TPU v7x, 256 devices: a whole 4x4x8 slice. The times are simulated.
256 devices in a mesh: walk: 32 (over z, x), chol: 8 (over y, core).
Axes of the slice: x: 4, y: 4, z: 8, core: 2. Of those that a mesh axis runs over, the one named last changes fastest.
Arguments:
- orbitals: bfloat16 [32, 400, 2048], P('walk', None, 'chol'), may hold values from -4 to 4
- intersection_inv: bfloat16 [32, 400, 400], P('walk'), may hold values from -0.18 to 0.18
- interp: bfloat16 [2048, 4096], P(None, 'chol'), may hold values from -0.079549513 to 0.079549513
- occ_interp: bfloat16 [400, 4096], P(None, 'chol'), may hold values from -0.18 to 0.18
- chol_factors: bfloat16 [4096, 8192], P('chol', 'walk'), may hold values from -2 to 2
- fields: float32 [32, 8192], P(None, 'walk'), may hold values from -4 to 4
Outputs:
- new_orbitals: bfloat16 [32, 400, 2048], P('walk', None, 'chol')
- force_bias: float32 [32, 8192], P(None, 'walk')
All inputs are finite; a program needn't handle non-finite values.
Results may differ from a plain program's by a relative error of at most 0.017.
Values may be sent and summed in bfloat16 or wider, within the bound.
No kernel may reach another device: no remote copies, remote signals or barrier semaphores. Data moves between devices by JAX's collectives and lax.ppermute only.
A program may use at most 64 MiB of HBM per device.

v0:
```python
import jax
import jax.numpy as jnp
from jax import lax
from jax.sharding import PartitionSpec as P

TERMS = 4


time_root = 2.2


def joined_along(blocks, dim):
    blocks = jnp.moveaxis(blocks, 0, dim)
    dims = blocks.shape
    return blocks.reshape(*dims[:dim], dims[dim] * dims[dim + 1], *dims[dim + 2 :])


def sent_to_all(value, axis):
    length = lax.axis_size(axis)
    return lax.all_to_all(
        jnp.broadcast_to(value[None], (length, *value.shape)), axis, 0, 0, tiled=True
    )


def collect(value, axis, dim):
    return joined_along(sent_to_all(value, axis), dim)


def of_everyone(value, axis):
    everything = sent_to_all(value, axis)
    return jnp.sum(everything, axis=0)


def cut_along(value, dim, length):
    dims = value.shape
    blocks = value.reshape(*dims[:dim], length, dims[dim] // length, *dims[dim + 1 :])
    return jnp.moveaxis(blocks, dim, 0)


def sum_at_owner(value, axis, dim):
    length = lax.axis_size(axis)
    blocks = lax.all_to_all(cut_along(value, dim, length), axis, 0, 0, tiled=True)
    return jnp.sum(blocks, axis=0)


def sent_and_summed(value, axis, dim):
    blocks = cut_along(value, dim, lax.axis_size(axis))
    arrived = lax.all_to_all(blocks, axis, split_axis=0, concat_axis=0, tiled=True)
    return arrived.astype(jnp.float32).sum(axis=0)


def on_device(orbitals, intersection_inv, interp, occ_interp, chol_factors, fields):
    piece = collect(orbitals, "chol", 2)
    green = jnp.einsum(
        "wij,wjm->wim", intersection_inv, piece, preferred_element_type=jnp.float32
    ).astype(jnp.bfloat16)
    projected = jnp.einsum("wim,mp->wip", green, interp, preferred_element_type=jnp.float32)
    applied = jnp.einsum("wim,mp->wip", piece, interp, preferred_element_type=jnp.float32)
    projected, current = (projected, applied)
    weights = jnp.sum(occ_interp.astype(jnp.float32)[None] * projected, axis=1)
    factors = chol_factors.astype(jnp.float32)
    all_weights = collect(weights, "walk", 0)
    partial_bias = jnp.dot(all_weights, factors, precision=lax.Precision.HIGHEST)
    force_bias = of_everyone(partial_bias, "chol")
    coeff = time_root * (fields - force_bias)
    field_part = jnp.dot(coeff, factors.T, precision=lax.Precision.HIGHEST)
    scales = sum_at_owner(field_part, "walk", 0)
    total = orbitals.astype(jnp.float32)
    for order in range(1, TERMS + 1):
        mixed = (current * scales[:, None, :] / order).astype(jnp.bfloat16)
        partial_value = jnp.einsum("wnp,mp->wnm", mixed, interp, preferred_element_type=jnp.float32)
        term_local = sent_and_summed(partial_value.astype(jnp.bfloat16), "chol", 2).astype(
            jnp.bfloat16
        )
        total = total + term_local.astype(jnp.float32)
        if order < TERMS:
            current = jnp.einsum(
                "wim,mp->wip",
                collect(term_local, "chol", 2),
                interp,
                preferred_element_type=jnp.float32,
            )
    return (total.astype(jnp.bfloat16), force_bias)


def solution(mesh):
    placed = (
        P("walk", None, "chol"),
        P("walk", None, None),
        P(None, "chol"),
        P(None, "chol"),
        P("chol", "walk"),
        P(None, "walk"),
    )
    return jax.shard_map(
        on_device,
        mesh=mesh,
        in_specs=placed,
        out_specs=(P("walk", None, "chol"), P(None, "walk")),
        check_vma=False,
    )
```

profile of v0, /device:TPU:1, one launch (start us, length us, event | category | flops | bytes accessed | tf_op | source)
XLA Modules:
  0.0 294.1 jit_solution(12566781795822847072)
XLA Ops:
  0.6 0.0 copy-start
  0.6 1.2 broadcast_in_dim.15
  1.8 27.3 %all_to_all.55 = bf16[8,1,400,256]{3,2,1,0:T(8,128)(2,1)S(1)} all-to-all(bf16[8,1,400,256]{3,2,1,0:T(8,128)(2,1)S(1)} %broadcast_in_dim.15), channel_id=1, replica_groups=mesh['walk'=32,'chol'=8] {'chol'}, dimensions={0} | all-to-all | bytes 3276800 | tf_op jit(solution)/shard_map/all_to_all | solution.py:20
  29.1 1.4 copy.27
  30.6 0.0 copy-done
  30.6 0.0 copy-done.5
  30.6 0.0 copy-done.6
  30.6 3.4 %fusion.7 = f32[512]{0:T(512)S(1)} fusion(bf16[2048,512]{1,0:T(8,128)(2,1)S(1)} %copy-done, bf16[400,2048]{1,0:T(8,128)(2,1)} %bitcast.98, bf16[400,512]{1,0:T(8,128)(2,1)S(1)} %copy-done.5, bf16[1,400,400]{2,1,0:T(8,128)(2,1)S(1)} %copy-done.6), kind=kOutput, calls=%fused_computation.21 | convolution fusion | flops 1495653888 | bytes 4467200 | tf_op jit(solution)/shard_map/wim,mp->wip/dot_general | solution.py:57
  33.9 0.0 copy-start.4
  34.0 19.7 %all_to_all.56 = f32[32,1,512]{2,1,0:T(1,128)S(1)} all-to-all(f32[32,1,512]{2,1,0:T(1,128)S(1)} %broadcast_in_dim.16), channel_id=1, replica_groups=mesh['walk'=32,'chol'=8] {'walk'}, dimensions={0} | all-to-all | bytes 131072 | tf_op jit(solution)/shard_map/all_to_all | solution.py:20
  53.6 0.0 copy-done.1
  53.6 0.2 fusion.18
  53.9 11.1 %all_to_all.57 = f32[8,32,256]{2,1,0:T(8,128)S(1)} all-to-all(f32[8,32,256]{2,1,0:T(8,128)S(1)} %broadcast_in_dim.17), channel_id=1, replica_groups=mesh['walk'=32,'chol'=8] {'chol'}, dimensions={0} | all-to-all | bytes 524288 | tf_op jit(solution)/shard_map/all_to_all | solution.py:20
  65.0 0.0 copy-start.3
  65.0 0.3 convolution_bitcast_fusion
  65.4 0.1 copy.18
  65.4 11.8 %all_to_all.58 = f32[32,1,512]{2,1,0:T(1,128)S(1)} all-to-all(f32[32,1,512]{2,1,0:T(1,128)S(1)} %copy.18), channel_id=1, replica_groups=mesh['walk'=32,'chol'=8] {'walk'}, dimensions={0} | all-to-all | bytes 131072 | tf_op jit(solution)/shard_map/all_to_all | solution.py:42
  77.3 0.1 reduce_sum.77
  77.3 4.5 %convolution_convert_fusion.3 = bf16[400,2048]{1,0:T(8,128)(2,1)} fusion(bf16[2048,512]{1,0:T(8,128)(2,1)S(1)} %copy-done, bf16[400,2048]{1,0:T(8,128)(2,1)} %bitcast.99, f32[512]{0:T(512)S(1)} %reduce_sum.77), kind=kOutput, calls=%fused_computation.3 | convolution fusion | flops 1678950400 | bytes 5376000 | tf_op jit(solution)/shard_map/wnp,mp->wnm/dot_general | solution.py:71
  81.8 1.9 copy.28
  83.8 0.3 copy.50
  84.1 27.0 %all_to_all.59 = bf16[8,1,400,256]{3,2,1,0:T(8,128)(2,1)} all-to-all(bf16[8,1,400,256]{3,2,1,0:T(8,128)(2,1)S(1)} %bitcast.88), channel_id=1, replica_groups=mesh['walk'=32,'chol'=8] {'chol'}, dimensions={0} | all-to-all | bytes 3276800 | tf_op jit(solution)/shard_map/all_to_all | solution.py:48
  111.1 1.7 reduce_sum.78
  112.8 0.1 broadcast_in_dim.18
  112.9 24.7 %all_to_all.60 = bf16[8,1,400,256]{3,2,1,0:T(8,128)(2,1)S(1)} all-to-all(bf16[8,1,400,256]{3,2,1,0:T(8,128)(2,1)S(1)} %broadcast_in_dim.18), channel_id=1, replica_groups=mesh['walk'=32,'chol'=8] {'chol'}, dimensions={0} | all-to-all | bytes 3276800 | tf_op jit(solution)/shard_map/all_to_all | solution.py:20
  137.6 1.4 copy.29
  139.0 4.5 %convolution_convert_fusion.2 = bf16[400,2048]{1,0:T(8,128)(2,1)} fusion(bf16[2048,512]{1,0:T(8,128)(2,1)S(1)} %copy-done, bf16[400,2048]{1,0:T(8,128)(2,1)} %bitcast.103, f32[512]{0:T(512)S(1)} %reduce_sum.77), kind=kOutput, calls=%fused_computation.2 | convolution fusion | flops 1679155200 | bytes 5376000 | tf_op jit(solution)/shard_map/wnp,mp->wnm/dot_general | solution.py:71
  143.5 1.9 copy.30
  145.4 0.3 copy.49
  145.8 25.4 %all_to_all.61 = bf16[8,1,400,256]{3,2,1,0:T(8,128)(2,1)} all-to-all(bf16[8,1,400,256]{3,2,1,0:T(8,128)(2,1)S(1)} %bitcast.91), channel_id=1, replica_groups=mesh['walk'=32,'chol'=8] {'chol'}, dimensions={0} | all-to-all | bytes 3276800 | tf_op jit(solution)/shard_map/all_to_all | solution.py:48
  171.2 1.7 reduce_sum.79
  172.9 0.1 broadcast_in_dim.19
  173.0 24.7 %all_to_all.62 = bf16[8,1,400,256]{3,2,1,0:T(8,128)(2,1)S(1)} all-to-all(bf16[8,1,400,256]{3,2,1,0:T(8,128)(2,1)S(1)} %broadcast_in_dim.19), channel_id=1, replica_groups=mesh['walk'=32,'chol'=8] {'chol'}, dimensions={0} | all-to-all | bytes 3276800 | tf_op jit(solution)/shard_map/all_to_all | solution.py:20
  197.7 1.4 copy.31
  199.1 4.5 %convolution_convert_fusion.1 = bf16[400,2048]{1,0:T(8,128)(2,1)} fusion(bf16[2048,512]{1,0:T(8,128)(2,1)S(1)} %copy-done, bf16[400,2048]{1,0:T(8,128)(2,1)} %bitcast.105, f32[512]{0:T(512)S(1)} %reduce_sum.77), kind=kOutput, calls=%fused_computation.1 | convolution fusion | flops 1679155200 | bytes 5376000 | tf_op jit(solution)/shard_map/wnp,mp->wnm/dot_general | solution.py:71
  203.6 1.9 copy.32
  205.6 0.3 copy.48
  205.9 25.4 %all_to_all.63 = bf16[8,1,400,256]{3,2,1,0:T(8,128)(2,1)} all-to-all(bf16[8,1,400,256]{3,2,1,0:T(8,128)(2,1)S(1)} %bitcast.94), channel_id=1, replica_groups=mesh['walk'=32,'chol'=8] {'chol'}, dimensions={0} | all-to-all | bytes 3276800 | tf_op jit(solution)/shard_map/all_to_all | solution.py:48
  231.3 1.7 reduce_sum.80
  233.0 0.1 broadcast_in_dim.20
  233.2 24.7 %all_to_all.64 = bf16[8,1,400,256]{3,2,1,0:T(8,128)(2,1)S(1)} all-to-all(bf16[8,1,400,256]{3,2,1,0:T(8,128)(2,1)S(1)} %broadcast_in_dim.20), channel_id=1, replica_groups=mesh['walk'=32,'chol'=8] {'chol'}, dimensions={0} | all-to-all | bytes 3276800 | tf_op jit(solution)/shard_map/all_to_all | solution.py:20
  257.9 1.4 copy.33
  259.3 4.5 %convolution_convert_fusion = bf16[400,2048]{1,0:T(8,128)(2,1)} fusion(bf16[2048,512]{1,0:T(8,128)(2,1)S(1)} %copy-done, bf16[400,2048]{1,0:T(8,128)(2,1)} %bitcast.100, f32[512]{0:T(512)S(1)} %reduce_sum.77), kind=kOutput, calls=%fused_computation | convolution fusion | flops 1679155200 | bytes 5376000 | tf_op jit(solution)/shard_map/wnp,mp->wnm/dot_general | solution.py:71
  263.8 1.9 copy.34
  265.7 0.3 copy.47
  266.0 25.4 %all_to_all.65 = bf16[8,1,400,256]{3,2,1,0:T(8,128)(2,1)} all-to-all(bf16[8,1,400,256]{3,2,1,0:T(8,128)(2,1)S(1)} %bitcast.97), channel_id=1, replica_groups=mesh['walk'=32,'chol'=8] {'chol'}, dimensions={0} | all-to-all | bytes 3276800 | tf_op jit(solution)/shard_map/all_to_all | solution.py:48
  291.5 1.7 reduce_sum.81
  293.2 0.8 fusion.8
  (10 shorter events, 0.1 us)
Async XLA Ops:
  0.6 29.9 %copy-start = (bf16[2048,512]{1,0:T(8,128)(2,1)S(1)}, bf16[2048,512]{1,0:T(8,128)(2,1)}, u32[]{:S(2)}) copy-start(bf16[2048,512]{1,0:T(8,128)(2,1)} %param.8) | copy-start | bytes 6291460
  29.1 1.4 copy-start.5
  29.1 1.4 copy-start.6
  30.6 23.1 %copy-start.1 = (bf16[512,256]{1,0:T(8,128)(2,1)S(1)}, bf16[512,256]{1,0:T(8,128)(2,1)}, u32[]{:S(2)}) copy-start(bf16[512,256]{1,0:T(8,128)(2,1)} %param.10) | copy-start | bytes 786436
  33.9 31.1 %copy-start.4 = (f32[32,256]{1,0:T(8,128)S(1)}, f32[32,256]{1,0:T(8,128)}, u32[]{:S(2)}) copy-start(f32[32,256]{1,0:T(8,128)} %param.11) | copy-start | bytes 98308
  65.0 16.8 %copy-start.3 = (f32[32,256]{1,0:T(8,128)}, f32[32,256]{1,0:T(8,128)S(1)}, u32[]{:S(2)}) copy-start(f32[32,256]{1,0:T(8,128)S(1)} %reduce_sum.76) | copy-start | bytes 98308
  291.5 1.7 copy-start.2
where the time goes:
time: 295 us; the launch traced here: 294 us
  blocking collectives  247 us (84%)
  matrix products  21.9 us (7%)
  local copies, waits for them, and re-layouts  16.3 us (6%)
  other arithmetic  7.76 us (3%)
    all_to_all x6, blocking collectives, sent_to_all(): lax.all_to_all(jnp.broadcast_to(value[None], (length, *value.shape)), axi...  132 us
    all_to_all x4, blocking collectives, sent_and_summed(): lax.all_to_all(blocks, axis, split_axis=0, concat_axis=0, tiled=True)  103 us
    dot_general x4, matrix products, on_device(): jnp.einsum('wnp,mp->wnm', mixed, interp, preferred_element_type=jnp.float32)  18 us
    unnamed x22, local copies, waits for them, and re-layouts  13.3 us
    all_to_all x1, blocking collectives, sum_at_owner(): lax.all_to_all(cut_along(value, dim, length), axis, 0, 0, tiled=True)  11.8 us
    reduce_sum x4, other arithmetic, sent_and_summed(): return arrived.astype(jnp.float32).sum(axis=0)  6.85 us

commit v1 on v0

v1 whole, which is shorter than its diff:
```python
import jax
import jax.numpy as jnp
from jax import lax
from jax.experimental import pallas as pl
from jax.experimental.pallas import tpu as pltpu
from jax.sharding import Mesh
from jax.sharding import PartitionSpec as P

TERMS = 4
time_root = 2.2

NZ, NX, NY, NC = 8, 4, 4, 2
ROWS = 400
SLAB = 104
PIECE = 56
TILES = (0, 6, 12, 18, 25, 31, 37, 43, 50)
f32 = jnp.float32
bf16 = jnp.bfloat16


def ring(n, k):
    return [(i, (i + k) % n) for i in range(n)]


PAIRS = [(i, (i + 1) % 8 if i % 2 else (i - 1) % 8) for i in range(8)]


def swap_core(value):
    return lax.ppermute(value, "core", ring(NC, 1))


def to_all(value, axis, length):
    return lax.all_to_all(
        jnp.broadcast_to(value[None], (length, *value.shape)), axis, 0, 0, tiled=True
    )


def one_term(term, scale_refs, interp_refs, out_ref):
    acc = None
    for scale, interp in zip(scale_refs, interp_refs):
        product = jnp.dot(term, interp[...], preferred_element_type=f32)
        mixed = (product * scale).astype(bf16)
        part = lax.dot_general(
            mixed, interp[...], (((1,), (1,)), ((), ())), preferred_element_type=f32
        )
        acc = part if acc is None else acc + part
    out_ref[...] = acc.astype(bf16)


def first_kernel(term_ref, scales_ref, a0, a1, a2, a3, out_ref):
    scales = [scales_ref[b : b + 1, :] for b in range(4)]
    one_term(term_ref[...], scales, (a0, a1, a2, a3), out_ref)


def next_kernel(mine_ref, other_ref, total_ref, scales_ref, a0, a1, a2, a3, out_ref, total_out):
    term = (mine_ref[...].astype(f32) + other_ref[...].astype(f32)).astype(bf16)
    total_out[...] = total_ref[...] + term.astype(f32)
    scales = [scales_ref[b : b + 1, :] for b in range(4)]
    one_term(term, scales, (a0, a1, a2, a3), out_ref)


def vmem(n):
    return [pl.BlockSpec(memory_space=pltpu.VMEM)] * n


def call_first(term, scales, halves):
    return pl.pallas_call(
        first_kernel,
        out_shape=jax.ShapeDtypeStruct((SLAB, 2048), bf16),
        in_specs=vmem(6),
        out_specs=vmem(1)[0],
        name="first_term",
    )(term, scales, *halves)


def call_next(mine, other, total, scales, halves):
    return pl.pallas_call(
        next_kernel,
        out_shape=(
            jax.ShapeDtypeStruct((SLAB, 2048), bf16),
            jax.ShapeDtypeStruct((SLAB, 2048), f32),
        ),
        in_specs=vmem(8),
        out_specs=tuple(vmem(2)),
        name="next_term",
    )(mine, other, total, scales, *halves)


def on_device(orbitals, intersection_inv, interp, occ_interp, chol_factors, fields):
    x = lax.axis_index("x")
    y = lax.axis_index("y")
    c = lax.axis_index("core")
    a_own = interp.reshape(4, 2, 256, 512).transpose(1, 0, 2, 3).reshape(2048, 512)
    a_par = swap_core(a_own)
    occ_par = swap_core(occ_interp)
    chol_par = swap_core(chol_factors)
    cols = to_all(orbitals[0], "y", NY)
    cols = jnp.moveaxis(cols, 0, 1).reshape(ROWS, 1024)
    part = lax.dynamic_slice(a_own, (x * 512, 0), (512, 512))
    part, _ = lax.optimization_barrier((part, cols))
    part = lax.ppermute(part, "y", ring(NY, 2))
    chol_far = lax.ppermute(jnp.concatenate([chol_factors, chol_par], 0), "y", ring(NY, 2))

    green = jnp.dot(intersection_inv[0], cols, preferred_element_type=f32).astype(bf16)
    weights = []
    for a, occ in ((a_own, occ_interp), (a_par, occ_par)):
        rows = lax.dynamic_slice(a, (c * 1024, 0), (1024, 512))
        projected = jnp.dot(green, rows, preferred_element_type=f32)
        weights.append(jnp.sum(occ.astype(f32) * projected, axis=0))
    weights = jnp.concatenate(weights)[None]
    all_weights = to_all(weights, ("z", "x"), NZ * NX).reshape(32, 1024)

    far_own = to_all(part, "x", NX).reshape(2048, 512)
    near = jnp.concatenate([chol_factors, chol_par], 0).astype(f32)
    partial_bias = jnp.dot(all_weights, near, precision=lax.Precision.HIGHEST)
    force_bias = jnp.sum(to_all(partial_bias, ("y", "core"), 8), axis=0)
    coeff = time_root * (fields - force_bias)
    half = jnp.concatenate([near, chol_far.astype(f32)], 0)
    field_part = jnp.dot(coeff, half.T, precision=lax.Precision.HIGHEST)
    arrived = lax.all_to_all(field_part.reshape(32, 4, 512), ("z", "x"), 0, 0, tiled=True)
    scales = jnp.sum(arrived, axis=0)
    far_par = swap_core(far_own)
    halves = (a_own, a_par, far_own, far_par)

    starts = jnp.array([8 * TILES[2 * e] for e in range(4)], jnp.int32)
    mine_at = jnp.where(c == 1, starts[y], starts[(y + 3) % 4])
    other_at = jnp.where(c == 1, starts[(y + 3) % 4], starts[y])
    own_cols = lax.dynamic_slice(cols, (mine_at, 0), (SLAB, 1024))
    par_cols = swap_core(lax.dynamic_slice(cols, (other_at, 0), (SLAB, 1024)))
    term = jnp.where(
        c == 0,
        jnp.concatenate([own_cols, par_cols], 1),
        jnp.concatenate([par_cols, own_cols], 1),
    )
    total = term.astype(f32)
    mine = call_first(term, scales, halves)
    for order in range(2, TERMS + 1):
        other = lax.ppermute(mine, ("y", "core"), PAIRS)
        mine, total = call_next(mine, other, total, scales / order, halves)
    keep_at = jnp.where(c == 1, 0, SLAB - PIECE)
    give_at = jnp.where(c == 1, SLAB - PIECE, 0)
    keep = lax.dynamic_slice(mine, (keep_at, 0), (PIECE, 2048))
    give = lax.dynamic_slice(mine, (give_at, 0), (PIECE, 2048))
    got = lax.ppermute(give, ("y", "core"), PAIRS)
    last = (keep.astype(f32) + got.astype(f32)).astype(bf16).astype(f32)
    total = lax.dynamic_slice(total, (keep_at, 0), (PIECE, 2048))
    rows = (total + last).astype(bf16)
    blocks = rows.reshape(PIECE, 2, 4, 256).transpose(2, 1, 0, 3).reshape(8, PIECE, 256)
    back = lax.all_to_all(blocks, ("y", "core"), 0, 0, tiled=True)
    out = [back[(i + 1) % 8, : 8 * (TILES[i + 1] - TILES[i])] for i in range(8)]
    return jnp.concatenate(out, 0)[None], force_bias


def solution(mesh):
    fine = Mesh(mesh.devices.reshape(NZ, NX, NY, NC), ("z", "x", "y", "core"))
    walk, chol = ("z", "x"), ("y", "core")
    return jax.shard_map(
        on_device,
        mesh=fine,
        in_specs=(
            P(walk, None, chol),
            P(walk, None, None),
            P(None, chol),
            P(None, chol),
            P(chol, walk),
            P(None, walk),
        ),
        out_specs=(P(walk, None, chol), P(None, walk)),
        check_vma=False,
    )
```

time: 295 us -> 211 us (0.72)
  blocking collectives: 247 us -> 14.1 us
  waiting for transfers between devices: 0 us -> 79.9 us
  starting transfers between devices: 0 us -> 49.7 us
  Pallas kernels: 0 us -> 35 us
  matrix products: 21.9 us -> 7.66 us
  other arithmetic: 7.76 us -> 3.66 us
    all_to_all x11 -> x1, blocking collectives: 247 us -> 14.1 us  [on_device(): back = lax.all_to_all(blocks, ('y', 'core'), 0, 0, tiled=True)]
    all_to_all x0 -> x5, waiting for transfers between devices: none -> 45.4 us  [the longest x4 38.5 us: to_all(): lax.all_to_all(jnp.broadcast_to(value[None], (length, *value.shape)), axi...]
    pallas_call x0 -> x4, Pallas kernels: none -> 35 us  [the longest x3 26.5 us: call_next(): pl.pallas_call(next_kernel, out_shape=(jax.ShapeDtypeStruct((SLAB, 2048),...]
    ppermute x0 -> x11, waiting for transfers between devices: none -> 34.5 us  [the longest x3 19.2 us: on_device(): other = lax.ppermute(mine, ('y', 'core'), PAIRS)]
    all_to_all x0 -> x5, starting transfers between devices: none -> 31.4 us  [the longest x4 24.8 us: to_all(): lax.all_to_all(jnp.broadcast_to(value[None], (length, *value.shape)), axi...]
    ppermute x0 -> x11, starting transfers between devices: none -> 18.2 us  [the longest x5 10.8 us: swap_core(): return lax.ppermute(value, 'core', ring(NC, 1))]
    dot_general x7 -> x5, matrix products: 21.9 us -> 7.66 us  [the longest x2 3.79 us: on_device(): projected = jnp.dot(green, rows, preferred_element_type=f32)]
    unnamed x22 -> x34, local copies, waits for them, and re-layouts: 13.3 us -> 3.99 us
  transfers between devices with their start and end apart: 0 -> 16, of which waited for: 0 -> 11; matrix products, arithmetic and copies ran while one was open for 0% -> 9% of each run, Pallas kernels for 0% -> 0%
where the time goes in v1:
time: 211 us; the launch traced here: 210 us
  waiting for transfers between devices  79.9 us (38%)
  starting transfers between devices  49.7 us (24%)
  Pallas kernels  35 us (17%)
  local copies, waits for them, and re-layouts  16.4 us (8%)
  blocking collectives  14.1 us (7%)
  matrix products  7.66 us (4%)
  other arithmetic  3.66 us (2%)
  between operations  3.52 us (2%)
    all_to_all x4, waiting for transfers between devices, to_all(): lax.all_to_all(jnp.broadcast_to(value[None], (length, *value.shape)), axi...  38.5 us
    pallas_call x3, Pallas kernels, call_next(): pl.pallas_call(next_kernel, out_shape=(jax.ShapeDtypeStruct((SLAB, 2048),...  26.5 us
    all_to_all x4, starting transfers between devices, to_all(): lax.all_to_all(jnp.broadcast_to(value[None], (length, *value.shape)), axi...  24.8 us
    ppermute x3, waiting for transfers between devices, on_device(): other = lax.ppermute(mine, ('y', 'core'), PAIRS)  19.2 us
    all_to_all x1, blocking collectives, on_device(): back = lax.all_to_all(blocks, ('y', 'core'), 0, 0, tiled=True)  14.1 us
    ppermute x5, starting transfers between devices, swap_core(): return lax.ppermute(value, 'core', ring(NC, 1))  10.8 us
    ppermute x1, waiting for transfers between devices, on_device(): part = lax.ppermute(part, 'y', ring(NY, 2))  9.59 us
    pallas_call x1, Pallas kernels, call_first(): pl.pallas_call(first_kernel, out_shape=jax.ShapeDtypeStruct((SLAB, 2048),...  8.47 us
  transfers between devices with their start and end apart: 16, of which 11 were waited for; matrix products, arithmetic and copies ran while one was open for 9% of the time, Pallas kernels for 0%

profile of v1, /device:TPU:1, one launch (start us, length us, event | category | flops | bytes accessed | tf_op | source)
XLA Modules:
  0.0 209.8 jit_solution(14162985977758231815)
XLA Ops:
  0.6 1.9 broadcast_in_dim.13
  2.6 5.0 %all-to-all-start = ((bf16[4,400,256]{2,1,0:T(8,128)(2,1)}), bf16[4,400,256]{2,1,0:T(8,128)(2,1)S(1)}, u32[]{:S(2)}, u32[]{:S(2)}) async-start(bf16[4,400,256]{2,1,0:T(8,128)(2,1)} %broadcast_in_dim.13), calls=%async_computation | async-start | bytes 1638400 | tf_op jit(solution)/shard_map/all_to_all | solution.py:33
  7.6 1.8 copy.15
  9.4 0.9 constant_dynamic-slice_fusion.1
  10.3 8.3 %all-to-all-done = bf16[4,400,256]{2,1,0:T(8,128)(2,1)S(1)} async-done(((bf16[4,400,256]{2,1,0:T(8,128)(2,1)}), bf16[4,400,256]{2,1,0:T(8,128)(2,1)S(1)}, u32[]{:S(2)}, u32[]{:S(2)}) %all-to-all-start) | async-done | bytes 819232 | tf_op jit(solution)/shard_map/all_to_all | solution.py:33
  18.7 1.1 copy.18
  20.0 2.8 %collective-permute-start.2 = (bf16[2048,512]{1,0:T(8,128)(2,1)S(1)}, bf16[2048,512]{1,0:T(8,128)(2,1)}, u32[]{:S(2)}, u32[]{:S(2)}) collective-permute-start(bf16[2048,512]{1,0:T(8,128)(2,1)S(1)} %bitcast.57), channel_id=1, source_target_pairs={{0,1},{1,0},{2,3},{3,2},{4,5},{5,4},{6,7},{7,6},{8,9},{9,8},{10,11... | collective-permute-start | bytes 6291464 | tf_op jit(solution)/shard_map/ppermute | solution.py:29
  22.8 9.6 %collective-permute-done.5 = bf16[512,512]{1,0:T(8,128)(2,1)S(1)} collective-permute-done((bf16[512,512]{1,0:T(8,128)(2,1)}, bf16[512,512]{1,0:T(8,128)(2,1)S(1)}, u32[]{:S(2)}, u32[]{:S(2)}) %collective-permute-start.5) | collective-permute-done | bytes 524320 | tf_op jit(solution)/shard_map/ppermute | solution.py:101
  32.4 1.6 broadcast_in_dim.31
  34.0 5.6 %all-to-all-start.4 = ((bf16[4,512,512]{2,1,0:T(8,128)(2,1)}), bf16[4,512,512]{2,1,0:T(8,128)(2,1)}, u32[]{:S(2)}, u32[]{:S(2)}) async-start(bf16[4,512,512]{2,1,0:T(8,128)(2,1)} %broadcast_in_dim.31), calls=%async_computation.4 | async-start | bytes 4194304 | tf_op jit(solution)/shard_map/all_to_all | solution.py:33
  39.6 2.9 %collective-permute-start.1 = (bf16[400,512]{1,0:T(8,128)(2,1)}, bf16[400,512]{1,0:T(8,128)(2,1)}, u32[]{:S(2)}, u32[]{:S(2)}) collective-permute-start(bf16[400,512]{1,0:T(8,128)(2,1)} %param.10), channel_id=1, source_target_pairs={{0,1},{1,0},{2,3},{3,2},{4,5},{5,4},{6,7},{7,6},{8,9},{9,8},{10,11... | collective-permute-start | bytes 1228808 | tf_op jit(solution)/shard_map/ppermute | solution.py:29
  42.5 1.6 convolution_convert_fusion
  44.1 19.4 %all-to-all-done.4 = bf16[4,512,512]{2,1,0:T(8,128)(2,1)} async-done(((bf16[4,512,512]{2,1,0:T(8,128)(2,1)}), bf16[4,512,512]{2,1,0:T(8,128)(2,1)}, u32[]{:S(2)}, u32[]{:S(2)}) %all-to-all-start.4) | async-done | bytes 2097184 | tf_op jit(solution)/shard_map/all_to_all | solution.py:33
  63.5 3.6 %collective-permute-start.6 = (bf16[2048,512]{1,0:T(8,128)(2,1)}, bf16[2048,512]{1,0:T(8,128)(2,1)}, u32[]{:S(2)}, u32[]{:S(2)}) collective-permute-start(bf16[2048,512]{1,0:T(8,128)(2,1)} %bitcast.9.a2), channel_id=1, source_target_pairs={{0,1},{1,0},{2,3},{3,2},{4,5},{5,4},{6,7},{7,6},{8,9},{9,8},{10,11... | collective-permute-start | bytes 6291464 | tf_op jit(solution)/shard_map/ppermute | solution.py:29
  67.1 1.8 fusion
  69.0 1.9 multiply_reduce_fusion
  71.7 9.4 %all-to-all-start.1 = ((f32[32,1,1024]{2,1,0:T(1,128)}), f32[32,1,1024]{2,1,0:T(1,128)S(1)}, u32[]{:S(2)}, u32[]{:S(2)}) async-start(f32[32,1,1024]{2,1,0:T(1,128)} %broadcast_in_dim.14), calls=%async_computation.1 | async-start | bytes 262144 | tf_op jit(solution)/shard_map/all_to_all | solution.py:33
  81.1 1.0 constant_dynamic-update-slice_fusion.1
  82.1 1.0 constant_dynamic-update-slice_fusion
  83.6 7.4 %all-to-all-done.1 = f32[32,1,1024]{2,1,0:T(1,128)S(1)} async-done(((f32[32,1,1024]{2,1,0:T(1,128)}), f32[32,1,1024]{2,1,0:T(1,128)S(1)}, u32[]{:S(2)}, u32[]{:S(2)}) %all-to-all-start.1) | async-done | bytes 131104 | tf_op jit(solution)/shard_map/all_to_all | solution.py:33
  91.3 0.7 broadcast_in_dim.30
  92.1 4.8 %all-to-all-start.2 = ((f32[8,32,256]{2,1,0:T(8,128)}), f32[8,32,256]{2,1,0:T(8,128)S(1)}, u32[]{:S(2)}, u32[]{:S(2)}) async-start(f32[8,32,256]{2,1,0:T(8,128)} %broadcast_in_dim.30), calls=%async_computation.2 | async-start | bytes 524288 | tf_op jit(solution)/shard_map/all_to_all | solution.py:33
  100.1 3.3 %all-to-all-done.2 = f32[8,32,256]{2,1,0:T(8,128)S(1)} async-done(((f32[8,32,256]{2,1,0:T(8,128)}), f32[8,32,256]{2,1,0:T(8,128)S(1)}, u32[]{:S(2)}, u32[]{:S(2)}) %all-to-all-start.2) | async-done | bytes 262176 | tf_op jit(solution)/shard_map/all_to_all | solution.py:33
  103.5 2.0 fusion.1
  105.4 0.9 reshape.37
  106.3 6.7 %all-to-all-start.3 = ((f32[32,4,512]{2,1,0:T(4,128)}), f32[32,4,512]{2,1,0:T(4,128)S(1)}, u32[]{:S(2)}, u32[]{:S(2)}) async-start(f32[32,4,512]{2,1,0:T(4,128)} %reshape.37), calls=%async_computation.3 | async-start | bytes 524288 | tf_op jit(solution)/shard_map/all_to_all | solution.py:120
  113.0 1.4 collective-permute-start
  114.4 1.1 collective-permute-done
  115.5 1.2 fusion.31
  116.7 6.9 %all-to-all-done.3 = f32[32,4,512]{2,1,0:T(4,128)S(1)} async-done(((f32[32,4,512]{2,1,0:T(4,128)}), f32[32,4,512]{2,1,0:T(4,128)S(1)}, u32[]{:S(2)}, u32[]{:S(2)}) %all-to-all-start.3) | async-done | bytes 262176 | tf_op jit(solution)/shard_map/all_to_all | solution.py:120
  124.3 8.5 %first_term.1.mine_ref = bf16[104,2048]{1,0:T(8,128)(2,1)} custom-call(bf16[104,2048]{1,0:T(8,128)(2,1)} %get-tuple-element.17.term_ref, f32[4,512]{1,0:T(4,128)} %reduce_sum.39.scales_ref, bf16[2048,512]{1,0:T(8,128)(2,1)} %bitcast.59, bf16[2048,512]{1,0:T(8,128)(2,1)} %collective-permute-done.2.a1, bf16[2048,512]{1,0:T(8,128)(2,1)} %bitcast.9.a2, ...), custom_call_target="tpu_custom_call" | custom-call | tf_op jit(solution)/shard_map/first_term/pallas_call | solution.py:67
  132.8 3.2 %collective-permute-start.7 = (bf16[104,2048]{1,0:T(8,128)(2,1)}, bf16[104,2048]{1,0:T(8,128)(2,1)S(1)}, u32[]{:S(2)}, u32[]{:S(2)}) collective-permute-start(bf16[104,2048]{1,0:T(8,128)(2,1)} %first_term.1.mine_ref), channel_id=1, source_target_pairs={{0,7},{1,2},{2,1},{3,4},{4,3},{5,6},{6,5},{7,0},{8,15},{9,10},{10,... | collective-permute-start | bytes 1277960 | tf_op jit(solution)/shard_map/ppermute | solution.py:138
  136.5 5.7 %collective-permute-done.7.other_ref = bf16[104,2048]{1,0:T(8,128)(2,1)S(1)} collective-permute-done((bf16[104,2048]{1,0:T(8,128)(2,1)}, bf16[104,2048]{1,0:T(8,128)(2,1)S(1)}, u32[]{:S(2)}, u32[]{:S(2)}) %collective-permute-start.7) | collective-permute-done | bytes 426016 | tf_op jit(solution)/shard_map/ppermute | solution.py:138
  142.2 0.7 copy-done.4
  143.0 8.8 %next_term.3 = (bf16[104,2048]{1,0:T(8,128)(2,1)}, f32[104,2048]{1,0:T(8,128)}) custom-call(bf16[104,2048]{1,0:T(8,128)(2,1)} %first_term.1.mine_ref, bf16[104,2048]{1,0:T(8,128)(2,1)} %copy-done.4, f32[104,2048]{1,0:T(8,128)} %get-tuple-element.16.total_ref, f32[4,512]{1,0:T(4,128)} %get-tuple-element.22.scales_ref, bf16[2048,512]{1,0:T(8,128)(2,1)} %bitcast.60, ...), custom_call_target="tpu_custom_call" | custom-call | tf_op jit(solution)/shard_map/next_term/pallas_call | solution.py:77
  151.8 1.5 collective-permute-start.8
  153.3 6.6 %collective-permute-done.8.other_ref = bf16[104,2048]{1,0:T(8,128)(2,1)S(1)} collective-permute-done((bf16[104,2048]{1,0:T(8,128)(2,1)}, bf16[104,2048]{1,0:T(8,128)(2,1)S(1)}, u32[]{:S(2)}, u32[]{:S(2)}) %collective-permute-start.8) | collective-permute-done | bytes 426016 | tf_op jit(solution)/shard_map/ppermute | solution.py:138
  159.9 0.7 copy-done.5
  160.6 8.8 %next_term.4 = (bf16[104,2048]{1,0:T(8,128)(2,1)}, f32[104,2048]{1,0:T(8,128)}) custom-call(bf16[104,2048]{1,0:T(8,128)(2,1)} %get-tuple-element.10.mine_ref, bf16[104,2048]{1,0:T(8,128)(2,1)} %copy-done.5, f32[104,2048]{1,0:T(8,128)} %get-tuple-element.11.total_ref, f32[4,512]{1,0:T(4,128)} %get-tuple-element.21.scales_ref, bf16[2048,512]{1,0:T(8,128)(2,1)} %bitcast.61, ...), custom_call_target="tpu_custom_call" | custom-call | tf_op jit(solution)/shard_map/next_term/pallas_call | solution.py:77
  169.5 1.2 collective-permute-start.9
  170.6 6.9 %collective-permute-done.9.other_ref = bf16[104,2048]{1,0:T(8,128)(2,1)S(1)} collective-permute-done((bf16[104,2048]{1,0:T(8,128)(2,1)}, bf16[104,2048]{1,0:T(8,128)(2,1)S(1)}, u32[]{:S(2)}, u32[]{:S(2)}) %collective-permute-start.9) | collective-permute-done | bytes 426016 | tf_op jit(solution)/shard_map/ppermute | solution.py:138
  177.5 0.8 copy-done.3
  178.3 8.8 %next_term.5 = (bf16[104,2048]{1,0:T(8,128)(2,1)}, f32[104,2048]{1,0:T(8,128)}) custom-call(bf16[104,2048]{1,0:T(8,128)(2,1)} %get-tuple-element.12.mine_ref, bf16[104,2048]{1,0:T(8,128)(2,1)} %copy-done.3, f32[104,2048]{1,0:T(8,128)} %get-tuple-element.13.total_ref, f32[4,512]{1,0:T(4,128)} %get-tuple-element.20.scales_ref, bf16[2048,512]{1,0:T(8,128)(2,1)} %bitcast.62, ...), custom_call_target="tpu_custom_call" | custom-call | tf_op jit(solution)/shard_map/next_term/pallas_call | solution.py:77
  187.1 1.0 constant_dynamic-slice_fusion
  188.1 0.9 collective-permute-start.10
  189.0 4.6 %collective-permute-done.10 = bf16[56,2048]{1,0:T(8,128)(2,1)S(1)} collective-permute-done((bf16[56,2048]{1,0:T(8,128)(2,1)S(1)}, bf16[56,2048]{1,0:T(8,128)(2,1)S(1)}, u32[]{:S(2)}, u32[]{:S(2)}) %collective-permute-start.10) | collective-permute-done | bytes 229408 | tf_op jit(solution)/shard_map/ppermute | solution.py:144
  193.6 1.1 add_convert_fusion
  195.0 14.1 %all_to_all.30 = bf16[8,56,256]{2,1,0:T(8,128)(2,1)S(1)} all-to-all(bf16[8,56,256]{2,1,0:T(8,128)(2,1)S(1)} %bitcast.68), channel_id=1, replica_groups=mesh['z'=8,'x'=4,'y'=4,'core'=2] {'y','core'}, dimensions={0} | all-to-all | bytes 458752 | tf_op jit(solution)/shard_map/all_to_all | solution.py:149
  (49 shorter events, 4.7 us)
Async XLA Ops:
  0.6 41.9 %copy-start = (bf16[1,400,400]{2,1,0:T(8,128)(2,1)S(1)}, bf16[1,400,400]{2,1,0:T(8,128)(2,1)}, u32[]{:S(2)}) copy-start(bf16[1,400,400]{2,1,0:T(8,128)(2,1)} %param.8) | copy-start | bytes 960004
  2.6 16.1 %all-to-all-start = ((bf16[4,400,256]{2,1,0:T(8,128)(2,1)}), bf16[4,400,256]{2,1,0:T(8,128)(2,1)S(1)}, u32[]{:S(2)}, u32[]{:S(2)}) async-start(bf16[4,400,256]{2,1,0:T(8,128)(2,1)} %broadcast_in_dim.13), calls=%async_computation | async-start | bytes 1638400 | tf_op jit(solution)/shard_map/all_to_all | solution.py:33
  9.4 57.7 %copy-start.1 = (bf16[4,2,256,512]{3,2,0,1:T(8,128)(2,1)}, bf16[4,2,256,512]{3,2,0,1:T(8,128)(2,1)S(1)}, u32[]{:S(2)}) copy-start(bf16[4,2,256,512]{3,2,0,1:T(8,128)(2,1)S(1)} %copy.15) | copy-start | bytes 6291460
  19.7 12.7 %collective-permute-start.5 = (bf16[512,512]{1,0:T(8,128)(2,1)}, bf16[512,512]{1,0:T(8,128)(2,1)S(1)}, u32[]{:S(2)}, u32[]{:S(2)}) collective-permute-start(bf16[512,512]{1,0:T(8,128)(2,1)} %constant_dynamic-slice_fusion.1), channel_id=1, source_target_pairs={{0,4},{2,6},{4,0},{6,2},{1,5},{3,7},{5,1},{7,3},{8,12},{10,14},{12... | collective-permute-start | bytes 1572872 | tf_op jit(solution)/shard_map/ppermute | solution.py:101
  20.0 49.0 %collective-permute-start.2 = (bf16[2048,512]{1,0:T(8,128)(2,1)S(1)}, bf16[2048,512]{1,0:T(8,128)(2,1)}, u32[]{:S(2)}, u32[]{:S(2)}) collective-permute-start(bf16[2048,512]{1,0:T(8,128)(2,1)S(1)} %bitcast.57), channel_id=1, source_target_pairs={{0,1},{1,0},{2,3},{3,2},{4,5},{5,4},{6,7},{7,6},{8,9},{9,8},{10,11... | collective-permute-start | bytes 6291464 | tf_op jit(solution)/shard_map/ppermute | solution.py:29
  34.0 8.5 %copy-start.2 = (bf16[4,50,8,256]{3,2,0,1:T(8,128)(2,1)S(1)}, bf16[4,50,8,256]{3,2,0,1:T(8,128)(2,1)}, u32[]{:S(2)}) copy-start(bf16[4,50,8,256]{3,2,0,1:T(8,128)(2,1)} %copy.18) | copy-start | bytes 2457604
  34.0 29.5 %all-to-all-start.4 = ((bf16[4,512,512]{2,1,0:T(8,128)(2,1)}), bf16[4,512,512]{2,1,0:T(8,128)(2,1)}, u32[]{:S(2)}, u32[]{:S(2)}) async-start(bf16[4,512,512]{2,1,0:T(8,128)(2,1)} %broadcast_in_dim.31), calls=%async_computation.4 | async-start | bytes 4194304 | tf_op jit(solution)/shard_map/all_to_all | solution.py:33
  39.6 29.4 %collective-permute-start.1 = (bf16[400,512]{1,0:T(8,128)(2,1)}, bf16[400,512]{1,0:T(8,128)(2,1)}, u32[]{:S(2)}, u32[]{:S(2)}) collective-permute-start(bf16[400,512]{1,0:T(8,128)(2,1)} %param.10), channel_id=1, source_target_pairs={{0,1},{1,0},{2,3},{3,2},{4,5},{5,4},{6,7},{7,6},{8,9},{9,8},{10,11... | collective-permute-start | bytes 1228808 | tf_op jit(solution)/shard_map/ppermute | solution.py:29
  42.5 39.6 %collective-permute-start.3 = (bf16[512,256]{1,0:T(8,128)(2,1)}, bf16[512,256]{1,0:T(8,128)(2,1)}, u32[]{:S(2)}, u32[]{:S(2)}) collective-permute-start(bf16[512,256]{1,0:T(8,128)(2,1)} %param.11), channel_id=1, source_target_pairs={{0,1},{1,0},{2,3},{3,2},{4,5},{5,4},{6,7},{7,6},{8,9},{9,8},{10,11... | collective-permute-start | bytes 786440 | tf_op jit(solution)/shard_map/ppermute | solution.py:29
  63.5 5.5 %copy-start.12 = (bf16[400,1024]{1,0:T(8,128)(2,1)S(1)}, bf16[400,1024]{1,0:T(8,128)(2,1)}, u32[]{:S(2)}) copy-start(bf16[400,1024]{1,0:T(8,128)(2,1)} %convolution_convert_fusion) | copy-start | bytes 2457604
  63.5 60.8 %collective-permute-start.6 = (bf16[2048,512]{1,0:T(8,128)(2,1)}, bf16[2048,512]{1,0:T(8,128)(2,1)}, u32[]{:S(2)}, u32[]{:S(2)}) collective-permute-start(bf16[2048,512]{1,0:T(8,128)(2,1)} %bitcast.9.a2), channel_id=1, source_target_pairs={{0,1},{1,0},{2,3},{3,2},{4,5},{5,4},{6,7},{7,6},{8,9},{9,8},{10,11... | collective-permute-start | bytes 6291464 | tf_op jit(solution)/shard_map/ppermute | solution.py:29
  71.0 26.0 %copy-start.10 = (s32[4]{0:T(128)S(1)}, s32[4]{0:T(128)}, u32[]{:S(2)}) copy-start(s32[4]{0:T(128)} %constant.58.clone) | copy-start | bytes 52
  71.0 32.5 %copy-start.6 = (bf16[512,256]{1,0:T(8,128)(2,1)S(1)}, bf16[512,256]{1,0:T(8,128)(2,1)}, u32[]{:S(2)}) copy-start(bf16[512,256]{1,0:T(8,128)(2,1)} %param.11) | copy-start | bytes 786436
  71.0 32.5 %copy-start.11 = (f32[32,256]{1,0:T(8,128)S(1)}, f32[32,256]{1,0:T(8,128)}, u32[]{:S(2)}) copy-start(f32[32,256]{1,0:T(8,128)} %param.12) | copy-start | bytes 98308
  71.7 19.3 %all-to-all-start.1 = ((f32[32,1,1024]{2,1,0:T(1,128)}), f32[32,1,1024]{2,1,0:T(1,128)S(1)}, u32[]{:S(2)}, u32[]{:S(2)}) async-start(f32[32,1,1024]{2,1,0:T(1,128)} %broadcast_in_dim.14), calls=%async_computation.1 | async-start | bytes 262144 | tf_op jit(solution)/shard_map/all_to_all | solution.py:33
  83.1 20.3 %collective-permute-start.4 = (bf16[1024,256]{1,0:T(8,128)(2,1)S(1)}, bf16[1024,256]{1,0:T(8,128)(2,1)S(1)}, u32[]{:S(2)}, u32[]{:S(2)}) collective-permute-start(bf16[1024,256]{1,0:T(8,128)(2,1)S(1)} %constant_dynamic-update-slice_fusion), channel_id=1, source_target_pairs={{0,4},{2,6},{4,0},{6,2},{1,5},{3,7},{5,1},{7,3},{8,12},{10,14},{12... | collective-permute-start | bytes 1572872 | tf_op jit(solution)/shard_map/ppermute | solution.py:102
  92.1 11.3 %all-to-all-start.2 = ((f32[8,32,256]{2,1,0:T(8,128)}), f32[8,32,256]{2,1,0:T(8,128)S(1)}, u32[]{:S(2)}, u32[]{:S(2)}) async-start(f32[8,32,256]{2,1,0:T(8,128)} %broadcast_in_dim.30), calls=%async_computation.2 | async-start | bytes 524288 | tf_op jit(solution)/shard_map/all_to_all | solution.py:33
  103.4 9.6 %copy-start.8 = (f32[32,256]{1,0:T(8,128)}, f32[32,256]{1,0:T(8,128)S(1)}, u32[]{:S(2)}) copy-start(f32[32,256]{1,0:T(8,128)S(1)} %reduce_sum.38) | copy-start | bytes 98308
  106.3 17.3 %all-to-all-start.3 = ((f32[32,4,512]{2,1,0:T(4,128)}), f32[32,4,512]{2,1,0:T(4,128)S(1)}, u32[]{:S(2)}, u32[]{:S(2)}) async-start(f32[32,4,512]{2,1,0:T(4,128)} %reshape.37), calls=%async_computation.3 | async-start | bytes 524288 | tf_op jit(solution)/shard_map/all_to_all | solution.py:120
  113.0 2.5 %collective-permute-start = (bf16[104,1024]{1,0:T(8,128)(2,1)S(1)}, bf16[104,1024]{1,0:T(8,128)(2,1)S(1)}, u32[]{:S(2)}, u32[]{:S(2)}) collective-permute-start(bf16[104,1024]{1,0:T(8,128)(2,1)S(1)} %get-tuple-element.18), channel_id=1, source_target_pairs={{0,1},{1,0},{2,3},{3,2},{4,5},{5,4},{6,7},{7,6},{8,9},{9,8},{10,11... | collective-permute-start | bytes 638984 | tf_op jit(solution)/shard_map/ppermute | solution.py:29
  124.3 11.6 %copy-start.7 = (f32[4,512]{1,0:T(4,128)S(1)}, f32[4,512]{1,0:T(4,128)}, u32[]{:S(2)}) copy-start(f32[4,512]{1,0:T(4,128)} %reduce_sum.39.scales_ref) | copy-start | bytes 24580
  132.8 9.5 %collective-permute-start.7 = (bf16[104,2048]{1,0:T(8,128)(2,1)}, bf16[104,2048]{1,0:T(8,128)(2,1)S(1)}, u32[]{:S(2)}, u32[]{:S(2)}) collective-permute-start(bf16[104,2048]{1,0:T(8,128)(2,1)} %first_term.1.mine_ref), channel_id=1, source_target_pairs={{0,7},{1,2},{2,1},{3,4},{4,3},{5,6},{6,5},{7,0},{8,15},{9,10},{10,... | collective-permute-start | bytes 1277960 | tf_op jit(solution)/shard_map/ppermute | solution.py:138
  142.2 0.8 copy-start.4
  151.8 8.1 %collective-permute-start.8 = (bf16[104,2048]{1,0:T(8,128)(2,1)}, bf16[104,2048]{1,0:T(8,128)(2,1)S(1)}, u32[]{:S(2)}, u32[]{:S(2)}) collective-permute-start(bf16[104,2048]{1,0:T(8,128)(2,1)} %get-tuple-element.10.mine_ref), channel_id=1, source_target_pairs={{0,7},{1,2},{2,1},{3,4},{4,3},{5,6},{6,5},{7,0},{8,15},{9,10},{10,... | collective-permute-start | bytes 1277960 | tf_op jit(solution)/shard_map/ppermute | solution.py:138
  159.9 0.8 copy-start.5
  169.5 8.1 %collective-permute-start.9 = (bf16[104,2048]{1,0:T(8,128)(2,1)}, bf16[104,2048]{1,0:T(8,128)(2,1)S(1)}, u32[]{:S(2)}, u32[]{:S(2)}) collective-permute-start(bf16[104,2048]{1,0:T(8,128)(2,1)} %get-tuple-element.12.mine_ref), channel_id=1, source_target_pairs={{0,7},{1,2},{2,1},{3,4},{4,3},{5,6},{6,5},{7,0},{8,15},{9,10},{10,... | collective-permute-start | bytes 1277960 | tf_op jit(solution)/shard_map/ppermute | solution.py:138
  177.5 0.8 copy-start.3
  188.1 5.5 %collective-permute-start.10 = (bf16[56,2048]{1,0:T(8,128)(2,1)S(1)}, bf16[56,2048]{1,0:T(8,128)(2,1)S(1)}, u32[]{:S(2)}, u32[]{:S(2)}) collective-permute-start(bf16[56,2048]{1,0:T(8,128)(2,1)S(1)} %constant_dynamic-slice_fusion), channel_id=1, source_target_pairs={{0,7},{1,2},{2,1},{3,4},{4,3},{5,6},{6,5},{7,0},{8,15},{9,10},{10,... | collective-permute-start | bytes 688136 | tf_op jit(solution)/shard_map/ppermute | solution.py:144
  209.2 0.7 copy-start.9

commit v2 on v1

v2 whole, which is shorter than its diff:
```python
import jax
import jax.numpy as jnp
from jax import lax
from jax.experimental import pallas as pl
from jax.experimental.pallas import tpu as pltpu
from jax.sharding import Mesh
from jax.sharding import PartitionSpec as P


TERMS = 4
time_root = 2.2

NZ, NX, NY, NC = 8, 4, 4, 2
ROWS = 400
SLAB = 104
PIECE = 56
TILES = (0, 6, 12, 18, 25, 31, 37, 43, 50)
VMEM_LIMIT = 12 * 2**20
f32 = jnp.float32
bf16 = jnp.bfloat16


def ring(n, k):
    return [(i, (i + k) % n) for i in range(n)]


PAIRS = [(i, (i + 1) % 8 if i % 2 else (i - 1) % 8) for i in range(8)]


def swap_core(value):
    return lax.ppermute(value, "core", ring(NC, 1))


def to_all(value, axis, length):
    return lax.all_to_all(
        jnp.broadcast_to(value[None], (length, *value.shape)), axis, 0, 0, tiled=True
    )


def spec(space):
    return pl.BlockSpec(memory_space=space)


PARAMS = pltpu.CompilerParams(vmem_limit_bytes=VMEM_LIMIT)


def edge_of(y, c):
    return jnp.where(c == 1, y, (y + 3) % 4)


def head_kernel(inv, o0, o1, o2, o3, a_own, a_par, occ_own, occ_par, weights_ref):
    y = lax.axis_index("y")
    c = lax.axis_index("core")
    sums = [None, None]
    for j, o in enumerate((o0, o1, o2, o3)):
        green = jnp.dot(inv[...], o[...], preferred_element_type=f32).astype(bf16)
        at = pl.multiple_of(((y + j) % 4) * 512 + c * 256, 256)
        for k, a in enumerate((a_own, a_par)):
            part = jnp.dot(green, a[pl.ds(at, 256), :], preferred_element_type=f32)
            sums[k] = part if sums[k] is None else sums[k] + part
    for k, occ in enumerate((occ_own, occ_par)):
        weights = jnp.sum(occ[...].astype(f32) * sums[k], axis=0, keepdims=True)
        weights_ref[:, :, 512 * k : 512 * k + 512] = jnp.broadcast_to(weights, (32, 1, 512))


def call_head(inv, cols, a_own, a_par, occ_own, occ_par):
    return pl.pallas_call(
        head_kernel,
        out_shape=jax.ShapeDtypeStruct((32, 1, 1024), f32),
        in_specs=[spec(pltpu.VMEM)] * 9,
        out_specs=spec(pltpu.VMEM),
        compiler_params=pltpu.CompilerParams(vmem_limit_bytes=24 * 2**20),
        name="head",
    )(inv, *cols, a_own, a_par, occ_own, occ_par)


def slab_kernel(o0, o1, o2, o3, mine_ref, other_ref, sems):
    y = lax.axis_index("y")
    c = lax.axis_index("core")
    copies = []
    for k, out in enumerate((mine_ref, other_ref)):
        edge = edge_of(y, c if k == 0 else 1 - c)
        row = edge * 96 + jnp.where(edge >= 2, 8, 0)
        for j, o in enumerate((o0, o1, o2, o3)):
            copy = pltpu.make_async_copy(
                o.at[pl.ds(pl.multiple_of(row, 8), SLAB), :],
                out.at[:, pl.ds(pl.multiple_of(((y + j) % 4) * 256, 256), 256)],
                sems.at[4 * k + j],
            )
            copy.start()
            copies.append(copy)
    for copy in copies:
        copy.wait()


def call_slabs(cols):
    return pl.pallas_call(
        slab_kernel,
        out_shape=(jax.ShapeDtypeStruct((SLAB, 1024), bf16),) * 2,
        in_specs=[spec(pl.ANY)] * 4,
        out_specs=(spec(pl.ANY),) * 2,
        scratch_shapes=[pltpu.SemaphoreType.DMA((8,))],
        compiler_params=PARAMS,
        name="slabs",
    )(*cols)


def join_kernel(own, par, term_ref):
    c = lax.axis_index("core")

    def put(first, second):
        for y in range(4):
            cols = slice(256 * y, 256 * y + 256)
            term_ref[:, 512 * y : 512 * y + 256] = first[:, cols]
            term_ref[:, 512 * y + 256 : 512 * y + 512] = second[:, cols]

    pl.when(c == 0)(lambda: put(own, par))
    pl.when(c == 1)(lambda: put(par, own))


def call_join(own, par):
    return pl.pallas_call(
        join_kernel,
        out_shape=jax.ShapeDtypeStruct((SLAB, 2048), bf16),
        in_specs=[spec(pltpu.VMEM)] * 2,
        out_specs=spec(pltpu.VMEM),
        compiler_params=PARAMS,
        name="join",
    )(own, par)


def load_kernel(a0, a1, f0, f1, out_ref, sems):
    x = lax.axis_index("x")
    copies = [pltpu.make_async_copy(a, out_ref.at[b], sems.at[b]) for b, a in enumerate((a0, a1))]
    for b, f in enumerate((f0, f1)):
        for j in range(NX):
            at = pl.multiple_of(((x + j) % NX) * 512, 512)
            copies.append(
                pltpu.make_async_copy(
                    f.at[pl.ds(512 * j, 512), :],
                    out_ref.at[2 + b, pl.ds(at, 512), :],
                    sems.at[2 + NX * b + j],
                )
            )
    for copy in copies:
        copy.start()
    for copy in copies:
        copy.wait()


def call_load(halves):
    out = pl.pallas_call(
        load_kernel,
        out_shape=pltpu.VMEM((4, 2048, 512), bf16),
        in_specs=[spec(pl.ANY)] * 4,
        out_specs=spec(pltpu.VMEM),
        scratch_shapes=[pltpu.SemaphoreType.DMA((2 + 2 * NX,))],
        compiler_params=PARAMS,
        name="load_halves",
    )(*halves)
    return pltpu.with_memory_space_constraint(out, pltpu.VMEM)


def one_term(term, scales_ref, order, interp_ref):
    acc = None
    for b in range(4):
        interp = interp_ref[b]
        product = jnp.dot(term, interp, preferred_element_type=f32)
        mixed = (product * (scales_ref[b : b + 1, :] / order)).astype(bf16)
        part = lax.dot_general(
            mixed, interp, (((1,), (1,)), ((), ())), preferred_element_type=f32
        )
        acc = part if acc is None else acc + part
    return acc


def first_kernel(term_ref, scales_ref, interp_ref, out_ref):
    out_ref[...] = one_term(term_ref[...], scales_ref, 1, interp_ref).astype(bf16)


def next_kernel(order, mine_ref, other_ref, total_ref, scales_ref, interp_ref, out_ref, total_out):
    term = (mine_ref[...].astype(f32) + other_ref[...].astype(f32)).astype(bf16)
    total_out[...] = total_ref[...].astype(f32) + term.astype(f32)
    out_ref[...] = one_term(term, scales_ref, order, interp_ref).astype(bf16)


def last_kernel(mine_ref, other_ref, total_ref, scales_ref, interp_ref, out_ref):
    c = lax.axis_index("core")
    term = (mine_ref[...].astype(f32) + other_ref[...].astype(f32)).astype(bf16)
    total = total_ref[...] + term.astype(f32)
    acc = one_term(term, scales_ref, TERMS, interp_ref)
    low, high = slice(0, PIECE), slice(SLAB - PIECE, SLAB)

    def put(keep, give):
        kept = (acc[keep] + total[keep]).astype(bf16)
        given = acc[give].astype(bf16)
        for b in range(8):
            out_ref[b, :PIECE, :] = kept[:, 256 * b : 256 * b + 256]
            out_ref[b, PIECE:, :] = given[:, 256 * b : 256 * b + 256]

    pl.when(c == 1)(lambda: put(low, high))
    pl.when(c == 0)(lambda: put(high, low))


def call_term(kernel, out_shape, *args):
    many = isinstance(out_shape, tuple)
    return pl.pallas_call(
        kernel,
        out_shape=out_shape,
        in_specs=[spec(pltpu.VMEM)] * len(args),
        out_specs=(spec(pltpu.VMEM),) * len(out_shape) if many else spec(pltpu.VMEM),
        compiler_params=PARAMS,
        name="term",
    )(*args)


def end_kernel(back_ref, out_ref):
    for i in range(8):
        start = 8 * TILES[i]
        n = 8 * (TILES[i + 1] - TILES[i])
        owner, partner = (i + 1) % 8, (i + 2) % 8 if i % 2 == 0 else i
        kept = back_ref[owner, :n, :].astype(f32)
        given = back_ref[partner, PIECE : PIECE + n, :].astype(f32)
        out_ref[0, start : start + n, :] = (kept + given).astype(bf16)


def call_end(back):
    return pl.pallas_call(
        end_kernel,
        out_shape=jax.ShapeDtypeStruct((1, ROWS, 256), bf16),
        in_specs=[spec(pltpu.VMEM)],
        out_specs=spec(pltpu.VMEM),
        compiler_params=PARAMS,
        name="end",
    )(back)


def on_device(orbitals, intersection_inv, interp, occ_interp, chol_factors, fields):
    x = lax.axis_index("x")
    cols = [orbitals[0]]
    for j in (1, 2, 3):
        cols.append(lax.ppermute(orbitals[0], "y", ring(NY, -j)))
    a_par = swap_core(interp)
    occ_par = swap_core(occ_interp)
    chol_par = swap_core(chol_factors)
    near = jnp.concatenate([chol_factors, chol_par], 0)
    part = lax.dynamic_slice(interp, (x * 512, 0), (512, 512))
    part = lax.ppermute(part, "y", ring(NY, 2))
    chol_far = lax.ppermute(near, "y", ring(NY, 2))

    weights = call_head(intersection_inv[0], cols, interp, a_par, occ_interp, occ_par)
    mine, other = call_slabs(cols)
    term = call_join(mine, swap_core(other))
    all_weights = lax.all_to_all(weights, ("z", "x"), 0, 0, tiled=True).reshape(32, 1024)

    parts = [part]
    for j in (1, 2, 3):
        parts.append(lax.ppermute(part, "x", ring(NX, -j)))
    far_own = jnp.concatenate(parts, 0)
    partial_bias = jnp.dot(all_weights, near.astype(f32), precision=lax.Precision.HIGHEST)
    force_bias = jnp.sum(to_all(partial_bias, ("y", "core"), 8), axis=0)
    coeff = time_root * (fields - force_bias)
    half = jnp.concatenate([near, chol_far], 0).astype(f32)
    field_part = jnp.dot(coeff, half.T, precision=lax.Precision.HIGHEST)
    arrived = lax.all_to_all(
        field_part.astype(bf16).reshape(32, 4, 512), ("z", "x"), 0, 0, tiled=True
    )
    scales = jnp.sum(arrived.astype(f32), axis=0)
    far_par = swap_core(far_own)
    halves = call_load((interp, a_par, far_own, far_par))

    part_shape = jax.ShapeDtypeStruct((SLAB, 2048), bf16)
    total_shape = jax.ShapeDtypeStruct((SLAB, 2048), f32)
    total = term
    mine = call_term(first_kernel, part_shape, term, scales, halves)
    for order in range(2, TERMS):
        other = lax.ppermute(mine, ("y", "core"), PAIRS)
        mine, total = call_term(
            lambda *refs, order=order: next_kernel(order, *refs),
            (part_shape, total_shape),
            *(mine, other, total, scales, halves),
        )
    other = lax.ppermute(mine, ("y", "core"), PAIRS)
    blocks = call_term(
        last_kernel,
        jax.ShapeDtypeStruct((8, 2 * PIECE, 256), bf16),
        *(mine, other, total, scales, halves),
    )
    back = lax.all_to_all(blocks, ("y", "core"), 0, 0, tiled=True)
    return call_end(back), force_bias


def solution(mesh):
    fine = Mesh(mesh.devices.reshape(NZ, NX, NY, NC), ("z", "x", "y", "core"))
    walk, chol = ("z", "x"), ("y", "core")
    return jax.shard_map(
        on_device,
        mesh=fine,
        in_specs=(
            P(walk, None, chol),
            P(walk, None, None),
            P(None, chol),
            P(None, chol),
            P(chol, walk),
            P(None, walk),
        ),
        out_specs=(P(walk, None, chol), P(None, walk)),
        check_vma=False,
    )
```

time: 211 us -> 185 us (0.88)
  starting transfers between devices: 49.7 us -> 34.5 us
  blocking collectives: 14.1 us -> 29.1 us
  Pallas kernels: 35 us -> 22.4 us
  local copies, waits for them, and re-layouts: 16.4 us -> 10 us
  matrix products: 7.66 us -> 3.44 us
  waiting for transfers between devices: 79.9 us -> 82.9 us
  between operations: 3.52 us -> 0.86 us
  other arithmetic: 3.66 us -> 1.05 us
    ppermute x2 -> x7, waiting for transfers between devices: 4.59 us -> 38.1 us  [the longest x3 23 us: on_device(): parts.append(lax.ppermute(part, 'x', ring(NX, -j)))]
    all_to_all x5 -> x2, waiting for transfers between devices: 45.4 us -> 13.6 us  [the longest x1 7.12 us: on_device(): lax.all_to_all(weights, ('z', 'x'), 0, 0, tiled=True).reshape(32, 1024)]
    all_to_all x5 -> x2, starting transfers between devices: 31.4 us -> 15.8 us  [the longest x1 9.94 us: on_device(): lax.all_to_all(weights, ('z', 'x'), 0, 0, tiled=True).reshape(32, 1024)]
    pallas_call x4 -> x9, Pallas kernels: 35 us -> 22.4 us  [the longest x4 16.4 us: call_term(): pl.pallas_call(kernel, out_shape=out_shape, in_specs=[spec(pltpu.VMEM)] *...]
    all_to_all x0 -> x1, blocking collectives: none -> 12.5 us  [to_all(): lax.all_to_all(jnp.broadcast_to(value[None], (length, *value.shape)), axi...]
    ppermute x5, starting transfers between devices: 10.8 us -> 4.17 us  [swap_core(): return lax.ppermute(value, 'core', ring(NC, 1))]
    ppermute x2 -> x7, starting transfers between devices: 1.4 us -> 7.73 us  [the longest x3 4.39 us: on_device(): parts.append(lax.ppermute(part, 'x', ring(NX, -j)))]
    broadcast_in_dim x4 -> x1, local copies, waits for them, and re-layouts: 4.97 us -> 0.02 us  [to_all(): jnp.broadcast_to(value[None], (length, *value.shape))]
  transfers between devices with their start and end apart: 16 -> 18, of which waited for: 11 -> 12; matrix products, arithmetic and copies ran while one was open for 9% -> 6% of each run, Pallas kernels for 0% -> 2%
where the time goes in v2:
time: 185 us; the launch traced here: 184 us
  waiting for transfers between devices  82.9 us (45%)
  starting transfers between devices  34.5 us (19%)
  blocking collectives  29.1 us (16%)
  Pallas kernels  22.4 us (12%)
  local copies, waits for them, and re-layouts  10 us (5%)
  matrix products  3.44 us (2%)
    ppermute x3, waiting for transfers between devices, on_device(): parts.append(lax.ppermute(part, 'x', ring(NX, -j)))  23 us
    ppermute x3, waiting for transfers between devices, on_device(): other = lax.ppermute(mine, ('y', 'core'), PAIRS)  20.5 us
    all_to_all x1, blocking collectives, on_device(): back = lax.all_to_all(blocks, ('y', 'core'), 0, 0, tiled=True)  16.6 us
    pallas_call x4, Pallas kernels, call_term(): pl.pallas_call(kernel, out_shape=out_shape, in_specs=[spec(pltpu.VMEM)] *...  16.4 us
    ppermute x3, waiting for transfers between devices, on_device(): cols.append(lax.ppermute(orbitals[0], 'y', ring(NY, -j)))  15.1 us
    all_to_all x1, blocking collectives, to_all(): lax.all_to_all(jnp.broadcast_to(value[None], (length, *value.shape)), axi...  12.5 us
    all_to_all x1, starting transfers between devices, on_device(): lax.all_to_all(weights, ('z', 'x'), 0, 0, tiled=True).reshape(32, 1024)  9.94 us
    ppermute x1, waiting for transfers between devices, on_device(): part = lax.ppermute(part, 'y', ring(NY, 2))  9.65 us
  transfers between devices with their start and end apart: 18, of which 12 were waited for; matrix products, arithmetic and copies ran while one was open for 6% of the time, Pallas kernels for 2%

profile of v2, /device:TPU:1, one launch (start us, length us, event | category | flops | bytes accessed | tf_op | source)
XLA Modules:
  0.0 184.3 jit_solution(17318789570258069001)
XLA Ops:
  0.6 1.1 constant_dynamic-slice_fusion
  1.8 3.8 %collective-permute-start.8 = (bf16[512,512]{1,0:T(8,128)(2,1)S(1)}, bf16[512,512]{1,0:T(8,128)(2,1)S(1)}, u32[]{:S(2)}, u32[]{:S(2)}) collective-permute-start(bf16[512,512]{1,0:T(8,128)(2,1)S(1)} %constant_dynamic-slice_fusion), channel_id=1, source_target_pairs={{0,4},{2,6},{4,0},{6,2},{1,5},{3,7},{5,1},{7,3},{8,12},{10,14},{12... | collective-permute-start | bytes 1572872 | tf_op jit(solution)/shard_map/ppermute | solution.py:248
  5.6 1.0 collective-permute-start.4
  6.5 9.7 %collective-permute-done.8 = bf16[512,512]{1,0:T(8,128)(2,1)S(1)} collective-permute-done((bf16[512,512]{1,0:T(8,128)(2,1)S(1)}, bf16[512,512]{1,0:T(8,128)(2,1)S(1)}, u32[]{:S(2)}, u32[]{:S(2)}) %collective-permute-start.8) | collective-permute-done | bytes 524320 | tf_op jit(solution)/shard_map/ppermute | solution.py:248
  16.2 3.3 %collective-permute-start.9 = (bf16[512,512]{1,0:T(8,128)(2,1)S(1)}, bf16[512,512]{1,0:T(8,128)(2,1)S(1)}, u32[]{:S(2)}, u32[]{:S(2)}) collective-permute-start(bf16[512,512]{1,0:T(8,128)(2,1)S(1)} %collective-permute-done.8), channel_id=1, source_target_pairs={{0,24},{8,0},{16,8},{24,16},{1,25},{9,1},{17,9},{25,17},{2,26},{10... | collective-permute-start | bytes 1572872 | tf_op jit(solution)/shard_map/ppermute | solution.py:258
  19.5 0.5 collective-permute-start.10
  20.0 0.6 collective-permute-start.11
  20.6 0.8 constant_dynamic-update-slice_fusion.5
  21.4 9.0 %collective-permute-done.9 = bf16[512,512]{1,0:T(8,128)(2,1)S(1)} collective-permute-done((bf16[512,512]{1,0:T(8,128)(2,1)S(1)}, bf16[512,512]{1,0:T(8,128)(2,1)S(1)}, u32[]{:S(2)}, u32[]{:S(2)}) %collective-permute-start.9) | collective-permute-done | bytes 524320 | tf_op jit(solution)/shard_map/ppermute | solution.py:258
  30.5 0.8 constant_dynamic-update-slice_fusion.4
  31.3 1.4 collective-permute-done.10
  32.7 0.8 constant_dynamic-update-slice_fusion.3
  33.5 12.5 %collective-permute-done.11 = bf16[512,512]{1,0:T(8,128)(2,1)S(1)} collective-permute-done((bf16[512,512]{1,0:T(8,128)(2,1)S(1)}, bf16[512,512]{1,0:T(8,128)(2,1)S(1)}, u32[]{:S(2)}, u32[]{:S(2)}) %collective-permute-start.11) | collective-permute-done | bytes 524320 | tf_op jit(solution)/shard_map/ppermute | solution.py:258
  46.0 0.8 constant_dynamic-update-slice_fusion.2.f0
  46.9 0.5 collective-permute-start.12
  47.4 2.7 %collective-permute-start = (bf16[400,256]{1,0:T(8,128)(2,1)S(1)}, bf16[400,256]{1,0:T(8,128)(2,1)S(1)}, u32[]{:S(2)}, u32[]{:S(2)}) collective-permute-start(bf16[400,256]{1,0:T(8,128)(2,1)S(1)} %bitcast.6), channel_id=1, source_target_pairs={{0,6},{2,0},{4,2},{6,4},{1,7},{3,1},{5,3},{7,5},{8,14},{10,8},{12,... | collective-permute-start | bytes 614408 | tf_op jit(solution)/shard_map/ppermute | solution.py:242
  50.8 8.0 %collective-permute-done.o1 = bf16[400,256]{1,0:T(8,128)(2,1)S(1)} collective-permute-done((bf16[400,256]{1,0:T(8,128)(2,1)S(1)}, bf16[400,256]{1,0:T(8,128)(2,1)S(1)}, u32[]{:S(2)}, u32[]{:S(2)}) %collective-permute-start) | collective-permute-done | bytes 204832 | tf_op jit(solution)/shard_map/ppermute | solution.py:242
  58.8 1.0 collective-permute-start.6
  59.8 7.1 %collective-permute-done.2.o3 = bf16[400,256]{1,0:T(8,128)(2,1)S(1)} collective-permute-done((bf16[400,256]{1,0:T(8,128)(2,1)S(1)}, bf16[400,256]{1,0:T(8,128)(2,1)S(1)}, u32[]{:S(2)}, u32[]{:S(2)}) %collective-permute-start.2) | collective-permute-done | bytes 204832 | tf_op jit(solution)/shard_map/ppermute | solution.py:242
  66.9 2.5 %head.1 = f32[32,1,1024]{2,1,0:T(1,128)} custom-call(bf16[400,400]{1,0:T(8,128)(2,1)S(1)} %bitcast.11, bf16[400,256]{1,0:T(8,128)(2,1)S(1)} %bitcast.9, bf16[400,256]{1,0:T(8,128)(2,1)S(1)} %collective-permute-done.o1, bf16[400,256]{1,0:T(8,128)(2,1)S(1)} %collective-permute-done.1.o2, bf16[400,256]{1,0:T(8,128)(2,1)S(1)} %collective-permute-done.2.o3, ...), custom_call_target="tpu_custom_call" | custom-call | tf_op jit(solution)/shard_map/head/pallas_call | solution.py:67
  69.4 1.3 copy-done.1
  70.7 9.9 %all-to-all-start = ((f32[32,1,1024]{2,1,0:T(1,128)}), f32[32,1,1024]{2,1,0:T(1,128)}, u32[]{:S(2)}, u32[]{:S(2)}) async-start(f32[32,1,1024]{2,1,0:T(1,128)} %head.1), calls=%async_computation | async-start | bytes 262144 | tf_op jit(solution)/shard_map/all_to_all | solution.py:254
  80.7 1.0 constant_dynamic-update-slice_fusion.1
  81.6 1.0 constant_dynamic-update-slice_fusion
  82.9 7.1 %all-to-all-done = f32[32,1,1024]{2,1,0:T(1,128)} async-done(((f32[32,1,1024]{2,1,0:T(1,128)}), f32[32,1,1024]{2,1,0:T(1,128)}, u32[]{:S(2)}, u32[]{:S(2)}) %all-to-all-start) | async-done | bytes 131104 | tf_op jit(solution)/shard_map/all_to_all | solution.py:254
  90.0 1.3 fusion.5
  91.3 12.5 %all_to_all.20 = f32[8,32,256]{2,1,0:T(8,128)} all-to-all(f32[8,32,256]{2,1,0:T(8,128)S(1)} %broadcast_in_dim.2), channel_id=1, replica_groups=mesh['z'=8,'x'=4,'y'=4,'core'=2] {'y','core'}, dimensions={0} | all-to-all | bytes 524288 | tf_op jit(solution)/shard_map/all_to_all | solution.py:35
  103.7 1.0 reduce_sum.18
  104.7 2.2 %convolution_convert_fusion = bf16[32,2048]{1,0:T(8,128)(2,1)S(1)} fusion(bf16[1024,256]{1,0:T(8,128)(2,1)} %collective-permute-done.7, bf16[512,256]{1,0:T(8,128)(2,1)} %collective-permute-done.6, bf16[512,256]{1,0:T(8,128)(2,1)} %param.10, f32[32,256]{1,0:T(8,128)S(1)} %copy-done.7, f32[32,256]{1,0:T(8,128)S(1)} %reduce_sum.18), kind=kOutput, calls=%fused_computation | convolution fusion | flops 204554240 | bytes 1245184 | tf_op jit(solution)/shard_map/dot_general | solution.py:264
  106.9 0.7 reshape.12
  107.7 5.8 %all-to-all-start.2 = ((bf16[32,4,512]{2,1,0:T(4,128)(2,1)}), bf16[32,4,512]{2,1,0:T(4,128)(2,1)S(1)}, u32[]{:S(2)}, u32[]{:S(2)}) async-start(bf16[32,4,512]{2,1,0:T(4,128)(2,1)} %reshape.12), calls=%async_computation.2 | async-start | bytes 262144 | tf_op jit(solution)/shard_map/all_to_all | solution.py:265
  113.7 1.4 collective-permute-start.3
  115.1 1.1 collective-permute-done.3.par
  116.4 6.4 %all-to-all-done.2 = bf16[32,4,512]{2,1,0:T(4,128)(2,1)S(1)} async-done(((bf16[32,4,512]{2,1,0:T(4,128)(2,1)}), bf16[32,4,512]{2,1,0:T(4,128)(2,1)S(1)}, u32[]{:S(2)}, u32[]{:S(2)}) %all-to-all-start.2) | async-done | bytes 131104 | tf_op jit(solution)/shard_map/all_to_all | solution.py:265
  122.9 1.6 copy-done.2
  124.5 2.5 %load_halves.1.interp_ref.refs_4_ = bf16[4,2048,512]{2,1,0:T(8,128)(2,1)S(1)} custom-call(bf16[2048,512]{1,0:T(8,128)(2,1)S(1)} %copy-done, bf16[2048,512]{1,0:T(8,128)(2,1)S(1)} %copy-done.2, bf16[2048,512]{1,0:T(8,128)(2,1)} %constant_dynamic-update-slice_fusion.2.f0, bf16[2048,512]{1,0:T(8,128)(2,1)} %collective-permute-done.12.f1), custom_call_target="tpu_custom_call" | custom-call | tf_op jit(solution)/shard_map/load_halves/pallas_call | solution.py:152
  127.0 4.1 %term.4.refs_0_ = bf16[104,2048]{1,0:T(8,128)(2,1)S(1)} custom-call(bf16[104,2048]{1,0:T(8,128)(2,1)S(1)} %join.1.term_ref.refs_2_, f32[4,512]{1,0:T(4,128)S(1)} %convert_reduce_fusion.scales_ref.refs_3_, bf16[4,2048,512]{2,1,0:T(8,128)(2,1)S(1)} %load_halves.1.interp_ref.refs_4_), custom_call_target="tpu_custom_call" | custom-call | tf_op jit(solution)/shard_map/term/pallas_call | solution.py:207
  131.1 1.3 collective-permute-start.13
  132.4 6.6 %collective-permute-done.13.refs_1_ = bf16[104,2048]{1,0:T(8,128)(2,1)S(1)} collective-permute-done((bf16[104,2048]{1,0:T(8,128)(2,1)S(1)}, bf16[104,2048]{1,0:T(8,128)(2,1)S(1)}, u32[]{:S(2)}, u32[]{:S(2)}) %collective-permute-start.13) | collective-permute-done | bytes 426016 | tf_op jit(solution)/shard_map/ppermute | solution.py:277
  139.1 4.1 %term.5 = (bf16[104,2048]{1,0:T(8,128)(2,1)S(1)}, f32[104,2048]{1,0:T(8,128)S(1)}) custom-call(bf16[104,2048]{1,0:T(8,128)(2,1)S(1)} %term.4.refs_0_, bf16[104,2048]{1,0:T(8,128)(2,1)S(1)} %collective-permute-done.13.refs_1_, bf16[104,2048]{1,0:T(8,128)(2,1)S(1)} %join.1.term_ref.refs_2_, f32[4,512]{1,0:T(4,128)S(1)} %convert_reduce_fusion.scales_ref.refs_3_, ...), custom_call_target="tpu_custom_call" | custom-call | tf_op jit(solution)/shard_map/term/pallas_call | solution.py:207
  143.1 1.0 collective-permute-start.14
  144.1 6.9 %collective-permute-done.14.refs_1_ = bf16[104,2048]{1,0:T(8,128)(2,1)S(1)} collective-permute-done((bf16[104,2048]{1,0:T(8,128)(2,1)S(1)}, bf16[104,2048]{1,0:T(8,128)(2,1)S(1)}, u32[]{:S(2)}, u32[]{:S(2)}) %collective-permute-start.14) | collective-permute-done | bytes 426016 | tf_op jit(solution)/shard_map/ppermute | solution.py:277
  151.1 4.1 %term.6 = (bf16[104,2048]{1,0:T(8,128)(2,1)S(1)}, f32[104,2048]{1,0:T(8,128)S(1)}) custom-call(bf16[104,2048]{1,0:T(8,128)(2,1)S(1)} %get-tuple-element.10.refs_0_, bf16[104,2048]{1,0:T(8,128)(2,1)S(1)} %collective-permute-done.14.refs_1_, f32[104,2048]{1,0:T(8,128)S(1)} %get-tuple-element.11.refs_2_, f32[4,512]{1,0:T(4,128)S(1)} %convert_reduce_fusion.scales_ref.refs_3_, ...), custom_call_target="tpu_custom_call" | custom-call | tf_op jit(solution)/shard_map/term/pallas_call | solution.py:207
  155.2 0.7 collective-permute-start.15
  155.9 6.9 %collective-permute-done.15.other_ref = bf16[104,2048]{1,0:T(8,128)(2,1)S(1)} collective-permute-done((bf16[104,2048]{1,0:T(8,128)(2,1)S(1)}, bf16[104,2048]{1,0:T(8,128)(2,1)S(1)}, u32[]{:S(2)}, u32[]{:S(2)}) %collective-permute-start.15) | collective-permute-done | bytes 426016 | tf_op jit(solution)/shard_map/ppermute | solution.py:283
  162.8 4.1 %term.7 = bf16[8,112,256]{2,1,0:T(8,128)(2,1)S(1)} custom-call(bf16[104,2048]{1,0:T(8,128)(2,1)S(1)} %get-tuple-element.12.mine_ref, bf16[104,2048]{1,0:T(8,128)(2,1)S(1)} %collective-permute-done.15.other_ref, f32[104,2048]{1,0:T(8,128)S(1)} %get-tuple-element.13.total_ref, f32[4,512]{1,0:T(4,128)S(1)} %convert_reduce_fusion.scales_ref.refs_3_, ...), custom_call_target="tpu_custom_call" | custom-call | tf_op jit(solution)/shard_map/term/pallas_call | solution.py:207
  167.0 16.6 %all_to_all.21.back_ref = bf16[8,112,256]{2,1,0:T(8,128)(2,1)S(1)} all-to-all(bf16[8,112,256]{2,1,0:T(8,128)(2,1)S(1)} %term.7), channel_id=1, replica_groups=mesh['z'=8,'x'=4,'y'=4,'core'=2] {'y','core'}, dimensions={0} | all-to-all | bytes 917504 | tf_op jit(solution)/shard_map/all_to_all | solution.py:289
  183.6 0.7 end.1
  (28 shorter events, 1.4 us)
Async XLA Ops:
  1.7 45.7 %copy-start.3 = (bf16[1,400,256]{2,1,0:T(8,128)(2,1)S(1)}, bf16[1,400,256]{2,1,0:T(8,128)(2,1)}, u32[]{:S(2)}) copy-start(bf16[1,400,256]{2,1,0:T(8,128)(2,1)} %param.6) | copy-start | bytes 614404
  1.7 48.4 %copy-start.5 = (bf16[400,512]{1,0:T(8,128)(2,1)S(1)}, bf16[400,512]{1,0:T(8,128)(2,1)}, u32[]{:S(2)}) copy-start(bf16[400,512]{1,0:T(8,128)(2,1)} %occ_own.1) | copy-start | bytes 1228804
  1.7 65.2 %copy-start = (bf16[2048,512]{1,0:T(8,128)(2,1)S(1)}, bf16[2048,512]{1,0:T(8,128)(2,1)}, u32[]{:S(2)}) copy-start(bf16[2048,512]{1,0:T(8,128)(2,1)} %a0.1) | copy-start | bytes 6291460
  1.8 65.2 %copy-start.4 = (bf16[1,400,400]{2,1,0:T(8,128)(2,1)S(1)}, bf16[1,400,400]{2,1,0:T(8,128)(2,1)}, u32[]{:S(2)}) copy-start(bf16[1,400,400]{2,1,0:T(8,128)(2,1)} %param.7) | copy-start | bytes 960004
  1.8 14.4 %collective-permute-start.8 = (bf16[512,512]{1,0:T(8,128)(2,1)S(1)}, bf16[512,512]{1,0:T(8,128)(2,1)S(1)}, u32[]{:S(2)}, u32[]{:S(2)}) collective-permute-start(bf16[512,512]{1,0:T(8,128)(2,1)S(1)} %constant_dynamic-slice_fusion), channel_id=1, source_target_pairs={{0,4},{2,6},{4,0},{6,2},{1,5},{3,7},{5,1},{7,3},{8,12},{10,14},{12... | collective-permute-start | bytes 1572872 | tf_op jit(solution)/shard_map/ppermute | solution.py:248
  5.6 61.3 %collective-permute-start.4 = (bf16[2048,512]{1,0:T(8,128)(2,1)}, bf16[2048,512]{1,0:T(8,128)(2,1)S(1)}, u32[]{:S(2)}, u32[]{:S(2)}) collective-permute-start(bf16[2048,512]{1,0:T(8,128)(2,1)} %a0.1), channel_id=1, source_target_pairs={{0,1},{1,0},{2,3},{3,2},{4,5},{5,4},{6,7},{7,6},{8,9},{9,8},{10,11... | collective-permute-start | bytes 6291464 | tf_op jit(solution)/shard_map/ppermute | solution.py:31
  16.2 14.3 %collective-permute-start.9 = (bf16[512,512]{1,0:T(8,128)(2,1)S(1)}, bf16[512,512]{1,0:T(8,128)(2,1)S(1)}, u32[]{:S(2)}, u32[]{:S(2)}) collective-permute-start(bf16[512,512]{1,0:T(8,128)(2,1)S(1)} %collective-permute-done.8), channel_id=1, source_target_pairs={{0,24},{8,0},{16,8},{24,16},{1,25},{9,1},{17,9},{25,17},{2,26},{10... | collective-permute-start | bytes 1572872 | tf_op jit(solution)/shard_map/ppermute | solution.py:258
  19.5 13.3 %collective-permute-start.10 = (bf16[512,512]{1,0:T(8,128)(2,1)S(1)}, bf16[512,512]{1,0:T(8,128)(2,1)S(1)}, u32[]{:S(2)}, u32[]{:S(2)}) collective-permute-start(bf16[512,512]{1,0:T(8,128)(2,1)S(1)} %collective-permute-done.8), channel_id=1, source_target_pairs={{0,16},{8,24},{16,0},{24,8},{1,17},{9,25},{17,1},{25,9},{2,18},{10... | collective-permute-start | bytes 1572872 | tf_op jit(solution)/shard_map/ppermute | solution.py:258
  20.0 26.1 %collective-permute-start.11 = (bf16[512,512]{1,0:T(8,128)(2,1)S(1)}, bf16[512,512]{1,0:T(8,128)(2,1)S(1)}, u32[]{:S(2)}, u32[]{:S(2)}) collective-permute-start(bf16[512,512]{1,0:T(8,128)(2,1)S(1)} %collective-permute-done.8), channel_id=1, source_target_pairs={{0,8},{8,16},{16,24},{24,0},{1,9},{9,17},{17,25},{25,1},{2,10},{10... | collective-permute-start | bytes 1572872 | tf_op jit(solution)/shard_map/ppermute | solution.py:258
  46.9 76.0 %collective-permute-start.12 = (bf16[2048,512]{1,0:T(8,128)(2,1)}, bf16[2048,512]{1,0:T(8,128)(2,1)}, u32[]{:S(2)}, u32[]{:S(2)}) collective-permute-start(bf16[2048,512]{1,0:T(8,128)(2,1)} %constant_dynamic-update-slice_fusion.2.f0), channel_id=1, source_target_pairs={{0,1},{1,0},{2,3},{3,2},{4,5},{5,4},{6,7},{7,6},{8,9},{9,8},{10,11... | collective-permute-start | bytes 6291464 | tf_op jit(solution)/shard_map/ppermute | solution.py:31
  47.4 11.4 %collective-permute-start = (bf16[400,256]{1,0:T(8,128)(2,1)S(1)}, bf16[400,256]{1,0:T(8,128)(2,1)S(1)}, u32[]{:S(2)}, u32[]{:S(2)}) collective-permute-start(bf16[400,256]{1,0:T(8,128)(2,1)S(1)} %bitcast.6), channel_id=1, source_target_pairs={{0,6},{2,0},{4,2},{6,4},{1,7},{3,1},{5,3},{7,5},{8,14},{10,8},{12,... | collective-permute-start | bytes 614408 | tf_op jit(solution)/shard_map/ppermute | solution.py:242
  50.1 16.8 %collective-permute-start.5 = (bf16[400,512]{1,0:T(8,128)(2,1)S(1)}, bf16[400,512]{1,0:T(8,128)(2,1)S(1)}, u32[]{:S(2)}, u32[]{:S(2)}) collective-permute-start(bf16[400,512]{1,0:T(8,128)(2,1)S(1)} %copy-done.5), channel_id=1, source_target_pairs={{0,1},{1,0},{2,3},{3,2},{4,5},{5,4},{6,7},{7,6},{8,9},{9,8},{10,11... | collective-permute-start | bytes 1228808 | tf_op jit(solution)/shard_map/ppermute | solution.py:31
  50.4 8.4 %collective-permute-start.1 = (bf16[400,256]{1,0:T(8,128)(2,1)S(1)}, bf16[400,256]{1,0:T(8,128)(2,1)S(1)}, u32[]{:S(2)}, u32[]{:S(2)}) collective-permute-start(bf16[400,256]{1,0:T(8,128)(2,1)S(1)} %bitcast.7), channel_id=1, source_target_pairs={{0,4},{2,6},{4,0},{6,2},{1,5},{3,7},{5,1},{7,3},{8,12},{10,14},{12... | collective-permute-start | bytes 614408 | tf_op jit(solution)/shard_map/ppermute | solution.py:242
  58.8 8.1 %collective-permute-start.2 = (bf16[400,256]{1,0:T(8,128)(2,1)S(1)}, bf16[400,256]{1,0:T(8,128)(2,1)S(1)}, u32[]{:S(2)}, u32[]{:S(2)}) collective-permute-start(bf16[400,256]{1,0:T(8,128)(2,1)S(1)} %bitcast.8), channel_id=1, source_target_pairs={{0,2},{2,4},{4,6},{6,0},{1,3},{3,5},{5,7},{7,1},{8,10},{10,12},{12... | collective-permute-start | bytes 614408 | tf_op jit(solution)/shard_map/ppermute | solution.py:242
  58.8 22.8 %collective-permute-start.6 = (bf16[512,256]{1,0:T(8,128)(2,1)}, bf16[512,256]{1,0:T(8,128)(2,1)}, u32[]{:S(2)}, u32[]{:S(2)}) collective-permute-start(bf16[512,256]{1,0:T(8,128)(2,1)} %param.10), channel_id=1, source_target_pairs={{0,1},{1,0},{2,3},{3,2},{4,5},{5,4},{6,7},{7,6},{8,9},{9,8},{10,11... | collective-permute-start | bytes 786440 | tf_op jit(solution)/shard_map/ppermute | solution.py:31
  69.4 1.3 copy-start.1
  70.7 34.0 %copy-start.7 = (f32[32,256]{1,0:T(8,128)S(1)}, f32[32,256]{1,0:T(8,128)}, u32[]{:S(2)}) copy-start(f32[32,256]{1,0:T(8,128)} %param.11) | copy-start | bytes 98308
  70.7 19.3 %all-to-all-start = ((f32[32,1,1024]{2,1,0:T(1,128)}), f32[32,1,1024]{2,1,0:T(1,128)}, u32[]{:S(2)}, u32[]{:S(2)}) async-start(f32[32,1,1024]{2,1,0:T(1,128)} %head.1), calls=%async_computation | async-start | bytes 262144 | tf_op jit(solution)/shard_map/all_to_all | solution.py:254
  82.6 22.1 %collective-permute-start.7 = (bf16[1024,256]{1,0:T(8,128)(2,1)S(1)}, bf16[1024,256]{1,0:T(8,128)(2,1)}, u32[]{:S(2)}, u32[]{:S(2)}) collective-permute-start(bf16[1024,256]{1,0:T(8,128)(2,1)S(1)} %constant_dynamic-update-slice_fusion), channel_id=1, source_target_pairs={{0,4},{2,6},{4,0},{6,2},{1,5},{3,7},{5,1},{7,3},{8,12},{10,14},{12... | collective-permute-start | bytes 1572872 | tf_op jit(solution)/shard_map/ppermute | solution.py:249
  104.7 11.7 %copy-start.6 = (f32[32,256]{1,0:T(8,128)}, f32[32,256]{1,0:T(8,128)S(1)}, u32[]{:S(2)}) copy-start(f32[32,256]{1,0:T(8,128)S(1)} %reduce_sum.18) | copy-start | bytes 98308
  107.7 15.2 %all-to-all-start.2 = ((bf16[32,4,512]{2,1,0:T(4,128)(2,1)}), bf16[32,4,512]{2,1,0:T(4,128)(2,1)S(1)}, u32[]{:S(2)}, u32[]{:S(2)}) async-start(bf16[32,4,512]{2,1,0:T(4,128)(2,1)} %reshape.12), calls=%async_computation.2 | async-start | bytes 262144 | tf_op jit(solution)/shard_map/all_to_all | solution.py:265
  113.7 2.5 %collective-permute-start.3 = (bf16[104,1024]{1,0:T(8,128)(2,1)S(1)}, bf16[104,1024]{1,0:T(8,128)(2,1)S(1)}, u32[]{:S(2)}, u32[]{:S(2)}) collective-permute-start(bf16[104,1024]{1,0:T(8,128)(2,1)S(1)} %get-tuple-element.9), channel_id=1, source_target_pairs={{0,1},{1,0},{2,3},{3,2},{4,5},{5,4},{6,7},{7,6},{8,9},{9,8},{10,11... | collective-permute-start | bytes 638984 | tf_op jit(solution)/shard_map/ppermute | solution.py:31
  122.9 1.6 copy-start.2
  131.1 7.9 %collective-permute-start.13 = (bf16[104,2048]{1,0:T(8,128)(2,1)S(1)}, bf16[104,2048]{1,0:T(8,128)(2,1)S(1)}, u32[]{:S(2)}, u32[]{:S(2)}) collective-permute-start(bf16[104,2048]{1,0:T(8,128)(2,1)S(1)} %term.4.refs_0_), channel_id=1, source_target_pairs={{0,7},{1,2},{2,1},{3,4},{4,3},{5,6},{6,5},{7,0},{8,15},{9,10},{10,... | collective-permute-start | bytes 1277960 | tf_op jit(solution)/shard_map/ppermute | solution.py:277
  143.1 7.9 %collective-permute-start.14 = (bf16[104,2048]{1,0:T(8,128)(2,1)S(1)}, bf16[104,2048]{1,0:T(8,128)(2,1)S(1)}, u32[]{:S(2)}, u32[]{:S(2)}) collective-permute-start(bf16[104,2048]{1,0:T(8,128)(2,1)S(1)} %get-tuple-element.10.refs_0_), channel_id=1, source_target_pairs={{0,7},{1,2},{2,1},{3,4},{4,3},{5,6},{6,5},{7,0},{8,15},{9,10},{10,... | collective-permute-start | bytes 1277960 | tf_op jit(solution)/shard_map/ppermute | solution.py:277
  155.2 7.6 %collective-permute-start.15 = (bf16[104,2048]{1,0:T(8,128)(2,1)S(1)}, bf16[104,2048]{1,0:T(8,128)(2,1)S(1)}, u32[]{:S(2)}, u32[]{:S(2)}) collective-permute-start(bf16[104,2048]{1,0:T(8,128)(2,1)S(1)} %get-tuple-element.12.mine_ref), channel_id=1, source_target_pairs={{0,7},{1,2},{2,1},{3,4},{4,3},{5,6},{6,5},{7,0},{8,15},{9,10},{10,... | collective-permute-start | bytes 1277960 | tf_op jit(solution)/shard_map/ppermute | solution.py:283

commit v3 on v2

--- a/solution.py
+++ b/solution.py
@@ -41,6 +41,10 @@
     return pl.BlockSpec(memory_space=space)
 
 
+def in_hbm(*values):
+    return [pltpu.with_memory_space_constraint(v, pltpu.HBM) for v in values]
+
+
 PARAMS = pltpu.CompilerParams(vmem_limit_bytes=VMEM_LIMIT)
 
 
@@ -48,22 +52,62 @@
     return jnp.where(c == 1, y, (y + 3) % 4)
 
 
-def head_kernel(inv, o0, o1, o2, o3, a_own, a_par, occ_own, occ_par, weights_ref):
+def start_kernel(interp, inv, orb, occ, part, rows_out, inv_out, orb_out, occ_out, sems):
+    x = lax.axis_index("x")
+    c = lax.axis_index("core")
+    at = pl.multiple_of(x * 512, 512)
+    copies = [pltpu.make_async_copy(interp.at[pl.ds(at, 512), :], part, sems.at[0])]
+    for y in range(NY):
+        at = pl.multiple_of(y * 512 + c * 256, 256)
+        rows = interp.at[pl.ds(at, 256), :]
+        copies.append(
+            pltpu.make_async_copy(rows, rows_out.at[pl.ds(256 * y, 256), :], sems.at[1 + y])
+        )
+    for k, (a, b) in enumerate(((inv, inv_out), (orb, orb_out), (occ, occ_out))):
+        copies.append(pltpu.make_async_copy(a, b, sems.at[5 + k]))
+    for copy in copies:
+        copy.start()
+    for copy in copies:
+        copy.wait()
+
+
+def call_start(interp, inv, orb, occ):
+    part, *rest = pl.pallas_call(
+        start_kernel,
+        out_shape=(
+            jax.ShapeDtypeStruct((512, 512), bf16),
+            pltpu.VMEM((1024, 512), bf16),
+            pltpu.VMEM((ROWS, ROWS), bf16),
+            pltpu.VMEM((ROWS, 256), bf16),
+            pltpu.VMEM((ROWS, 512), bf16),
+        ),
+        in_specs=[spec(pltpu.HBM)] * 4,
+        out_specs=(spec(pltpu.HBM),) + (spec(pltpu.VMEM),) * 4,
+        scratch_shapes=[pltpu.SemaphoreType.DMA((8,))],
+        compiler_params=PARAMS,
+        name="start",
+    )(*in_hbm(interp, inv, orb, occ))
+    return part, *[pltpu.with_memory_space_constraint(r, pltpu.VMEM) for r in rest]
+
+
+def head_kernel(inv, o0, o1, o2, o3, rows_own, a_par, occ_own, occ_par, weights_ref):
     y = lax.axis_index("y")
     c = lax.axis_index("core")
     sums = [None, None]
     for j, o in enumerate((o0, o1, o2, o3)):
         green = jnp.dot(inv[...], o[...], preferred_element_type=f32).astype(bf16)
-        at = pl.multiple_of(((y + j) % 4) * 512 + c * 256, 256)
-        for k, a in enumerate((a_own, a_par)):
-            part = jnp.dot(green, a[pl.ds(at, 256), :], preferred_element_type=f32)
+        of = (y + j) % NY
+        own = rows_own[pl.ds(pl.multiple_of(of * 256, 256), 256), :]
+        par = a_par[pl.ds(pl.multiple_of(of * 512 + c * 256, 256), 256), :]
+        for k, a in enumerate((own, par)):
+            part = jnp.dot(green, a, preferred_element_type=f32)
             sums[k] = part if sums[k] is None else sums[k] + part
     for k, occ in enumerate((occ_own, occ_par)):
         weights = jnp.sum(occ[...].astype(f32) * sums[k], axis=0, keepdims=True)
         weights_ref[:, :, 512 * k : 512 * k + 512] = jnp.broadcast_to(weights, (32, 1, 512))
 
 
-def call_head(inv, cols, a_own, a_par, occ_own, occ_par):
+def call_head(inv, cols, rows_own, a_par, occ_own, occ_par):
     return pl.pallas_call(
         head_kernel,
         out_shape=jax.ShapeDtypeStruct((32, 1, 1024), f32),
@@ -71,7 +115,40 @@
         out_specs=spec(pltpu.VMEM),
         compiler_params=pltpu.CompilerParams(vmem_limit_bytes=24 * 2**20),
         name="head",
-    )(inv, *cols, a_own, a_par, occ_own, occ_par)
+    )(inv, *cols, rows_own, a_par, occ_own, occ_par)
+
+
+def field_kernel(bias_ref, fields_ref, c0, c1, c2, c3, force_ref, out_ref):
+    bias = bias_ref[0]
+    for k in range(1, 8):
+        bias = bias + bias_ref[k]
+    force_ref[...] = bias
+    coeff = time_root * (fields_ref[...] - bias)
+    parts = [
+        lax.dot_general(
+            coeff,
+            c[...].astype(f32),
+            (((1,), (1,)), ((), ())),
+            precision=lax.Precision.HIGHEST,
+            preferred_element_type=f32,
+        )
+        for c in (c0, c1, c2, c3)
+    ]
+    out_ref[...] = jnp.concatenate(parts, 1).reshape(32, 4, 512).astype(bf16)
+
+
+def call_field(biases, fields, chols):
+    return pl.pallas_call(
+        field_kernel,
+        out_shape=(
+            jax.ShapeDtypeStruct((32, 256), f32),
+            jax.ShapeDtypeStruct((32, 4, 512), bf16),
+        ),
+        in_specs=[spec(pltpu.VMEM)] * 6,
+        out_specs=(spec(pltpu.VMEM),) * 2,
+        compiler_params=PARAMS,
+        name="field",
+    )(biases, fields, *chols)
 
 
 def slab_kernel(o0, o1, o2, o3, mine_ref, other_ref, sems):
@@ -129,41 +206,10 @@
     )(own, par)
 
 
-def load_kernel(a0, a1, f0, f1, out_ref, sems):
-    x = lax.axis_index("x")
-    copies = [pltpu.make_async_copy(a, out_ref.at[b], sems.at[b]) for b, a in enumerate((a0, a1))]
-    for b, f in enumerate((f0, f1)):
-        for j in range(NX):
-            at = pl.multiple_of(((x + j) % NX) * 512, 512)
-            copies.append(
-                pltpu.make_async_copy(
-                    f.at[pl.ds(512 * j, 512), :],
-                    out_ref.at[2 + b, pl.ds(at, 512), :],
-                    sems.at[2 + NX * b + j],
-                )
-            )
-    for copy in copies:
-        copy.start()
-    for copy in copies:
-        copy.wait()
-
-
-def call_load(halves):
-    out = pl.pallas_call(
-        load_kernel,
-        out_shape=pltpu.VMEM((4, 2048, 512), bf16),
-        in_specs=[spec(pl.ANY)] * 4,
-        out_specs=spec(pltpu.VMEM),
-        scratch_shapes=[pltpu.SemaphoreType.DMA((2 + 2 * NX,))],
-        compiler_params=PARAMS,
-        name="load_halves",
-    )(*halves)
-    return pltpu.with_memory_space_constraint(out, pltpu.VMEM)
-
-
-def one_term(term, scales_ref, order, interp_ref):
+def one_term(term, scales_ref, order, interp_ref, wait=lambda b: None):
     acc = None
     for b in range(4):
+        wait(b)
         interp = interp_ref[b]
         product = jnp.dot(term, interp, preferred_element_type=f32)
         mixed = (product * (scales_ref[b : b + 1, :] / order)).astype(bf16)
@@ -174,8 +220,47 @@
     return acc
 
 
-def first_kernel(term_ref, scales_ref, interp_ref, out_ref):
-    out_ref[...] = one_term(term_ref[...], scales_ref, 1, interp_ref).astype(bf16)
+def first_kernel(term_ref, arrived_ref, *refs):
+    near, far, (out_ref, scales_ref, interp_ref, sems) = refs[:2], (refs[2:6], refs[6:10]), refs[10:]
+    x = lax.axis_index("x")
+    copies = [
+        [pltpu.make_async_copy(a, interp_ref.at[b], sems.at[b])] for b, a in enumerate(near)
+    ]
+    for b in range(2):
+        copies.append([])
+        for j in range(NX):
+            at = pl.multiple_of(((x + j) % NX) * 512, 512)
+            copies[-1].append(
+                pltpu.make_async_copy(
+                    far[b][j], interp_ref.at[2 + b, pl.ds(at, 512), :], sems.at[2 + NX * b + j]
+                )
+            )
+    for copy in sum(copies, []):
+        copy.start()
+    scales_ref[...] = jnp.sum(arrived_ref[...].astype(f32), axis=0)
+
+    def wait(b):
+        for copy in copies[b]:
+            copy.wait()
+
+    out_ref[...] = one_term(term_ref[...], scales_ref, 1, interp_ref, wait).astype(bf16)
+
+
+def call_first(term, arrived, parts):
+    mine, scales, halves = pl.pallas_call(
+        first_kernel,
+        out_shape=(
+            jax.ShapeDtypeStruct((SLAB, 2048), bf16),
+            jax.ShapeDtypeStruct((4, 512), f32),
+            pltpu.VMEM((4, 2048, 512), bf16),
+        ),
+        in_specs=[spec(pltpu.VMEM)] * 2 + [spec(pltpu.HBM)] * 10,
+        out_specs=(spec(pltpu.VMEM),) * 3,
+        scratch_shapes=[pltpu.SemaphoreType.DMA((2 + 2 * NX,))],
+        compiler_params=PARAMS,
+        name="first",
+    )(term, arrived, *in_hbm(*parts))
+    return mine, scales, pltpu.with_memory_space_constraint(halves, pltpu.VMEM)
 
 
 def next_kernel(order, mine_ref, other_ref, total_ref, scales_ref, interp_ref, out_ref, total_out):
@@ -236,43 +321,40 @@
 
 
 def on_device(orbitals, intersection_inv, interp, occ_interp, chol_factors, fields):
-    x = lax.axis_index("x")
-    cols = [orbitals[0]]
-    for j in (1, 2, 3):
-        cols.append(lax.ppermute(orbitals[0], "y", ring(NY, -j)))
+    orb = orbitals[0]
+    part, rows, inv, orb_v, occ = call_start(interp, intersection_inv[0], orb, occ_interp)
+    others = [lax.ppermute(orb, "y", ring(NY, -j)) for j in (1, 2, 3)]
     a_par = swap_core(interp)
     occ_par = swap_core(occ_interp)
     chol_par = swap_core(chol_factors)
-    near = jnp.concatenate([chol_factors, chol_par], 0)
-    part = lax.dynamic_slice(interp, (x * 512, 0), (512, 512))
+    part, *others = lax.optimization_barrier((part, *others))
     part = lax.ppermute(part, "y", ring(NY, 2))
-    chol_far = lax.ppermute(near, "y", ring(NY, 2))
-
-    weights = call_head(intersection_inv[0], cols, interp, a_par, occ_interp, occ_par)
-    mine, other = call_slabs(cols)
+    chol_far = lax.ppermute(chol_factors, "y", ring(NY, 2))
+    chol_far_par = swap_core(chol_far)
+
+    weights = call_head(inv, [orb_v, *others], rows, a_par, occ, occ_par)
+    mine, other = call_slabs([orb, *others])
     term = call_join(mine, swap_core(other))
     all_weights = lax.all_to_all(weights, ("z", "x"), 0, 0, tiled=True).reshape(32, 1024)
 
-    parts = [part]
+    far = [part]
     for j in (1, 2, 3):
-        parts.append(lax.ppermute(part, "x", ring(NX, -j)))
-    far_own = jnp.concatenate(parts, 0)
-    partial_bias = jnp.dot(all_weights, near.astype(f32), precision=lax.Precision.HIGHEST)
-    force_bias = jnp.sum(to_all(partial_bias, ("y", "core"), 8), axis=0)
-    coeff = time_root * (fields - force_bias)
-    half = jnp.concatenate([near, chol_far], 0).astype(f32)
-    field_part = jnp.dot(coeff, half.T, precision=lax.Precision.HIGHEST)
-    arrived = lax.all_to_all(
-        field_part.astype(bf16).reshape(32, 4, 512), ("z", "x"), 0, 0, tiled=True
+        far.append(lax.ppermute(part, "x", ring(NX, -j)))
+    far_par = []
+    for j in range(4):
+        far_par.append(swap_core(far[j]))
+    near = jnp.concatenate([chol_factors, chol_par], 0).astype(f32)
+    partial_bias = jnp.dot(all_weights, near, precision=lax.Precision.HIGHEST)
+    biases = to_all(partial_bias, ("y", "core"), 8)
+    force_bias, field_part = call_field(
+        biases, fields, (chol_factors, chol_par, chol_far, chol_far_par)
     )
-    scales = jnp.sum(arrived.astype(f32), axis=0)
-    far_par = swap_core(far_own)
-    halves = call_load((interp, a_par, far_own, far_par))
+    arrived = lax.all_to_all(field_part, ("z", "x"), 0, 0, tiled=True)
 
     part_shape = jax.ShapeDtypeStruct((SLAB, 2048), bf16)
     total_shape = jax.ShapeDtypeStruct((SLAB, 2048), f32)
     total = term
-    mine = call_term(first_kernel, part_shape, term, scales, halves)
+    mine, scales, halves = call_first(term, arrived, (interp, a_par, *far, *far_par))
     for order in range(2, TERMS):
         other = lax.ppermute(mine, ("y", "core"), PAIRS)
         mine, total = call_term(

time: 185 us -> 156 us (0.84)
  waiting for transfers between devices: 82.9 us -> 57.2 us
  starting transfers between devices: 34.5 us -> 52.8 us
  blocking collectives: 29.1 us -> 15.4 us
  local copies, waits for them, and re-layouts: 10 us -> 0.74 us
  Pallas kernels: 22.4 us -> 27.1 us
  matrix products: 3.44 us -> 1.3 us
    ppermute x7, waiting for transfers between devices: 38.1 us -> 11.2 us  [the longest x3 7.68 us: on_device(): others = [lax.ppermute(orb, 'y', ring(NY, -j)) for j in (1, 2, 3)]]
    all_to_all x1 -> x0, blocking collectives: 12.5 us -> none  [to_all(): lax.all_to_all(jnp.broadcast_to(value[None], (length, *value.shape)), axi...]
    ppermute x5 -> x9, starting transfers between devices: 4.17 us -> 14.3 us  [swap_core(): return lax.ppermute(value, 'core', ring(NC, 1))]
    pallas_call x1 -> x3, Pallas kernels: 2.51 us -> 11.5 us  [the longest x1 6.16 us: call_first(): pl.pallas_call(first_kernel, out_shape=(jax.ShapeDtypeStruct((SLAB, 2048)...]
    all_to_all x1 -> x2, starting transfers between devices: 5.83 us -> 13.5 us  [the longest x1 8.8 us: on_device(): arrived = lax.all_to_all(field_part, ('z', 'x'), 0, 0, tiled=True)]
    all_to_all x1 -> x2, waiting for transfers between devices: 6.44 us -> 13.1 us  [the longest x1 6.56 us: on_device(): arrived = lax.all_to_all(field_part, ('z', 'x'), 0, 0, tiled=True)]
    unnamed x20 -> x14, local copies, waits for them, and re-layouts: 6.39 us -> 0.03 us
    all_to_all x1, waiting for transfers between devices: 7.12 us -> 1.49 us  [on_device(): lax.all_to_all(weights, ('z', 'x'), 0, 0, tiled=True).reshape(32, 1024)]
  transfers between devices with their start and end apart: 18 -> 23, of which waited for: 12 -> 12; matrix products, arithmetic and copies ran while one was open for 6% -> 1% of each run, Pallas kernels for 2% -> 5%
where the time goes in v3:
time: 156 us; the launch traced here: 155 us
  waiting for transfers between devices  57.2 us (37%)
  starting transfers between devices  52.8 us (34%)
  Pallas kernels  27.1 us (17%)
  blocking collectives  15.4 us (10%)
    ppermute x3, waiting for transfers between devices, on_device(): other = lax.ppermute(mine, ('y', 'core'), PAIRS)  19.2 us
    all_to_all x1, blocking collectives, on_device(): back = lax.all_to_all(blocks, ('y', 'core'), 0, 0, tiled=True)  15.4 us
    ppermute x9, starting transfers between devices, swap_core(): return lax.ppermute(value, 'core', ring(NC, 1))  14.3 us
    pallas_call x3, Pallas kernels, call_term(): pl.pallas_call(kernel, out_shape=out_shape, in_specs=[spec(pltpu.VMEM)] *...  12.3 us
    ppermute x1, waiting for transfers between devices, on_device(): part = lax.ppermute(part, 'y', ring(NY, 2))  11.1 us
    all_to_all x1, starting transfers between devices, on_device(): arrived = lax.all_to_all(field_part, ('z', 'x'), 0, 0, tiled=True)  8.8 us
    all_to_all x1, starting transfers between devices, on_device(): lax.all_to_all(weights, ('z', 'x'), 0, 0, tiled=True).reshape(32, 1024)  8.73 us
    ppermute x3, waiting for transfers between devices, on_device(): others = [lax.ppermute(orb, 'y', ring(NY, -j)) for j in (1, 2, 3)]  7.68 us
  transfers between devices with their start and end apart: 23, of which 12 were waited for; matrix products, arithmetic and copies ran while one was open for 1% of the time, Pallas kernels for 5%

profile of v3, /device:TPU:1, one launch (start us, length us, event | category | flops | bytes accessed | tf_op | source)
XLA Modules:
  0.0 155.4 jit_solution(14004090770497109096)
XLA Ops:
  0.7 3.3 %collective-permute-start.4 = (bf16[2048,512]{1,0:T(8,128)(2,1)}, bf16[2048,512]{1,0:T(8,128)(2,1)S(1)}, u32[]{:S(2)}, u32[]{:S(2)}) collective-permute-start(bf16[2048,512]{1,0:T(8,128)(2,1)} %refs_0_.1), channel_id=1, source_target_pairs={{0,1},{1,0},{2,3},{3,2},{4,5},{5,4},{6,7},{7,6},{8,9},{9,8},{10,11... | collective-permute-start | bytes 6291464 | tf_op jit(solution)/shard_map/ppermute | solution.py:31
  3.9 0.0 collective-permute-start.2
  3.9 2.2 %collective-permute-start.1 = (bf16[400,256]{1,0:T(8,128)(2,1)}, bf16[400,256]{1,0:T(8,128)(2,1)S(1)}, u32[]{:S(2)}, u32[]{:S(2)}) collective-permute-start(bf16[400,256]{1,0:T(8,128)(2,1)} %bitcast.6), channel_id=1, source_target_pairs={{0,4},{2,6},{4,0},{6,2},{1,5},{3,7},{5,1},{7,3},{8,12},{10,14},{12... | collective-permute-start | bytes 614408 | tf_op jit(solution)/shard_map/ppermute | solution.py:326
  6.1 1.1 collective-permute-start
  7.2 1.7 %start.1 = (bf16[512,512]{1,0:T(8,128)(2,1)S(1)}, bf16[1024,512]{1,0:T(8,128)(2,1)S(1)}, bf16[400,400]{1,0:T(8,128)(2,1)S(1)}, bf16[400,256]{1,0:T(8,128)(2,1)S(1)}, bf16[400,512]{1,0:T(8,128)(2,1)S(1)}) custom-call(bf16[2048,512]{1,0:T(8,128)(2,1)} %refs_0_.1, bf16[400,400]{1,0:T(8,128)(2,1)} %bitcast.10, bf16[400,256]{1,0:T(8,128)(2,1)} %bitcast.8, ...), custom_call_target="tpu_custom_call" | custom-call | tf_op jit(solution)/shard_map/start/pallas_call | solution.py:75
  9.0 3.4 %collective-permute-done.2.o3 = bf16[400,256]{1,0:T(8,128)(2,1)S(1)} collective-permute-done((bf16[400,256]{1,0:T(8,128)(2,1)}, bf16[400,256]{1,0:T(8,128)(2,1)S(1)}, u32[]{:S(2)}, u32[]{:S(2)}) %collective-permute-start.2) | collective-permute-done | bytes 204832 | tf_op jit(solution)/shard_map/ppermute | solution.py:326
  12.4 3.5 %collective-permute-done.1.o2 = bf16[400,256]{1,0:T(8,128)(2,1)S(1)} collective-permute-done((bf16[400,256]{1,0:T(8,128)(2,1)}, bf16[400,256]{1,0:T(8,128)(2,1)S(1)}, u32[]{:S(2)}, u32[]{:S(2)}) %collective-permute-start.1) | collective-permute-done | bytes 204832 | tf_op jit(solution)/shard_map/ppermute | solution.py:326
  15.9 0.8 collective-permute-done.o1
  16.6 1.2 collective-permute-start.9
  17.8 1.5 collective-permute-start.5
  19.4 11.1 %collective-permute-done.9.refs_2_ = bf16[512,512]{1,0:T(8,128)(2,1)} collective-permute-done((bf16[512,512]{1,0:T(8,128)(2,1)S(1)}, bf16[512,512]{1,0:T(8,128)(2,1)}, u32[]{:S(2)}, u32[]{:S(2)}) %collective-permute-start.9) | collective-permute-done | bytes 524320 | tf_op jit(solution)/shard_map/ppermute | solution.py:331
  30.5 0.7 collective-permute-start.12
  31.2 2.5 %collective-permute-start.11 = (bf16[512,512]{1,0:T(8,128)(2,1)}, bf16[512,512]{1,0:T(8,128)(2,1)}, u32[]{:S(2)}, u32[]{:S(2)}) collective-permute-start(bf16[512,512]{1,0:T(8,128)(2,1)} %collective-permute-done.9.refs_2_), channel_id=1, source_target_pairs={{0,16},{8,24},{16,0},{24,8},{1,17},{9,25},{17,1},{25,9},{2,18},{10... | collective-permute-start | bytes 1572872 | tf_op jit(solution)/shard_map/ppermute | solution.py:342
  33.6 1.2 collective-permute-start.10
  34.8 0.0 collective-permute-done.5.occ_par
  34.8 1.7 %collective-permute-start.7 = (bf16[512,256]{1,0:T(8,128)(2,1)S(1)}, bf16[512,256]{1,0:T(8,128)(2,1)S(1)}, u32[]{:S(2)}, u32[]{:S(2)}) collective-permute-start(bf16[512,256]{1,0:T(8,128)(2,1)S(1)} %copy-done.2), channel_id=1, source_target_pairs={{0,4},{2,6},{4,0},{6,2},{1,5},{3,7},{5,1},{7,3},{8,12},{10,14},{12... | collective-permute-start | bytes 786440 | tf_op jit(solution)/shard_map/ppermute | solution.py:332
  36.5 3.2 %collective-permute-start.6 = (bf16[512,256]{1,0:T(8,128)(2,1)S(1)}, bf16[512,256]{1,0:T(8,128)(2,1)}, u32[]{:S(2)}, u32[]{:S(2)}) collective-permute-start(bf16[512,256]{1,0:T(8,128)(2,1)S(1)} %copy-done.2), channel_id=1, source_target_pairs={{0,1},{1,0},{2,3},{3,2},{4,5},{5,4},{6,7},{7,6},{8,9},{9,8},{10,11... | collective-permute-start | bytes 786440 | tf_op jit(solution)/shard_map/ppermute | solution.py:31
  39.7 2.4 %head.1 = f32[32,1,1024]{2,1,0:T(1,128)} custom-call(bf16[400,400]{1,0:T(8,128)(2,1)S(1)} %get-tuple-element.28.inv, bf16[400,256]{1,0:T(8,128)(2,1)S(1)} %get-tuple-element.29.o0, bf16[400,256]{1,0:T(8,128)(2,1)S(1)} %collective-permute-done.o1, bf16[400,256]{1,0:T(8,128)(2,1)S(1)} %collective-permute-done.1.o2, ...), custom_call_target="tpu_custom_call" | custom-call | tf_op jit(solution)/shard_map/head/pallas_call | solution.py:111
  42.2 8.7 %all-to-all-start = ((f32[32,1,1024]{2,1,0:T(1,128)}), f32[32,1,1024]{2,1,0:T(1,128)S(1)}, u32[]{:S(2)}, u32[]{:S(2)}) async-start(f32[32,1,1024]{2,1,0:T(1,128)} %head.1), calls=%async_computation | async-start | bytes 262144 | tf_op jit(solution)/shard_map/all_to_all | solution.py:338
  50.9 0.4 collective-permute-start.8
  51.3 0.2 collective-permute-start.13
  51.5 0.3 collective-permute-start.16
  51.8 3.6 %collective-permute-done.11.refs_4_ = bf16[512,512]{1,0:T(8,128)(2,1)} collective-permute-done((bf16[512,512]{1,0:T(8,128)(2,1)}, bf16[512,512]{1,0:T(8,128)(2,1)}, u32[]{:S(2)}, u32[]{:S(2)}) %collective-permute-start.11) | collective-permute-done | bytes 524320 | tf_op jit(solution)/shard_map/ppermute | solution.py:342
  55.4 3.3 %collective-permute-start.15 = (bf16[512,512]{1,0:T(8,128)(2,1)}, bf16[512,512]{1,0:T(8,128)(2,1)}, u32[]{:S(2)}, u32[]{:S(2)}) collective-permute-start(bf16[512,512]{1,0:T(8,128)(2,1)} %collective-permute-done.11.refs_4_), channel_id=1, source_target_pairs={{0,1},{1,0},{2,3},{3,2},{4,5},{5,4},{6,7},{7,6},{8,9},{9,8},{10,11... | collective-permute-start | bytes 1572872 | tf_op jit(solution)/shard_map/ppermute | solution.py:31
  58.7 0.7 collective-permute-start.14
  59.4 1.5 all-to-all-done
  60.8 1.3 fusion
  62.2 0.7 broadcast_in_dim.2
  62.9 4.7 %all-to-all-start.1 = ((f32[8,32,256]{2,1,0:T(8,128)}), f32[8,32,256]{2,1,0:T(8,128)S(1)}, u32[]{:S(2)}, u32[]{:S(2)}) async-start(f32[8,32,256]{2,1,0:T(8,128)} %broadcast_in_dim.2), calls=%async_computation.1 | async-start | bytes 524288 | tf_op jit(solution)/shard_map/all_to_all | solution.py:35
  67.6 6.5 %all-to-all-done.1.bias_ref = f32[8,32,256]{2,1,0:T(8,128)S(1)} async-done(((f32[8,32,256]{2,1,0:T(8,128)}), f32[8,32,256]{2,1,0:T(8,128)S(1)}, u32[]{:S(2)}, u32[]{:S(2)}) %all-to-all-start.1) | async-done | bytes 262176 | tf_op jit(solution)/shard_map/all_to_all | solution.py:35
  74.1 3.6 %field.1 = (f32[32,256]{1,0:T(8,128)}, bf16[32,4,512]{2,1,0:T(4,128)(2,1)}) custom-call(f32[8,32,256]{2,1,0:T(8,128)S(1)} %all-to-all-done.1.bias_ref, f32[32,256]{1,0:T(8,128)S(1)} %copy-done.3, bf16[512,256]{1,0:T(8,128)(2,1)S(1)} %copy-done.2, bf16[512,256]{1,0:T(8,128)(2,1)} %collective-permute-done.6.c1, ...), custom_call_target="tpu_custom_call" | custom-call | tf_op jit(solution)/shard_map/field/pallas_call | solution.py:141
  77.7 8.8 %all-to-all-start.2 = ((bf16[32,4,512]{2,1,0:T(4,128)(2,1)}), bf16[32,4,512]{2,1,0:T(4,128)(2,1)S(1)}, u32[]{:S(2)}, u32[]{:S(2)}) async-start(bf16[32,4,512]{2,1,0:T(4,128)(2,1)} %get-tuple-element.32), calls=%async_computation.2 | async-start | bytes 262144 | tf_op jit(solution)/shard_map/all_to_all | solution.py:352
  86.5 0.2 slabs.1
  86.7 1.4 collective-permute-start.3
  88.1 1.1 collective-permute-done.3.par
  89.3 6.6 %all-to-all-done.2.arrived_ref = bf16[32,4,512]{2,1,0:T(4,128)(2,1)S(1)} async-done(((bf16[32,4,512]{2,1,0:T(4,128)(2,1)}), bf16[32,4,512]{2,1,0:T(4,128)(2,1)S(1)}, u32[]{:S(2)}, u32[]{:S(2)}) %all-to-all-start.2) | async-done | bytes 131104 | tf_op jit(solution)/shard_map/all_to_all | solution.py:352
  95.9 6.2 %first.1 = (bf16[104,2048]{1,0:T(8,128)(2,1)S(1)}, f32[4,512]{1,0:T(4,128)S(1)}, bf16[4,2048,512]{2,1,0:T(8,128)(2,1)S(1)}) custom-call(bf16[104,2048]{1,0:T(8,128)(2,1)S(1)} %join.1.term_ref.refs_2_, bf16[32,4,512]{2,1,0:T(4,128)(2,1)S(1)} %all-to-all-done.2.arrived_ref, bf16[2048,512]{1,0:T(8,128)(2,1)} %refs_0_.1, bf16[2048,512]{1,0:T(8,128)(2,1)} %copy-done, ...), custom_call_target="tpu_custom_call" | custom-call | tf_op jit(solution)/shard_map/first/pallas_call | solution.py:250
  102.0 2.8 %collective-permute-start.17 = (bf16[104,2048]{1,0:T(8,128)(2,1)S(1)}, bf16[104,2048]{1,0:T(8,128)(2,1)S(1)}, u32[]{:S(2)}, u32[]{:S(2)}) collective-permute-start(bf16[104,2048]{1,0:T(8,128)(2,1)S(1)} %get-tuple-element.34.refs_0_), channel_id=1, source_target_pairs={{0,7},{1,2},{2,1},{3,4},{4,3},{5,6},{6,5},{7,0},{8,15},{9,10},{10,... | collective-permute-start | bytes 1277960 | tf_op jit(solution)/shard_map/ppermute | solution.py:359
  104.8 6.1 %collective-permute-done.17.refs_1_ = bf16[104,2048]{1,0:T(8,128)(2,1)S(1)} collective-permute-done((bf16[104,2048]{1,0:T(8,128)(2,1)S(1)}, bf16[104,2048]{1,0:T(8,128)(2,1)S(1)}, u32[]{:S(2)}, u32[]{:S(2)}) %collective-permute-start.17) | collective-permute-done | bytes 426016 | tf_op jit(solution)/shard_map/ppermute | solution.py:359
  110.9 4.1 %term.3 = (bf16[104,2048]{1,0:T(8,128)(2,1)S(1)}, f32[104,2048]{1,0:T(8,128)S(1)}) custom-call(bf16[104,2048]{1,0:T(8,128)(2,1)S(1)} %get-tuple-element.34.refs_0_, bf16[104,2048]{1,0:T(8,128)(2,1)S(1)} %collective-permute-done.17.refs_1_, bf16[104,2048]{1,0:T(8,128)(2,1)S(1)} %join.1.term_ref.refs_2_, f32[4,512]{1,0:T(4,128)S(1)} %get-tuple-element.35.refs_3_.scales_ref, ...), custom_call_target="tpu_custom_call" | custom-call | tf_op jit(solution)/shard_map/term/pallas_call | solution.py:292
  115.0 1.5 collective-permute-start.18
  116.5 6.4 %collective-permute-done.18.refs_1_ = bf16[104,2048]{1,0:T(8,128)(2,1)S(1)} collective-permute-done((bf16[104,2048]{1,0:T(8,128)(2,1)S(1)}, bf16[104,2048]{1,0:T(8,128)(2,1)S(1)}, u32[]{:S(2)}, u32[]{:S(2)}) %collective-permute-start.18) | collective-permute-done | bytes 426016 | tf_op jit(solution)/shard_map/ppermute | solution.py:359
  122.9 4.1 %term.4 = (bf16[104,2048]{1,0:T(8,128)(2,1)S(1)}, f32[104,2048]{1,0:T(8,128)S(1)}) custom-call(bf16[104,2048]{1,0:T(8,128)(2,1)S(1)} %get-tuple-element.37.refs_0_, bf16[104,2048]{1,0:T(8,128)(2,1)S(1)} %collective-permute-done.18.refs_1_, f32[104,2048]{1,0:T(8,128)S(1)} %get-tuple-element.38.refs_2_, f32[4,512]{1,0:T(4,128)S(1)} %get-tuple-element.35.refs_3_.scales_ref, ...), custom_call_target="tpu_custom_call" | custom-call | tf_op jit(solution)/shard_map/term/pallas_call | solution.py:292
  127.0 1.5 collective-permute-start.19
  128.5 6.7 %collective-permute-done.19.other_ref = bf16[104,2048]{1,0:T(8,128)(2,1)S(1)} collective-permute-done((bf16[104,2048]{1,0:T(8,128)(2,1)S(1)}, bf16[104,2048]{1,0:T(8,128)(2,1)S(1)}, u32[]{:S(2)}, u32[]{:S(2)}) %collective-permute-start.19) | collective-permute-done | bytes 426016 | tf_op jit(solution)/shard_map/ppermute | solution.py:365
  135.2 4.1 %term.5 = bf16[8,112,256]{2,1,0:T(8,128)(2,1)S(1)} custom-call(bf16[104,2048]{1,0:T(8,128)(2,1)S(1)} %get-tuple-element.39.mine_ref, bf16[104,2048]{1,0:T(8,128)(2,1)S(1)} %collective-permute-done.19.other_ref, f32[104,2048]{1,0:T(8,128)S(1)} %get-tuple-element.40.total_ref, f32[4,512]{1,0:T(4,128)S(1)} %get-tuple-element.35.refs_3_.scales_ref, ...), custom_call_target="tpu_custom_call" | custom-call | tf_op jit(solution)/shard_map/term/pallas_call | solution.py:292
  139.3 15.4 %all_to_all.20.back_ref = bf16[8,112,256]{2,1,0:T(8,128)(2,1)S(1)} all-to-all(bf16[8,112,256]{2,1,0:T(8,128)(2,1)S(1)} %term.5), channel_id=1, replica_groups=mesh['z'=8,'x'=4,'y'=4,'core'=2] {'y','core'}, dimensions={0} | all-to-all | bytes 917504 | tf_op jit(solution)/shard_map/all_to_all | solution.py:371
  154.7 0.7 end.1
  (25 shorter events, 0.1 us)
Async XLA Ops:
  0.6 17.2 %copy-start.6 = (bf16[400,512]{1,0:T(8,128)(2,1)S(1)}, bf16[400,512]{1,0:T(8,128)(2,1)}, u32[]{:S(2)}) copy-start(bf16[400,512]{1,0:T(8,128)(2,1)} %occ.1) | copy-start | bytes 1228804
  0.6 34.2 %copy-start.2 = (bf16[512,256]{1,0:T(8,128)(2,1)S(1)}, bf16[512,256]{1,0:T(8,128)(2,1)}, u32[]{:S(2)}) copy-start(bf16[512,256]{1,0:T(8,128)(2,1)} %c0.1) | copy-start | bytes 786436
  0.7 35.9 %collective-permute-start.4 = (bf16[2048,512]{1,0:T(8,128)(2,1)}, bf16[2048,512]{1,0:T(8,128)(2,1)S(1)}, u32[]{:S(2)}, u32[]{:S(2)}) collective-permute-start(bf16[2048,512]{1,0:T(8,128)(2,1)} %refs_0_.1), channel_id=1, source_target_pairs={{0,1},{1,0},{2,3},{3,2},{4,5},{5,4},{6,7},{7,6},{8,9},{9,8},{10,11... | collective-permute-start | bytes 6291464 | tf_op jit(solution)/shard_map/ppermute | solution.py:31
  3.9 8.4 %collective-permute-start.2 = (bf16[400,256]{1,0:T(8,128)(2,1)}, bf16[400,256]{1,0:T(8,128)(2,1)S(1)}, u32[]{:S(2)}, u32[]{:S(2)}) collective-permute-start(bf16[400,256]{1,0:T(8,128)(2,1)} %bitcast.5), channel_id=1, source_target_pairs={{0,2},{2,4},{4,6},{6,0},{1,3},{3,5},{5,7},{7,1},{8,10},{10,12},{12... | collective-permute-start | bytes 614408 | tf_op jit(solution)/shard_map/ppermute | solution.py:326
  3.9 11.9 %collective-permute-start.1 = (bf16[400,256]{1,0:T(8,128)(2,1)}, bf16[400,256]{1,0:T(8,128)(2,1)S(1)}, u32[]{:S(2)}, u32[]{:S(2)}) collective-permute-start(bf16[400,256]{1,0:T(8,128)(2,1)} %bitcast.6), channel_id=1, source_target_pairs={{0,4},{2,6},{4,0},{6,2},{1,5},{3,7},{5,1},{7,3},{8,12},{10,14},{12... | collective-permute-start | bytes 614408 | tf_op jit(solution)/shard_map/ppermute | solution.py:326
  6.1 10.5 %collective-permute-start = (bf16[400,256]{1,0:T(8,128)(2,1)}, bf16[400,256]{1,0:T(8,128)(2,1)S(1)}, u32[]{:S(2)}, u32[]{:S(2)}) collective-permute-start(bf16[400,256]{1,0:T(8,128)(2,1)} %bitcast.7), channel_id=1, source_target_pairs={{0,6},{2,0},{4,2},{6,4},{1,7},{3,1},{5,3},{7,5},{8,14},{10,8},{12,... | collective-permute-start | bytes 614408 | tf_op jit(solution)/shard_map/ppermute | solution.py:326
  16.6 13.9 %collective-permute-start.9 = (bf16[512,512]{1,0:T(8,128)(2,1)S(1)}, bf16[512,512]{1,0:T(8,128)(2,1)}, u32[]{:S(2)}, u32[]{:S(2)}) collective-permute-start(bf16[512,512]{1,0:T(8,128)(2,1)S(1)} %get-tuple-element.33), channel_id=1, source_target_pairs={{0,4},{2,6},{4,0},{6,2},{1,5},{3,7},{5,1},{7,3},{8,12},{10,14},{12... | collective-permute-start | bytes 1572872 | tf_op jit(solution)/shard_map/ppermute | solution.py:331
  17.8 16.9 %collective-permute-start.5 = (bf16[400,512]{1,0:T(8,128)(2,1)S(1)}, bf16[400,512]{1,0:T(8,128)(2,1)S(1)}, u32[]{:S(2)}, u32[]{:S(2)}) collective-permute-start(bf16[400,512]{1,0:T(8,128)(2,1)S(1)} %copy-done.6), channel_id=1, source_target_pairs={{0,1},{1,0},{2,3},{3,2},{4,5},{5,4},{6,7},{7,6},{8,9},{9,8},{10,11... | collective-permute-start | bytes 1228808 | tf_op jit(solution)/shard_map/ppermute | solution.py:31
  30.5 21.0 %collective-permute-start.12 = (bf16[512,512]{1,0:T(8,128)(2,1)}, bf16[512,512]{1,0:T(8,128)(2,1)}, u32[]{:S(2)}, u32[]{:S(2)}) collective-permute-start(bf16[512,512]{1,0:T(8,128)(2,1)} %collective-permute-done.9.refs_2_), channel_id=1, source_target_pairs={{0,8},{8,16},{16,24},{24,0},{1,9},{9,17},{17,25},{25,1},{2,10},{10... | collective-permute-start | bytes 1572872 | tf_op jit(solution)/shard_map/ppermute | solution.py:342
  31.2 24.2 %collective-permute-start.11 = (bf16[512,512]{1,0:T(8,128)(2,1)}, bf16[512,512]{1,0:T(8,128)(2,1)}, u32[]{:S(2)}, u32[]{:S(2)}) collective-permute-start(bf16[512,512]{1,0:T(8,128)(2,1)} %collective-permute-done.9.refs_2_), channel_id=1, source_target_pairs={{0,16},{8,24},{16,0},{24,8},{1,17},{9,25},{17,1},{25,9},{2,18},{10... | collective-permute-start | bytes 1572872 | tf_op jit(solution)/shard_map/ppermute | solution.py:342
  33.6 25.0 %collective-permute-start.10 = (bf16[512,512]{1,0:T(8,128)(2,1)}, bf16[512,512]{1,0:T(8,128)(2,1)}, u32[]{:S(2)}, u32[]{:S(2)}) collective-permute-start(bf16[512,512]{1,0:T(8,128)(2,1)} %collective-permute-done.9.refs_2_), channel_id=1, source_target_pairs={{0,24},{8,0},{16,8},{24,16},{1,25},{9,1},{17,9},{25,17},{2,26},{10... | collective-permute-start | bytes 1572872 | tf_op jit(solution)/shard_map/ppermute | solution.py:342
  34.8 16.1 %collective-permute-start.7 = (bf16[512,256]{1,0:T(8,128)(2,1)S(1)}, bf16[512,256]{1,0:T(8,128)(2,1)S(1)}, u32[]{:S(2)}, u32[]{:S(2)}) collective-permute-start(bf16[512,256]{1,0:T(8,128)(2,1)S(1)} %copy-done.2), channel_id=1, source_target_pairs={{0,4},{2,6},{4,0},{6,2},{1,5},{3,7},{5,1},{7,3},{8,12},{10,14},{12... | collective-permute-start | bytes 786440 | tf_op jit(solution)/shard_map/ppermute | solution.py:332
  36.5 5.7 %copy-start = (bf16[2048,512]{1,0:T(8,128)(2,1)}, bf16[2048,512]{1,0:T(8,128)(2,1)S(1)}, u32[]{:S(2)}) copy-start(bf16[2048,512]{1,0:T(8,128)(2,1)S(1)} %collective-permute-done.4.a_par.refs_1_) | copy-start | bytes 6291460
  36.5 14.8 %collective-permute-start.6 = (bf16[512,256]{1,0:T(8,128)(2,1)S(1)}, bf16[512,256]{1,0:T(8,128)(2,1)}, u32[]{:S(2)}, u32[]{:S(2)}) collective-permute-start(bf16[512,256]{1,0:T(8,128)(2,1)S(1)} %copy-done.2), channel_id=1, source_target_pairs={{0,1},{1,0},{2,3},{3,2},{4,5},{5,4},{6,7},{7,6},{8,9},{9,8},{10,11... | collective-permute-start | bytes 786440 | tf_op jit(solution)/shard_map/ppermute | solution.py:31
  39.7 34.4 %copy-start.3 = (f32[32,256]{1,0:T(8,128)S(1)}, f32[32,256]{1,0:T(8,128)}, u32[]{:S(2)}) copy-start(f32[32,256]{1,0:T(8,128)} %fields_ref.1) | copy-start | bytes 98308
  42.2 44.3 %copy-start.1 = (bf16[1,400,256]{2,1,0:T(8,128)(2,1)S(1)}, bf16[1,400,256]{2,1,0:T(8,128)(2,1)}, u32[]{:S(2)}) copy-start(bf16[1,400,256]{2,1,0:T(8,128)(2,1)} %param.6) | copy-start | bytes 614404
  42.2 18.7 %all-to-all-start = ((f32[32,1,1024]{2,1,0:T(1,128)}), f32[32,1,1024]{2,1,0:T(1,128)S(1)}, u32[]{:S(2)}, u32[]{:S(2)}) async-start(f32[32,1,1024]{2,1,0:T(1,128)} %head.1), calls=%async_computation | async-start | bytes 262144 | tf_op jit(solution)/shard_map/all_to_all | solution.py:338
  50.9 16.7 %collective-permute-start.8 = (bf16[512,256]{1,0:T(8,128)(2,1)S(1)}, bf16[512,256]{1,0:T(8,128)(2,1)S(1)}, u32[]{:S(2)}, u32[]{:S(2)}) collective-permute-start(bf16[512,256]{1,0:T(8,128)(2,1)S(1)} %collective-permute-done.7.c2), channel_id=1, source_target_pairs={{0,1},{1,0},{2,3},{3,2},{4,5},{5,4},{6,7},{7,6},{8,9},{9,8},{10,11... | collective-permute-start | bytes 786440 | tf_op jit(solution)/shard_map/ppermute | solution.py:31
  51.3 37.9 %collective-permute-start.13 = (bf16[512,512]{1,0:T(8,128)(2,1)}, bf16[512,512]{1,0:T(8,128)(2,1)S(1)}, u32[]{:S(2)}, u32[]{:S(2)}) collective-permute-start(bf16[512,512]{1,0:T(8,128)(2,1)} %collective-permute-done.9.refs_2_), channel_id=1, source_target_pairs={{0,1},{1,0},{2,3},{3,2},{4,5},{5,4},{6,7},{7,6},{8,9},{9,8},{10,11... | collective-permute-start | bytes 1572872 | tf_op jit(solution)/shard_map/ppermute | solution.py:31
  51.5 37.7 %collective-permute-start.16 = (bf16[512,512]{1,0:T(8,128)(2,1)}, bf16[512,512]{1,0:T(8,128)(2,1)S(1)}, u32[]{:S(2)}, u32[]{:S(2)}) collective-permute-start(bf16[512,512]{1,0:T(8,128)(2,1)} %collective-permute-done.12.refs_5_), channel_id=1, source_target_pairs={{0,1},{1,0},{2,3},{3,2},{4,5},{5,4},{6,7},{7,6},{8,9},{9,8},{10,11... | collective-permute-start | bytes 1572872 | tf_op jit(solution)/shard_map/ppermute | solution.py:31
  55.4 33.9 %collective-permute-start.15 = (bf16[512,512]{1,0:T(8,128)(2,1)}, bf16[512,512]{1,0:T(8,128)(2,1)}, u32[]{:S(2)}, u32[]{:S(2)}) collective-permute-start(bf16[512,512]{1,0:T(8,128)(2,1)} %collective-permute-done.11.refs_4_), channel_id=1, source_target_pairs={{0,1},{1,0},{2,3},{3,2},{4,5},{5,4},{6,7},{7,6},{8,9},{9,8},{10,11... | collective-permute-start | bytes 1572872 | tf_op jit(solution)/shard_map/ppermute | solution.py:31
  58.7 30.6 %collective-permute-start.14 = (bf16[512,512]{1,0:T(8,128)(2,1)}, bf16[512,512]{1,0:T(8,128)(2,1)}, u32[]{:S(2)}, u32[]{:S(2)}) collective-permute-start(bf16[512,512]{1,0:T(8,128)(2,1)} %collective-permute-done.10.refs_3_), channel_id=1, source_target_pairs={{0,1},{1,0},{2,3},{3,2},{4,5},{5,4},{6,7},{7,6},{8,9},{9,8},{10,11... | collective-permute-start | bytes 1572872 | tf_op jit(solution)/shard_map/ppermute | solution.py:31
  62.9 11.2 %all-to-all-start.1 = ((f32[8,32,256]{2,1,0:T(8,128)}), f32[8,32,256]{2,1,0:T(8,128)S(1)}, u32[]{:S(2)}, u32[]{:S(2)}) async-start(f32[8,32,256]{2,1,0:T(8,128)} %broadcast_in_dim.2), calls=%async_computation.1 | async-start | bytes 524288 | tf_op jit(solution)/shard_map/all_to_all | solution.py:35
  77.7 18.2 %all-to-all-start.2 = ((bf16[32,4,512]{2,1,0:T(4,128)(2,1)}), bf16[32,4,512]{2,1,0:T(4,128)(2,1)S(1)}, u32[]{:S(2)}, u32[]{:S(2)}) async-start(bf16[32,4,512]{2,1,0:T(4,128)(2,1)} %get-tuple-element.32), calls=%async_computation.2 | async-start | bytes 262144 | tf_op jit(solution)/shard_map/all_to_all | solution.py:352
  86.7 2.5 %collective-permute-start.3 = (bf16[104,1024]{1,0:T(8,128)(2,1)S(1)}, bf16[104,1024]{1,0:T(8,128)(2,1)S(1)}, u32[]{:S(2)}, u32[]{:S(2)}) collective-permute-start(bf16[104,1024]{1,0:T(8,128)(2,1)S(1)} %get-tuple-element.27), channel_id=1, source_target_pairs={{0,1},{1,0},{2,3},{3,2},{4,5},{5,4},{6,7},{7,6},{8,9},{9,8},{10,11... | collective-permute-start | bytes 638984 | tf_op jit(solution)/shard_map/ppermute | solution.py:31
  89.2 6.6 %copy-start.4 = (bf16[512,512]{1,0:T(8,128)(2,1)}, bf16[512,512]{1,0:T(8,128)(2,1)S(1)}, u32[]{:S(2)}) copy-start(bf16[512,512]{1,0:T(8,128)(2,1)S(1)} %collective-permute-done.13.refs_6_) | copy-start | bytes 1572868
  89.3 6.6 %copy-start.5 = (bf16[512,512]{1,0:T(8,128)(2,1)}, bf16[512,512]{1,0:T(8,128)(2,1)S(1)}, u32[]{:S(2)}) copy-start(bf16[512,512]{1,0:T(8,128)(2,1)S(1)} %collective-permute-done.16.refs_9_) | copy-start | bytes 1572868
  102.0 8.9 %collective-permute-start.17 = (bf16[104,2048]{1,0:T(8,128)(2,1)S(1)}, bf16[104,2048]{1,0:T(8,128)(2,1)S(1)}, u32[]{:S(2)}, u32[]{:S(2)}) collective-permute-start(bf16[104,2048]{1,0:T(8,128)(2,1)S(1)} %get-tuple-element.34.refs_0_), channel_id=1, source_target_pairs={{0,7},{1,2},{2,1},{3,4},{4,3},{5,6},{6,5},{7,0},{8,15},{9,10},{10,... | collective-permute-start | bytes 1277960 | tf_op jit(solution)/shard_map/ppermute | solution.py:359
  115.0 7.9 %collective-permute-start.18 = (bf16[104,2048]{1,0:T(8,128)(2,1)S(1)}, bf16[104,2048]{1,0:T(8,128)(2,1)S(1)}, u32[]{:S(2)}, u32[]{:S(2)}) collective-permute-start(bf16[104,2048]{1,0:T(8,128)(2,1)S(1)} %get-tuple-element.37.refs_0_), channel_id=1, source_target_pairs={{0,7},{1,2},{2,1},{3,4},{4,3},{5,6},{6,5},{7,0},{8,15},{9,10},{10,... | collective-permute-start | bytes 1277960 | tf_op jit(solution)/shard_map/ppermute | solution.py:359
  127.0 8.2 %collective-permute-start.19 = (bf16[104,2048]{1,0:T(8,128)(2,1)S(1)}, bf16[104,2048]{1,0:T(8,128)(2,1)S(1)}, u32[]{:S(2)}, u32[]{:S(2)}) collective-permute-start(bf16[104,2048]{1,0:T(8,128)(2,1)S(1)} %get-tuple-element.39.mine_ref), channel_id=1, source_target_pairs={{0,7},{1,2},{2,1},{3,4},{4,3},{5,6},{6,5},{7,0},{8,15},{9,10},{10,... | collective-permute-start | bytes 1277960 | tf_op jit(solution)/shard_map/ppermute | solution.py:365

commit v4 on v3

--- a/solution.py
+++ b/solution.py
@@ -13,6 +13,7 @@
 NZ, NX, NY, NC = 8, 4, 4, 2
 ROWS = 400
 SLAB = 104
+HALF = 1024
 PIECE = 56
 TILES = (0, 6, 12, 18, 25, 31, 37, 43, 50)
 VMEM_LIMIT = 12 * 2**20
@@ -75,14 +76,14 @@
     part, *rest = pl.pallas_call(
         start_kernel,
         out_shape=(
-            jax.ShapeDtypeStruct((512, 512), bf16),
+            pltpu.VMEM((512, 512), bf16),
             pltpu.VMEM((1024, 512), bf16),
             pltpu.VMEM((ROWS, ROWS), bf16),
             pltpu.VMEM((ROWS, 256), bf16),
             pltpu.VMEM((ROWS, 512), bf16),
         ),
         in_specs=[spec(pltpu.HBM)] * 4,
-        out_specs=(spec(pltpu.HBM),) + (spec(pltpu.VMEM),) * 4,
+        out_specs=(spec(pltpu.VMEM),) * 5,
         scratch_shapes=[pltpu.SemaphoreType.DMA((8,))],
         compiler_params=PARAMS,
         name="start",
@@ -182,14 +183,14 @@
     )(*cols)
 
 
-def join_kernel(own, par, term_ref):
+def join_kernel(own, par, *outs):
     c = lax.axis_index("core")
 
     def put(first, second):
         for y in range(4):
-            cols = slice(256 * y, 256 * y + 256)
-            term_ref[:, 512 * y : 512 * y + 256] = first[:, cols]
-            term_ref[:, 512 * y + 256 : 512 * y + 512] = second[:, cols]
+            cols, out, at = slice(256 * y, 256 * y + 256), outs[y // 2], 512 * (y % 2)
+            out[:, at : at + 256] = first[:, cols]
+            out[:, at + 256 : at + 512] = second[:, cols]
 
     pl.when(c == 0)(lambda: put(own, par))
     pl.when(c == 1)(lambda: put(par, own))
@@ -198,30 +199,39 @@
 def call_join(own, par):
     return pl.pallas_call(
         join_kernel,
-        out_shape=jax.ShapeDtypeStruct((SLAB, 2048), bf16),
+        out_shape=(jax.ShapeDtypeStruct((SLAB, HALF), bf16),) * 2,
         in_specs=[spec(pltpu.VMEM)] * 2,
-        out_specs=spec(pltpu.VMEM),
+        out_specs=(spec(pltpu.VMEM),) * 2,
         compiler_params=PARAMS,
         name="join",
     )(own, par)
 
 
-def one_term(term, scales_ref, order, interp_ref, wait=lambda b: None):
+def times(term, interp_ref, b, h):
+    rows = interp_ref[b, HALF * h : HALF * h + HALF, :]
+    return jnp.dot(term, rows, preferred_element_type=f32)
+
+
+def back(mixed, interp_ref, h):
     acc = None
     for b in range(4):
-        wait(b)
-        interp = interp_ref[b]
-        product = jnp.dot(term, interp, preferred_element_type=f32)
-        mixed = (product * (scales_ref[b : b + 1, :] / order)).astype(bf16)
-        part = lax.dot_general(
-            mixed, interp, (((1,), (1,)), ((), ())), preferred_element_type=f32
-        )
+        rows = interp_ref[b, HALF * h : HALF * h + HALF, :]
+        part = lax.dot_general(mixed[b], rows, (((1,), (1,)), ((), ())), preferred_element_type=f32)
         acc = part if acc is None else acc + part
     return acc
 
 
-def first_kernel(term_ref, arrived_ref, *refs):
-    near, far, (out_ref, scales_ref, interp_ref, sems) = refs[:2], (refs[2:6], refs[6:10]), refs[10:]
+def mix(product, scales_ref, b, order):
+    return (product * (scales_ref[b : b + 1, :] / order)).astype(bf16)
+
+
+def added(mine_ref, other_ref):
+    return (mine_ref[...].astype(f32) + other_ref[...].astype(f32)).astype(bf16)
+
+
+def first_kernel(term_0, term_1, arrived_ref, *refs):
+    near, far = refs[:2], (refs[2:6], refs[6:10])
+    mixed_ref, out_ref, scales_ref, interp_ref, sems = refs[10:]
     x = lax.axis_index("x")
     copies = [
         [pltpu.make_async_copy(a, interp_ref.at[b], sems.at[b])] for b, a in enumerate(near)
@@ -238,53 +248,79 @@
     for copy in sum(copies, []):
         copy.start()
     scales_ref[...] = jnp.sum(arrived_ref[...].astype(f32), axis=0)
-
-    def wait(b):
+    mixed = []
+    for b in range(4):
         for copy in copies[b]:
             copy.wait()
-
-    out_ref[...] = one_term(term_ref[...], scales_ref, 1, interp_ref, wait).astype(bf16)
-
-
-def call_first(term, arrived, parts):
-    mine, scales, halves = pl.pallas_call(
+        product = times(term_0[...], interp_ref, b, 0) + times(term_1[...], interp_ref, b, 1)
+        mixed.append(mix(product, scales_ref, b, 1))
+        mixed_ref[b] = mixed[b]
+    out_ref[...] = back(mixed, interp_ref, 0).astype(bf16)
+
+
+def call_first(terms, arrived, parts):
+    mixed, mine, scales, halves = pl.pallas_call(
         first_kernel,
         out_shape=(
-            jax.ShapeDtypeStruct((SLAB, 2048), bf16),
+            jax.ShapeDtypeStruct((4, SLAB, 512), bf16),
+            jax.ShapeDtypeStruct((SLAB, HALF), bf16),
             jax.ShapeDtypeStruct((4, 512), f32),
             pltpu.VMEM((4, 2048, 512), bf16),
         ),
-        in_specs=[spec(pltpu.VMEM)] * 2 + [spec(pltpu.HBM)] * 10,
-        out_specs=(spec(pltpu.VMEM),) * 3,
+        in_specs=[spec(pltpu.VMEM)] * 3 + [spec(pltpu.HBM)] * 6 + [spec(pl.ANY)] * 4,
+        out_specs=(spec(pltpu.VMEM),) * 4,
         scratch_shapes=[pltpu.SemaphoreType.DMA((2 + 2 * NX,))],
         compiler_params=PARAMS,
         name="first",
-    )(term, arrived, *in_hbm(*parts))
-    return mine, scales, pltpu.with_memory_space_constraint(halves, pltpu.VMEM)
-
-
-def next_kernel(order, mine_ref, other_ref, total_ref, scales_ref, interp_ref, out_ref, total_out):
-    term = (mine_ref[...].astype(f32) + other_ref[...].astype(f32)).astype(bf16)
+    )(*terms, arrived, *in_hbm(*parts[:6]), *parts[6:])
+    return mixed, mine, scales, pltpu.with_memory_space_constraint(halves, pltpu.VMEM)
+
+
+def begin_kernel(mine_ref, other_ref, total_ref, interp_ref, product_ref, total_out):
+    term = added(mine_ref, other_ref)
     total_out[...] = total_ref[...].astype(f32) + term.astype(f32)
-    out_ref[...] = one_term(term, scales_ref, order, interp_ref).astype(bf16)
-
-
-def last_kernel(mine_ref, other_ref, total_ref, scales_ref, interp_ref, out_ref):
+    for b in range(4):
+        product_ref[b] = times(term, interp_ref, b, 0)
+
+
+def middle_kernel(order, mine_ref, other_ref, total_ref, product_ref, scales_ref, interp_ref, *outs):
+    mixed_ref, out_ref, total_out = outs
+    term = added(mine_ref, other_ref)
+    total_out[...] = total_ref[...].astype(f32) + term.astype(f32)
+    mixed = []
+    for b in range(4):
+        product = product_ref[b] + times(term, interp_ref, b, 1)
+        mixed.append(mix(product, scales_ref, b, order))
+        mixed_ref[b] = mixed[b]
+    out_ref[...] = back(mixed, interp_ref, 0).astype(bf16)
+
+
+def finish_kernel(mixed_ref, interp_ref, out_ref):
+    mixed = [mixed_ref[b] for b in range(4)]
+    out_ref[...] = back(mixed, interp_ref, 1).astype(bf16)
+
+
+def last_kernel(mine_ref, other_ref, total_0, total_1, product_ref, scales_ref, interp_ref, out_ref):
     c = lax.axis_index("core")
-    term = (mine_ref[...].astype(f32) + other_ref[...].astype(f32)).astype(bf16)
-    total = total_ref[...] + term.astype(f32)
-    acc = one_term(term, scales_ref, TERMS, interp_ref)
+    term = added(mine_ref, other_ref)
+    totals = (total_0[...], total_1[...] + term.astype(f32))
+    mixed = [
+        mix(product_ref[b] + times(term, interp_ref, b, 1), scales_ref, b, TERMS)
+        for b in range(4)
+    ]
     low, high = slice(0, PIECE), slice(SLAB - PIECE, SLAB)
-
-    def put(keep, give):
-        kept = (acc[keep] + total[keep]).astype(bf16)
-        given = acc[give].astype(bf16)
-        for b in range(8):
-            out_ref[b, :PIECE, :] = kept[:, 256 * b : 256 * b + 256]
-            out_ref[b, PIECE:, :] = given[:, 256 * b : 256 * b + 256]
-
-    pl.when(c == 1)(lambda: put(low, high))
-    pl.when(c == 0)(lambda: put(high, low))
+    for h in range(2):
+        acc = back(mixed, interp_ref, h)
+
+        def put(keep, give, h=h, acc=acc):
+            kept = (acc[keep] + totals[h][keep]).astype(bf16)
+            given = acc[give].astype(bf16)
+            for b in range(4):
+                out_ref[4 * h + b, :PIECE, :] = kept[:, 256 * b : 256 * b + 256]
+                out_ref[4 * h + b, PIECE:, :] = given[:, 256 * b : 256 * b + 256]
+
+        pl.when(c == 1)(lambda put=put: put(low, high))
+        pl.when(c == 0)(lambda put=put: put(high, low))
 
 
 def call_term(kernel, out_shape, *args):
@@ -334,7 +370,7 @@
 
     weights = call_head(inv, [orb_v, *others], rows, a_par, occ, occ_par)
     mine, other = call_slabs([orb, *others])
-    term = call_join(mine, swap_core(other))
+    terms = call_join(mine, swap_core(other))
     all_weights = lax.all_to_all(weights, ("z", "x"), 0, 0, tiled=True).reshape(32, 1024)
 
     far = [part]
@@ -351,25 +387,36 @@
     )
     arrived = lax.all_to_all(field_part, ("z", "x"), 0, 0, tiled=True)
 
-    part_shape = jax.ShapeDtypeStruct((SLAB, 2048), bf16)
-    total_shape = jax.ShapeDtypeStruct((SLAB, 2048), f32)
-    total = term
-    mine, scales, halves = call_first(term, arrived, (interp, a_par, *far, *far_par))
-    for order in range(2, TERMS):
-        other = lax.ppermute(mine, ("y", "core"), PAIRS)
-        mine, total = call_term(
-            lambda *refs, order=order: next_kernel(order, *refs),
-            (part_shape, total_shape),
-            *(mine, other, total, scales, halves),
+    part_shape = jax.ShapeDtypeStruct((SLAB, HALF), bf16)
+    total_shape = jax.ShapeDtypeStruct((SLAB, HALF), f32)
+    mixed_shape = jax.ShapeDtypeStruct((4, SLAB, 512), bf16)
+    product_shape = jax.ShapeDtypeStruct((4, SLAB, 512), f32)
+    blocks_shape = jax.ShapeDtypeStruct((8, 2 * PIECE, 256), bf16)
+    totals = terms
+    mixed, mine_0, scales, interp_v = call_first(
+        terms, arrived, (interp, a_par, *far, *far_par)
+    )
+    for order in range(2, TERMS + 1):
+        other_0 = lax.ppermute(mine_0, ("y", "core"), PAIRS)
+        mine_1 = call_term(finish_kernel, part_shape, mixed, interp_v)
+        other_1 = lax.ppermute(mine_1, ("y", "core"), PAIRS)
+        product, total_0 = call_term(
+            begin_kernel, (product_shape, total_shape), mine_0, other_0, totals[0], interp_v
         )
-    other = lax.ppermute(mine, ("y", "core"), PAIRS)
+        if order < TERMS:
+            mixed, mine_0, total_1 = call_term(
+                lambda *refs, order=order: middle_kernel(order, *refs),
+                (mixed_shape, part_shape, total_shape),
+                *(mine_1, other_1, totals[1], product, scales, interp_v),
+            )
+            totals = (total_0, total_1)
     blocks = call_term(
         last_kernel,
-        jax.ShapeDtypeStruct((8, 2 * PIECE, 256), bf16),
-        *(mine, other, total, scales, halves),
+        blocks_shape,
+        *(mine_1, other_1, total_0, totals[1], product, scales, interp_v),
     )
-    back = lax.all_to_all(blocks, ("y", "core"), 0, 0, tiled=True)
-    return call_end(back), force_bias
+    returned = lax.all_to_all(blocks, ("y", "core"), 0, 0, tiled=True)
+    return call_end(returned), force_bias
 
 
 def solution(mesh):

time: 156 us -> 153 us (0.981)
  waiting for transfers between devices: 57.2 us -> 49.7 us
  local copies, waits for them, and re-layouts: 0.74 us -> 3.07 us
    ppermute x3 -> x6, waiting for transfers between devices: 19.2 us -> 12.4 us  [the longest x3 6.67 us: on_device(): other_0 = lax.ppermute(mine_0, ('y', 'core'), PAIRS)]
    unnamed x14 -> x16, local copies, waits for them, and re-layouts: 0.03 us -> 2.34 us
    pallas_call x3 -> x9, Pallas kernels: 12.3 us -> 14 us  [call_term(): pl.pallas_call(kernel, out_shape=out_shape, in_specs=[spec(pltpu.VMEM)] *...]
    ppermute x3 -> x6, starting transfers between devices: 5.79 us -> 6.93 us  [the longest x3 4.55 us: on_device(): other_0 = lax.ppermute(mine_0, ('y', 'core'), PAIRS)]
  transfers between devices with their start and end apart: 23 -> 26, of which waited for: 12 -> 15; matrix products, arithmetic and copies ran while one was open for 1% -> 1% of each run, Pallas kernels for 5% -> 9%
where the time goes in v4:
time: 153 us
  starting transfers between devices  54 us (35%)
  waiting for transfers between devices  49.7 us (32%)
  Pallas kernels  27.3 us (18%)
  blocking collectives  16.8 us (11%)
  local copies, waits for them, and re-layouts  3.07 us (2%)
    all_to_all x1, blocking collectives, on_device(): returned = lax.all_to_all(blocks, ('y', 'core'), 0, 0, tiled=True)  16.8 us
    ppermute x9, starting transfers between devices, swap_core(): return lax.ppermute(value, 'core', ring(NC, 1))  14.3 us
    pallas_call x9, Pallas kernels, call_term(): pl.pallas_call(kernel, out_shape=out_shape, in_specs=[spec(pltpu.VMEM)] *...  14 us
    ppermute x1, waiting for transfers between devices, on_device(): part = lax.ppermute(part, 'y', ring(NY, 2))  11.1 us
    all_to_all x1, starting transfers between devices, on_device(): arrived = lax.all_to_all(field_part, ('z', 'x'), 0, 0, tiled=True)  8.8 us
    all_to_all x1, starting transfers between devices, on_device(): lax.all_to_all(weights, ('z', 'x'), 0, 0, tiled=True).reshape(32, 1024)  8.73 us
    ppermute x3, waiting for transfers between devices, on_device(): others = [lax.ppermute(orb, 'y', ring(NY, -j)) for j in (1, 2, 3)]  7.68 us
    ppermute x3, waiting for transfers between devices, on_device(): other_0 = lax.ppermute(mine_0, ('y', 'core'), PAIRS)  6.67 us
  transfers between devices with their start and end apart: 26, of which 15 were waited for; matrix products, arithmetic and copies ran while one was open for 1% of the time, Pallas kernels for 9%

profile of v4, /device:TPU:1, one launch (start us, length us, event | category | flops | bytes accessed | tf_op | source)
XLA Modules:
  0.0 153.0 jit_solution(8071742133164078803)
XLA Ops:
  0.7 3.3 %collective-permute-start.4 = (bf16[2048,512]{1,0:T(8,128)(2,1)}, bf16[2048,512]{1,0:T(8,128)(2,1)S(1)}, u32[]{:S(2)}, u32[]{:S(2)}) collective-permute-start(bf16[2048,512]{1,0:T(8,128)(2,1)} %refs_0_.1), channel_id=1, source_target_pairs={{0,1},{1,0},{2,3},{3,2},{4,5},{5,4},{6,7},{7,6},{8,9},{9,8},{10,11... | collective-permute-start | bytes 6291464 | tf_op jit(solution)/shard_map/ppermute | solution.py:32
  3.9 2.2 %collective-permute-start.1 = (bf16[400,256]{1,0:T(8,128)(2,1)}, bf16[400,256]{1,0:T(8,128)(2,1)S(1)}, u32[]{:S(2)}, u32[]{:S(2)}) collective-permute-start(bf16[400,256]{1,0:T(8,128)(2,1)} %bitcast.6), channel_id=1, source_target_pairs={{0,4},{2,6},{4,0},{6,2},{1,5},{3,7},{5,1},{7,3},{8,12},{10,14},{12... | collective-permute-start | bytes 614408 | tf_op jit(solution)/shard_map/ppermute | solution.py:362
  6.1 1.1 collective-permute-start
  7.2 1.7 %start.1 = (bf16[512,512]{1,0:T(8,128)(2,1)S(1)}, bf16[1024,512]{1,0:T(8,128)(2,1)S(1)}, bf16[400,400]{1,0:T(8,128)(2,1)S(1)}, bf16[400,256]{1,0:T(8,128)(2,1)S(1)}, bf16[400,512]{1,0:T(8,128)(2,1)S(1)}) custom-call(bf16[2048,512]{1,0:T(8,128)(2,1)} %refs_0_.1, bf16[400,400]{1,0:T(8,128)(2,1)} %bitcast.10, bf16[400,256]{1,0:T(8,128)(2,1)} %bitcast.8, ...), custom_call_target="tpu_custom_call" | custom-call | tf_op jit(solution)/shard_map/start/pallas_call | solution.py:76
  9.0 3.4 %collective-permute-done.2.o3 = bf16[400,256]{1,0:T(8,128)(2,1)S(1)} collective-permute-done((bf16[400,256]{1,0:T(8,128)(2,1)}, bf16[400,256]{1,0:T(8,128)(2,1)S(1)}, u32[]{:S(2)}, u32[]{:S(2)}) %collective-permute-start.2) | collective-permute-done | bytes 204832 | tf_op jit(solution)/shard_map/ppermute | solution.py:362
  12.4 3.5 %collective-permute-done.1.o2 = bf16[400,256]{1,0:T(8,128)(2,1)S(1)} collective-permute-done((bf16[400,256]{1,0:T(8,128)(2,1)}, bf16[400,256]{1,0:T(8,128)(2,1)S(1)}, u32[]{:S(2)}, u32[]{:S(2)}) %collective-permute-start.1) | collective-permute-done | bytes 204832 | tf_op jit(solution)/shard_map/ppermute | solution.py:362
  15.9 0.8 collective-permute-done.o1
  16.6 1.2 collective-permute-start.9
  17.8 1.5 collective-permute-start.5
  19.4 11.1 %collective-permute-done.9.refs_2_ = bf16[512,512]{1,0:T(8,128)(2,1)} collective-permute-done((bf16[512,512]{1,0:T(8,128)(2,1)S(1)}, bf16[512,512]{1,0:T(8,128)(2,1)}, u32[]{:S(2)}, u32[]{:S(2)}) %collective-permute-start.9) | collective-permute-done | bytes 524320 | tf_op jit(solution)/shard_map/ppermute | solution.py:367
  31.2 2.5 %collective-permute-start.11 = (bf16[512,512]{1,0:T(8,128)(2,1)}, bf16[512,512]{1,0:T(8,128)(2,1)}, u32[]{:S(2)}, u32[]{:S(2)}) collective-permute-start(bf16[512,512]{1,0:T(8,128)(2,1)} %collective-permute-done.9.refs_2_), channel_id=1, source_target_pairs={{0,16},{8,24},{16,0},{24,8},{1,17},{9,25},{17,1},{25,9},{2,18},{10... | collective-permute-start | bytes 1572872 | tf_op jit(solution)/shard_map/ppermute | solution.py:378
  33.6 1.2 collective-permute-start.10
  34.8 1.7 %collective-permute-start.7 = (bf16[512,256]{1,0:T(8,128)(2,1)S(1)}, bf16[512,256]{1,0:T(8,128)(2,1)S(1)}, u32[]{:S(2)}, u32[]{:S(2)}) collective-permute-start(bf16[512,256]{1,0:T(8,128)(2,1)S(1)} %copy-done.2), channel_id=1, source_target_pairs={{0,4},{2,6},{4,0},{6,2},{1,5},{3,7},{5,1},{7,3},{8,12},{10,14},{12... | collective-permute-start | bytes 786440 | tf_op jit(solution)/shard_map/ppermute | solution.py:368
  36.5 3.2 %collective-permute-start.6 = (bf16[512,256]{1,0:T(8,128)(2,1)S(1)}, bf16[512,256]{1,0:T(8,128)(2,1)}, u32[]{:S(2)}, u32[]{:S(2)}) collective-permute-start(bf16[512,256]{1,0:T(8,128)(2,1)S(1)} %copy-done.2), channel_id=1, source_target_pairs={{0,1},{1,0},{2,3},{3,2},{4,5},{5,4},{6,7},{7,6},{8,9},{9,8},{10,11... | collective-permute-start | bytes 786440 | tf_op jit(solution)/shard_map/ppermute | solution.py:32
  39.7 2.4 %head.1 = f32[32,1,1024]{2,1,0:T(1,128)} custom-call(bf16[400,400]{1,0:T(8,128)(2,1)S(1)} %get-tuple-element.41.inv, bf16[400,256]{1,0:T(8,128)(2,1)S(1)} %get-tuple-element.42.o0, bf16[400,256]{1,0:T(8,128)(2,1)S(1)} %collective-permute-done.o1, bf16[400,256]{1,0:T(8,128)(2,1)S(1)} %collective-permute-done.1.o2, ...), custom_call_target="tpu_custom_call" | custom-call | tf_op jit(solution)/shard_map/head/pallas_call | solution.py:112
  42.2 8.7 %all-to-all-start = ((f32[32,1,1024]{2,1,0:T(1,128)}), f32[32,1,1024]{2,1,0:T(1,128)S(1)}, u32[]{:S(2)}, u32[]{:S(2)}) async-start(f32[32,1,1024]{2,1,0:T(1,128)} %head.1), calls=%async_computation | async-start | bytes 262144 | tf_op jit(solution)/shard_map/all_to_all | solution.py:374
  51.8 3.6 %collective-permute-done.11.refs_4_ = bf16[512,512]{1,0:T(8,128)(2,1)} collective-permute-done((bf16[512,512]{1,0:T(8,128)(2,1)}, bf16[512,512]{1,0:T(8,128)(2,1)}, u32[]{:S(2)}, u32[]{:S(2)}) %collective-permute-start.11) | collective-permute-done | bytes 524320 | tf_op jit(solution)/shard_map/ppermute | solution.py:378
  55.4 3.3 %collective-permute-start.15 = (bf16[512,512]{1,0:T(8,128)(2,1)}, bf16[512,512]{1,0:T(8,128)(2,1)S(1)}, u32[]{:S(2)}, u32[]{:S(2)}) collective-permute-start(bf16[512,512]{1,0:T(8,128)(2,1)} %collective-permute-done.11.refs_4_), channel_id=1, source_target_pairs={{0,1},{1,0},{2,3},{3,2},{4,5},{5,4},{6,7},{7,6},{8,9},{9,8},{10,11... | collective-permute-start | bytes 1572872 | tf_op jit(solution)/shard_map/ppermute | solution.py:32
  59.4 1.5 all-to-all-done
  60.9 1.3 fusion
  62.9 4.7 %all-to-all-start.1 = ((f32[8,32,256]{2,1,0:T(8,128)}), f32[8,32,256]{2,1,0:T(8,128)S(1)}, u32[]{:S(2)}, u32[]{:S(2)}) async-start(f32[8,32,256]{2,1,0:T(8,128)} %broadcast_in_dim.2), calls=%async_computation.1 | async-start | bytes 524288 | tf_op jit(solution)/shard_map/all_to_all | solution.py:36
  68.4 5.8 %all-to-all-done.1.bias_ref = f32[8,32,256]{2,1,0:T(8,128)S(1)} async-done(((f32[8,32,256]{2,1,0:T(8,128)}), f32[8,32,256]{2,1,0:T(8,128)S(1)}, u32[]{:S(2)}, u32[]{:S(2)}) %all-to-all-start.1) | async-done | bytes 262176 | tf_op jit(solution)/shard_map/all_to_all | solution.py:36
  74.1 0.9 copy-done.4
  75.1 3.0 %field.1 = (f32[32,256]{1,0:T(8,128)}, bf16[32,4,512]{2,1,0:T(4,128)(2,1)S(1)}) custom-call(f32[8,32,256]{2,1,0:T(8,128)S(1)} %all-to-all-done.1.bias_ref, f32[32,256]{1,0:T(8,128)S(1)} %copy-done.6, bf16[512,256]{1,0:T(8,128)(2,1)S(1)} %copy-done.2, bf16[512,256]{1,0:T(8,128)(2,1)} %collective-permute-done.6.c1, ...), custom_call_target="tpu_custom_call" | custom-call | tf_op jit(solution)/shard_map/field/pallas_call | solution.py:142
  78.8 8.8 %all-to-all-start.2 = ((bf16[32,4,512]{2,1,0:T(4,128)(2,1)}), bf16[32,4,512]{2,1,0:T(4,128)(2,1)S(1)}, u32[]{:S(2)}, u32[]{:S(2)}) async-start(bf16[32,4,512]{2,1,0:T(4,128)(2,1)} %copy-done.5), calls=%async_computation.2 | async-start | bytes 262144 | tf_op jit(solution)/shard_map/all_to_all | solution.py:388
  87.8 1.4 collective-permute-start.3
  89.2 1.1 collective-permute-done.3.par
  90.4 6.6 %all-to-all-done.2.arrived_ref = bf16[32,4,512]{2,1,0:T(4,128)(2,1)S(1)} async-done(((bf16[32,4,512]{2,1,0:T(4,128)(2,1)}), bf16[32,4,512]{2,1,0:T(4,128)(2,1)S(1)}, u32[]{:S(2)}, u32[]{:S(2)}) %all-to-all-start.2) | async-done | bytes 131104 | tf_op jit(solution)/shard_map/all_to_all | solution.py:388
  97.0 5.1 %first.1 = (bf16[4,104,512]{2,1,0:T(8,128)(2,1)S(1)}, bf16[104,1024]{1,0:T(8,128)(2,1)S(1)}, f32[4,512]{1,0:T(4,128)S(1)}, bf16[4,2048,512]{2,1,0:T(8,128)(2,1)S(1)}) custom-call(bf16[104,1024]{1,0:T(8,128)(2,1)S(1)} %get-tuple-element.39.term_0.total_ref, bf16[104,1024]{1,0:T(8,128)(2,1)S(1)} %get-tuple-element.40.term_1.refs_2_, ...), custom_call_target="tpu_custom_call" | custom-call | tf_op jit(solution)/shard_map/first/pallas_call | solution.py:262
  102.0 2.8 %collective-permute-start.18 = (bf16[104,1024]{1,0:T(8,128)(2,1)S(1)}, bf16[104,1024]{1,0:T(8,128)(2,1)S(1)}, u32[]{:S(2)}, u32[]{:S(2)}) collective-permute-start(bf16[104,1024]{1,0:T(8,128)(2,1)S(1)} %get-tuple-element.49.mine_ref), channel_id=1, source_target_pairs={{0,7},{1,2},{2,1},{3,4},{4,3},{5,6},{6,5},{7,0},{8,15},{9,10},{10,... | collective-permute-start | bytes 638984 | tf_op jit(solution)/shard_map/ppermute | solution.py:400
  104.8 1.4 term.9.refs_0_
  106.3 2.3 %collective-permute-done.18.other_ref = bf16[104,1024]{1,0:T(8,128)(2,1)S(1)} collective-permute-done((bf16[104,1024]{1,0:T(8,128)(2,1)S(1)}, bf16[104,1024]{1,0:T(8,128)(2,1)S(1)}, u32[]{:S(2)}, u32[]{:S(2)}) %collective-permute-start.18) | collective-permute-done | bytes 213024 | tf_op jit(solution)/shard_map/ppermute | solution.py:400
  108.6 0.7 term.10
  109.4 2.5 %collective-permute-done.17.refs_1_ = bf16[104,1024]{1,0:T(8,128)(2,1)S(1)} collective-permute-done((bf16[104,1024]{1,0:T(8,128)(2,1)S(1)}, bf16[104,1024]{1,0:T(8,128)(2,1)S(1)}, u32[]{:S(2)}, u32[]{:S(2)}) %collective-permute-start.17) | collective-permute-done | bytes 213024 | tf_op jit(solution)/shard_map/ppermute | solution.py:402
  111.9 2.0 %term.11 = (bf16[4,104,512]{2,1,0:T(8,128)(2,1)S(1)}, bf16[104,1024]{1,0:T(8,128)(2,1)S(1)}, f32[104,1024]{1,0:T(8,128)S(1)}) custom-call(bf16[104,1024]{1,0:T(8,128)(2,1)S(1)} %term.9.refs_0_, bf16[104,1024]{1,0:T(8,128)(2,1)S(1)} %collective-permute-done.17.refs_1_, bf16[104,1024]{1,0:T(8,128)(2,1)S(1)} %get-tuple-element.40.term_1.refs_2_, ...), custom_call_target="tpu_custom_call" | custom-call | tf_op jit(solution)/shard_map/term/pallas_call | solution.py:328
  114.5 1.4 term.12.refs_0_
  115.9 1.3 collective-permute-start.19
  117.2 2.3 %collective-permute-done.20.other_ref = bf16[104,1024]{1,0:T(8,128)(2,1)S(1)} collective-permute-done((bf16[104,1024]{1,0:T(8,128)(2,1)S(1)}, bf16[104,1024]{1,0:T(8,128)(2,1)S(1)}, u32[]{:S(2)}, u32[]{:S(2)}) %collective-permute-start.20) | collective-permute-done | bytes 213024 | tf_op jit(solution)/shard_map/ppermute | solution.py:400
  119.5 0.8 term.13
  120.3 1.3 collective-permute-done.19.refs_1_
  121.6 2.0 %term.14 = (bf16[4,104,512]{2,1,0:T(8,128)(2,1)S(1)}, bf16[104,1024]{1,0:T(8,128)(2,1)S(1)}, f32[104,1024]{1,0:T(8,128)S(1)}) custom-call(bf16[104,1024]{1,0:T(8,128)(2,1)S(1)} %term.12.refs_0_, bf16[104,1024]{1,0:T(8,128)(2,1)S(1)} %collective-permute-done.19.refs_1_, f32[104,1024]{1,0:T(8,128)S(1)} %get-tuple-element.53.refs_2_, ...), custom_call_target="tpu_custom_call" | custom-call | tf_op jit(solution)/shard_map/term/pallas_call | solution.py:328
  123.6 1.2 collective-permute-start.22
  124.8 1.4 term.15.mine_ref
  126.2 0.9 collective-permute-start.21
  127.2 2.0 %collective-permute-done.22.other_ref = bf16[104,1024]{1,0:T(8,128)(2,1)S(1)} collective-permute-done((bf16[104,1024]{1,0:T(8,128)(2,1)S(1)}, bf16[104,1024]{1,0:T(8,128)(2,1)S(1)}, u32[]{:S(2)}, u32[]{:S(2)}) %collective-permute-start.22) | collective-permute-done | bytes 213024 | tf_op jit(solution)/shard_map/ppermute | solution.py:400
  130.0 1.9 %collective-permute-done.21.other_ref = bf16[104,1024]{1,0:T(8,128)(2,1)S(1)} collective-permute-done((bf16[104,1024]{1,0:T(8,128)(2,1)S(1)}, bf16[104,1024]{1,0:T(8,128)(2,1)S(1)}, u32[]{:S(2)}, u32[]{:S(2)}) %collective-permute-start.21) | collective-permute-done | bytes 213024 | tf_op jit(solution)/shard_map/ppermute | solution.py:402
  131.9 3.5 %term.17 = bf16[8,112,256]{2,1,0:T(8,128)(2,1)S(1)} custom-call(bf16[104,1024]{1,0:T(8,128)(2,1)S(1)} %term.15.mine_ref, bf16[104,1024]{1,0:T(8,128)(2,1)S(1)} %collective-permute-done.21.other_ref, f32[104,1024]{1,0:T(8,128)S(1)} %get-tuple-element.60.total_0, f32[104,1024]{1,0:T(8,128)S(1)} %get-tuple-element.61.total_1, ...), custom_call_target="tpu_custom_call" | custom-call | tf_op jit(solution)/shard_map/term/pallas_call | solution.py:328
  135.4 16.8 %all_to_all.20.back_ref = bf16[8,112,256]{2,1,0:T(8,128)(2,1)S(1)} all-to-all(bf16[8,112,256]{2,1,0:T(8,128)(2,1)S(1)} %term.17), channel_id=1, replica_groups=mesh['z'=8,'x'=4,'y'=4,'core'=2] {'y','core'}, dimensions={0} | all-to-all | bytes 917504 | tf_op jit(solution)/shard_map/all_to_all | solution.py:418
  (39 shorter events, 6.8 us)
Async XLA Ops:
  0.6 17.2 %copy-start.7 = (bf16[400,512]{1,0:T(8,128)(2,1)S(1)}, bf16[400,512]{1,0:T(8,128)(2,1)}, u32[]{:S(2)}) copy-start(bf16[400,512]{1,0:T(8,128)(2,1)} %occ.1) | copy-start | bytes 1228804
  0.6 34.2 %copy-start.2 = (bf16[512,256]{1,0:T(8,128)(2,1)S(1)}, bf16[512,256]{1,0:T(8,128)(2,1)}, u32[]{:S(2)}) copy-start(bf16[512,256]{1,0:T(8,128)(2,1)} %c0.1) | copy-start | bytes 786436
  0.7 35.9 %collective-permute-start.4 = (bf16[2048,512]{1,0:T(8,128)(2,1)}, bf16[2048,512]{1,0:T(8,128)(2,1)S(1)}, u32[]{:S(2)}, u32[]{:S(2)}) collective-permute-start(bf16[2048,512]{1,0:T(8,128)(2,1)} %refs_0_.1), channel_id=1, source_target_pairs={{0,1},{1,0},{2,3},{3,2},{4,5},{5,4},{6,7},{7,6},{8,9},{9,8},{10,11... | collective-permute-start | bytes 6291464 | tf_op jit(solution)/shard_map/ppermute | solution.py:32
  3.9 8.4 %collective-permute-start.2 = (bf16[400,256]{1,0:T(8,128)(2,1)}, bf16[400,256]{1,0:T(8,128)(2,1)S(1)}, u32[]{:S(2)}, u32[]{:S(2)}) collective-permute-start(bf16[400,256]{1,0:T(8,128)(2,1)} %bitcast.5), channel_id=1, source_target_pairs={{0,2},{2,4},{4,6},{6,0},{1,3},{3,5},{5,7},{7,1},{8,10},{10,12},{12... | collective-permute-start | bytes 614408 | tf_op jit(solution)/shard_map/ppermute | solution.py:362
  3.9 11.9 %collective-permute-start.1 = (bf16[400,256]{1,0:T(8,128)(2,1)}, bf16[400,256]{1,0:T(8,128)(2,1)S(1)}, u32[]{:S(2)}, u32[]{:S(2)}) collective-permute-start(bf16[400,256]{1,0:T(8,128)(2,1)} %bitcast.6), channel_id=1, source_target_pairs={{0,4},{2,6},{4,0},{6,2},{1,5},{3,7},{5,1},{7,3},{8,12},{10,14},{12... | collective-permute-start | bytes 614408 | tf_op jit(solution)/shard_map/ppermute | solution.py:362
  6.1 10.5 %collective-permute-start = (bf16[400,256]{1,0:T(8,128)(2,1)}, bf16[400,256]{1,0:T(8,128)(2,1)S(1)}, u32[]{:S(2)}, u32[]{:S(2)}) collective-permute-start(bf16[400,256]{1,0:T(8,128)(2,1)} %bitcast.7), channel_id=1, source_target_pairs={{0,6},{2,0},{4,2},{6,4},{1,7},{3,1},{5,3},{7,5},{8,14},{10,8},{12,... | collective-permute-start | bytes 614408 | tf_op jit(solution)/shard_map/ppermute | solution.py:362
  16.6 13.9 %collective-permute-start.9 = (bf16[512,512]{1,0:T(8,128)(2,1)S(1)}, bf16[512,512]{1,0:T(8,128)(2,1)}, u32[]{:S(2)}, u32[]{:S(2)}) collective-permute-start(bf16[512,512]{1,0:T(8,128)(2,1)S(1)} %get-tuple-element.46), channel_id=1, source_target_pairs={{0,4},{2,6},{4,0},{6,2},{1,5},{3,7},{5,1},{7,3},{8,12},{10,14},{12... | collective-permute-start | bytes 1572872 | tf_op jit(solution)/shard_map/ppermute | solution.py:367
  17.8 16.9 %collective-permute-start.5 = (bf16[400,512]{1,0:T(8,128)(2,1)S(1)}, bf16[400,512]{1,0:T(8,128)(2,1)S(1)}, u32[]{:S(2)}, u32[]{:S(2)}) collective-permute-start(bf16[400,512]{1,0:T(8,128)(2,1)S(1)} %copy-done.7), channel_id=1, source_target_pairs={{0,1},{1,0},{2,3},{3,2},{4,5},{5,4},{6,7},{7,6},{8,9},{9,8},{10,11... | collective-permute-start | bytes 1228808 | tf_op jit(solution)/shard_map/ppermute | solution.py:32
  30.5 21.1 %collective-permute-start.12 = (bf16[512,512]{1,0:T(8,128)(2,1)}, bf16[512,512]{1,0:T(8,128)(2,1)}, u32[]{:S(2)}, u32[]{:S(2)}) collective-permute-start(bf16[512,512]{1,0:T(8,128)(2,1)} %collective-permute-done.9.refs_2_), channel_id=1, source_target_pairs={{0,8},{8,16},{16,24},{24,0},{1,9},{9,17},{17,25},{25,1},{2,10},{10... | collective-permute-start | bytes 1572872 | tf_op jit(solution)/shard_map/ppermute | solution.py:378
  31.2 24.2 %collective-permute-start.11 = (bf16[512,512]{1,0:T(8,128)(2,1)}, bf16[512,512]{1,0:T(8,128)(2,1)}, u32[]{:S(2)}, u32[]{:S(2)}) collective-permute-start(bf16[512,512]{1,0:T(8,128)(2,1)} %collective-permute-done.9.refs_2_), channel_id=1, source_target_pairs={{0,16},{8,24},{16,0},{24,8},{1,17},{9,25},{17,1},{25,9},{2,18},{10... | collective-permute-start | bytes 1572872 | tf_op jit(solution)/shard_map/ppermute | solution.py:378
  33.6 25.0 %collective-permute-start.10 = (bf16[512,512]{1,0:T(8,128)(2,1)}, bf16[512,512]{1,0:T(8,128)(2,1)}, u32[]{:S(2)}, u32[]{:S(2)}) collective-permute-start(bf16[512,512]{1,0:T(8,128)(2,1)} %collective-permute-done.9.refs_2_), channel_id=1, source_target_pairs={{0,24},{8,0},{16,8},{24,16},{1,25},{9,1},{17,9},{25,17},{2,26},{10... | collective-permute-start | bytes 1572872 | tf_op jit(solution)/shard_map/ppermute | solution.py:378
  34.8 16.1 %collective-permute-start.7 = (bf16[512,256]{1,0:T(8,128)(2,1)S(1)}, bf16[512,256]{1,0:T(8,128)(2,1)S(1)}, u32[]{:S(2)}, u32[]{:S(2)}) collective-permute-start(bf16[512,256]{1,0:T(8,128)(2,1)S(1)} %copy-done.2), channel_id=1, source_target_pairs={{0,4},{2,6},{4,0},{6,2},{1,5},{3,7},{5,1},{7,3},{8,12},{10,14},{12... | collective-permute-start | bytes 786440 | tf_op jit(solution)/shard_map/ppermute | solution.py:368
  36.5 5.7 %copy-start = (bf16[2048,512]{1,0:T(8,128)(2,1)}, bf16[2048,512]{1,0:T(8,128)(2,1)S(1)}, u32[]{:S(2)}) copy-start(bf16[2048,512]{1,0:T(8,128)(2,1)S(1)} %collective-permute-done.4.a_par.refs_1_) | copy-start | bytes 6291460
  36.5 14.8 %collective-permute-start.6 = (bf16[512,256]{1,0:T(8,128)(2,1)S(1)}, bf16[512,256]{1,0:T(8,128)(2,1)}, u32[]{:S(2)}, u32[]{:S(2)}) collective-permute-start(bf16[512,256]{1,0:T(8,128)(2,1)S(1)} %copy-done.2), channel_id=1, source_target_pairs={{0,1},{1,0},{2,3},{3,2},{4,5},{5,4},{6,7},{7,6},{8,9},{9,8},{10,11... | collective-permute-start | bytes 786440 | tf_op jit(solution)/shard_map/ppermute | solution.py:32
  39.7 34.4 %copy-start.6 = (f32[32,256]{1,0:T(8,128)S(1)}, f32[32,256]{1,0:T(8,128)}, u32[]{:S(2)}) copy-start(f32[32,256]{1,0:T(8,128)} %fields_ref.1) | copy-start | bytes 98308
  42.2 45.4 %copy-start.1 = (bf16[1,400,256]{2,1,0:T(8,128)(2,1)S(1)}, bf16[1,400,256]{2,1,0:T(8,128)(2,1)}, u32[]{:S(2)}) copy-start(bf16[1,400,256]{2,1,0:T(8,128)(2,1)} %param.6) | copy-start | bytes 614404
  42.2 18.7 %all-to-all-start = ((f32[32,1,1024]{2,1,0:T(1,128)}), f32[32,1,1024]{2,1,0:T(1,128)S(1)}, u32[]{:S(2)}, u32[]{:S(2)}) async-start(f32[32,1,1024]{2,1,0:T(1,128)} %head.1), calls=%async_computation | async-start | bytes 262144 | tf_op jit(solution)/shard_map/all_to_all | solution.py:374
  50.9 16.7 %collective-permute-start.8 = (bf16[512,256]{1,0:T(8,128)(2,1)S(1)}, bf16[512,256]{1,0:T(8,128)(2,1)S(1)}, u32[]{:S(2)}, u32[]{:S(2)}) collective-permute-start(bf16[512,256]{1,0:T(8,128)(2,1)S(1)} %collective-permute-done.7.c2), channel_id=1, source_target_pairs={{0,1},{1,0},{2,3},{3,2},{4,5},{5,4},{6,7},{7,6},{8,9},{9,8},{10,11... | collective-permute-start | bytes 786440 | tf_op jit(solution)/shard_map/ppermute | solution.py:32
  51.3 39.0 %collective-permute-start.13 = (bf16[512,512]{1,0:T(8,128)(2,1)}, bf16[512,512]{1,0:T(8,128)(2,1)S(1)}, u32[]{:S(2)}, u32[]{:S(2)}) collective-permute-start(bf16[512,512]{1,0:T(8,128)(2,1)} %collective-permute-done.9.refs_2_), channel_id=1, source_target_pairs={{0,1},{1,0},{2,3},{3,2},{4,5},{5,4},{6,7},{7,6},{8,9},{9,8},{10,11... | collective-permute-start | bytes 1572872 | tf_op jit(solution)/shard_map/ppermute | solution.py:32
  51.5 38.8 %collective-permute-start.16 = (bf16[512,512]{1,0:T(8,128)(2,1)}, bf16[512,512]{1,0:T(8,128)(2,1)S(1)}, u32[]{:S(2)}, u32[]{:S(2)}) collective-permute-start(bf16[512,512]{1,0:T(8,128)(2,1)} %collective-permute-done.12.refs_5_), channel_id=1, source_target_pairs={{0,1},{1,0},{2,3},{3,2},{4,5},{5,4},{6,7},{7,6},{8,9},{9,8},{10,11... | collective-permute-start | bytes 1572872 | tf_op jit(solution)/shard_map/ppermute | solution.py:32
  55.4 34.9 %collective-permute-start.15 = (bf16[512,512]{1,0:T(8,128)(2,1)}, bf16[512,512]{1,0:T(8,128)(2,1)S(1)}, u32[]{:S(2)}, u32[]{:S(2)}) collective-permute-start(bf16[512,512]{1,0:T(8,128)(2,1)} %collective-permute-done.11.refs_4_), channel_id=1, source_target_pairs={{0,1},{1,0},{2,3},{3,2},{4,5},{5,4},{6,7},{7,6},{8,9},{9,8},{10,11... | collective-permute-start | bytes 1572872 | tf_op jit(solution)/shard_map/ppermute | solution.py:32
  58.7 31.7 %collective-permute-start.14 = (bf16[512,512]{1,0:T(8,128)(2,1)}, bf16[512,512]{1,0:T(8,128)(2,1)}, u32[]{:S(2)}, u32[]{:S(2)}) collective-permute-start(bf16[512,512]{1,0:T(8,128)(2,1)} %collective-permute-done.10.refs_3_), channel_id=1, source_target_pairs={{0,1},{1,0},{2,3},{3,2},{4,5},{5,4},{6,7},{7,6},{8,9},{9,8},{10,11... | collective-permute-start | bytes 1572872 | tf_op jit(solution)/shard_map/ppermute | solution.py:32
  62.9 11.2 %all-to-all-start.1 = ((f32[8,32,256]{2,1,0:T(8,128)}), f32[8,32,256]{2,1,0:T(8,128)S(1)}, u32[]{:S(2)}, u32[]{:S(2)}) async-start(f32[8,32,256]{2,1,0:T(8,128)} %broadcast_in_dim.2), calls=%async_computation.1 | async-start | bytes 524288 | tf_op jit(solution)/shard_map/all_to_all | solution.py:36
  67.6 0.7 copy-start.3
  74.1 1.0 copy-start.4
  78.1 0.7 copy-start.5
  78.8 18.2 %all-to-all-start.2 = ((bf16[32,4,512]{2,1,0:T(4,128)(2,1)}), bf16[32,4,512]{2,1,0:T(4,128)(2,1)S(1)}, u32[]{:S(2)}, u32[]{:S(2)}) async-start(bf16[32,4,512]{2,1,0:T(4,128)(2,1)} %copy-done.5), calls=%async_computation.2 | async-start | bytes 262144 | tf_op jit(solution)/shard_map/all_to_all | solution.py:388
  87.8 2.5 %collective-permute-start.3 = (bf16[104,1024]{1,0:T(8,128)(2,1)S(1)}, bf16[104,1024]{1,0:T(8,128)(2,1)S(1)}, u32[]{:S(2)}, u32[]{:S(2)}) collective-permute-start(bf16[104,1024]{1,0:T(8,128)(2,1)S(1)} %get-tuple-element.38), channel_id=1, source_target_pairs={{0,1},{1,0},{2,3},{3,2},{4,5},{5,4},{6,7},{7,6},{8,9},{9,8},{10,11... | collective-permute-start | bytes 638984 | tf_op jit(solution)/shard_map/ppermute | solution.py:32
  102.0 6.6 %collective-permute-start.18 = (bf16[104,1024]{1,0:T(8,128)(2,1)S(1)}, bf16[104,1024]{1,0:T(8,128)(2,1)S(1)}, u32[]{:S(2)}, u32[]{:S(2)}) collective-permute-start(bf16[104,1024]{1,0:T(8,128)(2,1)S(1)} %get-tuple-element.49.mine_ref), channel_id=1, source_target_pairs={{0,7},{1,2},{2,1},{3,4},{4,3},{5,6},{6,5},{7,0},{8,15},{9,10},{10,... | collective-permute-start | bytes 638984 | tf_op jit(solution)/shard_map/ppermute | solution.py:400
  106.2 5.7 %collective-permute-start.17 = (bf16[104,1024]{1,0:T(8,128)(2,1)S(1)}, bf16[104,1024]{1,0:T(8,128)(2,1)S(1)}, u32[]{:S(2)}, u32[]{:S(2)}) collective-permute-start(bf16[104,1024]{1,0:T(8,128)(2,1)S(1)} %term.9.refs_0_), channel_id=1, source_target_pairs={{0,7},{1,2},{2,1},{3,4},{4,3},{5,6},{6,5},{7,0},{8,15},{9,10},{10,... | collective-permute-start | bytes 638984 | tf_op jit(solution)/shard_map/ppermute | solution.py:402
  113.9 5.7 %collective-permute-start.20 = (bf16[104,1024]{1,0:T(8,128)(2,1)S(1)}, bf16[104,1024]{1,0:T(8,128)(2,1)S(1)}, u32[]{:S(2)}, u32[]{:S(2)}) collective-permute-start(bf16[104,1024]{1,0:T(8,128)(2,1)S(1)} %get-tuple-element.54.mine_ref), channel_id=1, source_target_pairs={{0,7},{1,2},{2,1},{3,4},{4,3},{5,6},{6,5},{7,0},{8,15},{9,10},{10,... | collective-permute-start | bytes 638984 | tf_op jit(solution)/shard_map/ppermute | solution.py:400
  115.9 5.7 %collective-permute-start.19 = (bf16[104,1024]{1,0:T(8,128)(2,1)S(1)}, bf16[104,1024]{1,0:T(8,128)(2,1)S(1)}, u32[]{:S(2)}, u32[]{:S(2)}) collective-permute-start(bf16[104,1024]{1,0:T(8,128)(2,1)S(1)} %term.12.refs_0_), channel_id=1, source_target_pairs={{0,7},{1,2},{2,1},{3,4},{4,3},{5,6},{6,5},{7,0},{8,15},{9,10},{10,... | collective-permute-start | bytes 638984 | tf_op jit(solution)/shard_map/ppermute | solution.py:402
  123.6 5.6 %collective-permute-start.22 = (bf16[104,1024]{1,0:T(8,128)(2,1)S(1)}, bf16[104,1024]{1,0:T(8,128)(2,1)S(1)}, u32[]{:S(2)}, u32[]{:S(2)}) collective-permute-start(bf16[104,1024]{1,0:T(8,128)(2,1)S(1)} %get-tuple-element.58.mine_ref), channel_id=1, source_target_pairs={{0,7},{1,2},{2,1},{3,4},{4,3},{5,6},{6,5},{7,0},{8,15},{9,10},{10,... | collective-permute-start | bytes 638984 | tf_op jit(solution)/shard_map/ppermute | solution.py:400
  126.2 5.7 %collective-permute-start.21 = (bf16[104,1024]{1,0:T(8,128)(2,1)S(1)}, bf16[104,1024]{1,0:T(8,128)(2,1)S(1)}, u32[]{:S(2)}, u32[]{:S(2)}) collective-permute-start(bf16[104,1024]{1,0:T(8,128)(2,1)S(1)} %term.15.mine_ref), channel_id=1, source_target_pairs={{0,7},{1,2},{2,1},{3,4},{4,3},{5,6},{6,5},{7,0},{8,15},{9,10},{10,... | collective-permute-start | bytes 638984 | tf_op jit(solution)/shard_map/ppermute | solution.py:402

commit v5 on v4

--- a/solution.py
+++ b/solution.py
@@ -125,16 +125,18 @@
         bias = bias + bias_ref[k]
     force_ref[...] = bias
     coeff = time_root * (fields_ref[...] - bias)
-    parts = [
-        lax.dot_general(
-            coeff,
-            c[...].astype(f32),
-            (((1,), (1,)), ((), ())),
-            precision=lax.Precision.HIGHEST,
-            preferred_element_type=f32,
+    coeff = jnp.concatenate([coeff[31 - w : 32 - w] for w in range(32)], 0)
+    split = []
+    for _ in range(3):
+        split.append(coeff.astype(bf16))
+        coeff = coeff - split[-1].astype(f32)
+    split = jnp.concatenate(split, 0)
+    parts = []
+    for c in (c0, c1, c2, c3):
+        part = lax.dot_general(
+            split, c[...], (((1,), (1,)), ((), ())), preferred_element_type=f32
         )
-        for c in (c0, c1, c2, c3)
-    ]
+        parts.append(part[:32] + (part[32:64] + part[64:]))
     out_ref[...] = jnp.concatenate(parts, 1).reshape(32, 4, 512).astype(bf16)
 
 
@@ -385,7 +387,9 @@
     force_bias, field_part = call_field(
         biases, fields, (chol_factors, chol_par, chol_far, chol_far_par)
     )
-    arrived = lax.all_to_all(field_part, ("z", "x"), 0, 0, tiled=True)
+    arrived = lax.all_to_all(
+        field_part, ("z", "x"), 0, 0, tiled=True, axis_index_groups=[list(range(31, -1, -1))]
+    )
 
     part_shape = jax.ShapeDtypeStruct((SLAB, HALF), bf16)
     total_shape = jax.ShapeDtypeStruct((SLAB, HALF), f32)

time: 153 us -> 150 us (0.980)
  waiting for transfers between devices: 49.7 us -> 45.6 us
  starting transfers between devices: 54 us -> 55.8 us
    all_to_all x1, waiting for transfers between devices: 6.59 us -> 2.49 us  [on_device(): lax.all_to_all(field_part, ('z', 'x'), 0, 0, tiled=True, axis_index_group...]
  transfers between devices with their start and end apart: 26 -> 26, of which waited for: 15 -> 15; matrix products, arithmetic and copies ran while one was open for 1% -> 1% of each run, Pallas kernels for 9% -> 8%
where the time goes in v5:
time: 150 us; the launch traced here: 149 us
  starting transfers between devices  55.8 us (37%)
  waiting for transfers between devices  45.6 us (30%)
  Pallas kernels  26.1 us (17%)
  blocking collectives  16.8 us (11%)
  local copies, waits for them, and re-layouts  3.07 us (2%)
    all_to_all x1, blocking collectives, on_device(): returned = lax.all_to_all(blocks, ('y', 'core'), 0, 0, tiled=True)  16.8 us
    ppermute x9, starting transfers between devices, swap_core(): return lax.ppermute(value, 'core', ring(NC, 1))  14.5 us
    pallas_call x9, Pallas kernels, call_term(): pl.pallas_call(kernel, out_shape=out_shape, in_specs=[spec(pltpu.VMEM)] *...  14 us
    ppermute x1, waiting for transfers between devices, on_device(): part = lax.ppermute(part, 'y', ring(NY, 2))  11.1 us
    all_to_all x1, starting transfers between devices, on_device(): lax.all_to_all(field_part, ('z', 'x'), 0, 0, tiled=True, axis_index_group...  10.3 us
    all_to_all x1, starting transfers between devices, on_device(): lax.all_to_all(weights, ('z', 'x'), 0, 0, tiled=True).reshape(32, 1024)  8.73 us
    ppermute x3, waiting for transfers between devices, on_device(): others = [lax.ppermute(orb, 'y', ring(NY, -j)) for j in (1, 2, 3)]  7.68 us
    ppermute x3, waiting for transfers between devices, on_device(): other_0 = lax.ppermute(mine_0, ('y', 'core'), PAIRS)  6.45 us
  transfers between devices with their start and end apart: 26, of which 15 were waited for; matrix products, arithmetic and copies ran while one was open for 1% of the time, Pallas kernels for 8%

profile of v5, /device:TPU:1, one launch (start us, length us, event | category | flops | bytes accessed | tf_op | source)
XLA Modules:
  0.0 149.5 jit_solution(17848659913219756102)
XLA Ops:
  0.7 3.3 %collective-permute-start.4 = (bf16[2048,512]{1,0:T(8,128)(2,1)}, bf16[2048,512]{1,0:T(8,128)(2,1)S(1)}, u32[]{:S(2)}, u32[]{:S(2)}) collective-permute-start(bf16[2048,512]{1,0:T(8,128)(2,1)} %refs_0_.1), channel_id=1, source_target_pairs={{0,1},{1,0},{2,3},{3,2},{4,5},{5,4},{6,7},{7,6},{8,9},{9,8},{10,11... | collective-permute-start | bytes 6291464 | tf_op jit(solution)/shard_map/ppermute | solution.py:32
  3.9 2.2 %collective-permute-start.1 = (bf16[400,256]{1,0:T(8,128)(2,1)}, bf16[400,256]{1,0:T(8,128)(2,1)S(1)}, u32[]{:S(2)}, u32[]{:S(2)}) collective-permute-start(bf16[400,256]{1,0:T(8,128)(2,1)} %bitcast.6), channel_id=1, source_target_pairs={{0,4},{2,6},{4,0},{6,2},{1,5},{3,7},{5,1},{7,3},{8,12},{10,14},{12... | collective-permute-start | bytes 614408 | tf_op jit(solution)/shard_map/ppermute | solution.py:364
  6.1 1.1 collective-permute-start
  7.2 1.7 %start.1 = (bf16[512,512]{1,0:T(8,128)(2,1)S(1)}, bf16[1024,512]{1,0:T(8,128)(2,1)S(1)}, bf16[400,400]{1,0:T(8,128)(2,1)S(1)}, bf16[400,256]{1,0:T(8,128)(2,1)S(1)}, bf16[400,512]{1,0:T(8,128)(2,1)S(1)}) custom-call(bf16[2048,512]{1,0:T(8,128)(2,1)} %refs_0_.1, bf16[400,400]{1,0:T(8,128)(2,1)} %bitcast.10, bf16[400,256]{1,0:T(8,128)(2,1)} %bitcast.8, ...), custom_call_target="tpu_custom_call" | custom-call | tf_op jit(solution)/shard_map/start/pallas_call | solution.py:76
  9.0 3.4 %collective-permute-done.2.o3 = bf16[400,256]{1,0:T(8,128)(2,1)S(1)} collective-permute-done((bf16[400,256]{1,0:T(8,128)(2,1)}, bf16[400,256]{1,0:T(8,128)(2,1)S(1)}, u32[]{:S(2)}, u32[]{:S(2)}) %collective-permute-start.2) | collective-permute-done | bytes 204832 | tf_op jit(solution)/shard_map/ppermute | solution.py:364
  12.4 3.5 %collective-permute-done.1.o2 = bf16[400,256]{1,0:T(8,128)(2,1)S(1)} collective-permute-done((bf16[400,256]{1,0:T(8,128)(2,1)}, bf16[400,256]{1,0:T(8,128)(2,1)S(1)}, u32[]{:S(2)}, u32[]{:S(2)}) %collective-permute-start.1) | collective-permute-done | bytes 204832 | tf_op jit(solution)/shard_map/ppermute | solution.py:364
  15.9 0.8 collective-permute-done.o1
  16.6 1.2 collective-permute-start.9
  17.8 1.5 %collective-permute-start.5 = (bf16[400,512]{1,0:T(8,128)(2,1)S(1)}, bf16[400,512]{1,0:T(8,128)(2,1)S(1)}, u32[]{:S(2)}, u32[]{:S(2)}) collective-permute-start(bf16[400,512]{1,0:T(8,128)(2,1)S(1)} %copy-done.7), channel_id=1, source_target_pairs={{0,1},{1,0},{2,3},{3,2},{4,5},{5,4},{6,7},{7,6},{8,9},{9,8},{10,11... | collective-permute-start | bytes 1228808 | tf_op jit(solution)/shard_map/ppermute | solution.py:32
  19.4 11.1 %collective-permute-done.9.refs_2_ = bf16[512,512]{1,0:T(8,128)(2,1)} collective-permute-done((bf16[512,512]{1,0:T(8,128)(2,1)S(1)}, bf16[512,512]{1,0:T(8,128)(2,1)}, u32[]{:S(2)}, u32[]{:S(2)}) %collective-permute-start.9) | collective-permute-done | bytes 524320 | tf_op jit(solution)/shard_map/ppermute | solution.py:369
  31.2 2.5 %collective-permute-start.11 = (bf16[512,512]{1,0:T(8,128)(2,1)}, bf16[512,512]{1,0:T(8,128)(2,1)}, u32[]{:S(2)}, u32[]{:S(2)}) collective-permute-start(bf16[512,512]{1,0:T(8,128)(2,1)} %collective-permute-done.9.refs_2_), channel_id=1, source_target_pairs={{0,16},{8,24},{16,0},{24,8},{1,17},{9,25},{17,1},{25,9},{2,18},{10... | collective-permute-start | bytes 1572872 | tf_op jit(solution)/shard_map/ppermute | solution.py:380
  33.6 1.2 collective-permute-start.10
  34.8 1.7 %collective-permute-start.7 = (bf16[512,256]{1,0:T(8,128)(2,1)S(1)}, bf16[512,256]{1,0:T(8,128)(2,1)S(1)}, u32[]{:S(2)}, u32[]{:S(2)}) collective-permute-start(bf16[512,256]{1,0:T(8,128)(2,1)S(1)} %copy-done.2), channel_id=1, source_target_pairs={{0,4},{2,6},{4,0},{6,2},{1,5},{3,7},{5,1},{7,3},{8,12},{10,14},{12... | collective-permute-start | bytes 786440 | tf_op jit(solution)/shard_map/ppermute | solution.py:370
  36.5 3.2 %collective-permute-start.6 = (bf16[512,256]{1,0:T(8,128)(2,1)S(1)}, bf16[512,256]{1,0:T(8,128)(2,1)}, u32[]{:S(2)}, u32[]{:S(2)}) collective-permute-start(bf16[512,256]{1,0:T(8,128)(2,1)S(1)} %copy-done.2), channel_id=1, source_target_pairs={{0,1},{1,0},{2,3},{3,2},{4,5},{5,4},{6,7},{7,6},{8,9},{9,8},{10,11... | collective-permute-start | bytes 786440 | tf_op jit(solution)/shard_map/ppermute | solution.py:32
  39.7 2.4 %head.1 = f32[32,1,1024]{2,1,0:T(1,128)} custom-call(bf16[400,400]{1,0:T(8,128)(2,1)S(1)} %get-tuple-element.41.inv, bf16[400,256]{1,0:T(8,128)(2,1)S(1)} %get-tuple-element.42.o0, bf16[400,256]{1,0:T(8,128)(2,1)S(1)} %collective-permute-done.o1, bf16[400,256]{1,0:T(8,128)(2,1)S(1)} %collective-permute-done.1.o2, ...), custom_call_target="tpu_custom_call" | custom-call | tf_op jit(solution)/shard_map/head/pallas_call | solution.py:112
  42.2 8.7 %all-to-all-start = ((f32[32,1,1024]{2,1,0:T(1,128)}), f32[32,1,1024]{2,1,0:T(1,128)S(1)}, u32[]{:S(2)}, u32[]{:S(2)}) async-start(f32[32,1,1024]{2,1,0:T(1,128)} %head.1), calls=%async_computation | async-start | bytes 262144 | tf_op jit(solution)/shard_map/all_to_all | solution.py:376
  51.8 3.6 %collective-permute-done.11.refs_4_ = bf16[512,512]{1,0:T(8,128)(2,1)} collective-permute-done((bf16[512,512]{1,0:T(8,128)(2,1)}, bf16[512,512]{1,0:T(8,128)(2,1)}, u32[]{:S(2)}, u32[]{:S(2)}) %collective-permute-start.11) | collective-permute-done | bytes 524320 | tf_op jit(solution)/shard_map/ppermute | solution.py:380
  55.4 3.3 %collective-permute-start.15 = (bf16[512,512]{1,0:T(8,128)(2,1)}, bf16[512,512]{1,0:T(8,128)(2,1)S(1)}, u32[]{:S(2)}, u32[]{:S(2)}) collective-permute-start(bf16[512,512]{1,0:T(8,128)(2,1)} %collective-permute-done.11.refs_4_), channel_id=1, source_target_pairs={{0,1},{1,0},{2,3},{3,2},{4,5},{5,4},{6,7},{7,6},{8,9},{9,8},{10,11... | collective-permute-start | bytes 1572872 | tf_op jit(solution)/shard_map/ppermute | solution.py:32
  59.4 1.5 %all-to-all-done = f32[32,1,1024]{2,1,0:T(1,128)S(1)} async-done(((f32[32,1,1024]{2,1,0:T(1,128)}), f32[32,1,1024]{2,1,0:T(1,128)S(1)}, u32[]{:S(2)}, u32[]{:S(2)}) %all-to-all-start) | async-done | bytes 131104 | tf_op jit(solution)/shard_map/all_to_all | solution.py:376
  60.9 1.3 fusion
  62.9 4.7 %all-to-all-start.1 = ((f32[8,32,256]{2,1,0:T(8,128)}), f32[8,32,256]{2,1,0:T(8,128)S(1)}, u32[]{:S(2)}, u32[]{:S(2)}) async-start(f32[8,32,256]{2,1,0:T(8,128)} %broadcast_in_dim.2), calls=%async_computation.1 | async-start | bytes 524288 | tf_op jit(solution)/shard_map/all_to_all | solution.py:36
  68.4 5.8 %all-to-all-done.1.bias_ref = f32[8,32,256]{2,1,0:T(8,128)S(1)} async-done(((f32[8,32,256]{2,1,0:T(8,128)}), f32[8,32,256]{2,1,0:T(8,128)S(1)}, u32[]{:S(2)}, u32[]{:S(2)}) %all-to-all-start.1) | async-done | bytes 262176 | tf_op jit(solution)/shard_map/all_to_all | solution.py:36
  74.1 0.9 copy-done.4
  75.1 1.8 %field.1 = (f32[32,256]{1,0:T(8,128)}, bf16[32,4,512]{2,1,0:T(4,128)(2,1)S(1)}) custom-call(f32[8,32,256]{2,1,0:T(8,128)S(1)} %all-to-all-done.1.bias_ref, f32[32,256]{1,0:T(8,128)S(1)} %copy-done.6, bf16[512,256]{1,0:T(8,128)(2,1)S(1)} %copy-done.2, bf16[512,256]{1,0:T(8,128)(2,1)} %collective-permute-done.6.c1, ...), custom_call_target="tpu_custom_call" | custom-call | tf_op jit(solution)/shard_map/field/pallas_call | solution.py:144
  77.6 10.3 %all-to-all-start.2 = ((bf16[32,4,512]{2,1,0:T(4,128)(2,1)}), bf16[32,4,512]{2,1,0:T(4,128)(2,1)S(1)}, u32[]{:S(2)}, u32[]{:S(2)}) async-start(bf16[32,4,512]{2,1,0:T(4,128)(2,1)} %copy-done.5), calls=%async_computation.2 | async-start | bytes 262144 | tf_op jit(solution)/shard_map/all_to_all | solution.py:390
  88.0 1.7 %collective-permute-start.3 = (bf16[104,1024]{1,0:T(8,128)(2,1)S(1)}, bf16[104,1024]{1,0:T(8,128)(2,1)S(1)}, u32[]{:S(2)}, u32[]{:S(2)}) collective-permute-start(bf16[104,1024]{1,0:T(8,128)(2,1)S(1)} %get-tuple-element.38), channel_id=1, source_target_pairs={{0,1},{1,0},{2,3},{3,2},{4,5},{5,4},{6,7},{7,6},{8,9},{9,8},{10,11... | collective-permute-start | bytes 638984 | tf_op jit(solution)/shard_map/ppermute | solution.py:32
  89.7 1.1 collective-permute-done.3.par
  90.9 2.5 %all-to-all-done.2.arrived_ref = bf16[32,4,512]{2,1,0:T(4,128)(2,1)S(1)} async-done(((bf16[32,4,512]{2,1,0:T(4,128)(2,1)}), bf16[32,4,512]{2,1,0:T(4,128)(2,1)S(1)}, u32[]{:S(2)}, u32[]{:S(2)}) %all-to-all-start.2) | async-done | bytes 131104 | tf_op jit(solution)/shard_map/all_to_all | solution.py:390
  93.4 5.1 %first.1 = (bf16[4,104,512]{2,1,0:T(8,128)(2,1)S(1)}, bf16[104,1024]{1,0:T(8,128)(2,1)S(1)}, f32[4,512]{1,0:T(4,128)S(1)}, bf16[4,2048,512]{2,1,0:T(8,128)(2,1)S(1)}) custom-call(bf16[104,1024]{1,0:T(8,128)(2,1)S(1)} %get-tuple-element.39.term_0.total_ref, bf16[104,1024]{1,0:T(8,128)(2,1)S(1)} %get-tuple-element.40.term_1.refs_2_, ...), custom_call_target="tpu_custom_call" | custom-call | tf_op jit(solution)/shard_map/first/pallas_call | solution.py:264
  98.5 2.9 %collective-permute-start.18 = (bf16[104,1024]{1,0:T(8,128)(2,1)S(1)}, bf16[104,1024]{1,0:T(8,128)(2,1)S(1)}, u32[]{:S(2)}, u32[]{:S(2)}) collective-permute-start(bf16[104,1024]{1,0:T(8,128)(2,1)S(1)} %get-tuple-element.49.mine_ref), channel_id=1, source_target_pairs={{0,7},{1,2},{2,1},{3,4},{4,3},{5,6},{6,5},{7,0},{8,15},{9,10},{10,... | collective-permute-start | bytes 638984 | tf_op jit(solution)/shard_map/ppermute | solution.py:404
  101.3 1.4 term.9.refs_0_
  102.8 2.3 %collective-permute-done.18.other_ref = bf16[104,1024]{1,0:T(8,128)(2,1)S(1)} collective-permute-done((bf16[104,1024]{1,0:T(8,128)(2,1)S(1)}, bf16[104,1024]{1,0:T(8,128)(2,1)S(1)}, u32[]{:S(2)}, u32[]{:S(2)}) %collective-permute-start.18) | collective-permute-done | bytes 213024 | tf_op jit(solution)/shard_map/ppermute | solution.py:404
  105.2 0.7 term.10
  105.9 2.5 %collective-permute-done.17.refs_1_ = bf16[104,1024]{1,0:T(8,128)(2,1)S(1)} collective-permute-done((bf16[104,1024]{1,0:T(8,128)(2,1)S(1)}, bf16[104,1024]{1,0:T(8,128)(2,1)S(1)}, u32[]{:S(2)}, u32[]{:S(2)}) %collective-permute-start.17) | collective-permute-done | bytes 213024 | tf_op jit(solution)/shard_map/ppermute | solution.py:406
  108.4 2.0 %term.11 = (bf16[4,104,512]{2,1,0:T(8,128)(2,1)S(1)}, bf16[104,1024]{1,0:T(8,128)(2,1)S(1)}, f32[104,1024]{1,0:T(8,128)S(1)}) custom-call(bf16[104,1024]{1,0:T(8,128)(2,1)S(1)} %term.9.refs_0_, bf16[104,1024]{1,0:T(8,128)(2,1)S(1)} %collective-permute-done.17.refs_1_, bf16[104,1024]{1,0:T(8,128)(2,1)S(1)} %get-tuple-element.40.term_1.refs_2_, ...), custom_call_target="tpu_custom_call" | custom-call | tf_op jit(solution)/shard_map/term/pallas_call | solution.py:330
  111.0 1.4 term.12.refs_0_
  112.4 1.3 collective-permute-start.19
  113.8 2.3 %collective-permute-done.20.other_ref = bf16[104,1024]{1,0:T(8,128)(2,1)S(1)} collective-permute-done((bf16[104,1024]{1,0:T(8,128)(2,1)S(1)}, bf16[104,1024]{1,0:T(8,128)(2,1)S(1)}, u32[]{:S(2)}, u32[]{:S(2)}) %collective-permute-start.20) | collective-permute-done | bytes 213024 | tf_op jit(solution)/shard_map/ppermute | solution.py:404
  116.1 0.8 term.13
  116.8 1.3 collective-permute-done.19.refs_1_
  118.1 2.0 %term.14 = (bf16[4,104,512]{2,1,0:T(8,128)(2,1)S(1)}, bf16[104,1024]{1,0:T(8,128)(2,1)S(1)}, f32[104,1024]{1,0:T(8,128)S(1)}) custom-call(bf16[104,1024]{1,0:T(8,128)(2,1)S(1)} %term.12.refs_0_, bf16[104,1024]{1,0:T(8,128)(2,1)S(1)} %collective-permute-done.19.refs_1_, f32[104,1024]{1,0:T(8,128)S(1)} %get-tuple-element.53.refs_2_, ...), custom_call_target="tpu_custom_call" | custom-call | tf_op jit(solution)/shard_map/term/pallas_call | solution.py:330
  120.2 1.0 collective-permute-start.22
  121.2 1.4 term.15.mine_ref
  122.6 1.2 collective-permute-start.21
  123.7 1.8 %collective-permute-done.22.other_ref = bf16[104,1024]{1,0:T(8,128)(2,1)S(1)} collective-permute-done((bf16[104,1024]{1,0:T(8,128)(2,1)S(1)}, bf16[104,1024]{1,0:T(8,128)(2,1)S(1)}, u32[]{:S(2)}, u32[]{:S(2)}) %collective-permute-start.22) | collective-permute-done | bytes 213024 | tf_op jit(solution)/shard_map/ppermute | solution.py:404
  126.3 2.1 %collective-permute-done.21.other_ref = bf16[104,1024]{1,0:T(8,128)(2,1)S(1)} collective-permute-done((bf16[104,1024]{1,0:T(8,128)(2,1)S(1)}, bf16[104,1024]{1,0:T(8,128)(2,1)S(1)}, u32[]{:S(2)}, u32[]{:S(2)}) %collective-permute-start.21) | collective-permute-done | bytes 213024 | tf_op jit(solution)/shard_map/ppermute | solution.py:406
  128.4 3.5 %term.17 = bf16[8,112,256]{2,1,0:T(8,128)(2,1)S(1)} custom-call(bf16[104,1024]{1,0:T(8,128)(2,1)S(1)} %term.15.mine_ref, bf16[104,1024]{1,0:T(8,128)(2,1)S(1)} %collective-permute-done.21.other_ref, f32[104,1024]{1,0:T(8,128)S(1)} %get-tuple-element.60.total_0, f32[104,1024]{1,0:T(8,128)S(1)} %get-tuple-element.61.total_1, ...), custom_call_target="tpu_custom_call" | custom-call | tf_op jit(solution)/shard_map/term/pallas_call | solution.py:330
  132.0 16.8 %all_to_all.20.back_ref = bf16[8,112,256]{2,1,0:T(8,128)(2,1)S(1)} all-to-all(bf16[8,112,256]{2,1,0:T(8,128)(2,1)S(1)} %term.17), channel_id=1, replica_groups=mesh['z'=8,'x'=4,'y'=4,'core'=2] {'y','core'}, dimensions={0} | all-to-all | bytes 917504 | tf_op jit(solution)/shard_map/all_to_all | solution.py:422
  (39 shorter events, 6.8 us)
Async XLA Ops:
  0.6 17.2 %copy-start.7 = (bf16[400,512]{1,0:T(8,128)(2,1)S(1)}, bf16[400,512]{1,0:T(8,128)(2,1)}, u32[]{:S(2)}) copy-start(bf16[400,512]{1,0:T(8,128)(2,1)} %occ.1) | copy-start | bytes 1228804
  0.6 34.2 %copy-start.2 = (bf16[512,256]{1,0:T(8,128)(2,1)S(1)}, bf16[512,256]{1,0:T(8,128)(2,1)}, u32[]{:S(2)}) copy-start(bf16[512,256]{1,0:T(8,128)(2,1)} %c0.1) | copy-start | bytes 786436
  0.7 35.9 %collective-permute-start.4 = (bf16[2048,512]{1,0:T(8,128)(2,1)}, bf16[2048,512]{1,0:T(8,128)(2,1)S(1)}, u32[]{:S(2)}, u32[]{:S(2)}) collective-permute-start(bf16[2048,512]{1,0:T(8,128)(2,1)} %refs_0_.1), channel_id=1, source_target_pairs={{0,1},{1,0},{2,3},{3,2},{4,5},{5,4},{6,7},{7,6},{8,9},{9,8},{10,11... | collective-permute-start | bytes 6291464 | tf_op jit(solution)/shard_map/ppermute | solution.py:32
  3.9 8.4 %collective-permute-start.2 = (bf16[400,256]{1,0:T(8,128)(2,1)}, bf16[400,256]{1,0:T(8,128)(2,1)S(1)}, u32[]{:S(2)}, u32[]{:S(2)}) collective-permute-start(bf16[400,256]{1,0:T(8,128)(2,1)} %bitcast.5), channel_id=1, source_target_pairs={{0,2},{2,4},{4,6},{6,0},{1,3},{3,5},{5,7},{7,1},{8,10},{10,12},{12... | collective-permute-start | bytes 614408 | tf_op jit(solution)/shard_map/ppermute | solution.py:364
  3.9 11.9 %collective-permute-start.1 = (bf16[400,256]{1,0:T(8,128)(2,1)}, bf16[400,256]{1,0:T(8,128)(2,1)S(1)}, u32[]{:S(2)}, u32[]{:S(2)}) collective-permute-start(bf16[400,256]{1,0:T(8,128)(2,1)} %bitcast.6), channel_id=1, source_target_pairs={{0,4},{2,6},{4,0},{6,2},{1,5},{3,7},{5,1},{7,3},{8,12},{10,14},{12... | collective-permute-start | bytes 614408 | tf_op jit(solution)/shard_map/ppermute | solution.py:364
  6.1 10.5 %collective-permute-start = (bf16[400,256]{1,0:T(8,128)(2,1)}, bf16[400,256]{1,0:T(8,128)(2,1)S(1)}, u32[]{:S(2)}, u32[]{:S(2)}) collective-permute-start(bf16[400,256]{1,0:T(8,128)(2,1)} %bitcast.7), channel_id=1, source_target_pairs={{0,6},{2,0},{4,2},{6,4},{1,7},{3,1},{5,3},{7,5},{8,14},{10,8},{12,... | collective-permute-start | bytes 614408 | tf_op jit(solution)/shard_map/ppermute | solution.py:364
  16.6 13.9 %collective-permute-start.9 = (bf16[512,512]{1,0:T(8,128)(2,1)S(1)}, bf16[512,512]{1,0:T(8,128)(2,1)}, u32[]{:S(2)}, u32[]{:S(2)}) collective-permute-start(bf16[512,512]{1,0:T(8,128)(2,1)S(1)} %get-tuple-element.46), channel_id=1, source_target_pairs={{0,4},{2,6},{4,0},{6,2},{1,5},{3,7},{5,1},{7,3},{8,12},{10,14},{12... | collective-permute-start | bytes 1572872 | tf_op jit(solution)/shard_map/ppermute | solution.py:369
  17.8 16.9 %collective-permute-start.5 = (bf16[400,512]{1,0:T(8,128)(2,1)S(1)}, bf16[400,512]{1,0:T(8,128)(2,1)S(1)}, u32[]{:S(2)}, u32[]{:S(2)}) collective-permute-start(bf16[400,512]{1,0:T(8,128)(2,1)S(1)} %copy-done.7), channel_id=1, source_target_pairs={{0,1},{1,0},{2,3},{3,2},{4,5},{5,4},{6,7},{7,6},{8,9},{9,8},{10,11... | collective-permute-start | bytes 1228808 | tf_op jit(solution)/shard_map/ppermute | solution.py:32
  30.5 21.1 %collective-permute-start.12 = (bf16[512,512]{1,0:T(8,128)(2,1)}, bf16[512,512]{1,0:T(8,128)(2,1)}, u32[]{:S(2)}, u32[]{:S(2)}) collective-permute-start(bf16[512,512]{1,0:T(8,128)(2,1)} %collective-permute-done.9.refs_2_), channel_id=1, source_target_pairs={{0,8},{8,16},{16,24},{24,0},{1,9},{9,17},{17,25},{25,1},{2,10},{10... | collective-permute-start | bytes 1572872 | tf_op jit(solution)/shard_map/ppermute | solution.py:380
  31.2 24.2 %collective-permute-start.11 = (bf16[512,512]{1,0:T(8,128)(2,1)}, bf16[512,512]{1,0:T(8,128)(2,1)}, u32[]{:S(2)}, u32[]{:S(2)}) collective-permute-start(bf16[512,512]{1,0:T(8,128)(2,1)} %collective-permute-done.9.refs_2_), channel_id=1, source_target_pairs={{0,16},{8,24},{16,0},{24,8},{1,17},{9,25},{17,1},{25,9},{2,18},{10... | collective-permute-start | bytes 1572872 | tf_op jit(solution)/shard_map/ppermute | solution.py:380
  33.6 25.0 %collective-permute-start.10 = (bf16[512,512]{1,0:T(8,128)(2,1)}, bf16[512,512]{1,0:T(8,128)(2,1)}, u32[]{:S(2)}, u32[]{:S(2)}) collective-permute-start(bf16[512,512]{1,0:T(8,128)(2,1)} %collective-permute-done.9.refs_2_), channel_id=1, source_target_pairs={{0,24},{8,0},{16,8},{24,16},{1,25},{9,1},{17,9},{25,17},{2,26},{10... | collective-permute-start | bytes 1572872 | tf_op jit(solution)/shard_map/ppermute | solution.py:380
  34.8 16.1 %collective-permute-start.7 = (bf16[512,256]{1,0:T(8,128)(2,1)S(1)}, bf16[512,256]{1,0:T(8,128)(2,1)S(1)}, u32[]{:S(2)}, u32[]{:S(2)}) collective-permute-start(bf16[512,256]{1,0:T(8,128)(2,1)S(1)} %copy-done.2), channel_id=1, source_target_pairs={{0,4},{2,6},{4,0},{6,2},{1,5},{3,7},{5,1},{7,3},{8,12},{10,14},{12... | collective-permute-start | bytes 786440 | tf_op jit(solution)/shard_map/ppermute | solution.py:370
  36.5 5.7 %copy-start = (bf16[2048,512]{1,0:T(8,128)(2,1)}, bf16[2048,512]{1,0:T(8,128)(2,1)S(1)}, u32[]{:S(2)}) copy-start(bf16[2048,512]{1,0:T(8,128)(2,1)S(1)} %collective-permute-done.4.a_par.refs_1_) | copy-start | bytes 6291460
  36.5 14.8 %collective-permute-start.6 = (bf16[512,256]{1,0:T(8,128)(2,1)S(1)}, bf16[512,256]{1,0:T(8,128)(2,1)}, u32[]{:S(2)}, u32[]{:S(2)}) collective-permute-start(bf16[512,256]{1,0:T(8,128)(2,1)S(1)} %copy-done.2), channel_id=1, source_target_pairs={{0,1},{1,0},{2,3},{3,2},{4,5},{5,4},{6,7},{7,6},{8,9},{9,8},{10,11... | collective-permute-start | bytes 786440 | tf_op jit(solution)/shard_map/ppermute | solution.py:32
  39.7 34.4 %copy-start.6 = (f32[32,256]{1,0:T(8,128)S(1)}, f32[32,256]{1,0:T(8,128)}, u32[]{:S(2)}) copy-start(f32[32,256]{1,0:T(8,128)} %fields_ref.1) | copy-start | bytes 98308
  42.2 45.7 %copy-start.1 = (bf16[1,400,256]{2,1,0:T(8,128)(2,1)S(1)}, bf16[1,400,256]{2,1,0:T(8,128)(2,1)}, u32[]{:S(2)}) copy-start(bf16[1,400,256]{2,1,0:T(8,128)(2,1)} %param.6) | copy-start | bytes 614404
  42.2 18.7 %all-to-all-start = ((f32[32,1,1024]{2,1,0:T(1,128)}), f32[32,1,1024]{2,1,0:T(1,128)S(1)}, u32[]{:S(2)}, u32[]{:S(2)}) async-start(f32[32,1,1024]{2,1,0:T(1,128)} %head.1), calls=%async_computation | async-start | bytes 262144 | tf_op jit(solution)/shard_map/all_to_all | solution.py:376
  50.9 16.7 %collective-permute-start.8 = (bf16[512,256]{1,0:T(8,128)(2,1)S(1)}, bf16[512,256]{1,0:T(8,128)(2,1)S(1)}, u32[]{:S(2)}, u32[]{:S(2)}) collective-permute-start(bf16[512,256]{1,0:T(8,128)(2,1)S(1)} %collective-permute-done.7.c2), channel_id=1, source_target_pairs={{0,1},{1,0},{2,3},{3,2},{4,5},{5,4},{6,7},{7,6},{8,9},{9,8},{10,11... | collective-permute-start | bytes 786440 | tf_op jit(solution)/shard_map/ppermute | solution.py:32
  51.3 39.5 %collective-permute-start.13 = (bf16[512,512]{1,0:T(8,128)(2,1)}, bf16[512,512]{1,0:T(8,128)(2,1)S(1)}, u32[]{:S(2)}, u32[]{:S(2)}) collective-permute-start(bf16[512,512]{1,0:T(8,128)(2,1)} %collective-permute-done.9.refs_2_), channel_id=1, source_target_pairs={{0,1},{1,0},{2,3},{3,2},{4,5},{5,4},{6,7},{7,6},{8,9},{9,8},{10,11... | collective-permute-start | bytes 1572872 | tf_op jit(solution)/shard_map/ppermute | solution.py:32
  51.5 39.3 %collective-permute-start.16 = (bf16[512,512]{1,0:T(8,128)(2,1)}, bf16[512,512]{1,0:T(8,128)(2,1)S(1)}, u32[]{:S(2)}, u32[]{:S(2)}) collective-permute-start(bf16[512,512]{1,0:T(8,128)(2,1)} %collective-permute-done.12.refs_5_), channel_id=1, source_target_pairs={{0,1},{1,0},{2,3},{3,2},{4,5},{5,4},{6,7},{7,6},{8,9},{9,8},{10,11... | collective-permute-start | bytes 1572872 | tf_op jit(solution)/shard_map/ppermute | solution.py:32
  55.4 35.5 %collective-permute-start.15 = (bf16[512,512]{1,0:T(8,128)(2,1)}, bf16[512,512]{1,0:T(8,128)(2,1)S(1)}, u32[]{:S(2)}, u32[]{:S(2)}) collective-permute-start(bf16[512,512]{1,0:T(8,128)(2,1)} %collective-permute-done.11.refs_4_), channel_id=1, source_target_pairs={{0,1},{1,0},{2,3},{3,2},{4,5},{5,4},{6,7},{7,6},{8,9},{9,8},{10,11... | collective-permute-start | bytes 1572872 | tf_op jit(solution)/shard_map/ppermute | solution.py:32
  58.7 32.2 %collective-permute-start.14 = (bf16[512,512]{1,0:T(8,128)(2,1)}, bf16[512,512]{1,0:T(8,128)(2,1)}, u32[]{:S(2)}, u32[]{:S(2)}) collective-permute-start(bf16[512,512]{1,0:T(8,128)(2,1)} %collective-permute-done.10.refs_3_), channel_id=1, source_target_pairs={{0,1},{1,0},{2,3},{3,2},{4,5},{5,4},{6,7},{7,6},{8,9},{9,8},{10,11... | collective-permute-start | bytes 1572872 | tf_op jit(solution)/shard_map/ppermute | solution.py:32
  62.9 11.2 %all-to-all-start.1 = ((f32[8,32,256]{2,1,0:T(8,128)}), f32[8,32,256]{2,1,0:T(8,128)S(1)}, u32[]{:S(2)}, u32[]{:S(2)}) async-start(f32[8,32,256]{2,1,0:T(8,128)} %broadcast_in_dim.2), calls=%async_computation.1 | async-start | bytes 524288 | tf_op jit(solution)/shard_map/all_to_all | solution.py:36
  67.6 0.7 copy-start.3
  74.1 1.0 copy-start.4
  76.9 0.7 copy-start.5
  77.6 15.8 %all-to-all-start.2 = ((bf16[32,4,512]{2,1,0:T(4,128)(2,1)}), bf16[32,4,512]{2,1,0:T(4,128)(2,1)S(1)}, u32[]{:S(2)}, u32[]{:S(2)}) async-start(bf16[32,4,512]{2,1,0:T(4,128)(2,1)} %copy-done.5), calls=%async_computation.2 | async-start | bytes 262144 | tf_op jit(solution)/shard_map/all_to_all | solution.py:390
  88.0 2.8 %collective-permute-start.3 = (bf16[104,1024]{1,0:T(8,128)(2,1)S(1)}, bf16[104,1024]{1,0:T(8,128)(2,1)S(1)}, u32[]{:S(2)}, u32[]{:S(2)}) collective-permute-start(bf16[104,1024]{1,0:T(8,128)(2,1)S(1)} %get-tuple-element.38), channel_id=1, source_target_pairs={{0,1},{1,0},{2,3},{3,2},{4,5},{5,4},{6,7},{7,6},{8,9},{9,8},{10,11... | collective-permute-start | bytes 638984 | tf_op jit(solution)/shard_map/ppermute | solution.py:32
  98.5 6.7 %collective-permute-start.18 = (bf16[104,1024]{1,0:T(8,128)(2,1)S(1)}, bf16[104,1024]{1,0:T(8,128)(2,1)S(1)}, u32[]{:S(2)}, u32[]{:S(2)}) collective-permute-start(bf16[104,1024]{1,0:T(8,128)(2,1)S(1)} %get-tuple-element.49.mine_ref), channel_id=1, source_target_pairs={{0,7},{1,2},{2,1},{3,4},{4,3},{5,6},{6,5},{7,0},{8,15},{9,10},{10,... | collective-permute-start | bytes 638984 | tf_op jit(solution)/shard_map/ppermute | solution.py:404
  102.7 5.7 %collective-permute-start.17 = (bf16[104,1024]{1,0:T(8,128)(2,1)S(1)}, bf16[104,1024]{1,0:T(8,128)(2,1)S(1)}, u32[]{:S(2)}, u32[]{:S(2)}) collective-permute-start(bf16[104,1024]{1,0:T(8,128)(2,1)S(1)} %term.9.refs_0_), channel_id=1, source_target_pairs={{0,7},{1,2},{2,1},{3,4},{4,3},{5,6},{6,5},{7,0},{8,15},{9,10},{10,... | collective-permute-start | bytes 638984 | tf_op jit(solution)/shard_map/ppermute | solution.py:406
  110.4 5.7 %collective-permute-start.20 = (bf16[104,1024]{1,0:T(8,128)(2,1)S(1)}, bf16[104,1024]{1,0:T(8,128)(2,1)S(1)}, u32[]{:S(2)}, u32[]{:S(2)}) collective-permute-start(bf16[104,1024]{1,0:T(8,128)(2,1)S(1)} %get-tuple-element.54.mine_ref), channel_id=1, source_target_pairs={{0,7},{1,2},{2,1},{3,4},{4,3},{5,6},{6,5},{7,0},{8,15},{9,10},{10,... | collective-permute-start | bytes 638984 | tf_op jit(solution)/shard_map/ppermute | solution.py:404
  112.4 5.7 %collective-permute-start.19 = (bf16[104,1024]{1,0:T(8,128)(2,1)S(1)}, bf16[104,1024]{1,0:T(8,128)(2,1)S(1)}, u32[]{:S(2)}, u32[]{:S(2)}) collective-permute-start(bf16[104,1024]{1,0:T(8,128)(2,1)S(1)} %term.12.refs_0_), channel_id=1, source_target_pairs={{0,7},{1,2},{2,1},{3,4},{4,3},{5,6},{6,5},{7,0},{8,15},{9,10},{10,... | collective-permute-start | bytes 638984 | tf_op jit(solution)/shard_map/ppermute | solution.py:406
  120.2 5.4 %collective-permute-start.22 = (bf16[104,1024]{1,0:T(8,128)(2,1)S(1)}, bf16[104,1024]{1,0:T(8,128)(2,1)S(1)}, u32[]{:S(2)}, u32[]{:S(2)}) collective-permute-start(bf16[104,1024]{1,0:T(8,128)(2,1)S(1)} %get-tuple-element.58.mine_ref), channel_id=1, source_target_pairs={{0,7},{1,2},{2,1},{3,4},{4,3},{5,6},{6,5},{7,0},{8,15},{9,10},{10,... | collective-permute-start | bytes 638984 | tf_op jit(solution)/shard_map/ppermute | solution.py:404
  122.6 5.9 %collective-permute-start.21 = (bf16[104,1024]{1,0:T(8,128)(2,1)S(1)}, bf16[104,1024]{1,0:T(8,128)(2,1)S(1)}, u32[]{:S(2)}, u32[]{:S(2)}) collective-permute-start(bf16[104,1024]{1,0:T(8,128)(2,1)S(1)} %term.15.mine_ref), channel_id=1, source_target_pairs={{0,7},{1,2},{2,1},{3,4},{4,3},{5,6},{6,5},{7,0},{8,15},{9,10},{10,... | collective-permute-start | bytes 638984 | tf_op jit(solution)/shard_map/ppermute | solution.py:406

commit v6 on v5

--- a/solution.py
+++ b/solution.py
@@ -25,17 +25,14 @@
     return [(i, (i + k) % n) for i in range(n)]
 
 
+Z_ORDER = (4, 3, 5, 2, 6, 1, 7, 0)
+WALK_RANKS = [[z * NX + x for z in Z_ORDER for x in range(NX)]]
+CHOL_RANKS = [list(range(7, -1, -1))]
 PAIRS = [(i, (i + 1) % 8 if i % 2 else (i - 1) % 8) for i in range(8)]
 
 
 def swap_core(value):
     return lax.ppermute(value, "core", ring(NC, 1))
-
-
-def to_all(value, axis, length):
-    return lax.all_to_all(
-        jnp.broadcast_to(value[None], (length, *value.shape)), axis, 0, 0, tiled=True
-    )
 
 
 def spec(space):
@@ -123,9 +120,10 @@
     bias = bias_ref[0]
     for k in range(1, 8):
         bias = bias + bias_ref[k]
-    force_ref[...] = bias
-    coeff = time_root * (fields_ref[...] - bias)
-    coeff = jnp.concatenate([coeff[31 - w : 32 - w] for w in range(32)], 0)
+    for rank, z in enumerate(Z_ORDER):
+        force_ref[NX * z : NX * z + NX, :] = bias[NX * rank : NX * rank + NX]
+    fields = jnp.concatenate([fields_ref[NX * z : NX * z + NX, :] for z in Z_ORDER], 0)
+    coeff = time_root * (fields - bias)
     split = []
     for _ in range(3):
         split.append(coeff.astype(bf16))
@@ -318,8 +316,8 @@
             kept = (acc[keep] + totals[h][keep]).astype(bf16)
             given = acc[give].astype(bf16)
             for b in range(4):
-                out_ref[4 * h + b, :PIECE, :] = kept[:, 256 * b : 256 * b + 256]
-                out_ref[4 * h + b, PIECE:, :] = given[:, 256 * b : 256 * b + 256]
+                out_ref[7 - 4 * h - b, :PIECE, :] = kept[:, 256 * b : 256 * b + 256]
+                out_ref[7 - 4 * h - b, PIECE:, :] = given[:, 256 * b : 256 * b + 256]
 
         pl.when(c == 1)(lambda put=put: put(low, high))
         pl.when(c == 0)(lambda put=put: put(high, low))
@@ -342,8 +340,8 @@
         start = 8 * TILES[i]
         n = 8 * (TILES[i + 1] - TILES[i])
         owner, partner = (i + 1) % 8, (i + 2) % 8 if i % 2 == 0 else i
-        kept = back_ref[owner, :n, :].astype(f32)
-        given = back_ref[partner, PIECE : PIECE + n, :].astype(f32)
+        kept = back_ref[7 - owner, :n, :].astype(f32)
+        given = back_ref[7 - partner, PIECE : PIECE + n, :].astype(f32)
         out_ref[0, start : start + n, :] = (kept + given).astype(bf16)
 
 
@@ -373,7 +371,9 @@
     weights = call_head(inv, [orb_v, *others], rows, a_par, occ, occ_par)
     mine, other = call_slabs([orb, *others])
     terms = call_join(mine, swap_core(other))
-    all_weights = lax.all_to_all(weights, ("z", "x"), 0, 0, tiled=True).reshape(32, 1024)
+    all_weights = lax.all_to_all(
+        weights, ("z", "x"), 0, 0, tiled=True, axis_index_groups=WALK_RANKS
+    ).reshape(32, 1024)
 
     far = [part]
     for j in (1, 2, 3):
@@ -383,13 +383,18 @@
         far_par.append(swap_core(far[j]))
     near = jnp.concatenate([chol_factors, chol_par], 0).astype(f32)
     partial_bias = jnp.dot(all_weights, near, precision=lax.Precision.HIGHEST)
-    biases = to_all(partial_bias, ("y", "core"), 8)
+    biases = lax.all_to_all(
+        jnp.broadcast_to(partial_bias[None], (8, 32, 256)),
+        ("y", "core"),
+        0,
+        0,
+        tiled=True,
+        axis_index_groups=CHOL_RANKS,
+    )
     force_bias, field_part = call_field(
         biases, fields, (chol_factors, chol_par, chol_far, chol_far_par)
     )
-    arrived = lax.all_to_all(
-        field_part, ("z", "x"), 0, 0, tiled=True, axis_index_groups=[list(range(31, -1, -1))]
-    )
+    arrived = lax.all_to_all(field_part, ("z", "x"), 0, 0, tiled=True, axis_index_groups=WALK_RANKS)
 
     part_shape = jax.ShapeDtypeStruct((SLAB, HALF), bf16)
     total_shape = jax.ShapeDtypeStruct((SLAB, HALF), f32)
@@ -419,7 +424,7 @@
         blocks_shape,
         *(mine_1, other_1, total_0, totals[1], product, scales, interp_v),
     )
-    returned = lax.all_to_all(blocks, ("y", "core"), 0, 0, tiled=True)
+    returned = lax.all_to_all(blocks, ("y", "core"), 0, 0, tiled=True, axis_index_groups=CHOL_RANKS)
     return call_end(returned), force_bias
 
 

time: 150 us -> 148 us (0.987)
  waiting for transfers between devices: 45.6 us -> 39.3 us
  starting transfers between devices: 55.8 us -> 60.9 us
    all_to_all x2, starting transfers between devices: 13.5 us -> 17.9 us  [the longest x1 10.7 us: on_device(): lax.all_to_all(weights, ('z', 'x'), 0, 0, tiled=True, axis_index_groups=W...]
    all_to_all x2, waiting for transfers between devices: 7.28 us -> 3.82 us  [the longest x1 3.81 us: on_device(): lax.all_to_all(jnp.broadcast_to(partial_bias[None], (8, 32, 256)), ('y',...]
    ppermute x3, waiting for transfers between devices: 3.56 us -> 1.56 us  [on_device(): far.append(lax.ppermute(part, 'x', ring(NX, -j)))]
  transfers between devices with their start and end apart: 26 -> 26, of which waited for: 15 -> 14; matrix products, arithmetic and copies ran while one was open for 1% -> 1% of each run, Pallas kernels for 8% -> 9%
where the time goes in v6:
time: 148 us
  starting transfers between devices  60.9 us (41%)
  waiting for transfers between devices  39.3 us (27%)
  Pallas kernels  26.1 us (18%)
  blocking collectives  16 us (11%)
  local copies, waits for them, and re-layouts  3.07 us (2%)
    all_to_all x1, blocking collectives, on_device(): lax.all_to_all(blocks, ('y', 'core'), 0, 0, tiled=True, axis_index_groups...  16 us
    ppermute x9, starting transfers between devices, swap_core(): return lax.ppermute(value, 'core', ring(NC, 1))  15 us
    pallas_call x9, Pallas kernels, call_term(): pl.pallas_call(kernel, out_shape=out_shape, in_specs=[spec(pltpu.VMEM)] *...  14.1 us
    ppermute x1, waiting for transfers between devices, on_device(): part = lax.ppermute(part, 'y', ring(NY, 2))  11.1 us
    all_to_all x1, starting transfers between devices, on_device(): lax.all_to_all(field_part, ('z', 'x'), 0, 0, tiled=True, axis_index_group...  10.9 us
    all_to_all x1, starting transfers between devices, on_device(): lax.all_to_all(weights, ('z', 'x'), 0, 0, tiled=True, axis_index_groups=W...  10.7 us
    ppermute x3, waiting for transfers between devices, on_device(): others = [lax.ppermute(orb, 'y', ring(NY, -j)) for j in (1, 2, 3)]  7.68 us
    all_to_all x1, starting transfers between devices, on_device(): lax.all_to_all(jnp.broadcast_to(partial_bias[None], (8, 32, 256)), ('y',...  7.17 us
  transfers between devices with their start and end apart: 26, of which 14 were waited for; matrix products, arithmetic and copies ran while one was open for 1% of the time, Pallas kernels for 9%

profile of v6, /device:TPU:1, one launch (start us, length us, event | category | flops | bytes accessed | tf_op | source)
XLA Modules:
  0.0 147.5 jit_solution(12997422527666631532)
XLA Ops:
  0.7 3.3 %collective-permute-start.4 = (bf16[2048,512]{1,0:T(8,128)(2,1)}, bf16[2048,512]{1,0:T(8,128)(2,1)S(1)}, u32[]{:S(2)}, u32[]{:S(2)}) collective-permute-start(bf16[2048,512]{1,0:T(8,128)(2,1)} %refs_0_.1), channel_id=1, source_target_pairs={{0,1},{1,0},{2,3},{3,2},{4,5},{5,4},{6,7},{7,6},{8,9},{9,8},{10,11... | collective-permute-start | bytes 6291464 | tf_op jit(solution)/shard_map/ppermute | solution.py:35
  3.9 2.2 %collective-permute-start.1 = (bf16[400,256]{1,0:T(8,128)(2,1)}, bf16[400,256]{1,0:T(8,128)(2,1)S(1)}, u32[]{:S(2)}, u32[]{:S(2)}) collective-permute-start(bf16[400,256]{1,0:T(8,128)(2,1)} %bitcast.6), channel_id=1, source_target_pairs={{0,4},{2,6},{4,0},{6,2},{1,5},{3,7},{5,1},{7,3},{8,12},{10,14},{12... | collective-permute-start | bytes 614408 | tf_op jit(solution)/shard_map/ppermute | solution.py:362
  6.1 1.1 collective-permute-start
  7.2 1.7 %start.1 = (bf16[512,512]{1,0:T(8,128)(2,1)S(1)}, bf16[1024,512]{1,0:T(8,128)(2,1)S(1)}, bf16[400,400]{1,0:T(8,128)(2,1)S(1)}, bf16[400,256]{1,0:T(8,128)(2,1)S(1)}, bf16[400,512]{1,0:T(8,128)(2,1)S(1)}) custom-call(bf16[2048,512]{1,0:T(8,128)(2,1)} %refs_0_.1, bf16[400,400]{1,0:T(8,128)(2,1)} %bitcast.10, bf16[400,256]{1,0:T(8,128)(2,1)} %bitcast.8, ...), custom_call_target="tpu_custom_call" | custom-call | tf_op jit(solution)/shard_map/start/pallas_call | solution.py:73
  9.0 3.4 %collective-permute-done.2.o3 = bf16[400,256]{1,0:T(8,128)(2,1)S(1)} collective-permute-done((bf16[400,256]{1,0:T(8,128)(2,1)}, bf16[400,256]{1,0:T(8,128)(2,1)S(1)}, u32[]{:S(2)}, u32[]{:S(2)}) %collective-permute-start.2) | collective-permute-done | bytes 204832 | tf_op jit(solution)/shard_map/ppermute | solution.py:362
  12.4 3.5 %collective-permute-done.1.o2 = bf16[400,256]{1,0:T(8,128)(2,1)S(1)} collective-permute-done((bf16[400,256]{1,0:T(8,128)(2,1)}, bf16[400,256]{1,0:T(8,128)(2,1)S(1)}, u32[]{:S(2)}, u32[]{:S(2)}) %collective-permute-start.1) | collective-permute-done | bytes 204832 | tf_op jit(solution)/shard_map/ppermute | solution.py:362
  15.9 0.8 collective-permute-done.o1
  16.6 1.2 collective-permute-start.9
  17.8 1.5 %collective-permute-start.5 = (bf16[400,512]{1,0:T(8,128)(2,1)S(1)}, bf16[400,512]{1,0:T(8,128)(2,1)S(1)}, u32[]{:S(2)}, u32[]{:S(2)}) collective-permute-start(bf16[400,512]{1,0:T(8,128)(2,1)S(1)} %copy-done.7), channel_id=1, source_target_pairs={{0,1},{1,0},{2,3},{3,2},{4,5},{5,4},{6,7},{7,6},{8,9},{9,8},{10,11... | collective-permute-start | bytes 1228808 | tf_op jit(solution)/shard_map/ppermute | solution.py:35
  19.4 11.1 %collective-permute-done.9.refs_2_ = bf16[512,512]{1,0:T(8,128)(2,1)} collective-permute-done((bf16[512,512]{1,0:T(8,128)(2,1)S(1)}, bf16[512,512]{1,0:T(8,128)(2,1)}, u32[]{:S(2)}, u32[]{:S(2)}) %collective-permute-start.9) | collective-permute-done | bytes 524320 | tf_op jit(solution)/shard_map/ppermute | solution.py:367
  31.2 2.5 %collective-permute-start.11 = (bf16[512,512]{1,0:T(8,128)(2,1)}, bf16[512,512]{1,0:T(8,128)(2,1)}, u32[]{:S(2)}, u32[]{:S(2)}) collective-permute-start(bf16[512,512]{1,0:T(8,128)(2,1)} %collective-permute-done.9.refs_2_), channel_id=1, source_target_pairs={{0,16},{8,24},{16,0},{24,8},{1,17},{9,25},{17,1},{25,9},{2,18},{10... | collective-permute-start | bytes 1572872 | tf_op jit(solution)/shard_map/ppermute | solution.py:380
  33.6 1.2 collective-permute-start.10
  34.8 1.7 %collective-permute-start.7 = (bf16[512,256]{1,0:T(8,128)(2,1)S(1)}, bf16[512,256]{1,0:T(8,128)(2,1)S(1)}, u32[]{:S(2)}, u32[]{:S(2)}) collective-permute-start(bf16[512,256]{1,0:T(8,128)(2,1)S(1)} %copy-done.2), channel_id=1, source_target_pairs={{0,4},{2,6},{4,0},{6,2},{1,5},{3,7},{5,1},{7,3},{8,12},{10,14},{12... | collective-permute-start | bytes 786440 | tf_op jit(solution)/shard_map/ppermute | solution.py:368
  36.5 3.2 %collective-permute-start.6 = (bf16[512,256]{1,0:T(8,128)(2,1)S(1)}, bf16[512,256]{1,0:T(8,128)(2,1)}, u32[]{:S(2)}, u32[]{:S(2)}) collective-permute-start(bf16[512,256]{1,0:T(8,128)(2,1)S(1)} %copy-done.2), channel_id=1, source_target_pairs={{0,1},{1,0},{2,3},{3,2},{4,5},{5,4},{6,7},{7,6},{8,9},{9,8},{10,11... | collective-permute-start | bytes 786440 | tf_op jit(solution)/shard_map/ppermute | solution.py:35
  39.7 2.4 %head.1 = f32[32,1,1024]{2,1,0:T(1,128)} custom-call(bf16[400,400]{1,0:T(8,128)(2,1)S(1)} %get-tuple-element.41.inv, bf16[400,256]{1,0:T(8,128)(2,1)S(1)} %get-tuple-element.42.o0, bf16[400,256]{1,0:T(8,128)(2,1)S(1)} %collective-permute-done.o1, bf16[400,256]{1,0:T(8,128)(2,1)S(1)} %collective-permute-done.1.o2, ...), custom_call_target="tpu_custom_call" | custom-call | tf_op jit(solution)/shard_map/head/pallas_call | solution.py:109
  42.2 10.7 %all-to-all-start = ((f32[32,1,1024]{2,1,0:T(1,128)}), f32[32,1,1024]{2,1,0:T(1,128)S(1)}, u32[]{:S(2)}, u32[]{:S(2)}) async-start(f32[32,1,1024]{2,1,0:T(1,128)} %head.1), calls=%async_computation | async-start | bytes 262144 | tf_op jit(solution)/shard_map/all_to_all | solution.py:374
  53.8 1.6 %collective-permute-done.11.refs_4_ = bf16[512,512]{1,0:T(8,128)(2,1)} collective-permute-done((bf16[512,512]{1,0:T(8,128)(2,1)}, bf16[512,512]{1,0:T(8,128)(2,1)}, u32[]{:S(2)}, u32[]{:S(2)}) %collective-permute-start.11) | collective-permute-done | bytes 524320 | tf_op jit(solution)/shard_map/ppermute | solution.py:380
  55.4 3.6 %collective-permute-start.15 = (bf16[512,512]{1,0:T(8,128)(2,1)}, bf16[512,512]{1,0:T(8,128)(2,1)S(1)}, u32[]{:S(2)}, u32[]{:S(2)}) collective-permute-start(bf16[512,512]{1,0:T(8,128)(2,1)} %collective-permute-done.11.refs_4_), channel_id=1, source_target_pairs={{0,1},{1,0},{2,3},{3,2},{4,5},{5,4},{6,7},{7,6},{8,9},{9,8},{10,11... | collective-permute-start | bytes 1572872 | tf_op jit(solution)/shard_map/ppermute | solution.py:35
  59.5 1.3 fusion
  61.6 7.2 %all-to-all-start.1 = ((f32[8,32,256]{2,1,0:T(8,128)}), f32[8,32,256]{2,1,0:T(8,128)S(1)}, u32[]{:S(2)}, u32[]{:S(2)}) async-start(f32[8,32,256]{2,1,0:T(8,128)} %broadcast_in_dim.2), calls=%async_computation.1 | async-start | bytes 524288 | tf_op jit(solution)/shard_map/all_to_all | solution.py:386
  69.5 3.8 %all-to-all-done.1.bias_ref = f32[8,32,256]{2,1,0:T(8,128)S(1)} async-done(((f32[8,32,256]{2,1,0:T(8,128)}), f32[8,32,256]{2,1,0:T(8,128)S(1)}, u32[]{:S(2)}, u32[]{:S(2)}) %all-to-all-start.1) | async-done | bytes 262176 | tf_op jit(solution)/shard_map/all_to_all | solution.py:386
  73.3 0.9 copy-done.4
  74.2 1.8 %field.1 = (f32[32,256]{1,0:T(8,128)}, bf16[32,4,512]{2,1,0:T(4,128)(2,1)S(1)}) custom-call(f32[8,32,256]{2,1,0:T(8,128)S(1)} %all-to-all-done.1.bias_ref, f32[32,256]{1,0:T(8,128)S(1)} %copy-done.6, bf16[512,256]{1,0:T(8,128)(2,1)S(1)} %copy-done.2, bf16[512,256]{1,0:T(8,128)(2,1)} %collective-permute-done.6.c1, ...), custom_call_target="tpu_custom_call" | custom-call | tf_op jit(solution)/shard_map/field/pallas_call | solution.py:142
  76.7 10.9 %all-to-all-start.2 = ((bf16[32,4,512]{2,1,0:T(4,128)(2,1)}), bf16[32,4,512]{2,1,0:T(4,128)(2,1)S(1)}, u32[]{:S(2)}, u32[]{:S(2)}) async-start(bf16[32,4,512]{2,1,0:T(4,128)(2,1)} %copy-done.5), calls=%async_computation.2 | async-start | bytes 262144 | tf_op jit(solution)/shard_map/all_to_all | solution.py:397
  87.8 1.9 %collective-permute-start.3 = (bf16[104,1024]{1,0:T(8,128)(2,1)S(1)}, bf16[104,1024]{1,0:T(8,128)(2,1)S(1)}, u32[]{:S(2)}, u32[]{:S(2)}) collective-permute-start(bf16[104,1024]{1,0:T(8,128)(2,1)S(1)} %get-tuple-element.38), channel_id=1, source_target_pairs={{0,1},{1,0},{2,3},{3,2},{4,5},{5,4},{6,7},{7,6},{8,9},{9,8},{10,11... | collective-permute-start | bytes 638984 | tf_op jit(solution)/shard_map/ppermute | solution.py:35
  89.7 1.1 collective-permute-done.3.par
  90.9 1.7 %all-to-all-done.2.arrived_ref = bf16[32,4,512]{2,1,0:T(4,128)(2,1)S(1)} async-done(((bf16[32,4,512]{2,1,0:T(4,128)(2,1)}), bf16[32,4,512]{2,1,0:T(4,128)(2,1)S(1)}, u32[]{:S(2)}, u32[]{:S(2)}) %all-to-all-start.2) | async-done | bytes 131104 | tf_op jit(solution)/shard_map/all_to_all | solution.py:397
  92.6 5.1 %first.1 = (bf16[4,104,512]{2,1,0:T(8,128)(2,1)S(1)}, bf16[104,1024]{1,0:T(8,128)(2,1)S(1)}, f32[4,512]{1,0:T(4,128)S(1)}, bf16[4,2048,512]{2,1,0:T(8,128)(2,1)S(1)}) custom-call(bf16[104,1024]{1,0:T(8,128)(2,1)S(1)} %get-tuple-element.39.term_0.total_ref, bf16[104,1024]{1,0:T(8,128)(2,1)S(1)} %get-tuple-element.40.term_1.refs_2_, ...), custom_call_target="tpu_custom_call" | custom-call | tf_op jit(solution)/shard_map/first/pallas_call | solution.py:262
  97.6 2.5 %collective-permute-start.18 = (bf16[104,1024]{1,0:T(8,128)(2,1)S(1)}, bf16[104,1024]{1,0:T(8,128)(2,1)S(1)}, u32[]{:S(2)}, u32[]{:S(2)}) collective-permute-start(bf16[104,1024]{1,0:T(8,128)(2,1)S(1)} %get-tuple-element.49.mine_ref), channel_id=1, source_target_pairs={{0,7},{1,2},{2,1},{3,4},{4,3},{5,6},{6,5},{7,0},{8,15},{9,10},{10,... | collective-permute-start | bytes 638984 | tf_op jit(solution)/shard_map/ppermute | solution.py:409
  100.2 1.4 term.9.refs_0_
  101.7 2.0 %collective-permute-done.18.other_ref = bf16[104,1024]{1,0:T(8,128)(2,1)S(1)} collective-permute-done((bf16[104,1024]{1,0:T(8,128)(2,1)S(1)}, bf16[104,1024]{1,0:T(8,128)(2,1)S(1)}, u32[]{:S(2)}, u32[]{:S(2)}) %collective-permute-start.18) | collective-permute-done | bytes 213024 | tf_op jit(solution)/shard_map/ppermute | solution.py:409
  103.7 0.8 term.10
  104.4 2.8 %collective-permute-done.17.refs_1_ = bf16[104,1024]{1,0:T(8,128)(2,1)S(1)} collective-permute-done((bf16[104,1024]{1,0:T(8,128)(2,1)S(1)}, bf16[104,1024]{1,0:T(8,128)(2,1)S(1)}, u32[]{:S(2)}, u32[]{:S(2)}) %collective-permute-start.17) | collective-permute-done | bytes 213024 | tf_op jit(solution)/shard_map/ppermute | solution.py:411
  107.2 2.0 %term.11 = (bf16[4,104,512]{2,1,0:T(8,128)(2,1)S(1)}, bf16[104,1024]{1,0:T(8,128)(2,1)S(1)}, f32[104,1024]{1,0:T(8,128)S(1)}) custom-call(bf16[104,1024]{1,0:T(8,128)(2,1)S(1)} %term.9.refs_0_, bf16[104,1024]{1,0:T(8,128)(2,1)S(1)} %collective-permute-done.17.refs_1_, bf16[104,1024]{1,0:T(8,128)(2,1)S(1)} %get-tuple-element.40.term_1.refs_2_, ...), custom_call_target="tpu_custom_call" | custom-call | tf_op jit(solution)/shard_map/term/pallas_call | solution.py:328
  109.8 1.4 term.12.refs_0_
  111.2 1.3 collective-permute-start.19
  112.6 2.0 %collective-permute-done.20.other_ref = bf16[104,1024]{1,0:T(8,128)(2,1)S(1)} collective-permute-done((bf16[104,1024]{1,0:T(8,128)(2,1)S(1)}, bf16[104,1024]{1,0:T(8,128)(2,1)S(1)}, u32[]{:S(2)}, u32[]{:S(2)}) %collective-permute-start.20) | collective-permute-done | bytes 213024 | tf_op jit(solution)/shard_map/ppermute | solution.py:409
  114.6 0.8 term.13
  115.4 1.8 %collective-permute-done.19.refs_1_ = bf16[104,1024]{1,0:T(8,128)(2,1)S(1)} collective-permute-done((bf16[104,1024]{1,0:T(8,128)(2,1)S(1)}, bf16[104,1024]{1,0:T(8,128)(2,1)S(1)}, u32[]{:S(2)}, u32[]{:S(2)}) %collective-permute-start.19) | collective-permute-done | bytes 213024 | tf_op jit(solution)/shard_map/ppermute | solution.py:411
  117.2 2.0 %term.14 = (bf16[4,104,512]{2,1,0:T(8,128)(2,1)S(1)}, bf16[104,1024]{1,0:T(8,128)(2,1)S(1)}, f32[104,1024]{1,0:T(8,128)S(1)}) custom-call(bf16[104,1024]{1,0:T(8,128)(2,1)S(1)} %term.12.refs_0_, bf16[104,1024]{1,0:T(8,128)(2,1)S(1)} %collective-permute-done.19.refs_1_, f32[104,1024]{1,0:T(8,128)S(1)} %get-tuple-element.53.refs_2_, ...), custom_call_target="tpu_custom_call" | custom-call | tf_op jit(solution)/shard_map/term/pallas_call | solution.py:328
  119.2 0.7 collective-permute-start.22
  120.0 1.4 term.15.mine_ref
  121.4 1.4 collective-permute-start.21
  122.8 1.8 %collective-permute-done.22.other_ref = bf16[104,1024]{1,0:T(8,128)(2,1)S(1)} collective-permute-done((bf16[104,1024]{1,0:T(8,128)(2,1)S(1)}, bf16[104,1024]{1,0:T(8,128)(2,1)S(1)}, u32[]{:S(2)}, u32[]{:S(2)}) %collective-permute-start.22) | collective-permute-done | bytes 213024 | tf_op jit(solution)/shard_map/ppermute | solution.py:409
  124.6 0.7 term.16
  125.3 1.9 %collective-permute-done.21.other_ref = bf16[104,1024]{1,0:T(8,128)(2,1)S(1)} collective-permute-done((bf16[104,1024]{1,0:T(8,128)(2,1)S(1)}, bf16[104,1024]{1,0:T(8,128)(2,1)S(1)}, u32[]{:S(2)}, u32[]{:S(2)}) %collective-permute-start.21) | collective-permute-done | bytes 213024 | tf_op jit(solution)/shard_map/ppermute | solution.py:411
  127.3 3.5 %term.17 = bf16[8,112,256]{2,1,0:T(8,128)(2,1)S(1)} custom-call(bf16[104,1024]{1,0:T(8,128)(2,1)S(1)} %term.15.mine_ref, bf16[104,1024]{1,0:T(8,128)(2,1)S(1)} %collective-permute-done.21.other_ref, f32[104,1024]{1,0:T(8,128)S(1)} %get-tuple-element.60.total_0, f32[104,1024]{1,0:T(8,128)S(1)} %get-tuple-element.61.total_1, ...), custom_call_target="tpu_custom_call" | custom-call | tf_op jit(solution)/shard_map/term/pallas_call | solution.py:328
  130.8 16.0 %all_to_all.20.back_ref = bf16[8,112,256]{2,1,0:T(8,128)(2,1)S(1)} all-to-all(bf16[8,112,256]{2,1,0:T(8,128)(2,1)S(1)} %term.17), channel_id=1, replica_groups={{7,6,5,4,3,2,1,0},{15,14,13,12,11,10,9,8},{23,22,21,20,19,18,17,16},{31..., dimensions={0} | all-to-all | bytes 917504 | tf_op jit(solution)/shard_map/all_to_all | solution.py:427
  (39 shorter events, 5.9 us)
Async XLA Ops:
  0.6 17.2 %copy-start.7 = (bf16[400,512]{1,0:T(8,128)(2,1)S(1)}, bf16[400,512]{1,0:T(8,128)(2,1)}, u32[]{:S(2)}) copy-start(bf16[400,512]{1,0:T(8,128)(2,1)} %occ.1) | copy-start | bytes 1228804
  0.6 34.2 %copy-start.2 = (bf16[512,256]{1,0:T(8,128)(2,1)S(1)}, bf16[512,256]{1,0:T(8,128)(2,1)}, u32[]{:S(2)}) copy-start(bf16[512,256]{1,0:T(8,128)(2,1)} %c0.1) | copy-start | bytes 786436
  0.7 35.9 %collective-permute-start.4 = (bf16[2048,512]{1,0:T(8,128)(2,1)}, bf16[2048,512]{1,0:T(8,128)(2,1)S(1)}, u32[]{:S(2)}, u32[]{:S(2)}) collective-permute-start(bf16[2048,512]{1,0:T(8,128)(2,1)} %refs_0_.1), channel_id=1, source_target_pairs={{0,1},{1,0},{2,3},{3,2},{4,5},{5,4},{6,7},{7,6},{8,9},{9,8},{10,11... | collective-permute-start | bytes 6291464 | tf_op jit(solution)/shard_map/ppermute | solution.py:35
  3.9 8.4 %collective-permute-start.2 = (bf16[400,256]{1,0:T(8,128)(2,1)}, bf16[400,256]{1,0:T(8,128)(2,1)S(1)}, u32[]{:S(2)}, u32[]{:S(2)}) collective-permute-start(bf16[400,256]{1,0:T(8,128)(2,1)} %bitcast.5), channel_id=1, source_target_pairs={{0,2},{2,4},{4,6},{6,0},{1,3},{3,5},{5,7},{7,1},{8,10},{10,12},{12... | collective-permute-start | bytes 614408 | tf_op jit(solution)/shard_map/ppermute | solution.py:362
  3.9 11.9 %collective-permute-start.1 = (bf16[400,256]{1,0:T(8,128)(2,1)}, bf16[400,256]{1,0:T(8,128)(2,1)S(1)}, u32[]{:S(2)}, u32[]{:S(2)}) collective-permute-start(bf16[400,256]{1,0:T(8,128)(2,1)} %bitcast.6), channel_id=1, source_target_pairs={{0,4},{2,6},{4,0},{6,2},{1,5},{3,7},{5,1},{7,3},{8,12},{10,14},{12... | collective-permute-start | bytes 614408 | tf_op jit(solution)/shard_map/ppermute | solution.py:362
  6.1 10.5 %collective-permute-start = (bf16[400,256]{1,0:T(8,128)(2,1)}, bf16[400,256]{1,0:T(8,128)(2,1)S(1)}, u32[]{:S(2)}, u32[]{:S(2)}) collective-permute-start(bf16[400,256]{1,0:T(8,128)(2,1)} %bitcast.7), channel_id=1, source_target_pairs={{0,6},{2,0},{4,2},{6,4},{1,7},{3,1},{5,3},{7,5},{8,14},{10,8},{12,... | collective-permute-start | bytes 614408 | tf_op jit(solution)/shard_map/ppermute | solution.py:362
  16.6 13.9 %collective-permute-start.9 = (bf16[512,512]{1,0:T(8,128)(2,1)S(1)}, bf16[512,512]{1,0:T(8,128)(2,1)}, u32[]{:S(2)}, u32[]{:S(2)}) collective-permute-start(bf16[512,512]{1,0:T(8,128)(2,1)S(1)} %get-tuple-element.46), channel_id=1, source_target_pairs={{0,4},{2,6},{4,0},{6,2},{1,5},{3,7},{5,1},{7,3},{8,12},{10,14},{12... | collective-permute-start | bytes 1572872 | tf_op jit(solution)/shard_map/ppermute | solution.py:367
  17.8 16.9 %collective-permute-start.5 = (bf16[400,512]{1,0:T(8,128)(2,1)S(1)}, bf16[400,512]{1,0:T(8,128)(2,1)S(1)}, u32[]{:S(2)}, u32[]{:S(2)}) collective-permute-start(bf16[400,512]{1,0:T(8,128)(2,1)S(1)} %copy-done.7), channel_id=1, source_target_pairs={{0,1},{1,0},{2,3},{3,2},{4,5},{5,4},{6,7},{7,6},{8,9},{9,8},{10,11... | collective-permute-start | bytes 1228808 | tf_op jit(solution)/shard_map/ppermute | solution.py:35
  30.5 23.0 %collective-permute-start.12 = (bf16[512,512]{1,0:T(8,128)(2,1)}, bf16[512,512]{1,0:T(8,128)(2,1)}, u32[]{:S(2)}, u32[]{:S(2)}) collective-permute-start(bf16[512,512]{1,0:T(8,128)(2,1)} %collective-permute-done.9.refs_2_), channel_id=1, source_target_pairs={{0,8},{8,16},{16,24},{24,0},{1,9},{9,17},{17,25},{25,1},{2,10},{10... | collective-permute-start | bytes 1572872 | tf_op jit(solution)/shard_map/ppermute | solution.py:380
  31.2 24.2 %collective-permute-start.11 = (bf16[512,512]{1,0:T(8,128)(2,1)}, bf16[512,512]{1,0:T(8,128)(2,1)}, u32[]{:S(2)}, u32[]{:S(2)}) collective-permute-start(bf16[512,512]{1,0:T(8,128)(2,1)} %collective-permute-done.9.refs_2_), channel_id=1, source_target_pairs={{0,16},{8,24},{16,0},{24,8},{1,17},{9,25},{17,1},{25,9},{2,18},{10... | collective-permute-start | bytes 1572872 | tf_op jit(solution)/shard_map/ppermute | solution.py:380
  33.6 25.4 %collective-permute-start.10 = (bf16[512,512]{1,0:T(8,128)(2,1)}, bf16[512,512]{1,0:T(8,128)(2,1)}, u32[]{:S(2)}, u32[]{:S(2)}) collective-permute-start(bf16[512,512]{1,0:T(8,128)(2,1)} %collective-permute-done.9.refs_2_), channel_id=1, source_target_pairs={{0,24},{8,0},{16,8},{24,16},{1,25},{9,1},{17,9},{25,17},{2,26},{10... | collective-permute-start | bytes 1572872 | tf_op jit(solution)/shard_map/ppermute | solution.py:380
  34.8 18.1 %collective-permute-start.7 = (bf16[512,256]{1,0:T(8,128)(2,1)S(1)}, bf16[512,256]{1,0:T(8,128)(2,1)S(1)}, u32[]{:S(2)}, u32[]{:S(2)}) collective-permute-start(bf16[512,256]{1,0:T(8,128)(2,1)S(1)} %copy-done.2), channel_id=1, source_target_pairs={{0,4},{2,6},{4,0},{6,2},{1,5},{3,7},{5,1},{7,3},{8,12},{10,14},{12... | collective-permute-start | bytes 786440 | tf_op jit(solution)/shard_map/ppermute | solution.py:368
  36.5 5.7 %copy-start = (bf16[2048,512]{1,0:T(8,128)(2,1)}, bf16[2048,512]{1,0:T(8,128)(2,1)S(1)}, u32[]{:S(2)}) copy-start(bf16[2048,512]{1,0:T(8,128)(2,1)S(1)} %collective-permute-done.4.a_par.refs_1_) | copy-start | bytes 6291460
  36.5 16.8 %collective-permute-start.6 = (bf16[512,256]{1,0:T(8,128)(2,1)S(1)}, bf16[512,256]{1,0:T(8,128)(2,1)}, u32[]{:S(2)}, u32[]{:S(2)}) collective-permute-start(bf16[512,256]{1,0:T(8,128)(2,1)S(1)} %copy-done.2), channel_id=1, source_target_pairs={{0,1},{1,0},{2,3},{3,2},{4,5},{5,4},{6,7},{7,6},{8,9},{9,8},{10,11... | collective-permute-start | bytes 786440 | tf_op jit(solution)/shard_map/ppermute | solution.py:35
  39.7 33.5 %copy-start.6 = (f32[32,256]{1,0:T(8,128)S(1)}, f32[32,256]{1,0:T(8,128)}, u32[]{:S(2)}) copy-start(f32[32,256]{1,0:T(8,128)} %fields_ref.1) | copy-start | bytes 98308
  42.2 45.4 %copy-start.1 = (bf16[1,400,256]{2,1,0:T(8,128)(2,1)S(1)}, bf16[1,400,256]{2,1,0:T(8,128)(2,1)}, u32[]{:S(2)}) copy-start(bf16[1,400,256]{2,1,0:T(8,128)(2,1)} %param.6) | copy-start | bytes 614404
  42.2 17.3 %all-to-all-start = ((f32[32,1,1024]{2,1,0:T(1,128)}), f32[32,1,1024]{2,1,0:T(1,128)S(1)}, u32[]{:S(2)}, u32[]{:S(2)}) async-start(f32[32,1,1024]{2,1,0:T(1,128)} %head.1), calls=%async_computation | async-start | bytes 262144 | tf_op jit(solution)/shard_map/all_to_all | solution.py:374
  52.9 15.8 %collective-permute-start.8 = (bf16[512,256]{1,0:T(8,128)(2,1)S(1)}, bf16[512,256]{1,0:T(8,128)(2,1)S(1)}, u32[]{:S(2)}, u32[]{:S(2)}) collective-permute-start(bf16[512,256]{1,0:T(8,128)(2,1)S(1)} %collective-permute-done.7.c2), channel_id=1, source_target_pairs={{0,1},{1,0},{2,3},{3,2},{4,5},{5,4},{6,7},{7,6},{8,9},{9,8},{10,11... | collective-permute-start | bytes 786440 | tf_op jit(solution)/shard_map/ppermute | solution.py:35
  53.3 37.5 %collective-permute-start.13 = (bf16[512,512]{1,0:T(8,128)(2,1)}, bf16[512,512]{1,0:T(8,128)(2,1)S(1)}, u32[]{:S(2)}, u32[]{:S(2)}) collective-permute-start(bf16[512,512]{1,0:T(8,128)(2,1)} %collective-permute-done.9.refs_2_), channel_id=1, source_target_pairs={{0,1},{1,0},{2,3},{3,2},{4,5},{5,4},{6,7},{7,6},{8,9},{9,8},{10,11... | collective-permute-start | bytes 1572872 | tf_op jit(solution)/shard_map/ppermute | solution.py:35
  53.5 37.3 %collective-permute-start.16 = (bf16[512,512]{1,0:T(8,128)(2,1)}, bf16[512,512]{1,0:T(8,128)(2,1)S(1)}, u32[]{:S(2)}, u32[]{:S(2)}) collective-permute-start(bf16[512,512]{1,0:T(8,128)(2,1)} %collective-permute-done.12.refs_5_), channel_id=1, source_target_pairs={{0,1},{1,0},{2,3},{3,2},{4,5},{5,4},{6,7},{7,6},{8,9},{9,8},{10,11... | collective-permute-start | bytes 1572872 | tf_op jit(solution)/shard_map/ppermute | solution.py:35
  55.4 35.5 %collective-permute-start.15 = (bf16[512,512]{1,0:T(8,128)(2,1)}, bf16[512,512]{1,0:T(8,128)(2,1)S(1)}, u32[]{:S(2)}, u32[]{:S(2)}) collective-permute-start(bf16[512,512]{1,0:T(8,128)(2,1)} %collective-permute-done.11.refs_4_), channel_id=1, source_target_pairs={{0,1},{1,0},{2,3},{3,2},{4,5},{5,4},{6,7},{7,6},{8,9},{9,8},{10,11... | collective-permute-start | bytes 1572872 | tf_op jit(solution)/shard_map/ppermute | solution.py:35
  59.0 31.9 %collective-permute-start.14 = (bf16[512,512]{1,0:T(8,128)(2,1)}, bf16[512,512]{1,0:T(8,128)(2,1)}, u32[]{:S(2)}, u32[]{:S(2)}) collective-permute-start(bf16[512,512]{1,0:T(8,128)(2,1)} %collective-permute-done.10.refs_3_), channel_id=1, source_target_pairs={{0,1},{1,0},{2,3},{3,2},{4,5},{5,4},{6,7},{7,6},{8,9},{9,8},{10,11... | collective-permute-start | bytes 1572872 | tf_op jit(solution)/shard_map/ppermute | solution.py:35
  61.6 11.7 %all-to-all-start.1 = ((f32[8,32,256]{2,1,0:T(8,128)}), f32[8,32,256]{2,1,0:T(8,128)S(1)}, u32[]{:S(2)}, u32[]{:S(2)}) async-start(f32[8,32,256]{2,1,0:T(8,128)} %broadcast_in_dim.2), calls=%async_computation.1 | async-start | bytes 524288 | tf_op jit(solution)/shard_map/all_to_all | solution.py:386
  68.8 0.7 copy-start.3
  73.3 1.0 copy-start.4
  76.1 0.7 copy-start.5
  76.7 15.8 %all-to-all-start.2 = ((bf16[32,4,512]{2,1,0:T(4,128)(2,1)}), bf16[32,4,512]{2,1,0:T(4,128)(2,1)S(1)}, u32[]{:S(2)}, u32[]{:S(2)}) async-start(bf16[32,4,512]{2,1,0:T(4,128)(2,1)} %copy-done.5), calls=%async_computation.2 | async-start | bytes 262144 | tf_op jit(solution)/shard_map/all_to_all | solution.py:397
  87.8 3.0 %collective-permute-start.3 = (bf16[104,1024]{1,0:T(8,128)(2,1)S(1)}, bf16[104,1024]{1,0:T(8,128)(2,1)S(1)}, u32[]{:S(2)}, u32[]{:S(2)}) collective-permute-start(bf16[104,1024]{1,0:T(8,128)(2,1)S(1)} %get-tuple-element.38), channel_id=1, source_target_pairs={{0,1},{1,0},{2,3},{3,2},{4,5},{5,4},{6,7},{7,6},{8,9},{9,8},{10,11... | collective-permute-start | bytes 638984 | tf_op jit(solution)/shard_map/ppermute | solution.py:35
  97.6 6.1 %collective-permute-start.18 = (bf16[104,1024]{1,0:T(8,128)(2,1)S(1)}, bf16[104,1024]{1,0:T(8,128)(2,1)S(1)}, u32[]{:S(2)}, u32[]{:S(2)}) collective-permute-start(bf16[104,1024]{1,0:T(8,128)(2,1)S(1)} %get-tuple-element.49.mine_ref), channel_id=1, source_target_pairs={{0,7},{1,2},{2,1},{3,4},{4,3},{5,6},{6,5},{7,0},{8,15},{9,10},{10,... | collective-permute-start | bytes 638984 | tf_op jit(solution)/shard_map/ppermute | solution.py:409
  101.6 5.7 %collective-permute-start.17 = (bf16[104,1024]{1,0:T(8,128)(2,1)S(1)}, bf16[104,1024]{1,0:T(8,128)(2,1)S(1)}, u32[]{:S(2)}, u32[]{:S(2)}) collective-permute-start(bf16[104,1024]{1,0:T(8,128)(2,1)S(1)} %term.9.refs_0_), channel_id=1, source_target_pairs={{0,7},{1,2},{2,1},{3,4},{4,3},{5,6},{6,5},{7,0},{8,15},{9,10},{10,... | collective-permute-start | bytes 638984 | tf_op jit(solution)/shard_map/ppermute | solution.py:411
  109.2 5.4 %collective-permute-start.20 = (bf16[104,1024]{1,0:T(8,128)(2,1)S(1)}, bf16[104,1024]{1,0:T(8,128)(2,1)S(1)}, u32[]{:S(2)}, u32[]{:S(2)}) collective-permute-start(bf16[104,1024]{1,0:T(8,128)(2,1)S(1)} %get-tuple-element.54.mine_ref), channel_id=1, source_target_pairs={{0,7},{1,2},{2,1},{3,4},{4,3},{5,6},{6,5},{7,0},{8,15},{9,10},{10,... | collective-permute-start | bytes 638984 | tf_op jit(solution)/shard_map/ppermute | solution.py:409
  111.2 5.9 %collective-permute-start.19 = (bf16[104,1024]{1,0:T(8,128)(2,1)S(1)}, bf16[104,1024]{1,0:T(8,128)(2,1)S(1)}, u32[]{:S(2)}, u32[]{:S(2)}) collective-permute-start(bf16[104,1024]{1,0:T(8,128)(2,1)S(1)} %term.12.refs_0_), channel_id=1, source_target_pairs={{0,7},{1,2},{2,1},{3,4},{4,3},{5,6},{6,5},{7,0},{8,15},{9,10},{10,... | collective-permute-start | bytes 638984 | tf_op jit(solution)/shard_map/ppermute | solution.py:411
  119.2 5.4 %collective-permute-start.22 = (bf16[104,1024]{1,0:T(8,128)(2,1)S(1)}, bf16[104,1024]{1,0:T(8,128)(2,1)S(1)}, u32[]{:S(2)}, u32[]{:S(2)}) collective-permute-start(bf16[104,1024]{1,0:T(8,128)(2,1)S(1)} %get-tuple-element.58.mine_ref), channel_id=1, source_target_pairs={{0,7},{1,2},{2,1},{3,4},{4,3},{5,6},{6,5},{7,0},{8,15},{9,10},{10,... | collective-permute-start | bytes 638984 | tf_op jit(solution)/shard_map/ppermute | solution.py:409
  121.4 5.9 %collective-permute-start.21 = (bf16[104,1024]{1,0:T(8,128)(2,1)S(1)}, bf16[104,1024]{1,0:T(8,128)(2,1)S(1)}, u32[]{:S(2)}, u32[]{:S(2)}) collective-permute-start(bf16[104,1024]{1,0:T(8,128)(2,1)S(1)} %term.15.mine_ref), channel_id=1, source_target_pairs={{0,7},{1,2},{2,1},{3,4},{4,3},{5,6},{6,5},{7,0},{8,15},{9,10},{10,... | collective-permute-start | bytes 638984 | tf_op jit(solution)/shard_map/ppermute | solution.py:411

commit v7 on v6

--- a/solution.py
+++ b/solution.py
@@ -359,18 +359,21 @@
 def on_device(orbitals, intersection_inv, interp, occ_interp, chol_factors, fields):
     orb = orbitals[0]
     part, rows, inv, orb_v, occ = call_start(interp, intersection_inv[0], orb, occ_interp)
-    others = [lax.ppermute(orb, "y", ring(NY, -j)) for j in (1, 2, 3)]
+    others = []
+    for j in (1, 2, 3):
+        others.append(lax.ppermute(orb, "y", ring(NY, -j)))
     a_par = swap_core(interp)
     occ_par = swap_core(occ_interp)
     chol_par = swap_core(chol_factors)
-    part, *others = lax.optimization_barrier((part, *others))
+    part, others[0], others[2] = lax.optimization_barrier((part, others[0], others[2]))
     part = lax.ppermute(part, "y", ring(NY, 2))
     chol_far = lax.ppermute(chol_factors, "y", ring(NY, 2))
     chol_far_par = swap_core(chol_far)
 
     weights = call_head(inv, [orb_v, *others], rows, a_par, occ, occ_par)
     mine, other = call_slabs([orb, *others])
-    terms = call_join(mine, swap_core(other))
+    other = swap_core(other)
+    terms = call_join(mine, other)
     all_weights = lax.all_to_all(
         weights, ("z", "x"), 0, 0, tiled=True, axis_index_groups=WALK_RANKS
     ).reshape(32, 1024)

time: 148 us -> 141 us (0.953)
  waiting for transfers between devices: 39.3 us -> 35.3 us
  local copies, waits for them, and re-layouts: 3.07 us -> 1.42 us
    ppermute x3, waiting for transfers between devices: 7.68 us -> 5.72 us  [on_device(): others.append(lax.ppermute(orb, 'y', ring(NY, -j)))]
    all_to_all x1, starting transfers between devices: 7.17 us -> 5.25 us  [on_device(): lax.all_to_all(jnp.broadcast_to(partial_bias[None], (8, 32, 256)), ('y',...]
    unnamed x16 -> x12, local copies, waits for them, and re-layouts: 2.34 us -> 0.67 us
    ppermute x3, waiting for transfers between devices: 1.56 us -> 0.06 us  [on_device(): far.append(lax.ppermute(part, 'x', ring(NX, -j)))]
    ppermute x1, waiting for transfers between devices: 11.1 us -> 9.66 us  [on_device(): part = lax.ppermute(part, 'y', ring(NY, 2))]
where the time goes in v7:
time: 141 us
  starting transfers between devices  59.6 us (42%)
  waiting for transfers between devices  35.3 us (25%)
  Pallas kernels  26 us (18%)
  blocking collectives  16 us (11%)
  local copies, waits for them, and re-layouts  1.42 us (1%)
    all_to_all x1, blocking collectives, on_device(): lax.all_to_all(blocks, ('y', 'core'), 0, 0, tiled=True, axis_index_groups...  16 us
    ppermute x9, starting transfers between devices, swap_core(): return lax.ppermute(value, 'core', ring(NC, 1))  15.4 us
    pallas_call x9, Pallas kernels, call_term(): pl.pallas_call(kernel, out_shape=out_shape, in_specs=[spec(pltpu.VMEM)] *...  14 us
    all_to_all x1, starting transfers between devices, on_device(): lax.all_to_all(field_part, ('z', 'x'), 0, 0, tiled=True, axis_index_group...  11 us
    all_to_all x1, starting transfers between devices, on_device(): lax.all_to_all(weights, ('z', 'x'), 0, 0, tiled=True, axis_index_groups=W...  10.6 us
    ppermute x1, waiting for transfers between devices, on_device(): part = lax.ppermute(part, 'y', ring(NY, 2))  9.66 us
    ppermute x3, waiting for transfers between devices, on_device(): other_1 = lax.ppermute(mine_1, ('y', 'core'), PAIRS)  6.52 us
    ppermute x3, waiting for transfers between devices, on_device(): other_0 = lax.ppermute(mine_0, ('y', 'core'), PAIRS)  5.86 us
  transfers between devices with their start and end apart: 26, of which 14 were waited for; matrix products, arithmetic and copies ran while one was open for 1% of the time, Pallas kernels for 9%

profile of v7, /device:TPU:1, one launch (start us, length us, event | category | flops | bytes accessed | tf_op | source)
XLA Modules:
  0.0 140.5 jit_solution(7987472614077987498)
XLA Ops:
  0.7 3.3 %collective-permute-start.4 = (bf16[2048,512]{1,0:T(8,128)(2,1)}, bf16[2048,512]{1,0:T(8,128)(2,1)S(1)}, u32[]{:S(2)}, u32[]{:S(2)}) collective-permute-start(bf16[2048,512]{1,0:T(8,128)(2,1)} %refs_0_.1), channel_id=1, source_target_pairs={{0,1},{1,0},{2,3},{3,2},{4,5},{5,4},{6,7},{7,6},{8,9},{9,8},{10,11... | collective-permute-start | bytes 6291464 | tf_op jit(solution)/shard_map/ppermute | solution.py:35
  4.0 2.7 %collective-permute-start = (bf16[400,256]{1,0:T(8,128)(2,1)}, bf16[400,256]{1,0:T(8,128)(2,1)S(1)}, u32[]{:S(2)}, u32[]{:S(2)}) collective-permute-start(bf16[400,256]{1,0:T(8,128)(2,1)} %bitcast.6), channel_id=1, source_target_pairs={{0,6},{2,0},{4,2},{6,4},{1,7},{3,1},{5,3},{7,5},{8,14},{10,8},{12,... | collective-permute-start | bytes 614408 | tf_op jit(solution)/shard_map/ppermute | solution.py:364
  6.6 1.7 %start.1 = (bf16[512,512]{1,0:T(8,128)(2,1)S(1)}, bf16[1024,512]{1,0:T(8,128)(2,1)S(1)}, bf16[400,400]{1,0:T(8,128)(2,1)S(1)}, bf16[400,256]{1,0:T(8,128)(2,1)S(1)}, bf16[400,512]{1,0:T(8,128)(2,1)S(1)}) custom-call(bf16[2048,512]{1,0:T(8,128)(2,1)} %refs_0_.1, bf16[400,400]{1,0:T(8,128)(2,1)} %bitcast.10, bf16[400,256]{1,0:T(8,128)(2,1)} %bitcast.7, ...), custom_call_target="tpu_custom_call" | custom-call | tf_op jit(solution)/shard_map/start/pallas_call | solution.py:73
  8.4 3.6 %collective-permute-done.1.o3 = bf16[400,256]{1,0:T(8,128)(2,1)S(1)} collective-permute-done((bf16[400,256]{1,0:T(8,128)(2,1)}, bf16[400,256]{1,0:T(8,128)(2,1)S(1)}, u32[]{:S(2)}, u32[]{:S(2)}) %collective-permute-start.1) | collective-permute-done | bytes 204832 | tf_op jit(solution)/shard_map/ppermute | solution.py:364
  11.9 1.2 collective-permute-start.9
  13.1 1.8 %collective-permute-start.2 = (bf16[400,256]{1,0:T(8,128)(2,1)S(1)}, bf16[400,256]{1,0:T(8,128)(2,1)S(1)}, u32[]{:S(2)}, u32[]{:S(2)}) collective-permute-start(bf16[400,256]{1,0:T(8,128)(2,1)S(1)} %bitcast.8), channel_id=1, source_target_pairs={{0,4},{2,6},{4,0},{6,2},{1,5},{3,7},{5,1},{7,3},{8,12},{10,14},{12... | collective-permute-start | bytes 614408 | tf_op jit(solution)/shard_map/ppermute | solution.py:364
  14.9 1.5 %collective-permute-start.5 = (bf16[400,512]{1,0:T(8,128)(2,1)S(1)}, bf16[400,512]{1,0:T(8,128)(2,1)S(1)}, u32[]{:S(2)}, u32[]{:S(2)}) collective-permute-start(bf16[400,512]{1,0:T(8,128)(2,1)S(1)} %copy-done.5), channel_id=1, source_target_pairs={{0,1},{1,0},{2,3},{3,2},{4,5},{5,4},{6,7},{7,6},{8,9},{9,8},{10,11... | collective-permute-start | bytes 1228808 | tf_op jit(solution)/shard_map/ppermute | solution.py:35
  16.4 9.7 %collective-permute-done.9.refs_2_ = bf16[512,512]{1,0:T(8,128)(2,1)} collective-permute-done((bf16[512,512]{1,0:T(8,128)(2,1)S(1)}, bf16[512,512]{1,0:T(8,128)(2,1)}, u32[]{:S(2)}, u32[]{:S(2)}) %collective-permute-start.9) | collective-permute-done | bytes 524320 | tf_op jit(solution)/shard_map/ppermute | solution.py:369
  26.1 2.1 %collective-permute-start.11 = (bf16[512,512]{1,0:T(8,128)(2,1)}, bf16[512,512]{1,0:T(8,128)(2,1)}, u32[]{:S(2)}, u32[]{:S(2)}) collective-permute-start(bf16[512,512]{1,0:T(8,128)(2,1)} %collective-permute-done.9.refs_2_), channel_id=1, source_target_pairs={{0,16},{8,24},{16,0},{24,8},{1,17},{9,25},{17,1},{25,9},{2,18},{10... | collective-permute-start | bytes 1572872 | tf_op jit(solution)/shard_map/ppermute | solution.py:383
  28.2 2.2 %collective-permute-done.2.o2 = bf16[400,256]{1,0:T(8,128)(2,1)S(1)} collective-permute-done((bf16[400,256]{1,0:T(8,128)(2,1)S(1)}, bf16[400,256]{1,0:T(8,128)(2,1)S(1)}, u32[]{:S(2)}, u32[]{:S(2)}) %collective-permute-start.2) | collective-permute-done | bytes 204832 | tf_op jit(solution)/shard_map/ppermute | solution.py:364
  30.3 0.9 collective-permute-start.10
  31.3 2.0 %collective-permute-start.7 = (bf16[512,256]{1,0:T(8,128)(2,1)S(1)}, bf16[512,256]{1,0:T(8,128)(2,1)S(1)}, u32[]{:S(2)}, u32[]{:S(2)}) collective-permute-start(bf16[512,256]{1,0:T(8,128)(2,1)S(1)} %copy-done.2), channel_id=1, source_target_pairs={{0,4},{2,6},{4,0},{6,2},{1,5},{3,7},{5,1},{7,3},{8,12},{10,14},{12... | collective-permute-start | bytes 786440 | tf_op jit(solution)/shard_map/ppermute | solution.py:370
  33.3 2.9 %collective-permute-start.6 = (bf16[512,256]{1,0:T(8,128)(2,1)S(1)}, bf16[512,256]{1,0:T(8,128)(2,1)}, u32[]{:S(2)}, u32[]{:S(2)}) collective-permute-start(bf16[512,256]{1,0:T(8,128)(2,1)S(1)} %copy-done.2), channel_id=1, source_target_pairs={{0,1},{1,0},{2,3},{3,2},{4,5},{5,4},{6,7},{7,6},{8,9},{9,8},{10,11... | collective-permute-start | bytes 786440 | tf_op jit(solution)/shard_map/ppermute | solution.py:35
  36.2 2.5 %head.1 = f32[32,1,1024]{2,1,0:T(1,128)} custom-call(bf16[400,400]{1,0:T(8,128)(2,1)S(1)} %get-tuple-element.39.inv, bf16[400,256]{1,0:T(8,128)(2,1)S(1)} %get-tuple-element.40.o0, bf16[400,256]{1,0:T(8,128)(2,1)S(1)} %collective-permute-done.o1, bf16[400,256]{1,0:T(8,128)(2,1)S(1)} %collective-permute-done.2.o2, ...), custom_call_target="tpu_custom_call" | custom-call | tf_op jit(solution)/shard_map/head/pallas_call | solution.py:109
  38.7 10.6 %all-to-all-start = ((f32[32,1,1024]{2,1,0:T(1,128)}), f32[32,1,1024]{2,1,0:T(1,128)S(1)}, u32[]{:S(2)}, u32[]{:S(2)}) async-start(f32[32,1,1024]{2,1,0:T(1,128)} %head.1), calls=%async_computation | async-start | bytes 262144 | tf_op jit(solution)/shard_map/all_to_all | solution.py:377
  49.9 3.3 %collective-permute-start.16 = (bf16[512,512]{1,0:T(8,128)(2,1)}, bf16[512,512]{1,0:T(8,128)(2,1)S(1)}, u32[]{:S(2)}, u32[]{:S(2)}) collective-permute-start(bf16[512,512]{1,0:T(8,128)(2,1)} %collective-permute-done.12.refs_5_), channel_id=1, source_target_pairs={{0,1},{1,0},{2,3},{3,2},{4,5},{5,4},{6,7},{7,6},{8,9},{9,8},{10,11... | collective-permute-start | bytes 1572872 | tf_op jit(solution)/shard_map/ppermute | solution.py:35
  53.2 1.9 %collective-permute-start.14 = (bf16[512,512]{1,0:T(8,128)(2,1)}, bf16[512,512]{1,0:T(8,128)(2,1)}, u32[]{:S(2)}, u32[]{:S(2)}) collective-permute-start(bf16[512,512]{1,0:T(8,128)(2,1)} %collective-permute-done.10.refs_3_), channel_id=1, source_target_pairs={{0,1},{1,0},{2,3},{3,2},{4,5},{5,4},{6,7},{7,6},{8,9},{9,8},{10,11... | collective-permute-start | bytes 1572872 | tf_op jit(solution)/shard_map/ppermute | solution.py:35
  55.3 1.3 fusion
  56.6 0.7 broadcast_in_dim.2
  57.4 5.2 %all-to-all-start.1 = ((f32[8,32,256]{2,1,0:T(8,128)}), f32[8,32,256]{2,1,0:T(8,128)S(1)}, u32[]{:S(2)}, u32[]{:S(2)}) async-start(f32[8,32,256]{2,1,0:T(8,128)} %broadcast_in_dim.2), calls=%async_computation.1 | async-start | bytes 524288 | tf_op jit(solution)/shard_map/all_to_all | solution.py:389
  62.6 4.5 %all-to-all-done.1.bias_ref = f32[8,32,256]{2,1,0:T(8,128)S(1)} async-done(((f32[8,32,256]{2,1,0:T(8,128)}), f32[8,32,256]{2,1,0:T(8,128)S(1)}, u32[]{:S(2)}, u32[]{:S(2)}) %all-to-all-start.1) | async-done | bytes 262176 | tf_op jit(solution)/shard_map/all_to_all | solution.py:389
  67.2 1.8 %field.1 = (f32[32,256]{1,0:T(8,128)}, bf16[32,4,512]{2,1,0:T(4,128)(2,1)S(1)}) custom-call(f32[8,32,256]{2,1,0:T(8,128)S(1)} %all-to-all-done.1.bias_ref, f32[32,256]{1,0:T(8,128)S(1)} %copy-done.4, bf16[512,256]{1,0:T(8,128)(2,1)S(1)} %copy-done.2, bf16[512,256]{1,0:T(8,128)(2,1)} %collective-permute-done.6.c1, ...), custom_call_target="tpu_custom_call" | custom-call | tf_op jit(solution)/shard_map/field/pallas_call | solution.py:142
  69.6 11.0 %all-to-all-start.2 = ((bf16[32,4,512]{2,1,0:T(4,128)(2,1)}), bf16[32,4,512]{2,1,0:T(4,128)(2,1)S(1)}, u32[]{:S(2)}, u32[]{:S(2)}) async-start(bf16[32,4,512]{2,1,0:T(4,128)(2,1)} %copy-done.3), calls=%async_computation.2 | async-start | bytes 262144 | tf_op jit(solution)/shard_map/all_to_all | solution.py:400
  80.8 1.9 %collective-permute-start.3 = (bf16[104,1024]{1,0:T(8,128)(2,1)S(1)}, bf16[104,1024]{1,0:T(8,128)(2,1)S(1)}, u32[]{:S(2)}, u32[]{:S(2)}) collective-permute-start(bf16[104,1024]{1,0:T(8,128)(2,1)S(1)} %get-tuple-element.36), channel_id=1, source_target_pairs={{0,1},{1,0},{2,3},{3,2},{4,5},{5,4},{6,7},{7,6},{8,9},{9,8},{10,11... | collective-permute-start | bytes 638984 | tf_op jit(solution)/shard_map/ppermute | solution.py:35
  82.8 1.1 collective-permute-done.3.par
  83.9 1.7 %all-to-all-done.2.arrived_ref = bf16[32,4,512]{2,1,0:T(4,128)(2,1)S(1)} async-done(((bf16[32,4,512]{2,1,0:T(4,128)(2,1)}), bf16[32,4,512]{2,1,0:T(4,128)(2,1)S(1)}, u32[]{:S(2)}, u32[]{:S(2)}) %all-to-all-start.2) | async-done | bytes 131104 | tf_op jit(solution)/shard_map/all_to_all | solution.py:400
  85.6 5.1 %first.1 = (bf16[4,104,512]{2,1,0:T(8,128)(2,1)S(1)}, bf16[104,1024]{1,0:T(8,128)(2,1)S(1)}, f32[4,512]{1,0:T(4,128)S(1)}, bf16[4,2048,512]{2,1,0:T(8,128)(2,1)S(1)}) custom-call(bf16[104,1024]{1,0:T(8,128)(2,1)S(1)} %get-tuple-element.37.term_0.total_ref, bf16[104,1024]{1,0:T(8,128)(2,1)S(1)} %get-tuple-element.38.term_1.refs_2_, ...), custom_call_target="tpu_custom_call" | custom-call | tf_op jit(solution)/shard_map/first/pallas_call | solution.py:262
  90.7 2.5 %collective-permute-start.18 = (bf16[104,1024]{1,0:T(8,128)(2,1)S(1)}, bf16[104,1024]{1,0:T(8,128)(2,1)S(1)}, u32[]{:S(2)}, u32[]{:S(2)}) collective-permute-start(bf16[104,1024]{1,0:T(8,128)(2,1)S(1)} %get-tuple-element.47.mine_ref), channel_id=1, source_target_pairs={{0,7},{1,2},{2,1},{3,4},{4,3},{5,6},{6,5},{7,0},{8,15},{9,10},{10,... | collective-permute-start | bytes 638984 | tf_op jit(solution)/shard_map/ppermute | solution.py:412
  93.2 1.4 term.9.refs_0_
  94.7 2.0 %collective-permute-done.18.other_ref = bf16[104,1024]{1,0:T(8,128)(2,1)S(1)} collective-permute-done((bf16[104,1024]{1,0:T(8,128)(2,1)S(1)}, bf16[104,1024]{1,0:T(8,128)(2,1)S(1)}, u32[]{:S(2)}, u32[]{:S(2)}) %collective-permute-start.18) | collective-permute-done | bytes 213024 | tf_op jit(solution)/shard_map/ppermute | solution.py:412
  96.7 0.7 term.10
  97.5 2.8 %collective-permute-done.17.refs_1_ = bf16[104,1024]{1,0:T(8,128)(2,1)S(1)} collective-permute-done((bf16[104,1024]{1,0:T(8,128)(2,1)S(1)}, bf16[104,1024]{1,0:T(8,128)(2,1)S(1)}, u32[]{:S(2)}, u32[]{:S(2)}) %collective-permute-start.17) | collective-permute-done | bytes 213024 | tf_op jit(solution)/shard_map/ppermute | solution.py:414
  100.3 2.0 %term.11 = (bf16[4,104,512]{2,1,0:T(8,128)(2,1)S(1)}, bf16[104,1024]{1,0:T(8,128)(2,1)S(1)}, f32[104,1024]{1,0:T(8,128)S(1)}) custom-call(bf16[104,1024]{1,0:T(8,128)(2,1)S(1)} %term.9.refs_0_, bf16[104,1024]{1,0:T(8,128)(2,1)S(1)} %collective-permute-done.17.refs_1_, bf16[104,1024]{1,0:T(8,128)(2,1)S(1)} %get-tuple-element.38.term_1.refs_2_, ...), custom_call_target="tpu_custom_call" | custom-call | tf_op jit(solution)/shard_map/term/pallas_call | solution.py:328
  102.9 1.4 term.12.refs_0_
  104.3 1.3 collective-permute-start.19
  105.6 2.0 %collective-permute-done.20.other_ref = bf16[104,1024]{1,0:T(8,128)(2,1)S(1)} collective-permute-done((bf16[104,1024]{1,0:T(8,128)(2,1)S(1)}, bf16[104,1024]{1,0:T(8,128)(2,1)S(1)}, u32[]{:S(2)}, u32[]{:S(2)}) %collective-permute-start.20) | collective-permute-done | bytes 213024 | tf_op jit(solution)/shard_map/ppermute | solution.py:412
  107.7 0.7 term.13
  108.4 1.8 %collective-permute-done.19.refs_1_ = bf16[104,1024]{1,0:T(8,128)(2,1)S(1)} collective-permute-done((bf16[104,1024]{1,0:T(8,128)(2,1)S(1)}, bf16[104,1024]{1,0:T(8,128)(2,1)S(1)}, u32[]{:S(2)}, u32[]{:S(2)}) %collective-permute-start.19) | collective-permute-done | bytes 213024 | tf_op jit(solution)/shard_map/ppermute | solution.py:414
  110.2 2.0 %term.14 = (bf16[4,104,512]{2,1,0:T(8,128)(2,1)S(1)}, bf16[104,1024]{1,0:T(8,128)(2,1)S(1)}, f32[104,1024]{1,0:T(8,128)S(1)}) custom-call(bf16[104,1024]{1,0:T(8,128)(2,1)S(1)} %term.12.refs_0_, bf16[104,1024]{1,0:T(8,128)(2,1)S(1)} %collective-permute-done.19.refs_1_, f32[104,1024]{1,0:T(8,128)S(1)} %get-tuple-element.51.refs_2_, ...), custom_call_target="tpu_custom_call" | custom-call | tf_op jit(solution)/shard_map/term/pallas_call | solution.py:328
  112.3 0.8 collective-permute-start.22
  113.0 1.4 term.15.mine_ref
  114.4 1.4 collective-permute-start.21
  115.8 1.8 %collective-permute-done.22.other_ref = bf16[104,1024]{1,0:T(8,128)(2,1)S(1)} collective-permute-done((bf16[104,1024]{1,0:T(8,128)(2,1)S(1)}, bf16[104,1024]{1,0:T(8,128)(2,1)S(1)}, u32[]{:S(2)}, u32[]{:S(2)}) %collective-permute-start.22) | collective-permute-done | bytes 213024 | tf_op jit(solution)/shard_map/ppermute | solution.py:412
  117.6 0.7 term.16
  118.4 1.9 %collective-permute-done.21.other_ref = bf16[104,1024]{1,0:T(8,128)(2,1)S(1)} collective-permute-done((bf16[104,1024]{1,0:T(8,128)(2,1)S(1)}, bf16[104,1024]{1,0:T(8,128)(2,1)S(1)}, u32[]{:S(2)}, u32[]{:S(2)}) %collective-permute-start.21) | collective-permute-done | bytes 213024 | tf_op jit(solution)/shard_map/ppermute | solution.py:414
  120.3 3.5 %term.17 = bf16[8,112,256]{2,1,0:T(8,128)(2,1)S(1)} custom-call(bf16[104,1024]{1,0:T(8,128)(2,1)S(1)} %term.15.mine_ref, bf16[104,1024]{1,0:T(8,128)(2,1)S(1)} %collective-permute-done.21.other_ref, f32[104,1024]{1,0:T(8,128)S(1)} %get-tuple-element.58.total_0, f32[104,1024]{1,0:T(8,128)S(1)} %get-tuple-element.59.total_1, ...), custom_call_target="tpu_custom_call" | custom-call | tf_op jit(solution)/shard_map/term/pallas_call | solution.py:328
  123.8 16.0 %all_to_all.20.back_ref = bf16[8,112,256]{2,1,0:T(8,128)(2,1)S(1)} all-to-all(bf16[8,112,256]{2,1,0:T(8,128)(2,1)S(1)} %term.17), channel_id=1, replica_groups={{7,6,5,4,3,2,1,0},{15,14,13,12,11,10,9,8},{23,22,21,20,19,18,17,16},{31..., dimensions={0} | all-to-all | bytes 917504 | tf_op jit(solution)/shard_map/all_to_all | solution.py:430
  139.8 0.7 end.1
  (35 shorter events, 2.5 us)
Async XLA Ops:
  0.6 12.4 %copy-start.1 = (bf16[1,400,256]{2,1,0:T(8,128)(2,1)S(1)}, bf16[1,400,256]{2,1,0:T(8,128)(2,1)}, u32[]{:S(2)}) copy-start(bf16[1,400,256]{2,1,0:T(8,128)(2,1)} %param.6) | copy-start | bytes 614404
  0.6 14.3 %copy-start.5 = (bf16[400,512]{1,0:T(8,128)(2,1)S(1)}, bf16[400,512]{1,0:T(8,128)(2,1)}, u32[]{:S(2)}) copy-start(bf16[400,512]{1,0:T(8,128)(2,1)} %occ.1) | copy-start | bytes 1228804
  0.7 30.6 %copy-start.2 = (bf16[512,256]{1,0:T(8,128)(2,1)S(1)}, bf16[512,256]{1,0:T(8,128)(2,1)}, u32[]{:S(2)}) copy-start(bf16[512,256]{1,0:T(8,128)(2,1)} %c0.1) | copy-start | bytes 786436
  0.7 32.6 %collective-permute-start.4 = (bf16[2048,512]{1,0:T(8,128)(2,1)}, bf16[2048,512]{1,0:T(8,128)(2,1)S(1)}, u32[]{:S(2)}, u32[]{:S(2)}) collective-permute-start(bf16[2048,512]{1,0:T(8,128)(2,1)} %refs_0_.1), channel_id=1, source_target_pairs={{0,1},{1,0},{2,3},{3,2},{4,5},{5,4},{6,7},{7,6},{8,9},{9,8},{10,11... | collective-permute-start | bytes 6291464 | tf_op jit(solution)/shard_map/ppermute | solution.py:35
  3.9 8.0 %collective-permute-start.1 = (bf16[400,256]{1,0:T(8,128)(2,1)}, bf16[400,256]{1,0:T(8,128)(2,1)S(1)}, u32[]{:S(2)}, u32[]{:S(2)}) collective-permute-start(bf16[400,256]{1,0:T(8,128)(2,1)} %bitcast.5), channel_id=1, source_target_pairs={{0,2},{2,4},{4,6},{6,0},{1,3},{3,5},{5,7},{7,1},{8,10},{10,12},{12... | collective-permute-start | bytes 614408 | tf_op jit(solution)/shard_map/ppermute | solution.py:364
  4.0 8.0 %collective-permute-start = (bf16[400,256]{1,0:T(8,128)(2,1)}, bf16[400,256]{1,0:T(8,128)(2,1)S(1)}, u32[]{:S(2)}, u32[]{:S(2)}) collective-permute-start(bf16[400,256]{1,0:T(8,128)(2,1)} %bitcast.6), channel_id=1, source_target_pairs={{0,6},{2,0},{4,2},{6,4},{1,7},{3,1},{5,3},{7,5},{8,14},{10,8},{12,... | collective-permute-start | bytes 614408 | tf_op jit(solution)/shard_map/ppermute | solution.py:364
  11.9 14.1 %collective-permute-start.9 = (bf16[512,512]{1,0:T(8,128)(2,1)S(1)}, bf16[512,512]{1,0:T(8,128)(2,1)}, u32[]{:S(2)}, u32[]{:S(2)}) collective-permute-start(bf16[512,512]{1,0:T(8,128)(2,1)S(1)} %get-tuple-element.44), channel_id=1, source_target_pairs={{0,4},{2,6},{4,0},{6,2},{1,5},{3,7},{5,1},{7,3},{8,12},{10,14},{12... | collective-permute-start | bytes 1572872 | tf_op jit(solution)/shard_map/ppermute | solution.py:369
  13.1 17.3 %collective-permute-start.2 = (bf16[400,256]{1,0:T(8,128)(2,1)S(1)}, bf16[400,256]{1,0:T(8,128)(2,1)S(1)}, u32[]{:S(2)}, u32[]{:S(2)}) collective-permute-start(bf16[400,256]{1,0:T(8,128)(2,1)S(1)} %bitcast.8), channel_id=1, source_target_pairs={{0,4},{2,6},{4,0},{6,2},{1,5},{3,7},{5,1},{7,3},{8,12},{10,14},{12... | collective-permute-start | bytes 614408 | tf_op jit(solution)/shard_map/ppermute | solution.py:364
  14.9 16.4 %collective-permute-start.5 = (bf16[400,512]{1,0:T(8,128)(2,1)S(1)}, bf16[400,512]{1,0:T(8,128)(2,1)S(1)}, u32[]{:S(2)}, u32[]{:S(2)}) collective-permute-start(bf16[400,512]{1,0:T(8,128)(2,1)S(1)} %copy-done.5), channel_id=1, source_target_pairs={{0,1},{1,0},{2,3},{3,2},{4,5},{5,4},{6,7},{7,6},{8,9},{9,8},{10,11... | collective-permute-start | bytes 1228808 | tf_op jit(solution)/shard_map/ppermute | solution.py:35
  26.1 23.8 %collective-permute-start.12 = (bf16[512,512]{1,0:T(8,128)(2,1)}, bf16[512,512]{1,0:T(8,128)(2,1)}, u32[]{:S(2)}, u32[]{:S(2)}) collective-permute-start(bf16[512,512]{1,0:T(8,128)(2,1)} %collective-permute-done.9.refs_2_), channel_id=1, source_target_pairs={{0,8},{8,16},{16,24},{24,0},{1,9},{9,17},{17,25},{25,1},{2,10},{10... | collective-permute-start | bytes 1572872 | tf_op jit(solution)/shard_map/ppermute | solution.py:383
  26.1 27.1 %collective-permute-start.11 = (bf16[512,512]{1,0:T(8,128)(2,1)}, bf16[512,512]{1,0:T(8,128)(2,1)}, u32[]{:S(2)}, u32[]{:S(2)}) collective-permute-start(bf16[512,512]{1,0:T(8,128)(2,1)} %collective-permute-done.9.refs_2_), channel_id=1, source_target_pairs={{0,16},{8,24},{16,0},{24,8},{1,17},{9,25},{17,1},{25,9},{2,18},{10... | collective-permute-start | bytes 1572872 | tf_op jit(solution)/shard_map/ppermute | solution.py:383
  30.3 22.9 %collective-permute-start.10 = (bf16[512,512]{1,0:T(8,128)(2,1)}, bf16[512,512]{1,0:T(8,128)(2,1)}, u32[]{:S(2)}, u32[]{:S(2)}) collective-permute-start(bf16[512,512]{1,0:T(8,128)(2,1)} %collective-permute-done.9.refs_2_), channel_id=1, source_target_pairs={{0,24},{8,0},{16,8},{24,16},{1,25},{9,1},{17,9},{25,17},{2,26},{10... | collective-permute-start | bytes 1572872 | tf_op jit(solution)/shard_map/ppermute | solution.py:383
  31.3 18.0 %collective-permute-start.7 = (bf16[512,256]{1,0:T(8,128)(2,1)S(1)}, bf16[512,256]{1,0:T(8,128)(2,1)S(1)}, u32[]{:S(2)}, u32[]{:S(2)}) collective-permute-start(bf16[512,256]{1,0:T(8,128)(2,1)S(1)} %copy-done.2), channel_id=1, source_target_pairs={{0,4},{2,6},{4,0},{6,2},{1,5},{3,7},{5,1},{7,3},{8,12},{10,14},{12... | collective-permute-start | bytes 786440 | tf_op jit(solution)/shard_map/ppermute | solution.py:370
  33.3 5.4 %copy-start = (bf16[2048,512]{1,0:T(8,128)(2,1)}, bf16[2048,512]{1,0:T(8,128)(2,1)S(1)}, u32[]{:S(2)}) copy-start(bf16[2048,512]{1,0:T(8,128)(2,1)S(1)} %collective-permute-done.4.a_par.refs_1_) | copy-start | bytes 6291460
  33.3 16.4 %collective-permute-start.6 = (bf16[512,256]{1,0:T(8,128)(2,1)S(1)}, bf16[512,256]{1,0:T(8,128)(2,1)}, u32[]{:S(2)}, u32[]{:S(2)}) collective-permute-start(bf16[512,256]{1,0:T(8,128)(2,1)S(1)} %copy-done.2), channel_id=1, source_target_pairs={{0,1},{1,0},{2,3},{3,2},{4,5},{5,4},{6,7},{7,6},{8,9},{9,8},{10,11... | collective-permute-start | bytes 786440 | tf_op jit(solution)/shard_map/ppermute | solution.py:35
  36.2 30.9 %copy-start.4 = (f32[32,256]{1,0:T(8,128)S(1)}, f32[32,256]{1,0:T(8,128)}, u32[]{:S(2)}) copy-start(f32[32,256]{1,0:T(8,128)} %fields_ref.1) | copy-start | bytes 98308
  38.7 16.6 %all-to-all-start = ((f32[32,1,1024]{2,1,0:T(1,128)}), f32[32,1,1024]{2,1,0:T(1,128)S(1)}, u32[]{:S(2)}, u32[]{:S(2)}) async-start(f32[32,1,1024]{2,1,0:T(1,128)} %head.1), calls=%async_computation | async-start | bytes 262144 | tf_op jit(solution)/shard_map/all_to_all | solution.py:377
  49.3 13.3 %collective-permute-start.8 = (bf16[512,256]{1,0:T(8,128)(2,1)S(1)}, bf16[512,256]{1,0:T(8,128)(2,1)S(1)}, u32[]{:S(2)}, u32[]{:S(2)}) collective-permute-start(bf16[512,256]{1,0:T(8,128)(2,1)S(1)} %collective-permute-done.7.c2), channel_id=1, source_target_pairs={{0,1},{1,0},{2,3},{3,2},{4,5},{5,4},{6,7},{7,6},{8,9},{9,8},{10,11... | collective-permute-start | bytes 786440 | tf_op jit(solution)/shard_map/ppermute | solution.py:35
  49.7 34.2 %collective-permute-start.13 = (bf16[512,512]{1,0:T(8,128)(2,1)}, bf16[512,512]{1,0:T(8,128)(2,1)S(1)}, u32[]{:S(2)}, u32[]{:S(2)}) collective-permute-start(bf16[512,512]{1,0:T(8,128)(2,1)} %collective-permute-done.9.refs_2_), channel_id=1, source_target_pairs={{0,1},{1,0},{2,3},{3,2},{4,5},{5,4},{6,7},{7,6},{8,9},{9,8},{10,11... | collective-permute-start | bytes 1572872 | tf_op jit(solution)/shard_map/ppermute | solution.py:35
  49.9 34.0 %collective-permute-start.16 = (bf16[512,512]{1,0:T(8,128)(2,1)}, bf16[512,512]{1,0:T(8,128)(2,1)S(1)}, u32[]{:S(2)}, u32[]{:S(2)}) collective-permute-start(bf16[512,512]{1,0:T(8,128)(2,1)} %collective-permute-done.12.refs_5_), channel_id=1, source_target_pairs={{0,1},{1,0},{2,3},{3,2},{4,5},{5,4},{6,7},{7,6},{8,9},{9,8},{10,11... | collective-permute-start | bytes 1572872 | tf_op jit(solution)/shard_map/ppermute | solution.py:35
  53.2 30.7 %collective-permute-start.15 = (bf16[512,512]{1,0:T(8,128)(2,1)}, bf16[512,512]{1,0:T(8,128)(2,1)S(1)}, u32[]{:S(2)}, u32[]{:S(2)}) collective-permute-start(bf16[512,512]{1,0:T(8,128)(2,1)} %collective-permute-done.11.refs_4_), channel_id=1, source_target_pairs={{0,1},{1,0},{2,3},{3,2},{4,5},{5,4},{6,7},{7,6},{8,9},{9,8},{10,11... | collective-permute-start | bytes 1572872 | tf_op jit(solution)/shard_map/ppermute | solution.py:35
  53.2 30.7 %collective-permute-start.14 = (bf16[512,512]{1,0:T(8,128)(2,1)}, bf16[512,512]{1,0:T(8,128)(2,1)}, u32[]{:S(2)}, u32[]{:S(2)}) collective-permute-start(bf16[512,512]{1,0:T(8,128)(2,1)} %collective-permute-done.10.refs_3_), channel_id=1, source_target_pairs={{0,1},{1,0},{2,3},{3,2},{4,5},{5,4},{6,7},{7,6},{8,9},{9,8},{10,11... | collective-permute-start | bytes 1572872 | tf_op jit(solution)/shard_map/ppermute | solution.py:35
  57.4 9.8 %all-to-all-start.1 = ((f32[8,32,256]{2,1,0:T(8,128)}), f32[8,32,256]{2,1,0:T(8,128)S(1)}, u32[]{:S(2)}, u32[]{:S(2)}) async-start(f32[8,32,256]{2,1,0:T(8,128)} %broadcast_in_dim.2), calls=%async_computation.1 | async-start | bytes 524288 | tf_op jit(solution)/shard_map/all_to_all | solution.py:389
  69.0 0.7 copy-start.3
  69.6 15.9 %all-to-all-start.2 = ((bf16[32,4,512]{2,1,0:T(4,128)(2,1)}), bf16[32,4,512]{2,1,0:T(4,128)(2,1)S(1)}, u32[]{:S(2)}, u32[]{:S(2)}) async-start(bf16[32,4,512]{2,1,0:T(4,128)(2,1)} %copy-done.3), calls=%async_computation.2 | async-start | bytes 262144 | tf_op jit(solution)/shard_map/all_to_all | solution.py:400
  80.8 3.0 %collective-permute-start.3 = (bf16[104,1024]{1,0:T(8,128)(2,1)S(1)}, bf16[104,1024]{1,0:T(8,128)(2,1)S(1)}, u32[]{:S(2)}, u32[]{:S(2)}) collective-permute-start(bf16[104,1024]{1,0:T(8,128)(2,1)S(1)} %get-tuple-element.36), channel_id=1, source_target_pairs={{0,1},{1,0},{2,3},{3,2},{4,5},{5,4},{6,7},{7,6},{8,9},{9,8},{10,11... | collective-permute-start | bytes 638984 | tf_op jit(solution)/shard_map/ppermute | solution.py:35
  90.7 6.1 %collective-permute-start.18 = (bf16[104,1024]{1,0:T(8,128)(2,1)S(1)}, bf16[104,1024]{1,0:T(8,128)(2,1)S(1)}, u32[]{:S(2)}, u32[]{:S(2)}) collective-permute-start(bf16[104,1024]{1,0:T(8,128)(2,1)S(1)} %get-tuple-element.47.mine_ref), channel_id=1, source_target_pairs={{0,7},{1,2},{2,1},{3,4},{4,3},{5,6},{6,5},{7,0},{8,15},{9,10},{10,... | collective-permute-start | bytes 638984 | tf_op jit(solution)/shard_map/ppermute | solution.py:412
  94.6 5.7 %collective-permute-start.17 = (bf16[104,1024]{1,0:T(8,128)(2,1)S(1)}, bf16[104,1024]{1,0:T(8,128)(2,1)S(1)}, u32[]{:S(2)}, u32[]{:S(2)}) collective-permute-start(bf16[104,1024]{1,0:T(8,128)(2,1)S(1)} %term.9.refs_0_), channel_id=1, source_target_pairs={{0,7},{1,2},{2,1},{3,4},{4,3},{5,6},{6,5},{7,0},{8,15},{9,10},{10,... | collective-permute-start | bytes 638984 | tf_op jit(solution)/shard_map/ppermute | solution.py:414
  102.3 5.4 %collective-permute-start.20 = (bf16[104,1024]{1,0:T(8,128)(2,1)S(1)}, bf16[104,1024]{1,0:T(8,128)(2,1)S(1)}, u32[]{:S(2)}, u32[]{:S(2)}) collective-permute-start(bf16[104,1024]{1,0:T(8,128)(2,1)S(1)} %get-tuple-element.52.mine_ref), channel_id=1, source_target_pairs={{0,7},{1,2},{2,1},{3,4},{4,3},{5,6},{6,5},{7,0},{8,15},{9,10},{10,... | collective-permute-start | bytes 638984 | tf_op jit(solution)/shard_map/ppermute | solution.py:412
  104.3 5.9 %collective-permute-start.19 = (bf16[104,1024]{1,0:T(8,128)(2,1)S(1)}, bf16[104,1024]{1,0:T(8,128)(2,1)S(1)}, u32[]{:S(2)}, u32[]{:S(2)}) collective-permute-start(bf16[104,1024]{1,0:T(8,128)(2,1)S(1)} %term.12.refs_0_), channel_id=1, source_target_pairs={{0,7},{1,2},{2,1},{3,4},{4,3},{5,6},{6,5},{7,0},{8,15},{9,10},{10,... | collective-permute-start | bytes 638984 | tf_op jit(solution)/shard_map/ppermute | solution.py:414
  112.3 5.4 %collective-permute-start.22 = (bf16[104,1024]{1,0:T(8,128)(2,1)S(1)}, bf16[104,1024]{1,0:T(8,128)(2,1)S(1)}, u32[]{:S(2)}, u32[]{:S(2)}) collective-permute-start(bf16[104,1024]{1,0:T(8,128)(2,1)S(1)} %get-tuple-element.56.mine_ref), channel_id=1, source_target_pairs={{0,7},{1,2},{2,1},{3,4},{4,3},{5,6},{6,5},{7,0},{8,15},{9,10},{10,... | collective-permute-start | bytes 638984 | tf_op jit(solution)/shard_map/ppermute | solution.py:412
  114.4 5.9 %collective-permute-start.21 = (bf16[104,1024]{1,0:T(8,128)(2,1)S(1)}, bf16[104,1024]{1,0:T(8,128)(2,1)S(1)}, u32[]{:S(2)}, u32[]{:S(2)}) collective-permute-start(bf16[104,1024]{1,0:T(8,128)(2,1)S(1)} %term.15.mine_ref), channel_id=1, source_target_pairs={{0,7},{1,2},{2,1},{3,4},{4,3},{5,6},{6,5},{7,0},{8,15},{9,10},{10,... | collective-permute-start | bytes 638984 | tf_op jit(solution)/shard_map/ppermute | solution.py:414

commit v8 on v7

--- a/solution.py
+++ b/solution.py
@@ -28,7 +28,8 @@
 Z_ORDER = (4, 3, 5, 2, 6, 1, 7, 0)
 WALK_RANKS = [[z * NX + x for z in Z_ORDER for x in range(NX)]]
 CHOL_RANKS = [list(range(7, -1, -1))]
-PAIRS = [(i, (i + 1) % 8 if i % 2 else (i - 1) % 8) for i in range(8)]
+OWNERS = (0, 2, 5, 3, 4, 6, 1, 7)
+PAIRS = [(OWNERS[i], OWNERS[i ^ 1]) for i in range(8)]
 
 
 def swap_core(value):
@@ -47,7 +48,7 @@
 
 
 def edge_of(y, c):
-    return jnp.where(c == 1, y, (y + 3) % 4)
+    return jnp.where(c == 0, y // 2 * 2, jnp.where((y == 1) | (y == 2), 1, 3))
 
 
 def start_kernel(interp, inv, orb, occ, part, rows_out, inv_out, orb_out, occ_out, sems):
@@ -301,7 +302,7 @@
 
 
 def last_kernel(mine_ref, other_ref, total_0, total_1, product_ref, scales_ref, interp_ref, out_ref):
-    c = lax.axis_index("core")
+    y = lax.axis_index("y")
     term = added(mine_ref, other_ref)
     totals = (total_0[...], total_1[...] + term.astype(f32))
     mixed = [
@@ -319,8 +320,8 @@
                 out_ref[7 - 4 * h - b, :PIECE, :] = kept[:, 256 * b : 256 * b + 256]
                 out_ref[7 - 4 * h - b, PIECE:, :] = given[:, 256 * b : 256 * b + 256]
 
-        pl.when(c == 1)(lambda put=put: put(low, high))
-        pl.when(c == 0)(lambda put=put: put(high, low))
+        pl.when(y % 2 == 0)(lambda put=put: put(low, high))
+        pl.when(y % 2 == 1)(lambda put=put: put(high, low))
 
 
 def call_term(kernel, out_shape, *args):
@@ -339,7 +340,7 @@
     for i in range(8):
         start = 8 * TILES[i]
         n = 8 * (TILES[i + 1] - TILES[i])
-        owner, partner = (i + 1) % 8, (i + 2) % 8 if i % 2 == 0 else i
+        owner, partner = OWNERS[i], OWNERS[i ^ 1]
         kept = back_ref[7 - owner, :n, :].astype(f32)
         given = back_ref[7 - partner, PIECE : PIECE + n, :].astype(f32)
         out_ref[0, start : start + n, :] = (kept + given).astype(bf16)

time: 141 us -> 138 us (0.979)
  blocking collectives: 16 us -> 11.7 us
  starting transfers between devices: 59.6 us -> 61.7 us
    all_to_all x1, blocking collectives: 16 us -> 11.7 us  [on_device(): lax.all_to_all(blocks, ('y', 'core'), 0, 0, tiled=True, axis_index_groups...]
where the time goes in v8:
time: 138 us
  starting transfers between devices  61.7 us (45%)
  waiting for transfers between devices  34.9 us (25%)
  Pallas kernels  26.1 us (19%)
  blocking collectives  11.7 us (8%)
  local copies, waits for them, and re-layouts  1.42 us (1%)
    ppermute x9, starting transfers between devices, swap_core(): return lax.ppermute(value, 'core', ring(NC, 1))  15.4 us
    pallas_call x9, Pallas kernels, call_term(): pl.pallas_call(kernel, out_shape=out_shape, in_specs=[spec(pltpu.VMEM)] *...  14.1 us
    all_to_all x1, blocking collectives, on_device(): lax.all_to_all(blocks, ('y', 'core'), 0, 0, tiled=True, axis_index_groups...  11.7 us
    all_to_all x1, starting transfers between devices, on_device(): lax.all_to_all(field_part, ('z', 'x'), 0, 0, tiled=True, axis_index_group...  11 us
    all_to_all x1, starting transfers between devices, on_device(): lax.all_to_all(weights, ('z', 'x'), 0, 0, tiled=True, axis_index_groups=W...  10.6 us
    ppermute x1, waiting for transfers between devices, on_device(): part = lax.ppermute(part, 'y', ring(NY, 2))  9.66 us
    ppermute x3, waiting for transfers between devices, on_device(): other_1 = lax.ppermute(mine_1, ('y', 'core'), PAIRS)  6.92 us
    ppermute x3, waiting for transfers between devices, on_device(): others.append(lax.ppermute(orb, 'y', ring(NY, -j)))  5.72 us
  transfers between devices with their start and end apart: 26, of which 14 were waited for; matrix products, arithmetic and copies ran while one was open for 1% of the time, Pallas kernels for 9%

profile of v8, /device:TPU:1, one launch (start us, length us, event | category | flops | bytes accessed | tf_op | source)
XLA Modules:
  0.0 137.9 jit_solution(6347674344670937158)
XLA Ops:
  0.7 3.3 %collective-permute-start.4 = (bf16[2048,512]{1,0:T(8,128)(2,1)}, bf16[2048,512]{1,0:T(8,128)(2,1)S(1)}, u32[]{:S(2)}, u32[]{:S(2)}) collective-permute-start(bf16[2048,512]{1,0:T(8,128)(2,1)} %refs_0_.1), channel_id=1, source_target_pairs={{0,1},{1,0},{2,3},{3,2},{4,5},{5,4},{6,7},{7,6},{8,9},{9,8},{10,11... | collective-permute-start | bytes 6291464 | tf_op jit(solution)/shard_map/ppermute | solution.py:36
  4.0 2.7 %collective-permute-start = (bf16[400,256]{1,0:T(8,128)(2,1)}, bf16[400,256]{1,0:T(8,128)(2,1)S(1)}, u32[]{:S(2)}, u32[]{:S(2)}) collective-permute-start(bf16[400,256]{1,0:T(8,128)(2,1)} %bitcast.6), channel_id=1, source_target_pairs={{0,6},{2,0},{4,2},{6,4},{1,7},{3,1},{5,3},{7,5},{8,14},{10,8},{12,... | collective-permute-start | bytes 614408 | tf_op jit(solution)/shard_map/ppermute | solution.py:365
  6.6 1.7 %start.1 = (bf16[512,512]{1,0:T(8,128)(2,1)S(1)}, bf16[1024,512]{1,0:T(8,128)(2,1)S(1)}, bf16[400,400]{1,0:T(8,128)(2,1)S(1)}, bf16[400,256]{1,0:T(8,128)(2,1)S(1)}, bf16[400,512]{1,0:T(8,128)(2,1)S(1)}) custom-call(bf16[2048,512]{1,0:T(8,128)(2,1)} %refs_0_.1, bf16[400,400]{1,0:T(8,128)(2,1)} %bitcast.10, bf16[400,256]{1,0:T(8,128)(2,1)} %bitcast.7, ...), custom_call_target="tpu_custom_call" | custom-call | tf_op jit(solution)/shard_map/start/pallas_call | solution.py:74
  8.4 3.6 %collective-permute-done.1.o3 = bf16[400,256]{1,0:T(8,128)(2,1)S(1)} collective-permute-done((bf16[400,256]{1,0:T(8,128)(2,1)}, bf16[400,256]{1,0:T(8,128)(2,1)S(1)}, u32[]{:S(2)}, u32[]{:S(2)}) %collective-permute-start.1) | collective-permute-done | bytes 204832 | tf_op jit(solution)/shard_map/ppermute | solution.py:365
  11.9 1.2 collective-permute-start.9
  13.1 1.8 %collective-permute-start.2 = (bf16[400,256]{1,0:T(8,128)(2,1)S(1)}, bf16[400,256]{1,0:T(8,128)(2,1)S(1)}, u32[]{:S(2)}, u32[]{:S(2)}) collective-permute-start(bf16[400,256]{1,0:T(8,128)(2,1)S(1)} %bitcast.8), channel_id=1, source_target_pairs={{0,4},{2,6},{4,0},{6,2},{1,5},{3,7},{5,1},{7,3},{8,12},{10,14},{12... | collective-permute-start | bytes 614408 | tf_op jit(solution)/shard_map/ppermute | solution.py:365
  14.9 1.5 %collective-permute-start.5 = (bf16[400,512]{1,0:T(8,128)(2,1)S(1)}, bf16[400,512]{1,0:T(8,128)(2,1)S(1)}, u32[]{:S(2)}, u32[]{:S(2)}) collective-permute-start(bf16[400,512]{1,0:T(8,128)(2,1)S(1)} %copy-done.5), channel_id=1, source_target_pairs={{0,1},{1,0},{2,3},{3,2},{4,5},{5,4},{6,7},{7,6},{8,9},{9,8},{10,11... | collective-permute-start | bytes 1228808 | tf_op jit(solution)/shard_map/ppermute | solution.py:36
  16.4 9.7 %collective-permute-done.9.refs_2_ = bf16[512,512]{1,0:T(8,128)(2,1)} collective-permute-done((bf16[512,512]{1,0:T(8,128)(2,1)S(1)}, bf16[512,512]{1,0:T(8,128)(2,1)}, u32[]{:S(2)}, u32[]{:S(2)}) %collective-permute-start.9) | collective-permute-done | bytes 524320 | tf_op jit(solution)/shard_map/ppermute | solution.py:370
  26.1 2.1 %collective-permute-start.11 = (bf16[512,512]{1,0:T(8,128)(2,1)}, bf16[512,512]{1,0:T(8,128)(2,1)}, u32[]{:S(2)}, u32[]{:S(2)}) collective-permute-start(bf16[512,512]{1,0:T(8,128)(2,1)} %collective-permute-done.9.refs_2_), channel_id=1, source_target_pairs={{0,16},{8,24},{16,0},{24,8},{1,17},{9,25},{17,1},{25,9},{2,18},{10... | collective-permute-start | bytes 1572872 | tf_op jit(solution)/shard_map/ppermute | solution.py:384
  28.2 2.2 %collective-permute-done.2.o2 = bf16[400,256]{1,0:T(8,128)(2,1)S(1)} collective-permute-done((bf16[400,256]{1,0:T(8,128)(2,1)S(1)}, bf16[400,256]{1,0:T(8,128)(2,1)S(1)}, u32[]{:S(2)}, u32[]{:S(2)}) %collective-permute-start.2) | collective-permute-done | bytes 204832 | tf_op jit(solution)/shard_map/ppermute | solution.py:365
  30.3 0.9 collective-permute-start.10
  31.3 2.0 %collective-permute-start.7 = (bf16[512,256]{1,0:T(8,128)(2,1)S(1)}, bf16[512,256]{1,0:T(8,128)(2,1)S(1)}, u32[]{:S(2)}, u32[]{:S(2)}) collective-permute-start(bf16[512,256]{1,0:T(8,128)(2,1)S(1)} %copy-done.2), channel_id=1, source_target_pairs={{0,4},{2,6},{4,0},{6,2},{1,5},{3,7},{5,1},{7,3},{8,12},{10,14},{12... | collective-permute-start | bytes 786440 | tf_op jit(solution)/shard_map/ppermute | solution.py:371
  33.3 2.9 %collective-permute-start.6 = (bf16[512,256]{1,0:T(8,128)(2,1)S(1)}, bf16[512,256]{1,0:T(8,128)(2,1)}, u32[]{:S(2)}, u32[]{:S(2)}) collective-permute-start(bf16[512,256]{1,0:T(8,128)(2,1)S(1)} %copy-done.2), channel_id=1, source_target_pairs={{0,1},{1,0},{2,3},{3,2},{4,5},{5,4},{6,7},{7,6},{8,9},{9,8},{10,11... | collective-permute-start | bytes 786440 | tf_op jit(solution)/shard_map/ppermute | solution.py:36
  36.2 2.5 %head.1 = f32[32,1,1024]{2,1,0:T(1,128)} custom-call(bf16[400,400]{1,0:T(8,128)(2,1)S(1)} %get-tuple-element.39.inv, bf16[400,256]{1,0:T(8,128)(2,1)S(1)} %get-tuple-element.40.o0, bf16[400,256]{1,0:T(8,128)(2,1)S(1)} %collective-permute-done.o1, bf16[400,256]{1,0:T(8,128)(2,1)S(1)} %collective-permute-done.2.o2, ...), custom_call_target="tpu_custom_call" | custom-call | tf_op jit(solution)/shard_map/head/pallas_call | solution.py:110
  38.7 10.6 %all-to-all-start = ((f32[32,1,1024]{2,1,0:T(1,128)}), f32[32,1,1024]{2,1,0:T(1,128)S(1)}, u32[]{:S(2)}, u32[]{:S(2)}) async-start(f32[32,1,1024]{2,1,0:T(1,128)} %head.1), calls=%async_computation | async-start | bytes 262144 | tf_op jit(solution)/shard_map/all_to_all | solution.py:378
  49.9 3.3 %collective-permute-start.16 = (bf16[512,512]{1,0:T(8,128)(2,1)}, bf16[512,512]{1,0:T(8,128)(2,1)S(1)}, u32[]{:S(2)}, u32[]{:S(2)}) collective-permute-start(bf16[512,512]{1,0:T(8,128)(2,1)} %collective-permute-done.12.refs_5_), channel_id=1, source_target_pairs={{0,1},{1,0},{2,3},{3,2},{4,5},{5,4},{6,7},{7,6},{8,9},{9,8},{10,11... | collective-permute-start | bytes 1572872 | tf_op jit(solution)/shard_map/ppermute | solution.py:36
  53.2 1.9 %collective-permute-start.14 = (bf16[512,512]{1,0:T(8,128)(2,1)}, bf16[512,512]{1,0:T(8,128)(2,1)}, u32[]{:S(2)}, u32[]{:S(2)}) collective-permute-start(bf16[512,512]{1,0:T(8,128)(2,1)} %collective-permute-done.10.refs_3_), channel_id=1, source_target_pairs={{0,1},{1,0},{2,3},{3,2},{4,5},{5,4},{6,7},{7,6},{8,9},{9,8},{10,11... | collective-permute-start | bytes 1572872 | tf_op jit(solution)/shard_map/ppermute | solution.py:36
  55.3 1.3 fusion
  57.4 5.2 %all-to-all-start.1 = ((f32[8,32,256]{2,1,0:T(8,128)}), f32[8,32,256]{2,1,0:T(8,128)S(1)}, u32[]{:S(2)}, u32[]{:S(2)}) async-start(f32[8,32,256]{2,1,0:T(8,128)} %broadcast_in_dim.2), calls=%async_computation.1 | async-start | bytes 524288 | tf_op jit(solution)/shard_map/all_to_all | solution.py:390
  62.6 4.5 %all-to-all-done.1.bias_ref = f32[8,32,256]{2,1,0:T(8,128)S(1)} async-done(((f32[8,32,256]{2,1,0:T(8,128)}), f32[8,32,256]{2,1,0:T(8,128)S(1)}, u32[]{:S(2)}, u32[]{:S(2)}) %all-to-all-start.1) | async-done | bytes 262176 | tf_op jit(solution)/shard_map/all_to_all | solution.py:390
  67.2 1.8 %field.1 = (f32[32,256]{1,0:T(8,128)}, bf16[32,4,512]{2,1,0:T(4,128)(2,1)S(1)}) custom-call(f32[8,32,256]{2,1,0:T(8,128)S(1)} %all-to-all-done.1.bias_ref, f32[32,256]{1,0:T(8,128)S(1)} %copy-done.4, bf16[512,256]{1,0:T(8,128)(2,1)S(1)} %copy-done.2, bf16[512,256]{1,0:T(8,128)(2,1)} %collective-permute-done.6.c1, ...), custom_call_target="tpu_custom_call" | custom-call | tf_op jit(solution)/shard_map/field/pallas_call | solution.py:143
  69.6 11.0 %all-to-all-start.2 = ((bf16[32,4,512]{2,1,0:T(4,128)(2,1)}), bf16[32,4,512]{2,1,0:T(4,128)(2,1)S(1)}, u32[]{:S(2)}, u32[]{:S(2)}) async-start(bf16[32,4,512]{2,1,0:T(4,128)(2,1)} %copy-done.3), calls=%async_computation.2 | async-start | bytes 262144 | tf_op jit(solution)/shard_map/all_to_all | solution.py:401
  80.8 1.9 %collective-permute-start.3 = (bf16[104,1024]{1,0:T(8,128)(2,1)S(1)}, bf16[104,1024]{1,0:T(8,128)(2,1)S(1)}, u32[]{:S(2)}, u32[]{:S(2)}) collective-permute-start(bf16[104,1024]{1,0:T(8,128)(2,1)S(1)} %get-tuple-element.36), channel_id=1, source_target_pairs={{0,1},{1,0},{2,3},{3,2},{4,5},{5,4},{6,7},{7,6},{8,9},{9,8},{10,11... | collective-permute-start | bytes 638984 | tf_op jit(solution)/shard_map/ppermute | solution.py:36
  82.8 1.1 collective-permute-done.3.par
  83.9 1.7 %all-to-all-done.2.arrived_ref = bf16[32,4,512]{2,1,0:T(4,128)(2,1)S(1)} async-done(((bf16[32,4,512]{2,1,0:T(4,128)(2,1)}), bf16[32,4,512]{2,1,0:T(4,128)(2,1)S(1)}, u32[]{:S(2)}, u32[]{:S(2)}) %all-to-all-start.2) | async-done | bytes 131104 | tf_op jit(solution)/shard_map/all_to_all | solution.py:401
  85.6 5.1 %first.1 = (bf16[4,104,512]{2,1,0:T(8,128)(2,1)S(1)}, bf16[104,1024]{1,0:T(8,128)(2,1)S(1)}, f32[4,512]{1,0:T(4,128)S(1)}, bf16[4,2048,512]{2,1,0:T(8,128)(2,1)S(1)}) custom-call(bf16[104,1024]{1,0:T(8,128)(2,1)S(1)} %get-tuple-element.37.term_0.total_ref, bf16[104,1024]{1,0:T(8,128)(2,1)S(1)} %get-tuple-element.38.term_1.refs_2_, ...), custom_call_target="tpu_custom_call" | custom-call | tf_op jit(solution)/shard_map/first/pallas_call | solution.py:263
  90.7 1.9 %collective-permute-start.18 = (bf16[104,1024]{1,0:T(8,128)(2,1)S(1)}, bf16[104,1024]{1,0:T(8,128)(2,1)S(1)}, u32[]{:S(2)}, u32[]{:S(2)}) collective-permute-start(bf16[104,1024]{1,0:T(8,128)(2,1)S(1)} %get-tuple-element.47.mine_ref), channel_id=1, source_target_pairs={{0,2},{2,0},{5,3},{3,5},{4,6},{6,4},{1,7},{7,1},{8,10},{10,8},{13,... | collective-permute-start | bytes 638984 | tf_op jit(solution)/shard_map/ppermute | solution.py:413
  92.6 1.4 %term.9.refs_0_ = bf16[104,1024]{1,0:T(8,128)(2,1)S(1)} custom-call(bf16[4,104,512]{2,1,0:T(8,128)(2,1)S(1)} %get-tuple-element.45.mixed_ref, bf16[4,2048,512]{2,1,0:T(8,128)(2,1)S(1)} %get-tuple-element.46.interp_ref.refs_5_), custom_call_target="tpu_custom_call" | custom-call | tf_op jit(solution)/shard_map/term/pallas_call | solution.py:329
  94.0 1.0 collective-permute-start.17
  94.9 1.7 %collective-permute-done.18.other_ref = bf16[104,1024]{1,0:T(8,128)(2,1)S(1)} collective-permute-done((bf16[104,1024]{1,0:T(8,128)(2,1)S(1)}, bf16[104,1024]{1,0:T(8,128)(2,1)S(1)}, u32[]{:S(2)}, u32[]{:S(2)}) %collective-permute-start.18) | collective-permute-done | bytes 213024 | tf_op jit(solution)/shard_map/ppermute | solution.py:413
  96.7 0.8 term.10
  97.4 2.5 %collective-permute-done.17.refs_1_ = bf16[104,1024]{1,0:T(8,128)(2,1)S(1)} collective-permute-done((bf16[104,1024]{1,0:T(8,128)(2,1)S(1)}, bf16[104,1024]{1,0:T(8,128)(2,1)S(1)}, u32[]{:S(2)}, u32[]{:S(2)}) %collective-permute-start.17) | collective-permute-done | bytes 213024 | tf_op jit(solution)/shard_map/ppermute | solution.py:415
  100.0 2.0 %term.11 = (bf16[4,104,512]{2,1,0:T(8,128)(2,1)S(1)}, bf16[104,1024]{1,0:T(8,128)(2,1)S(1)}, f32[104,1024]{1,0:T(8,128)S(1)}) custom-call(bf16[104,1024]{1,0:T(8,128)(2,1)S(1)} %term.9.refs_0_, bf16[104,1024]{1,0:T(8,128)(2,1)S(1)} %collective-permute-done.17.refs_1_, bf16[104,1024]{1,0:T(8,128)(2,1)S(1)} %get-tuple-element.38.term_1.refs_2_, ...), custom_call_target="tpu_custom_call" | custom-call | tf_op jit(solution)/shard_map/term/pallas_call | solution.py:329
  102.0 1.0 collective-permute-start.20
  103.0 1.4 %term.12.refs_0_ = bf16[104,1024]{1,0:T(8,128)(2,1)S(1)} custom-call(bf16[4,104,512]{2,1,0:T(8,128)(2,1)S(1)} %get-tuple-element.50.mixed_ref, bf16[4,2048,512]{2,1,0:T(8,128)(2,1)S(1)} %get-tuple-element.46.interp_ref.refs_5_), custom_call_target="tpu_custom_call" | custom-call | tf_op jit(solution)/shard_map/term/pallas_call | solution.py:329
  104.4 1.9 %collective-permute-start.19 = (bf16[104,1024]{1,0:T(8,128)(2,1)S(1)}, bf16[104,1024]{1,0:T(8,128)(2,1)S(1)}, u32[]{:S(2)}, u32[]{:S(2)}) collective-permute-start(bf16[104,1024]{1,0:T(8,128)(2,1)S(1)} %term.12.refs_0_), channel_id=1, source_target_pairs={{0,2},{2,0},{5,3},{3,5},{4,6},{6,4},{1,7},{7,1},{8,10},{10,8},{13,... | collective-permute-start | bytes 638984 | tf_op jit(solution)/shard_map/ppermute | solution.py:415
  106.3 1.7 %collective-permute-done.20.other_ref = bf16[104,1024]{1,0:T(8,128)(2,1)S(1)} collective-permute-done((bf16[104,1024]{1,0:T(8,128)(2,1)S(1)}, bf16[104,1024]{1,0:T(8,128)(2,1)S(1)}, u32[]{:S(2)}, u32[]{:S(2)}) %collective-permute-start.20) | collective-permute-done | bytes 213024 | tf_op jit(solution)/shard_map/ppermute | solution.py:413
  108.0 0.8 term.13
  108.8 1.6 %collective-permute-done.19.refs_1_ = bf16[104,1024]{1,0:T(8,128)(2,1)S(1)} collective-permute-done((bf16[104,1024]{1,0:T(8,128)(2,1)S(1)}, bf16[104,1024]{1,0:T(8,128)(2,1)S(1)}, u32[]{:S(2)}, u32[]{:S(2)}) %collective-permute-start.19) | collective-permute-done | bytes 213024 | tf_op jit(solution)/shard_map/ppermute | solution.py:415
  110.4 2.0 %term.14 = (bf16[4,104,512]{2,1,0:T(8,128)(2,1)S(1)}, bf16[104,1024]{1,0:T(8,128)(2,1)S(1)}, f32[104,1024]{1,0:T(8,128)S(1)}) custom-call(bf16[104,1024]{1,0:T(8,128)(2,1)S(1)} %term.12.refs_0_, bf16[104,1024]{1,0:T(8,128)(2,1)S(1)} %collective-permute-done.19.refs_1_, f32[104,1024]{1,0:T(8,128)S(1)} %get-tuple-element.51.refs_2_, ...), custom_call_target="tpu_custom_call" | custom-call | tf_op jit(solution)/shard_map/term/pallas_call | solution.py:329
  112.4 1.9 %collective-permute-start.22 = (bf16[104,1024]{1,0:T(8,128)(2,1)S(1)}, bf16[104,1024]{1,0:T(8,128)(2,1)S(1)}, u32[]{:S(2)}, u32[]{:S(2)}) collective-permute-start(bf16[104,1024]{1,0:T(8,128)(2,1)S(1)} %get-tuple-element.56.mine_ref), channel_id=1, source_target_pairs={{0,2},{2,0},{5,3},{3,5},{4,6},{6,4},{1,7},{7,1},{8,10},{10,8},{13,... | collective-permute-start | bytes 638984 | tf_op jit(solution)/shard_map/ppermute | solution.py:413
  114.3 1.4 %term.15.mine_ref = bf16[104,1024]{1,0:T(8,128)(2,1)S(1)} custom-call(bf16[4,104,512]{2,1,0:T(8,128)(2,1)S(1)} %get-tuple-element.55.mixed_ref, bf16[4,2048,512]{2,1,0:T(8,128)(2,1)S(1)} %get-tuple-element.46.interp_ref.refs_5_), custom_call_target="tpu_custom_call" | custom-call | tf_op jit(solution)/shard_map/term/pallas_call | solution.py:329
  115.7 1.2 collective-permute-start.21
  116.9 1.5 %collective-permute-done.22.other_ref = bf16[104,1024]{1,0:T(8,128)(2,1)S(1)} collective-permute-done((bf16[104,1024]{1,0:T(8,128)(2,1)S(1)}, bf16[104,1024]{1,0:T(8,128)(2,1)S(1)}, u32[]{:S(2)}, u32[]{:S(2)}) %collective-permute-start.22) | collective-permute-done | bytes 213024 | tf_op jit(solution)/shard_map/ppermute | solution.py:413
  118.4 0.8 term.16
  119.2 2.8 %collective-permute-done.21.other_ref = bf16[104,1024]{1,0:T(8,128)(2,1)S(1)} collective-permute-done((bf16[104,1024]{1,0:T(8,128)(2,1)S(1)}, bf16[104,1024]{1,0:T(8,128)(2,1)S(1)}, u32[]{:S(2)}, u32[]{:S(2)}) %collective-permute-start.21) | collective-permute-done | bytes 213024 | tf_op jit(solution)/shard_map/ppermute | solution.py:415
  121.9 3.5 %term.17 = bf16[8,112,256]{2,1,0:T(8,128)(2,1)S(1)} custom-call(bf16[104,1024]{1,0:T(8,128)(2,1)S(1)} %term.15.mine_ref, bf16[104,1024]{1,0:T(8,128)(2,1)S(1)} %collective-permute-done.21.other_ref, f32[104,1024]{1,0:T(8,128)S(1)} %get-tuple-element.58.total_0, f32[104,1024]{1,0:T(8,128)S(1)} %get-tuple-element.59.total_1, ...), custom_call_target="tpu_custom_call" | custom-call | tf_op jit(solution)/shard_map/term/pallas_call | solution.py:329
  125.5 11.7 %all_to_all.20.back_ref = bf16[8,112,256]{2,1,0:T(8,128)(2,1)S(1)} all-to-all(bf16[8,112,256]{2,1,0:T(8,128)(2,1)S(1)} %term.17), channel_id=1, replica_groups={{7,6,5,4,3,2,1,0},{15,14,13,12,11,10,9,8},{23,22,21,20,19,18,17,16},{31..., dimensions={0} | all-to-all | bytes 917504 | tf_op jit(solution)/shard_map/all_to_all | solution.py:431
  (35 shorter events, 3.3 us)
Async XLA Ops:
  0.6 12.4 %copy-start.1 = (bf16[1,400,256]{2,1,0:T(8,128)(2,1)S(1)}, bf16[1,400,256]{2,1,0:T(8,128)(2,1)}, u32[]{:S(2)}) copy-start(bf16[1,400,256]{2,1,0:T(8,128)(2,1)} %param.6) | copy-start | bytes 614404
  0.6 14.3 %copy-start.5 = (bf16[400,512]{1,0:T(8,128)(2,1)S(1)}, bf16[400,512]{1,0:T(8,128)(2,1)}, u32[]{:S(2)}) copy-start(bf16[400,512]{1,0:T(8,128)(2,1)} %occ.1) | copy-start | bytes 1228804
  0.7 30.6 %copy-start.2 = (bf16[512,256]{1,0:T(8,128)(2,1)S(1)}, bf16[512,256]{1,0:T(8,128)(2,1)}, u32[]{:S(2)}) copy-start(bf16[512,256]{1,0:T(8,128)(2,1)} %c0.1) | copy-start | bytes 786436
  0.7 32.6 %collective-permute-start.4 = (bf16[2048,512]{1,0:T(8,128)(2,1)}, bf16[2048,512]{1,0:T(8,128)(2,1)S(1)}, u32[]{:S(2)}, u32[]{:S(2)}) collective-permute-start(bf16[2048,512]{1,0:T(8,128)(2,1)} %refs_0_.1), channel_id=1, source_target_pairs={{0,1},{1,0},{2,3},{3,2},{4,5},{5,4},{6,7},{7,6},{8,9},{9,8},{10,11... | collective-permute-start | bytes 6291464 | tf_op jit(solution)/shard_map/ppermute | solution.py:36
  3.9 8.0 %collective-permute-start.1 = (bf16[400,256]{1,0:T(8,128)(2,1)}, bf16[400,256]{1,0:T(8,128)(2,1)S(1)}, u32[]{:S(2)}, u32[]{:S(2)}) collective-permute-start(bf16[400,256]{1,0:T(8,128)(2,1)} %bitcast.5), channel_id=1, source_target_pairs={{0,2},{2,4},{4,6},{6,0},{1,3},{3,5},{5,7},{7,1},{8,10},{10,12},{12... | collective-permute-start | bytes 614408 | tf_op jit(solution)/shard_map/ppermute | solution.py:365
  4.0 8.0 %collective-permute-start = (bf16[400,256]{1,0:T(8,128)(2,1)}, bf16[400,256]{1,0:T(8,128)(2,1)S(1)}, u32[]{:S(2)}, u32[]{:S(2)}) collective-permute-start(bf16[400,256]{1,0:T(8,128)(2,1)} %bitcast.6), channel_id=1, source_target_pairs={{0,6},{2,0},{4,2},{6,4},{1,7},{3,1},{5,3},{7,5},{8,14},{10,8},{12,... | collective-permute-start | bytes 614408 | tf_op jit(solution)/shard_map/ppermute | solution.py:365
  11.9 14.1 %collective-permute-start.9 = (bf16[512,512]{1,0:T(8,128)(2,1)S(1)}, bf16[512,512]{1,0:T(8,128)(2,1)}, u32[]{:S(2)}, u32[]{:S(2)}) collective-permute-start(bf16[512,512]{1,0:T(8,128)(2,1)S(1)} %get-tuple-element.44), channel_id=1, source_target_pairs={{0,4},{2,6},{4,0},{6,2},{1,5},{3,7},{5,1},{7,3},{8,12},{10,14},{12... | collective-permute-start | bytes 1572872 | tf_op jit(solution)/shard_map/ppermute | solution.py:370
  13.1 17.3 %collective-permute-start.2 = (bf16[400,256]{1,0:T(8,128)(2,1)S(1)}, bf16[400,256]{1,0:T(8,128)(2,1)S(1)}, u32[]{:S(2)}, u32[]{:S(2)}) collective-permute-start(bf16[400,256]{1,0:T(8,128)(2,1)S(1)} %bitcast.8), channel_id=1, source_target_pairs={{0,4},{2,6},{4,0},{6,2},{1,5},{3,7},{5,1},{7,3},{8,12},{10,14},{12... | collective-permute-start | bytes 614408 | tf_op jit(solution)/shard_map/ppermute | solution.py:365
  14.9 16.4 %collective-permute-start.5 = (bf16[400,512]{1,0:T(8,128)(2,1)S(1)}, bf16[400,512]{1,0:T(8,128)(2,1)S(1)}, u32[]{:S(2)}, u32[]{:S(2)}) collective-permute-start(bf16[400,512]{1,0:T(8,128)(2,1)S(1)} %copy-done.5), channel_id=1, source_target_pairs={{0,1},{1,0},{2,3},{3,2},{4,5},{5,4},{6,7},{7,6},{8,9},{9,8},{10,11... | collective-permute-start | bytes 1228808 | tf_op jit(solution)/shard_map/ppermute | solution.py:36
  26.1 23.8 %collective-permute-start.12 = (bf16[512,512]{1,0:T(8,128)(2,1)}, bf16[512,512]{1,0:T(8,128)(2,1)}, u32[]{:S(2)}, u32[]{:S(2)}) collective-permute-start(bf16[512,512]{1,0:T(8,128)(2,1)} %collective-permute-done.9.refs_2_), channel_id=1, source_target_pairs={{0,8},{8,16},{16,24},{24,0},{1,9},{9,17},{17,25},{25,1},{2,10},{10... | collective-permute-start | bytes 1572872 | tf_op jit(solution)/shard_map/ppermute | solution.py:384
  26.1 27.1 %collective-permute-start.11 = (bf16[512,512]{1,0:T(8,128)(2,1)}, bf16[512,512]{1,0:T(8,128)(2,1)}, u32[]{:S(2)}, u32[]{:S(2)}) collective-permute-start(bf16[512,512]{1,0:T(8,128)(2,1)} %collective-permute-done.9.refs_2_), channel_id=1, source_target_pairs={{0,16},{8,24},{16,0},{24,8},{1,17},{9,25},{17,1},{25,9},{2,18},{10... | collective-permute-start | bytes 1572872 | tf_op jit(solution)/shard_map/ppermute | solution.py:384
  30.3 22.9 %collective-permute-start.10 = (bf16[512,512]{1,0:T(8,128)(2,1)}, bf16[512,512]{1,0:T(8,128)(2,1)}, u32[]{:S(2)}, u32[]{:S(2)}) collective-permute-start(bf16[512,512]{1,0:T(8,128)(2,1)} %collective-permute-done.9.refs_2_), channel_id=1, source_target_pairs={{0,24},{8,0},{16,8},{24,16},{1,25},{9,1},{17,9},{25,17},{2,26},{10... | collective-permute-start | bytes 1572872 | tf_op jit(solution)/shard_map/ppermute | solution.py:384
  31.3 18.0 %collective-permute-start.7 = (bf16[512,256]{1,0:T(8,128)(2,1)S(1)}, bf16[512,256]{1,0:T(8,128)(2,1)S(1)}, u32[]{:S(2)}, u32[]{:S(2)}) collective-permute-start(bf16[512,256]{1,0:T(8,128)(2,1)S(1)} %copy-done.2), channel_id=1, source_target_pairs={{0,4},{2,6},{4,0},{6,2},{1,5},{3,7},{5,1},{7,3},{8,12},{10,14},{12... | collective-permute-start | bytes 786440 | tf_op jit(solution)/shard_map/ppermute | solution.py:371
  33.3 5.4 %copy-start = (bf16[2048,512]{1,0:T(8,128)(2,1)}, bf16[2048,512]{1,0:T(8,128)(2,1)S(1)}, u32[]{:S(2)}) copy-start(bf16[2048,512]{1,0:T(8,128)(2,1)S(1)} %collective-permute-done.4.a_par.refs_1_) | copy-start | bytes 6291460
  33.3 16.4 %collective-permute-start.6 = (bf16[512,256]{1,0:T(8,128)(2,1)S(1)}, bf16[512,256]{1,0:T(8,128)(2,1)}, u32[]{:S(2)}, u32[]{:S(2)}) collective-permute-start(bf16[512,256]{1,0:T(8,128)(2,1)S(1)} %copy-done.2), channel_id=1, source_target_pairs={{0,1},{1,0},{2,3},{3,2},{4,5},{5,4},{6,7},{7,6},{8,9},{9,8},{10,11... | collective-permute-start | bytes 786440 | tf_op jit(solution)/shard_map/ppermute | solution.py:36
  36.2 30.9 %copy-start.4 = (f32[32,256]{1,0:T(8,128)S(1)}, f32[32,256]{1,0:T(8,128)}, u32[]{:S(2)}) copy-start(f32[32,256]{1,0:T(8,128)} %fields_ref.1) | copy-start | bytes 98308
  38.7 16.6 %all-to-all-start = ((f32[32,1,1024]{2,1,0:T(1,128)}), f32[32,1,1024]{2,1,0:T(1,128)S(1)}, u32[]{:S(2)}, u32[]{:S(2)}) async-start(f32[32,1,1024]{2,1,0:T(1,128)} %head.1), calls=%async_computation | async-start | bytes 262144 | tf_op jit(solution)/shard_map/all_to_all | solution.py:378
  49.3 13.3 %collective-permute-start.8 = (bf16[512,256]{1,0:T(8,128)(2,1)S(1)}, bf16[512,256]{1,0:T(8,128)(2,1)S(1)}, u32[]{:S(2)}, u32[]{:S(2)}) collective-permute-start(bf16[512,256]{1,0:T(8,128)(2,1)S(1)} %collective-permute-done.7.c2), channel_id=1, source_target_pairs={{0,1},{1,0},{2,3},{3,2},{4,5},{5,4},{6,7},{7,6},{8,9},{9,8},{10,11... | collective-permute-start | bytes 786440 | tf_op jit(solution)/shard_map/ppermute | solution.py:36
  49.7 34.2 %collective-permute-start.13 = (bf16[512,512]{1,0:T(8,128)(2,1)}, bf16[512,512]{1,0:T(8,128)(2,1)S(1)}, u32[]{:S(2)}, u32[]{:S(2)}) collective-permute-start(bf16[512,512]{1,0:T(8,128)(2,1)} %collective-permute-done.9.refs_2_), channel_id=1, source_target_pairs={{0,1},{1,0},{2,3},{3,2},{4,5},{5,4},{6,7},{7,6},{8,9},{9,8},{10,11... | collective-permute-start | bytes 1572872 | tf_op jit(solution)/shard_map/ppermute | solution.py:36
  49.9 34.0 %collective-permute-start.16 = (bf16[512,512]{1,0:T(8,128)(2,1)}, bf16[512,512]{1,0:T(8,128)(2,1)S(1)}, u32[]{:S(2)}, u32[]{:S(2)}) collective-permute-start(bf16[512,512]{1,0:T(8,128)(2,1)} %collective-permute-done.12.refs_5_), channel_id=1, source_target_pairs={{0,1},{1,0},{2,3},{3,2},{4,5},{5,4},{6,7},{7,6},{8,9},{9,8},{10,11... | collective-permute-start | bytes 1572872 | tf_op jit(solution)/shard_map/ppermute | solution.py:36
  53.2 30.7 %collective-permute-start.15 = (bf16[512,512]{1,0:T(8,128)(2,1)}, bf16[512,512]{1,0:T(8,128)(2,1)S(1)}, u32[]{:S(2)}, u32[]{:S(2)}) collective-permute-start(bf16[512,512]{1,0:T(8,128)(2,1)} %collective-permute-done.11.refs_4_), channel_id=1, source_target_pairs={{0,1},{1,0},{2,3},{3,2},{4,5},{5,4},{6,7},{7,6},{8,9},{9,8},{10,11... | collective-permute-start | bytes 1572872 | tf_op jit(solution)/shard_map/ppermute | solution.py:36
  53.2 30.7 %collective-permute-start.14 = (bf16[512,512]{1,0:T(8,128)(2,1)}, bf16[512,512]{1,0:T(8,128)(2,1)}, u32[]{:S(2)}, u32[]{:S(2)}) collective-permute-start(bf16[512,512]{1,0:T(8,128)(2,1)} %collective-permute-done.10.refs_3_), channel_id=1, source_target_pairs={{0,1},{1,0},{2,3},{3,2},{4,5},{5,4},{6,7},{7,6},{8,9},{9,8},{10,11... | collective-permute-start | bytes 1572872 | tf_op jit(solution)/shard_map/ppermute | solution.py:36
  57.4 9.8 %all-to-all-start.1 = ((f32[8,32,256]{2,1,0:T(8,128)}), f32[8,32,256]{2,1,0:T(8,128)S(1)}, u32[]{:S(2)}, u32[]{:S(2)}) async-start(f32[8,32,256]{2,1,0:T(8,128)} %broadcast_in_dim.2), calls=%async_computation.1 | async-start | bytes 524288 | tf_op jit(solution)/shard_map/all_to_all | solution.py:390
  69.0 0.7 copy-start.3
  69.6 15.9 %all-to-all-start.2 = ((bf16[32,4,512]{2,1,0:T(4,128)(2,1)}), bf16[32,4,512]{2,1,0:T(4,128)(2,1)S(1)}, u32[]{:S(2)}, u32[]{:S(2)}) async-start(bf16[32,4,512]{2,1,0:T(4,128)(2,1)} %copy-done.3), calls=%async_computation.2 | async-start | bytes 262144 | tf_op jit(solution)/shard_map/all_to_all | solution.py:401
  80.8 3.0 %collective-permute-start.3 = (bf16[104,1024]{1,0:T(8,128)(2,1)S(1)}, bf16[104,1024]{1,0:T(8,128)(2,1)S(1)}, u32[]{:S(2)}, u32[]{:S(2)}) collective-permute-start(bf16[104,1024]{1,0:T(8,128)(2,1)S(1)} %get-tuple-element.36), channel_id=1, source_target_pairs={{0,1},{1,0},{2,3},{3,2},{4,5},{5,4},{6,7},{7,6},{8,9},{9,8},{10,11... | collective-permute-start | bytes 638984 | tf_op jit(solution)/shard_map/ppermute | solution.py:36
  90.7 6.0 %collective-permute-start.18 = (bf16[104,1024]{1,0:T(8,128)(2,1)S(1)}, bf16[104,1024]{1,0:T(8,128)(2,1)S(1)}, u32[]{:S(2)}, u32[]{:S(2)}) collective-permute-start(bf16[104,1024]{1,0:T(8,128)(2,1)S(1)} %get-tuple-element.47.mine_ref), channel_id=1, source_target_pairs={{0,2},{2,0},{5,3},{3,5},{4,6},{6,4},{1,7},{7,1},{8,10},{10,8},{13,... | collective-permute-start | bytes 638984 | tf_op jit(solution)/shard_map/ppermute | solution.py:413
  94.0 6.0 %collective-permute-start.17 = (bf16[104,1024]{1,0:T(8,128)(2,1)S(1)}, bf16[104,1024]{1,0:T(8,128)(2,1)S(1)}, u32[]{:S(2)}, u32[]{:S(2)}) collective-permute-start(bf16[104,1024]{1,0:T(8,128)(2,1)S(1)} %term.9.refs_0_), channel_id=1, source_target_pairs={{0,2},{2,0},{5,3},{3,5},{4,6},{6,4},{1,7},{7,1},{8,10},{10,8},{13,... | collective-permute-start | bytes 638984 | tf_op jit(solution)/shard_map/ppermute | solution.py:415
  102.0 6.0 %collective-permute-start.20 = (bf16[104,1024]{1,0:T(8,128)(2,1)S(1)}, bf16[104,1024]{1,0:T(8,128)(2,1)S(1)}, u32[]{:S(2)}, u32[]{:S(2)}) collective-permute-start(bf16[104,1024]{1,0:T(8,128)(2,1)S(1)} %get-tuple-element.52.mine_ref), channel_id=1, source_target_pairs={{0,2},{2,0},{5,3},{3,5},{4,6},{6,4},{1,7},{7,1},{8,10},{10,8},{13,... | collective-permute-start | bytes 638984 | tf_op jit(solution)/shard_map/ppermute | solution.py:413
  104.4 6.0 %collective-permute-start.19 = (bf16[104,1024]{1,0:T(8,128)(2,1)S(1)}, bf16[104,1024]{1,0:T(8,128)(2,1)S(1)}, u32[]{:S(2)}, u32[]{:S(2)}) collective-permute-start(bf16[104,1024]{1,0:T(8,128)(2,1)S(1)} %term.12.refs_0_), channel_id=1, source_target_pairs={{0,2},{2,0},{5,3},{3,5},{4,6},{6,4},{1,7},{7,1},{8,10},{10,8},{13,... | collective-permute-start | bytes 638984 | tf_op jit(solution)/shard_map/ppermute | solution.py:415
  112.4 6.0 %collective-permute-start.22 = (bf16[104,1024]{1,0:T(8,128)(2,1)S(1)}, bf16[104,1024]{1,0:T(8,128)(2,1)S(1)}, u32[]{:S(2)}, u32[]{:S(2)}) collective-permute-start(bf16[104,1024]{1,0:T(8,128)(2,1)S(1)} %get-tuple-element.56.mine_ref), channel_id=1, source_target_pairs={{0,2},{2,0},{5,3},{3,5},{4,6},{6,4},{1,7},{7,1},{8,10},{10,8},{13,... | collective-permute-start | bytes 638984 | tf_op jit(solution)/shard_map/ppermute | solution.py:413
  115.7 6.2 %collective-permute-start.21 = (bf16[104,1024]{1,0:T(8,128)(2,1)S(1)}, bf16[104,1024]{1,0:T(8,128)(2,1)S(1)}, u32[]{:S(2)}, u32[]{:S(2)}) collective-permute-start(bf16[104,1024]{1,0:T(8,128)(2,1)S(1)} %term.15.mine_ref), channel_id=1, source_target_pairs={{0,2},{2,0},{5,3},{3,5},{4,6},{6,4},{1,7},{7,1},{8,10},{10,8},{13,... | collective-permute-start | bytes 638984 | tf_op jit(solution)/shard_map/ppermute | solution.py:415

commit v9 on v8

--- a/solution.py
+++ b/solution.py
@@ -246,15 +246,16 @@
                     far[b][j], interp_ref.at[2 + b, pl.ds(at, 512), :], sems.at[2 + NX * b + j]
                 )
             )
-    for copy in sum(copies, []):
-        copy.start()
+    for b in (3, 0, 1, 2):
+        for copy in copies[b]:
+            copy.start()
     scales_ref[...] = jnp.sum(arrived_ref[...].astype(f32), axis=0)
-    mixed = []
-    for b in range(4):
+    mixed = [None] * 4
+    for b in (3, 0, 1, 2):
         for copy in copies[b]:
             copy.wait()
         product = times(term_0[...], interp_ref, b, 0) + times(term_1[...], interp_ref, b, 1)
-        mixed.append(mix(product, scales_ref, b, 1))
+        mixed[b] = mix(product, scales_ref, b, 1)
         mixed_ref[b] = mixed[b]
     out_ref[...] = back(mixed, interp_ref, 0).astype(bf16)
 

time: 138 us -> 138 us (level)
  no operation moved by 1% of the time
where the time goes in v9:
time: 138 us
  starting transfers between devices  61.7 us (45%)
  waiting for transfers between devices  34.9 us (25%)
  Pallas kernels  25.8 us (19%)
  blocking collectives  11.7 us (8%)
  local copies, waits for them, and re-layouts  1.42 us (1%)
    ppermute x9, starting transfers between devices, swap_core(): return lax.ppermute(value, 'core', ring(NC, 1))  15.4 us
    pallas_call x9, Pallas kernels, call_term(): pl.pallas_call(kernel, out_shape=out_shape, in_specs=[spec(pltpu.VMEM)] *...  14 us
    all_to_all x1, blocking collectives, on_device(): lax.all_to_all(blocks, ('y', 'core'), 0, 0, tiled=True, axis_index_groups...  11.7 us
    all_to_all x1, starting transfers between devices, on_device(): lax.all_to_all(field_part, ('z', 'x'), 0, 0, tiled=True, axis_index_group...  11 us
    all_to_all x1, starting transfers between devices, on_device(): lax.all_to_all(weights, ('z', 'x'), 0, 0, tiled=True, axis_index_groups=W...  10.6 us
    ppermute x1, waiting for transfers between devices, on_device(): part = lax.ppermute(part, 'y', ring(NY, 2))  9.66 us
    ppermute x3, waiting for transfers between devices, on_device(): other_1 = lax.ppermute(mine_1, ('y', 'core'), PAIRS)  6.93 us
    ppermute x3, waiting for transfers between devices, on_device(): others.append(lax.ppermute(orb, 'y', ring(NY, -j)))  5.72 us
  transfers between devices with their start and end apart: 26, of which 14 were waited for; matrix products, arithmetic and copies ran while one was open for 1% of the time, Pallas kernels for 9%

profile of v9, /device:TPU:1, one launch (start us, length us, event | category | flops | bytes accessed | tf_op | source)
XLA Modules:
  0.0 137.6 jit_solution(1942417998337077437)
XLA Ops:
  0.7 3.3 %collective-permute-start.4 = (bf16[2048,512]{1,0:T(8,128)(2,1)}, bf16[2048,512]{1,0:T(8,128)(2,1)S(1)}, u32[]{:S(2)}, u32[]{:S(2)}) collective-permute-start(bf16[2048,512]{1,0:T(8,128)(2,1)} %refs_0_.1), channel_id=1, source_target_pairs={{0,1},{1,0},{2,3},{3,2},{4,5},{5,4},{6,7},{7,6},{8,9},{9,8},{10,11... | collective-permute-start | bytes 6291464 | tf_op jit(solution)/shard_map/ppermute | solution.py:36
  4.0 2.7 %collective-permute-start = (bf16[400,256]{1,0:T(8,128)(2,1)}, bf16[400,256]{1,0:T(8,128)(2,1)S(1)}, u32[]{:S(2)}, u32[]{:S(2)}) collective-permute-start(bf16[400,256]{1,0:T(8,128)(2,1)} %bitcast.6), channel_id=1, source_target_pairs={{0,6},{2,0},{4,2},{6,4},{1,7},{3,1},{5,3},{7,5},{8,14},{10,8},{12,... | collective-permute-start | bytes 614408 | tf_op jit(solution)/shard_map/ppermute | solution.py:366
  6.6 1.7 %start.1 = (bf16[512,512]{1,0:T(8,128)(2,1)S(1)}, bf16[1024,512]{1,0:T(8,128)(2,1)S(1)}, bf16[400,400]{1,0:T(8,128)(2,1)S(1)}, bf16[400,256]{1,0:T(8,128)(2,1)S(1)}, bf16[400,512]{1,0:T(8,128)(2,1)S(1)}) custom-call(bf16[2048,512]{1,0:T(8,128)(2,1)} %refs_0_.1, bf16[400,400]{1,0:T(8,128)(2,1)} %bitcast.10, bf16[400,256]{1,0:T(8,128)(2,1)} %bitcast.7, ...), custom_call_target="tpu_custom_call" | custom-call | tf_op jit(solution)/shard_map/start/pallas_call | solution.py:74
  8.4 3.6 %collective-permute-done.1.o3 = bf16[400,256]{1,0:T(8,128)(2,1)S(1)} collective-permute-done((bf16[400,256]{1,0:T(8,128)(2,1)}, bf16[400,256]{1,0:T(8,128)(2,1)S(1)}, u32[]{:S(2)}, u32[]{:S(2)}) %collective-permute-start.1) | collective-permute-done | bytes 204832 | tf_op jit(solution)/shard_map/ppermute | solution.py:366
  11.9 1.2 collective-permute-start.9
  13.1 1.8 %collective-permute-start.2 = (bf16[400,256]{1,0:T(8,128)(2,1)S(1)}, bf16[400,256]{1,0:T(8,128)(2,1)S(1)}, u32[]{:S(2)}, u32[]{:S(2)}) collective-permute-start(bf16[400,256]{1,0:T(8,128)(2,1)S(1)} %bitcast.8), channel_id=1, source_target_pairs={{0,4},{2,6},{4,0},{6,2},{1,5},{3,7},{5,1},{7,3},{8,12},{10,14},{12... | collective-permute-start | bytes 614408 | tf_op jit(solution)/shard_map/ppermute | solution.py:366
  14.9 1.5 %collective-permute-start.5 = (bf16[400,512]{1,0:T(8,128)(2,1)S(1)}, bf16[400,512]{1,0:T(8,128)(2,1)S(1)}, u32[]{:S(2)}, u32[]{:S(2)}) collective-permute-start(bf16[400,512]{1,0:T(8,128)(2,1)S(1)} %copy-done.5), channel_id=1, source_target_pairs={{0,1},{1,0},{2,3},{3,2},{4,5},{5,4},{6,7},{7,6},{8,9},{9,8},{10,11... | collective-permute-start | bytes 1228808 | tf_op jit(solution)/shard_map/ppermute | solution.py:36
  16.4 9.7 %collective-permute-done.9.refs_2_ = bf16[512,512]{1,0:T(8,128)(2,1)} collective-permute-done((bf16[512,512]{1,0:T(8,128)(2,1)S(1)}, bf16[512,512]{1,0:T(8,128)(2,1)}, u32[]{:S(2)}, u32[]{:S(2)}) %collective-permute-start.9) | collective-permute-done | bytes 524320 | tf_op jit(solution)/shard_map/ppermute | solution.py:371
  26.1 2.1 %collective-permute-start.11 = (bf16[512,512]{1,0:T(8,128)(2,1)}, bf16[512,512]{1,0:T(8,128)(2,1)}, u32[]{:S(2)}, u32[]{:S(2)}) collective-permute-start(bf16[512,512]{1,0:T(8,128)(2,1)} %collective-permute-done.9.refs_2_), channel_id=1, source_target_pairs={{0,16},{8,24},{16,0},{24,8},{1,17},{9,25},{17,1},{25,9},{2,18},{10... | collective-permute-start | bytes 1572872 | tf_op jit(solution)/shard_map/ppermute | solution.py:385
  28.2 2.2 %collective-permute-done.2.o2 = bf16[400,256]{1,0:T(8,128)(2,1)S(1)} collective-permute-done((bf16[400,256]{1,0:T(8,128)(2,1)S(1)}, bf16[400,256]{1,0:T(8,128)(2,1)S(1)}, u32[]{:S(2)}, u32[]{:S(2)}) %collective-permute-start.2) | collective-permute-done | bytes 204832 | tf_op jit(solution)/shard_map/ppermute | solution.py:366
  30.3 0.9 collective-permute-start.10
  31.3 2.0 %collective-permute-start.7 = (bf16[512,256]{1,0:T(8,128)(2,1)S(1)}, bf16[512,256]{1,0:T(8,128)(2,1)S(1)}, u32[]{:S(2)}, u32[]{:S(2)}) collective-permute-start(bf16[512,256]{1,0:T(8,128)(2,1)S(1)} %copy-done.2), channel_id=1, source_target_pairs={{0,4},{2,6},{4,0},{6,2},{1,5},{3,7},{5,1},{7,3},{8,12},{10,14},{12... | collective-permute-start | bytes 786440 | tf_op jit(solution)/shard_map/ppermute | solution.py:372
  33.3 2.9 %collective-permute-start.6 = (bf16[512,256]{1,0:T(8,128)(2,1)S(1)}, bf16[512,256]{1,0:T(8,128)(2,1)}, u32[]{:S(2)}, u32[]{:S(2)}) collective-permute-start(bf16[512,256]{1,0:T(8,128)(2,1)S(1)} %copy-done.2), channel_id=1, source_target_pairs={{0,1},{1,0},{2,3},{3,2},{4,5},{5,4},{6,7},{7,6},{8,9},{9,8},{10,11... | collective-permute-start | bytes 786440 | tf_op jit(solution)/shard_map/ppermute | solution.py:36
  36.2 2.5 %head.1 = f32[32,1,1024]{2,1,0:T(1,128)} custom-call(bf16[400,400]{1,0:T(8,128)(2,1)S(1)} %get-tuple-element.39.inv, bf16[400,256]{1,0:T(8,128)(2,1)S(1)} %get-tuple-element.40.o0, bf16[400,256]{1,0:T(8,128)(2,1)S(1)} %collective-permute-done.o1, bf16[400,256]{1,0:T(8,128)(2,1)S(1)} %collective-permute-done.2.o2, ...), custom_call_target="tpu_custom_call" | custom-call | tf_op jit(solution)/shard_map/head/pallas_call | solution.py:110
  38.7 10.6 %all-to-all-start = ((f32[32,1,1024]{2,1,0:T(1,128)}), f32[32,1,1024]{2,1,0:T(1,128)S(1)}, u32[]{:S(2)}, u32[]{:S(2)}) async-start(f32[32,1,1024]{2,1,0:T(1,128)} %head.1), calls=%async_computation | async-start | bytes 262144 | tf_op jit(solution)/shard_map/all_to_all | solution.py:379
  49.9 3.3 %collective-permute-start.16 = (bf16[512,512]{1,0:T(8,128)(2,1)}, bf16[512,512]{1,0:T(8,128)(2,1)S(1)}, u32[]{:S(2)}, u32[]{:S(2)}) collective-permute-start(bf16[512,512]{1,0:T(8,128)(2,1)} %collective-permute-done.12.refs_5_), channel_id=1, source_target_pairs={{0,1},{1,0},{2,3},{3,2},{4,5},{5,4},{6,7},{7,6},{8,9},{9,8},{10,11... | collective-permute-start | bytes 1572872 | tf_op jit(solution)/shard_map/ppermute | solution.py:36
  53.2 1.9 %collective-permute-start.14 = (bf16[512,512]{1,0:T(8,128)(2,1)}, bf16[512,512]{1,0:T(8,128)(2,1)}, u32[]{:S(2)}, u32[]{:S(2)}) collective-permute-start(bf16[512,512]{1,0:T(8,128)(2,1)} %collective-permute-done.10.refs_3_), channel_id=1, source_target_pairs={{0,1},{1,0},{2,3},{3,2},{4,5},{5,4},{6,7},{7,6},{8,9},{9,8},{10,11... | collective-permute-start | bytes 1572872 | tf_op jit(solution)/shard_map/ppermute | solution.py:36
  55.3 1.3 fusion
  56.6 0.7 broadcast_in_dim.2
  57.4 5.2 %all-to-all-start.1 = ((f32[8,32,256]{2,1,0:T(8,128)}), f32[8,32,256]{2,1,0:T(8,128)S(1)}, u32[]{:S(2)}, u32[]{:S(2)}) async-start(f32[8,32,256]{2,1,0:T(8,128)} %broadcast_in_dim.2), calls=%async_computation.1 | async-start | bytes 524288 | tf_op jit(solution)/shard_map/all_to_all | solution.py:391
  62.6 4.5 %all-to-all-done.1.bias_ref = f32[8,32,256]{2,1,0:T(8,128)S(1)} async-done(((f32[8,32,256]{2,1,0:T(8,128)}), f32[8,32,256]{2,1,0:T(8,128)S(1)}, u32[]{:S(2)}, u32[]{:S(2)}) %all-to-all-start.1) | async-done | bytes 262176 | tf_op jit(solution)/shard_map/all_to_all | solution.py:391
  67.2 1.8 %field.1 = (f32[32,256]{1,0:T(8,128)}, bf16[32,4,512]{2,1,0:T(4,128)(2,1)S(1)}) custom-call(f32[8,32,256]{2,1,0:T(8,128)S(1)} %all-to-all-done.1.bias_ref, f32[32,256]{1,0:T(8,128)S(1)} %copy-done.4, bf16[512,256]{1,0:T(8,128)(2,1)S(1)} %copy-done.2, bf16[512,256]{1,0:T(8,128)(2,1)} %collective-permute-done.6.c1, ...), custom_call_target="tpu_custom_call" | custom-call | tf_op jit(solution)/shard_map/field/pallas_call | solution.py:143
  69.6 11.0 %all-to-all-start.2 = ((bf16[32,4,512]{2,1,0:T(4,128)(2,1)}), bf16[32,4,512]{2,1,0:T(4,128)(2,1)S(1)}, u32[]{:S(2)}, u32[]{:S(2)}) async-start(bf16[32,4,512]{2,1,0:T(4,128)(2,1)} %copy-done.3), calls=%async_computation.2 | async-start | bytes 262144 | tf_op jit(solution)/shard_map/all_to_all | solution.py:402
  80.8 1.9 %collective-permute-start.3 = (bf16[104,1024]{1,0:T(8,128)(2,1)S(1)}, bf16[104,1024]{1,0:T(8,128)(2,1)S(1)}, u32[]{:S(2)}, u32[]{:S(2)}) collective-permute-start(bf16[104,1024]{1,0:T(8,128)(2,1)S(1)} %get-tuple-element.36), channel_id=1, source_target_pairs={{0,1},{1,0},{2,3},{3,2},{4,5},{5,4},{6,7},{7,6},{8,9},{9,8},{10,11... | collective-permute-start | bytes 638984 | tf_op jit(solution)/shard_map/ppermute | solution.py:36
  82.8 1.1 collective-permute-done.3.par
  83.9 1.7 %all-to-all-done.2.arrived_ref = bf16[32,4,512]{2,1,0:T(4,128)(2,1)S(1)} async-done(((bf16[32,4,512]{2,1,0:T(4,128)(2,1)}), bf16[32,4,512]{2,1,0:T(4,128)(2,1)S(1)}, u32[]{:S(2)}, u32[]{:S(2)}) %all-to-all-start.2) | async-done | bytes 131104 | tf_op jit(solution)/shard_map/all_to_all | solution.py:402
  85.6 4.8 %first.1 = (bf16[4,104,512]{2,1,0:T(8,128)(2,1)S(1)}, bf16[104,1024]{1,0:T(8,128)(2,1)S(1)}, f32[4,512]{1,0:T(4,128)S(1)}, bf16[4,2048,512]{2,1,0:T(8,128)(2,1)S(1)}) custom-call(bf16[104,1024]{1,0:T(8,128)(2,1)S(1)} %get-tuple-element.37.term_0.total_ref, bf16[104,1024]{1,0:T(8,128)(2,1)S(1)} %get-tuple-element.38.term_1.refs_2_, ...), custom_call_target="tpu_custom_call" | custom-call | tf_op jit(solution)/shard_map/first/pallas_call | solution.py:264
  90.4 1.9 %collective-permute-start.18 = (bf16[104,1024]{1,0:T(8,128)(2,1)S(1)}, bf16[104,1024]{1,0:T(8,128)(2,1)S(1)}, u32[]{:S(2)}, u32[]{:S(2)}) collective-permute-start(bf16[104,1024]{1,0:T(8,128)(2,1)S(1)} %get-tuple-element.47.mine_ref), channel_id=1, source_target_pairs={{0,2},{2,0},{5,3},{3,5},{4,6},{6,4},{1,7},{7,1},{8,10},{10,8},{13,... | collective-permute-start | bytes 638984 | tf_op jit(solution)/shard_map/ppermute | solution.py:414
  92.3 1.4 %term.9.refs_0_ = bf16[104,1024]{1,0:T(8,128)(2,1)S(1)} custom-call(bf16[4,104,512]{2,1,0:T(8,128)(2,1)S(1)} %get-tuple-element.45.mixed_ref, bf16[4,2048,512]{2,1,0:T(8,128)(2,1)S(1)} %get-tuple-element.46.interp_ref.refs_5_), custom_call_target="tpu_custom_call" | custom-call | tf_op jit(solution)/shard_map/term/pallas_call | solution.py:330
  93.7 1.0 collective-permute-start.17
  94.7 1.7 %collective-permute-done.18.other_ref = bf16[104,1024]{1,0:T(8,128)(2,1)S(1)} collective-permute-done((bf16[104,1024]{1,0:T(8,128)(2,1)S(1)}, bf16[104,1024]{1,0:T(8,128)(2,1)S(1)}, u32[]{:S(2)}, u32[]{:S(2)}) %collective-permute-start.18) | collective-permute-done | bytes 213024 | tf_op jit(solution)/shard_map/ppermute | solution.py:414
  97.1 2.6 %collective-permute-done.17.refs_1_ = bf16[104,1024]{1,0:T(8,128)(2,1)S(1)} collective-permute-done((bf16[104,1024]{1,0:T(8,128)(2,1)S(1)}, bf16[104,1024]{1,0:T(8,128)(2,1)S(1)}, u32[]{:S(2)}, u32[]{:S(2)}) %collective-permute-start.17) | collective-permute-done | bytes 213024 | tf_op jit(solution)/shard_map/ppermute | solution.py:416
  99.7 2.0 %term.11 = (bf16[4,104,512]{2,1,0:T(8,128)(2,1)S(1)}, bf16[104,1024]{1,0:T(8,128)(2,1)S(1)}, f32[104,1024]{1,0:T(8,128)S(1)}) custom-call(bf16[104,1024]{1,0:T(8,128)(2,1)S(1)} %term.9.refs_0_, bf16[104,1024]{1,0:T(8,128)(2,1)S(1)} %collective-permute-done.17.refs_1_, bf16[104,1024]{1,0:T(8,128)(2,1)S(1)} %get-tuple-element.38.term_1.refs_2_, ...), custom_call_target="tpu_custom_call" | custom-call | tf_op jit(solution)/shard_map/term/pallas_call | solution.py:330
  101.7 1.0 collective-permute-start.20
  102.7 1.4 %term.12.refs_0_ = bf16[104,1024]{1,0:T(8,128)(2,1)S(1)} custom-call(bf16[4,104,512]{2,1,0:T(8,128)(2,1)S(1)} %get-tuple-element.50.mixed_ref, bf16[4,2048,512]{2,1,0:T(8,128)(2,1)S(1)} %get-tuple-element.46.interp_ref.refs_5_), custom_call_target="tpu_custom_call" | custom-call | tf_op jit(solution)/shard_map/term/pallas_call | solution.py:330
  104.1 1.9 %collective-permute-start.19 = (bf16[104,1024]{1,0:T(8,128)(2,1)S(1)}, bf16[104,1024]{1,0:T(8,128)(2,1)S(1)}, u32[]{:S(2)}, u32[]{:S(2)}) collective-permute-start(bf16[104,1024]{1,0:T(8,128)(2,1)S(1)} %term.12.refs_0_), channel_id=1, source_target_pairs={{0,2},{2,0},{5,3},{3,5},{4,6},{6,4},{1,7},{7,1},{8,10},{10,8},{13,... | collective-permute-start | bytes 638984 | tf_op jit(solution)/shard_map/ppermute | solution.py:416
  106.0 1.7 %collective-permute-done.20.other_ref = bf16[104,1024]{1,0:T(8,128)(2,1)S(1)} collective-permute-done((bf16[104,1024]{1,0:T(8,128)(2,1)S(1)}, bf16[104,1024]{1,0:T(8,128)(2,1)S(1)}, u32[]{:S(2)}, u32[]{:S(2)}) %collective-permute-start.20) | collective-permute-done | bytes 213024 | tf_op jit(solution)/shard_map/ppermute | solution.py:414
  107.7 0.8 term.13
  108.5 1.6 %collective-permute-done.19.refs_1_ = bf16[104,1024]{1,0:T(8,128)(2,1)S(1)} collective-permute-done((bf16[104,1024]{1,0:T(8,128)(2,1)S(1)}, bf16[104,1024]{1,0:T(8,128)(2,1)S(1)}, u32[]{:S(2)}, u32[]{:S(2)}) %collective-permute-start.19) | collective-permute-done | bytes 213024 | tf_op jit(solution)/shard_map/ppermute | solution.py:416
  110.1 2.0 %term.14 = (bf16[4,104,512]{2,1,0:T(8,128)(2,1)S(1)}, bf16[104,1024]{1,0:T(8,128)(2,1)S(1)}, f32[104,1024]{1,0:T(8,128)S(1)}) custom-call(bf16[104,1024]{1,0:T(8,128)(2,1)S(1)} %term.12.refs_0_, bf16[104,1024]{1,0:T(8,128)(2,1)S(1)} %collective-permute-done.19.refs_1_, f32[104,1024]{1,0:T(8,128)S(1)} %get-tuple-element.51.refs_2_, ...), custom_call_target="tpu_custom_call" | custom-call | tf_op jit(solution)/shard_map/term/pallas_call | solution.py:330
  112.1 1.9 %collective-permute-start.22 = (bf16[104,1024]{1,0:T(8,128)(2,1)S(1)}, bf16[104,1024]{1,0:T(8,128)(2,1)S(1)}, u32[]{:S(2)}, u32[]{:S(2)}) collective-permute-start(bf16[104,1024]{1,0:T(8,128)(2,1)S(1)} %get-tuple-element.56.mine_ref), channel_id=1, source_target_pairs={{0,2},{2,0},{5,3},{3,5},{4,6},{6,4},{1,7},{7,1},{8,10},{10,8},{13,... | collective-permute-start | bytes 638984 | tf_op jit(solution)/shard_map/ppermute | solution.py:414
  114.0 1.4 %term.15.mine_ref = bf16[104,1024]{1,0:T(8,128)(2,1)S(1)} custom-call(bf16[4,104,512]{2,1,0:T(8,128)(2,1)S(1)} %get-tuple-element.55.mixed_ref, bf16[4,2048,512]{2,1,0:T(8,128)(2,1)S(1)} %get-tuple-element.46.interp_ref.refs_5_), custom_call_target="tpu_custom_call" | custom-call | tf_op jit(solution)/shard_map/term/pallas_call | solution.py:330
  115.4 1.2 collective-permute-start.21
  116.6 1.5 %collective-permute-done.22.other_ref = bf16[104,1024]{1,0:T(8,128)(2,1)S(1)} collective-permute-done((bf16[104,1024]{1,0:T(8,128)(2,1)S(1)}, bf16[104,1024]{1,0:T(8,128)(2,1)S(1)}, u32[]{:S(2)}, u32[]{:S(2)}) %collective-permute-start.22) | collective-permute-done | bytes 213024 | tf_op jit(solution)/shard_map/ppermute | solution.py:414
  118.1 0.8 term.16
  118.9 2.8 %collective-permute-done.21.other_ref = bf16[104,1024]{1,0:T(8,128)(2,1)S(1)} collective-permute-done((bf16[104,1024]{1,0:T(8,128)(2,1)S(1)}, bf16[104,1024]{1,0:T(8,128)(2,1)S(1)}, u32[]{:S(2)}, u32[]{:S(2)}) %collective-permute-start.21) | collective-permute-done | bytes 213024 | tf_op jit(solution)/shard_map/ppermute | solution.py:416
  121.6 3.5 %term.17 = bf16[8,112,256]{2,1,0:T(8,128)(2,1)S(1)} custom-call(bf16[104,1024]{1,0:T(8,128)(2,1)S(1)} %term.15.mine_ref, bf16[104,1024]{1,0:T(8,128)(2,1)S(1)} %collective-permute-done.21.other_ref, f32[104,1024]{1,0:T(8,128)S(1)} %get-tuple-element.58.total_0, f32[104,1024]{1,0:T(8,128)S(1)} %get-tuple-element.59.total_1, ...), custom_call_target="tpu_custom_call" | custom-call | tf_op jit(solution)/shard_map/term/pallas_call | solution.py:330
  125.2 11.7 %all_to_all.20.back_ref = bf16[8,112,256]{2,1,0:T(8,128)(2,1)S(1)} all-to-all(bf16[8,112,256]{2,1,0:T(8,128)(2,1)S(1)} %term.17), channel_id=1, replica_groups={{7,6,5,4,3,2,1,0},{15,14,13,12,11,10,9,8},{23,22,21,20,19,18,17,16},{31..., dimensions={0} | all-to-all | bytes 917504 | tf_op jit(solution)/shard_map/all_to_all | solution.py:432
  (35 shorter events, 3.3 us)
Async XLA Ops:
  0.6 12.4 %copy-start.1 = (bf16[1,400,256]{2,1,0:T(8,128)(2,1)S(1)}, bf16[1,400,256]{2,1,0:T(8,128)(2,1)}, u32[]{:S(2)}) copy-start(bf16[1,400,256]{2,1,0:T(8,128)(2,1)} %param.6) | copy-start | bytes 614404
  0.6 14.3 %copy-start.5 = (bf16[400,512]{1,0:T(8,128)(2,1)S(1)}, bf16[400,512]{1,0:T(8,128)(2,1)}, u32[]{:S(2)}) copy-start(bf16[400,512]{1,0:T(8,128)(2,1)} %occ.1) | copy-start | bytes 1228804
  0.7 30.6 %copy-start.2 = (bf16[512,256]{1,0:T(8,128)(2,1)S(1)}, bf16[512,256]{1,0:T(8,128)(2,1)}, u32[]{:S(2)}) copy-start(bf16[512,256]{1,0:T(8,128)(2,1)} %c0.1) | copy-start | bytes 786436
  0.7 32.6 %collective-permute-start.4 = (bf16[2048,512]{1,0:T(8,128)(2,1)}, bf16[2048,512]{1,0:T(8,128)(2,1)S(1)}, u32[]{:S(2)}, u32[]{:S(2)}) collective-permute-start(bf16[2048,512]{1,0:T(8,128)(2,1)} %refs_0_.1), channel_id=1, source_target_pairs={{0,1},{1,0},{2,3},{3,2},{4,5},{5,4},{6,7},{7,6},{8,9},{9,8},{10,11... | collective-permute-start | bytes 6291464 | tf_op jit(solution)/shard_map/ppermute | solution.py:36
  3.9 8.0 %collective-permute-start.1 = (bf16[400,256]{1,0:T(8,128)(2,1)}, bf16[400,256]{1,0:T(8,128)(2,1)S(1)}, u32[]{:S(2)}, u32[]{:S(2)}) collective-permute-start(bf16[400,256]{1,0:T(8,128)(2,1)} %bitcast.5), channel_id=1, source_target_pairs={{0,2},{2,4},{4,6},{6,0},{1,3},{3,5},{5,7},{7,1},{8,10},{10,12},{12... | collective-permute-start | bytes 614408 | tf_op jit(solution)/shard_map/ppermute | solution.py:366
  4.0 8.0 %collective-permute-start = (bf16[400,256]{1,0:T(8,128)(2,1)}, bf16[400,256]{1,0:T(8,128)(2,1)S(1)}, u32[]{:S(2)}, u32[]{:S(2)}) collective-permute-start(bf16[400,256]{1,0:T(8,128)(2,1)} %bitcast.6), channel_id=1, source_target_pairs={{0,6},{2,0},{4,2},{6,4},{1,7},{3,1},{5,3},{7,5},{8,14},{10,8},{12,... | collective-permute-start | bytes 614408 | tf_op jit(solution)/shard_map/ppermute | solution.py:366
  11.9 14.1 %collective-permute-start.9 = (bf16[512,512]{1,0:T(8,128)(2,1)S(1)}, bf16[512,512]{1,0:T(8,128)(2,1)}, u32[]{:S(2)}, u32[]{:S(2)}) collective-permute-start(bf16[512,512]{1,0:T(8,128)(2,1)S(1)} %get-tuple-element.44), channel_id=1, source_target_pairs={{0,4},{2,6},{4,0},{6,2},{1,5},{3,7},{5,1},{7,3},{8,12},{10,14},{12... | collective-permute-start | bytes 1572872 | tf_op jit(solution)/shard_map/ppermute | solution.py:371
  13.1 17.3 %collective-permute-start.2 = (bf16[400,256]{1,0:T(8,128)(2,1)S(1)}, bf16[400,256]{1,0:T(8,128)(2,1)S(1)}, u32[]{:S(2)}, u32[]{:S(2)}) collective-permute-start(bf16[400,256]{1,0:T(8,128)(2,1)S(1)} %bitcast.8), channel_id=1, source_target_pairs={{0,4},{2,6},{4,0},{6,2},{1,5},{3,7},{5,1},{7,3},{8,12},{10,14},{12... | collective-permute-start | bytes 614408 | tf_op jit(solution)/shard_map/ppermute | solution.py:366
  14.9 16.4 %collective-permute-start.5 = (bf16[400,512]{1,0:T(8,128)(2,1)S(1)}, bf16[400,512]{1,0:T(8,128)(2,1)S(1)}, u32[]{:S(2)}, u32[]{:S(2)}) collective-permute-start(bf16[400,512]{1,0:T(8,128)(2,1)S(1)} %copy-done.5), channel_id=1, source_target_pairs={{0,1},{1,0},{2,3},{3,2},{4,5},{5,4},{6,7},{7,6},{8,9},{9,8},{10,11... | collective-permute-start | bytes 1228808 | tf_op jit(solution)/shard_map/ppermute | solution.py:36
  26.1 23.8 %collective-permute-start.12 = (bf16[512,512]{1,0:T(8,128)(2,1)}, bf16[512,512]{1,0:T(8,128)(2,1)}, u32[]{:S(2)}, u32[]{:S(2)}) collective-permute-start(bf16[512,512]{1,0:T(8,128)(2,1)} %collective-permute-done.9.refs_2_), channel_id=1, source_target_pairs={{0,8},{8,16},{16,24},{24,0},{1,9},{9,17},{17,25},{25,1},{2,10},{10... | collective-permute-start | bytes 1572872 | tf_op jit(solution)/shard_map/ppermute | solution.py:385
  26.1 27.1 %collective-permute-start.11 = (bf16[512,512]{1,0:T(8,128)(2,1)}, bf16[512,512]{1,0:T(8,128)(2,1)}, u32[]{:S(2)}, u32[]{:S(2)}) collective-permute-start(bf16[512,512]{1,0:T(8,128)(2,1)} %collective-permute-done.9.refs_2_), channel_id=1, source_target_pairs={{0,16},{8,24},{16,0},{24,8},{1,17},{9,25},{17,1},{25,9},{2,18},{10... | collective-permute-start | bytes 1572872 | tf_op jit(solution)/shard_map/ppermute | solution.py:385
  30.3 22.9 %collective-permute-start.10 = (bf16[512,512]{1,0:T(8,128)(2,1)}, bf16[512,512]{1,0:T(8,128)(2,1)}, u32[]{:S(2)}, u32[]{:S(2)}) collective-permute-start(bf16[512,512]{1,0:T(8,128)(2,1)} %collective-permute-done.9.refs_2_), channel_id=1, source_target_pairs={{0,24},{8,0},{16,8},{24,16},{1,25},{9,1},{17,9},{25,17},{2,26},{10... | collective-permute-start | bytes 1572872 | tf_op jit(solution)/shard_map/ppermute | solution.py:385
  31.3 18.0 %collective-permute-start.7 = (bf16[512,256]{1,0:T(8,128)(2,1)S(1)}, bf16[512,256]{1,0:T(8,128)(2,1)S(1)}, u32[]{:S(2)}, u32[]{:S(2)}) collective-permute-start(bf16[512,256]{1,0:T(8,128)(2,1)S(1)} %copy-done.2), channel_id=1, source_target_pairs={{0,4},{2,6},{4,0},{6,2},{1,5},{3,7},{5,1},{7,3},{8,12},{10,14},{12... | collective-permute-start | bytes 786440 | tf_op jit(solution)/shard_map/ppermute | solution.py:372
  33.3 5.4 %copy-start = (bf16[2048,512]{1,0:T(8,128)(2,1)}, bf16[2048,512]{1,0:T(8,128)(2,1)S(1)}, u32[]{:S(2)}) copy-start(bf16[2048,512]{1,0:T(8,128)(2,1)S(1)} %collective-permute-done.4.a_par.refs_1_) | copy-start | bytes 6291460
  33.3 16.4 %collective-permute-start.6 = (bf16[512,256]{1,0:T(8,128)(2,1)S(1)}, bf16[512,256]{1,0:T(8,128)(2,1)}, u32[]{:S(2)}, u32[]{:S(2)}) collective-permute-start(bf16[512,256]{1,0:T(8,128)(2,1)S(1)} %copy-done.2), channel_id=1, source_target_pairs={{0,1},{1,0},{2,3},{3,2},{4,5},{5,4},{6,7},{7,6},{8,9},{9,8},{10,11... | collective-permute-start | bytes 786440 | tf_op jit(solution)/shard_map/ppermute | solution.py:36
  36.2 30.9 %copy-start.4 = (f32[32,256]{1,0:T(8,128)S(1)}, f32[32,256]{1,0:T(8,128)}, u32[]{:S(2)}) copy-start(f32[32,256]{1,0:T(8,128)} %fields_ref.1) | copy-start | bytes 98308
  38.7 16.6 %all-to-all-start = ((f32[32,1,1024]{2,1,0:T(1,128)}), f32[32,1,1024]{2,1,0:T(1,128)S(1)}, u32[]{:S(2)}, u32[]{:S(2)}) async-start(f32[32,1,1024]{2,1,0:T(1,128)} %head.1), calls=%async_computation | async-start | bytes 262144 | tf_op jit(solution)/shard_map/all_to_all | solution.py:379
  49.3 13.3 %collective-permute-start.8 = (bf16[512,256]{1,0:T(8,128)(2,1)S(1)}, bf16[512,256]{1,0:T(8,128)(2,1)S(1)}, u32[]{:S(2)}, u32[]{:S(2)}) collective-permute-start(bf16[512,256]{1,0:T(8,128)(2,1)S(1)} %collective-permute-done.7.c2), channel_id=1, source_target_pairs={{0,1},{1,0},{2,3},{3,2},{4,5},{5,4},{6,7},{7,6},{8,9},{9,8},{10,11... | collective-permute-start | bytes 786440 | tf_op jit(solution)/shard_map/ppermute | solution.py:36
  49.7 34.2 %collective-permute-start.13 = (bf16[512,512]{1,0:T(8,128)(2,1)}, bf16[512,512]{1,0:T(8,128)(2,1)S(1)}, u32[]{:S(2)}, u32[]{:S(2)}) collective-permute-start(bf16[512,512]{1,0:T(8,128)(2,1)} %collective-permute-done.9.refs_2_), channel_id=1, source_target_pairs={{0,1},{1,0},{2,3},{3,2},{4,5},{5,4},{6,7},{7,6},{8,9},{9,8},{10,11... | collective-permute-start | bytes 1572872 | tf_op jit(solution)/shard_map/ppermute | solution.py:36
  49.9 34.0 %collective-permute-start.16 = (bf16[512,512]{1,0:T(8,128)(2,1)}, bf16[512,512]{1,0:T(8,128)(2,1)S(1)}, u32[]{:S(2)}, u32[]{:S(2)}) collective-permute-start(bf16[512,512]{1,0:T(8,128)(2,1)} %collective-permute-done.12.refs_5_), channel_id=1, source_target_pairs={{0,1},{1,0},{2,3},{3,2},{4,5},{5,4},{6,7},{7,6},{8,9},{9,8},{10,11... | collective-permute-start | bytes 1572872 | tf_op jit(solution)/shard_map/ppermute | solution.py:36
  53.2 30.7 %collective-permute-start.15 = (bf16[512,512]{1,0:T(8,128)(2,1)}, bf16[512,512]{1,0:T(8,128)(2,1)S(1)}, u32[]{:S(2)}, u32[]{:S(2)}) collective-permute-start(bf16[512,512]{1,0:T(8,128)(2,1)} %collective-permute-done.11.refs_4_), channel_id=1, source_target_pairs={{0,1},{1,0},{2,3},{3,2},{4,5},{5,4},{6,7},{7,6},{8,9},{9,8},{10,11... | collective-permute-start | bytes 1572872 | tf_op jit(solution)/shard_map/ppermute | solution.py:36
  53.2 30.7 %collective-permute-start.14 = (bf16[512,512]{1,0:T(8,128)(2,1)}, bf16[512,512]{1,0:T(8,128)(2,1)}, u32[]{:S(2)}, u32[]{:S(2)}) collective-permute-start(bf16[512,512]{1,0:T(8,128)(2,1)} %collective-permute-done.10.refs_3_), channel_id=1, source_target_pairs={{0,1},{1,0},{2,3},{3,2},{4,5},{5,4},{6,7},{7,6},{8,9},{9,8},{10,11... | collective-permute-start | bytes 1572872 | tf_op jit(solution)/shard_map/ppermute | solution.py:36
  57.4 9.8 %all-to-all-start.1 = ((f32[8,32,256]{2,1,0:T(8,128)}), f32[8,32,256]{2,1,0:T(8,128)S(1)}, u32[]{:S(2)}, u32[]{:S(2)}) async-start(f32[8,32,256]{2,1,0:T(8,128)} %broadcast_in_dim.2), calls=%async_computation.1 | async-start | bytes 524288 | tf_op jit(solution)/shard_map/all_to_all | solution.py:391
  69.0 0.7 copy-start.3
  69.6 15.9 %all-to-all-start.2 = ((bf16[32,4,512]{2,1,0:T(4,128)(2,1)}), bf16[32,4,512]{2,1,0:T(4,128)(2,1)S(1)}, u32[]{:S(2)}, u32[]{:S(2)}) async-start(bf16[32,4,512]{2,1,0:T(4,128)(2,1)} %copy-done.3), calls=%async_computation.2 | async-start | bytes 262144 | tf_op jit(solution)/shard_map/all_to_all | solution.py:402
  80.8 3.0 %collective-permute-start.3 = (bf16[104,1024]{1,0:T(8,128)(2,1)S(1)}, bf16[104,1024]{1,0:T(8,128)(2,1)S(1)}, u32[]{:S(2)}, u32[]{:S(2)}) collective-permute-start(bf16[104,1024]{1,0:T(8,128)(2,1)S(1)} %get-tuple-element.36), channel_id=1, source_target_pairs={{0,1},{1,0},{2,3},{3,2},{4,5},{5,4},{6,7},{7,6},{8,9},{9,8},{10,11... | collective-permute-start | bytes 638984 | tf_op jit(solution)/shard_map/ppermute | solution.py:36
  90.4 6.0 %collective-permute-start.18 = (bf16[104,1024]{1,0:T(8,128)(2,1)S(1)}, bf16[104,1024]{1,0:T(8,128)(2,1)S(1)}, u32[]{:S(2)}, u32[]{:S(2)}) collective-permute-start(bf16[104,1024]{1,0:T(8,128)(2,1)S(1)} %get-tuple-element.47.mine_ref), channel_id=1, source_target_pairs={{0,2},{2,0},{5,3},{3,5},{4,6},{6,4},{1,7},{7,1},{8,10},{10,8},{13,... | collective-permute-start | bytes 638984 | tf_op jit(solution)/shard_map/ppermute | solution.py:414
  93.7 6.0 %collective-permute-start.17 = (bf16[104,1024]{1,0:T(8,128)(2,1)S(1)}, bf16[104,1024]{1,0:T(8,128)(2,1)S(1)}, u32[]{:S(2)}, u32[]{:S(2)}) collective-permute-start(bf16[104,1024]{1,0:T(8,128)(2,1)S(1)} %term.9.refs_0_), channel_id=1, source_target_pairs={{0,2},{2,0},{5,3},{3,5},{4,6},{6,4},{1,7},{7,1},{8,10},{10,8},{13,... | collective-permute-start | bytes 638984 | tf_op jit(solution)/shard_map/ppermute | solution.py:416
  101.7 6.0 %collective-permute-start.20 = (bf16[104,1024]{1,0:T(8,128)(2,1)S(1)}, bf16[104,1024]{1,0:T(8,128)(2,1)S(1)}, u32[]{:S(2)}, u32[]{:S(2)}) collective-permute-start(bf16[104,1024]{1,0:T(8,128)(2,1)S(1)} %get-tuple-element.52.mine_ref), channel_id=1, source_target_pairs={{0,2},{2,0},{5,3},{3,5},{4,6},{6,4},{1,7},{7,1},{8,10},{10,8},{13,... | collective-permute-start | bytes 638984 | tf_op jit(solution)/shard_map/ppermute | solution.py:414
  104.1 6.0 %collective-permute-start.19 = (bf16[104,1024]{1,0:T(8,128)(2,1)S(1)}, bf16[104,1024]{1,0:T(8,128)(2,1)S(1)}, u32[]{:S(2)}, u32[]{:S(2)}) collective-permute-start(bf16[104,1024]{1,0:T(8,128)(2,1)S(1)} %term.12.refs_0_), channel_id=1, source_target_pairs={{0,2},{2,0},{5,3},{3,5},{4,6},{6,4},{1,7},{7,1},{8,10},{10,8},{13,... | collective-permute-start | bytes 638984 | tf_op jit(solution)/shard_map/ppermute | solution.py:416
  112.1 6.0 %collective-permute-start.22 = (bf16[104,1024]{1,0:T(8,128)(2,1)S(1)}, bf16[104,1024]{1,0:T(8,128)(2,1)S(1)}, u32[]{:S(2)}, u32[]{:S(2)}) collective-permute-start(bf16[104,1024]{1,0:T(8,128)(2,1)S(1)} %get-tuple-element.56.mine_ref), channel_id=1, source_target_pairs={{0,2},{2,0},{5,3},{3,5},{4,6},{6,4},{1,7},{7,1},{8,10},{10,8},{13,... | collective-permute-start | bytes 638984 | tf_op jit(solution)/shard_map/ppermute | solution.py:414
  115.4 6.2 %collective-permute-start.21 = (bf16[104,1024]{1,0:T(8,128)(2,1)S(1)}, bf16[104,1024]{1,0:T(8,128)(2,1)S(1)}, u32[]{:S(2)}, u32[]{:S(2)}) collective-permute-start(bf16[104,1024]{1,0:T(8,128)(2,1)S(1)} %term.15.mine_ref), channel_id=1, source_target_pairs={{0,2},{2,0},{5,3},{3,5},{4,6},{6,4},{1,7},{7,1},{8,10},{10,8},{13,... | collective-permute-start | bytes 638984 | tf_op jit(solution)/shard_map/ppermute | solution.py:416
